TPU v7x, 8 devices: a whole 2x2x1 slice. The times are simulated.
8 devices in a mesh: dp: 8 (over z, y, x, core).
Axes of the slice: x: 2, y: 2, z: 1, core: 2. Of those that a mesh axis runs over, the one named last changes fastest.
Arguments:
- query: bfloat16 [256, 24, 128], P('dp')
- k_cache: bfloat16 [256, 512, 8, 128], P('dp')
- v_cache: bfloat16 [256, 512, 8, 128], P('dp')
- cache_lens: int32 [256], P('dp')
- dest_slot: int32 [256], replicated
- k_new: bfloat16 [256, 8, 128], P('dp')
- v_new: bfloat16 [256, 8, 128], P('dp')
Outputs:
- output 1: bfloat16 [256, 24, 128], P('dp')
- output 2: bfloat16 [256, 512, 8, 128], P('dp')
- output 3: bfloat16 [256, 512, 8, 128], P('dp')
- output 4: int32 [256], P('dp')
All inputs are finite; a program needn't handle non-finite values.
Results may differ from a plain program's by a relative error of at most 0.001.
Values are sent between devices in bfloat16 or wider.
A program may use at most 1 GiB of HBM per device.

v0:
```python
import functools

import jax
import jax.numpy as jnp
from jax import lax
from jax.experimental import pallas as pl
from jax.experimental.pallas import tpu as pltpu
from jax.sharding import PartitionSpec as P


BP = 16
NB = 32
NX = 24
A = 4
SL = 32
BL = 32
IT = 136
S0, S1, R0, R1, XS, XR = range(6)
RDY, MLEN, SRC = 6 * 2 * IT, 6 * 2 * IT + 40, 6 * 2 * IT + 80
ROUNDS, CORE = 6 * 2 * IT + 120, 6 * 2 * IT + 121
TAB = 6 * 2 * IT + 128
U_PART, U_MERGE, U_OWN, U_POST, U_XS, U_XR = 0, 2, 4, 6, 8, 9
STEP, DONE, STATE = 24, 32, 64
END = 1 << 30
bf16 = jnp.bfloat16
f32 = jnp.float32
i32 = jnp.int32


def gray(c):
    return c ^ (c >> 1)


def lens_kernel(x, o, bsem, ssem, rsem):
    me = lax.axis_index('dp')
    barrier = pltpu.get_barrier_semaphore()
    for k in range(1, 8):
        pl.semaphore_signal(barrier, inc=1, device_id=(lax.rem(me + k, 8),), device_id_type=pl.DeviceIdType.MESH)
    pl.semaphore_wait(barrier, 7)
    here = pltpu.make_async_copy(x, o.at[me], bsem)
    here.start()
    sends = []
    for k in range(1, 8):
        c = pltpu.make_async_remote_copy(src_ref=x, dst_ref=o.at[me], send_sem=ssem.at[k], recv_sem=rsem.at[k],
                                         device_id=(lax.rem(me + k, 8),), device_id_type=pl.DeviceIdType.MESH)
        c.start()
        sends.append(c)
    here.wait()
    for c in sends:
        c.wait()


def plan_kernel(me_ref, dest_ref, len_ref, tab, lens_out, nbv, kindv, load, dload, xload):
    me = me_ref[0]
    core = me & 1
    mychip = me >> 1
    for i in range(9):
        load[i] = 0
        dload[i] = 0
        xload[i] = 0
    tab[CORE] = core

    def first(i, _):
        n = len_ref[i >> 5, 0, i & 31]
        d = dest_ref[i]
        nb = (n + (BP - 1)) >> 4
        ra = gray(i >> 6)
        delta = (gray(d >> 6) - ra) & 3
        nbv[i] = nb
        kindv[i] = delta
        slot = jnp.where(delta == 1, ra, jnp.where(delta == 3, 4 + ra, 8))
        load[slot] = load[slot] + nb
        cross = (delta == 0) & ((i >> 5) != (d >> 5))
        xslot = jnp.where(cross, i >> 5, 8)
        xload[xslot] = xload[xslot] + nb
        mine = jnp.where((d >> 5) == me, d & 31, 32)
        tab[MLEN + mine] = n
        tab[RDY + mine] = 0
        tab[SRC + mine] = jnp.where((i >> 5) == me, i & 31, -1)
        return 0

    lax.fori_loop(0, 8 * SL, first, 0)

    def lens(j, _):
        lens_out[j] = tab[MLEN + j] + 1
        return 0

    lax.fori_loop(0, SL, lens, 0)

    def choose(i, _):
        @pl.when(kindv[i] == 2)
        def _():
            nb = nbv[i]
            ra = gray(i >> 6)
            a1, a2, b1, b2 = ra, (ra + 1) & 3, 4 + ra, 4 + ((ra - 1) & 3)
            la, lb = jnp.maximum(load[a1], load[a2]), jnp.maximum(load[b1], load[b2])
            sa, sb = load[a1] + load[a2], load[b1] + load[b2]
            cw = (la < lb) | ((la == lb) & (sa <= sb))
            x1, x2 = jnp.where(cw, a1, b1), jnp.where(cw, a2, b2)
            load[x1] = load[x1] + nb
            load[x2] = load[x2] + nb
            dload[x1] = dload[x1] + nb
            kindv[i] = jnp.where(cw, 2, 4)

        return 0

    lax.fori_loop(0, 8 * SL, choose, 0)

    def own_and_total(d, x):
        up = (x - 1) & 3 if d == 0 else (x + 1) & 3
        fwd = dload[4 * d + up]
        own = load[4 * d + x] - fwd
        start = jnp.where(fwd > 0, jnp.maximum(own, 2 * NB), own)
        return start, start + fwd

    rounds = jnp.int32(0)
    for d in range(2):
        for x in range(4):
            _, total = own_and_total(d, jnp.int32(x))
            rounds = jnp.maximum(rounds, (total + NB - 1) // NB)
    for d in range(8):
        rounds = jnp.maximum(rounds, (xload[d] + NX - 1) // NX)
    tab[ROUNDS] = (rounds + 1) & -2

    def build(lid, d, x, recv):
        base = lid * 2 * IT
        up = (x - 1) & 3 if d == 0 else (x + 1) & 3
        first_kind, direct_kind = (2, 1) if d == 0 else (4, 3)

        def scan(ring, want, mode, c0):
            chip = gray(ring)

            def body(s, c):
                k, pos, fpos = c
                i = chip * 64 + s
                nb = nbv[i]
                hit = kindv[i] == want
                dst = dest_ref[i]
                if mode == 'src':
                    code = ((s >> 5) << 16) + (s & 31) * BL
                elif mode == 'fwd_in':
                    code = (2 << 16) + pos
                elif mode == 'fwd_out':
                    code = (2 << 16) + fpos
                else:
                    code = (((dst >> 5) & 1) << 16) + (dst & 31) * BL
                    mine = hit & ((dst >> 5) == me)
                    tab[RDY + jnp.where(mine, dst & 31, 33)] = (pos + nb - 1) // NB + 2
                tab[base + 2 * k] = nb
                tab[base + 2 * k + 1] = code
                inc = jnp.where(hit, nb, 0)
                return k + jnp.where(hit, 1, 0), pos + inc, fpos + inc

            return lax.fori_loop(0, 64, body, c0)

        k, pos, _ = scan(x, first_kind, 'fwd_in' if recv else 'src', (jnp.int32(0), jnp.int32(0), jnp.int32(0)))
        k, pos, _ = scan(x, direct_kind, 'dst' if recv else 'src', (k, pos, jnp.int32(0)))
        start, _ = own_and_total(d, x)
        tab[base + 2 * k] = start - pos
        tab[base + 2 * k + 1] = 3 << 16
        k = k + jnp.where(start > pos, 1, 0)
        k, pos, _ = scan(up, first_kind, 'dst' if recv else 'fwd_out', (k, start, jnp.int32(0)))
        tab[base + 2 * k] = END
        tab[base + 2 * k + 1] = 3 << 16

    x = gray(mychip)
    build(S0, 0, x, False)
    build(S1, 1, x, False)
    build(R0, 0, (x - 1) & 3, True)
    build(R1, 1, (x + 1) & 3, True)

    def cross_list(lid, sender, receiver, recv):
        base = lid * 2 * IT

        def body(s, c):
            k, pos = c
            i = sender * SL + s
            nb = nbv[i]
            dst = dest_ref[i]
            hit = (dst >> 5) == receiver
            tab[base + 2 * k] = nb
            if recv:
                tab[base + 2 * k + 1] = (dst & 31) * BL
                tab[RDY + jnp.where(hit, dst & 31, 33)] = (pos + nb - 1) // NX + 1
            else:
                tab[base + 2 * k + 1] = s * BL
            return k + jnp.where(hit, 1, 0), pos + jnp.where(hit, nb, 0)

        k, _ = lax.fori_loop(0, SL, body, (jnp.int32(0), jnp.int32(0)))
        tab[base + 2 * k] = END
        tab[base + 2 * k + 1] = 3 << 16

    cross_list(XS, me, me ^ 1, False)
    cross_list(XR, me ^ 1, me, True)


class Mover:
    def __init__(self, tab, st_in, st):
        self.tab, self.st = tab, st
        self.core = tab[CORE]

        def cp(i, _):
            st[i] = st_in[i]
            return 0

        lax.fori_loop(0, STATE, cp, 0)

    def walk(self, lid, use, n, fn):
        tab, st = self.tab, self.st
        base = lid * 2 * IT

        def body(c):
            p, item, off, cnt = c
            width = tab[base + 2 * item]
            code = tab[base + 2 * item + 1]
            take = jnp.minimum(n - p, width - off)
            cnt = cnt + fn(p, take, code >> 16, (code & 0xffff) + off)
            off = off + take
            adv = off >= width
            return p + take, jnp.where(adv, item + 1, item), jnp.where(adv, 0, off), cnt

        c0 = (jnp.int32(0), st[2 * use], st[2 * use + 1], jnp.int32(0))
        _, item, off, cnt = lax.while_loop(lambda c: c[0] < n, body, c0)
        st[2 * use] = item
        st[2 * use + 1] = off
        return cnt

    @staticmethod
    def drain(cnt, ref, sem):
        @pl.when(cnt > 0)
        def _():
            part = ref.at[pl.ds(0, cnt)]
            pltpu.make_async_copy(part, part, sem).wait()

    def partial(self, d, kc, vc, buf, sem):
        core = self.core

        def fn(p, take, kind, idx):
            mine = kind == core

            @pl.when(mine & (core == 0))
            def _():
                pltpu.make_async_copy(vc.at[pl.ds(idx, take)], buf.at[d, pl.ds(p, take)], sem).start()

            @pl.when(mine & (core == 1))
            def _():
                pltpu.make_async_copy(kc.at[pl.ds(idx, take)], buf.at[d, pl.ds(p, take)], sem).start()

            return jnp.where(mine, take, 0)

        return self.walk(S0 + d, U_PART + d, NB, fn)

    def merge(self, d, kc, vc, pre, fwd, buf, sem):
        core = self.core

        def fn(p, take, kind, idx):
            mine = kind == core

            @pl.when(mine & (core == 0))
            def _():
                pltpu.make_async_copy(kc.at[pl.ds(idx, take)], buf.at[d, pl.ds(p, take)], sem).start()

            @pl.when(mine & (core == 1))
            def _():
                pltpu.make_async_copy(vc.at[pl.ds(idx, take)], buf.at[d, pl.ds(p, take)], sem).start()

            @pl.when(kind == 1 - core)
            def _():
                pltpu.make_async_copy(pre.at[d, pl.ds(p, take)], buf.at[d, pl.ds(p, take)], sem).start()

            if fwd is not None:
                @pl.when(kind == 2)
                def _():
                    pltpu.make_async_copy(fwd.at[pl.ds(idx, take)], buf.at[d, pl.ds(p, take)], sem).start()
            return jnp.where(kind < 3, take, 0)

        return self.walk(S0 + d, U_MERGE + d, NB, fn)

    def cross_send(self, kc, vc, buf, sem):
        def fn(p, take, kind, idx):
            @pl.when(kind == 0)
            def _():
                pltpu.make_async_copy(kc.at[pl.ds(idx, take)], buf.at[0, pl.ds(p, take)], sem).start()
                pltpu.make_async_copy(vc.at[pl.ds(idx, take)], buf.at[1, pl.ds(p, take)], sem).start()

            return jnp.where(kind == 0, 2 * take, 0)

        return self.walk(XS, U_XS, NX, fn)

    def cross_recv(self, n, ko, vo, buf, sem):
        def fn(p, take, kind, idx):
            @pl.when(kind == 0)
            def _():
                pltpu.make_async_copy(buf.at[0, pl.ds(p, take)], ko.at[pl.ds(idx, take)], sem).start()
                pltpu.make_async_copy(buf.at[1, pl.ds(p, take)], vo.at[pl.ds(idx, take)], sem).start()

            return jnp.where(kind == 0, 2 * take, 0)

        return self.walk(XR, U_XR, n, fn)

    def unpack(self, d, use, n, flip, ko, vo, fwd, buf, sem):
        core = self.core
        plane = 1 - core if flip else core

        def fn(p, take, kind, idx):
            mine = kind == core

            @pl.when(mine & (plane == 0))
            def _():
                pltpu.make_async_copy(buf.at[d, pl.ds(p, take)], ko.at[pl.ds(idx, take)], sem).start()

            @pl.when(mine & (plane == 1))
            def _():
                pltpu.make_async_copy(buf.at[d, pl.ds(p, take)], vo.at[pl.ds(idx, take)], sem).start()

            cnt = jnp.where(mine, take, 0)
            if fwd is not None:
                @pl.when(kind == 2)
                def _():
                    pltpu.make_async_copy(buf.at[d, pl.ds(p, take)], fwd.at[pl.ds(idx, take)], sem).start()

                cnt = cnt + jnp.where(kind == 2, take, 0)
            return cnt

        return self.walk(R0 + d, use + d, n, fn)


def open_kernel(tab, st_in, kc, vc, st, part0, part1, dxs, vpart, vdx, sem):
    mv = Mover(tab, st_in, st)
    outs = [pltpu.make_async_copy(vpart.at[0], part0, sem.at[0]),
            pltpu.make_async_copy(vpart.at[1], part1, sem.at[1]),
            pltpu.make_async_copy(vdx, dxs, sem.at[2])]
    cnt = [mv.partial(0, kc, vc, vpart.at[c], sem.at[c]) + mv.partial(1, kc, vc, vpart.at[c], sem.at[c]) for c in range(2)]
    cnt.append(mv.cross_send(kc, vc, vdx, sem.at[2]))
    for c in range(3):
        mv.drain(cnt[c], kc, sem.at[c])
        outs[c].start()
    for c in outs:
        c.wait()


def open_merge_kernel(tab, st_in, kc, vc, pre, st, send0, send1, part, vsend, vpart, sem):
    mv = Mover(tab, st_in, st)
    c0 = mv.merge(0, kc, vc, pre, None, vsend, sem.at[0])
    c1 = mv.merge(1, kc, vc, pre, None, vsend, sem.at[1])
    c2 = mv.partial(0, kc, vc, vpart, sem.at[2]) + mv.partial(1, kc, vc, vpart, sem.at[2])
    mv.drain(c0, kc, sem.at[0])
    mv.drain(c1, kc, sem.at[1])
    mv.drain(c2, kc, sem.at[2])
    outs = [pltpu.make_async_copy(vsend.at[0], send0, sem.at[0]),
            pltpu.make_async_copy(vsend.at[1], send1, sem.at[1]),
            pltpu.make_async_copy(vpart, part, sem.at[2])]
    for c in outs:
        c.start()
    for c in outs:
        c.wait()


def round_kernel(tab, st_in, kc, vc, pre, rc0, rc1, po0, po1, dxr, f0i, f1i, koi, voi,
                 st, send0, send1, part, dxs, f0, f1, ko, vo,
                 vsend, vpart, vrecv, vpost, vdxs, vdxr, sem):
    mv = Mover(tab, st_in, st)
    r = st_in[STEP]
    st[STEP] = r + 1
    ins = [pltpu.make_async_copy(rc0, vrecv.at[0], sem.at[0]),
           pltpu.make_async_copy(rc1, vrecv.at[1], sem.at[1]),
           pltpu.make_async_copy(po0, vpost.at[0], sem.at[2]),
           pltpu.make_async_copy(po1, vpost.at[1], sem.at[3]),
           pltpu.make_async_copy(dxr, vdxr, sem.at[4])]
    for c in ins:
        c.start()
    n1 = jnp.where(r >= 1, NB, 0)
    n2 = jnp.where(r >= 2, NB, 0)
    nx = jnp.where(r >= 1, NX, 0)
    cp = mv.partial(0, kc, vc, vpart, sem.at[5]) + mv.partial(1, kc, vc, vpart, sem.at[5])
    cx = mv.cross_send(kc, vc, vdxs, sem.at[6])
    ins[0].wait()
    o0 = mv.unpack(0, U_OWN, n1, False, ko, vo, f0, vrecv, sem.at[7])
    ins[1].wait()
    o1 = mv.unpack(1, U_OWN, n1, False, ko, vo, f1, vrecv, sem.at[7])
    mv.drain(o0 + o1, kc, sem.at[7])
    c0 = mv.merge(0, kc, vc, pre, f0, vsend, sem.at[8])
    c1 = mv.merge(1, kc, vc, pre, f1, vsend, sem.at[9])
    ins[2].wait()
    ins[3].wait()
    o2 = mv.unpack(0, U_POST, n2, True, ko, vo, None, vpost, sem.at[7])
    o3 = mv.unpack(1, U_POST, n2, True, ko, vo, None, vpost, sem.at[7])
    ins[4].wait()
    o4 = mv.cross_recv(nx, ko, vo, vdxr, sem.at[7])
    mv.drain(cp, kc, sem.at[5])
    mv.drain(cx, kc, sem.at[6])
    mv.drain(c0, kc, sem.at[8])
    mv.drain(c1, kc, sem.at[9])
    outs = [pltpu.make_async_copy(vsend.at[0], send0, sem.at[0]),
            pltpu.make_async_copy(vsend.at[1], send1, sem.at[1]),
            pltpu.make_async_copy(vpart, part, sem.at[2]),
            pltpu.make_async_copy(vdxs, dxs, sem.at[3])]
    for c in outs:
        c.start()
    mv.drain(o2 + o3 + o4, kc, sem.at[7])
    for c in outs:
        c.wait()


def close_kernel(last, tab, st_in, *refs):
    if last:
        (po0, po1, koi, voi, st, ko, vo, vpost, sem) = refs
    else:
        (rc0, rc1, po0, po1, dxr, koi, voi, st, ko, vo, vpost, vrecv, vdxr, sem) = refs
    mv = Mover(tab, st_in, st)
    r = st_in[STEP]
    st[STEP] = r + 1
    ins = [pltpu.make_async_copy(po0, vpost.at[0], sem.at[0]),
           pltpu.make_async_copy(po1, vpost.at[1], sem.at[1])]
    if not last:
        ins += [pltpu.make_async_copy(rc0, vrecv.at[0], sem.at[2]),
                pltpu.make_async_copy(rc1, vrecv.at[1], sem.at[3]),
                pltpu.make_async_copy(dxr, vdxr, sem.at[4])]
    for c in ins:
        c.start()
    n1 = jnp.where(r >= 1, NB, 0)
    n2 = jnp.where(r >= 2, NB, 0)
    nx = jnp.where(r >= 1, NX, 0)
    for c in ins:
        c.wait()
    cnt = mv.unpack(0, U_POST, n2, True, ko, vo, None, vpost, sem.at[5])
    cnt += mv.unpack(1, U_POST, n2, True, ko, vo, None, vpost, sem.at[5])
    if not last:
        cnt += mv.unpack(0, U_OWN, n1, False, ko, vo, None, vrecv, sem.at[5])
        cnt += mv.unpack(1, U_OWN, n1, False, ko, vo, None, vrecv, sem.at[5])
        cnt += mv.cross_recv(nx, ko, vo, vdxr, sem.at[5])
    mv.drain(cnt, ko, sem.at[5])


def attn_kernel(batches, tab, st_in, q, kn, vn, kc, vc, koi, voi, aoi, st, ko, vo, ao,
                kb, vb, ob, sel, lsem, wsem, osem):
    def cp(i, _):
        st[i] = st_in[i]
        return 0

    lax.fori_loop(0, STATE, cp, 0)
    r = st_in[STEP]

    def load(a, j):
        s = tab[SRC + j]

        @pl.when(s >= 0)
        def _():
            pltpu.make_async_copy(kc.at[pl.ds(s * BL, BL)], kb.at[a], lsem.at[a]).start()
            pltpu.make_async_copy(vc.at[pl.ds(s * BL, BL)], vb.at[a], lsem.at[a]).start()

        @pl.when(s < 0)
        def _():
            pltpu.make_async_copy(ko.at[pl.ds(j * BL, BL)], kb.at[a], lsem.at[a]).start()
            pltpu.make_async_copy(vo.at[pl.ds(j * BL, BL)], vb.at[a], lsem.at[a]).start()

    def compute(a, j):
        pltpu.make_async_copy(kb.at[a], kb.at[a], lsem.at[a]).wait()
        pltpu.make_async_copy(vb.at[a], vb.at[a], lsem.at[a]).wait()
        m = tab[MLEN + j]
        s = tab[SRC + j]
        b0 = m >> 4
        row = lax.broadcasted_iota(i32, (128, 128), 0) >> 3
        for buf, new in ((kb, kn), (vb, vn)):
            x = buf[a, b0].astype(f32)
            fresh = jnp.concatenate([new[j].astype(f32)] * BP, axis=0)
            t = b0 * BP + row
            buf[a, b0] = jnp.where(t < m, x, jnp.where(t == m, fresh, 0.0)).astype(bf16)

        def wipe(b, _):
            kb[a, b] = jnp.zeros((128, 128), bf16)
            vb[a, b] = jnp.zeros((128, 128), bf16)
            return 0

        lax.fori_loop(b0 + 1, BL, wipe, 0)
        kf = kb[a].reshape(BL * 128, 128)
        vf = vb[a].reshape(BL * 128, 128)
        sc = lax.dot_general(q[j], kf, (((1,), (1,)), ((), ())), preferred_element_type=f32) * (128 ** -0.5)
        col = lax.broadcasted_iota(i32, sc.shape, 1)
        head = lax.broadcasted_iota(i32, sc.shape, 0) // 3
        ok = ((col & 7) == head) & ((col >> 3) <= m)
        sc = jnp.where(ok, sc, -1e30)
        top = jnp.max(sc, axis=1, keepdims=True)
        w = jnp.exp(sc - top)
        tot = jnp.sum(w, axis=1, keepdims=True)
        acc = lax.dot_general(w.astype(bf16), vf, (((1,), (0,)), ((), ())), preferred_element_type=f32)
        ob[a] = (acc / tot).astype(bf16)
        bw = jnp.where(s >= 0, 0, b0)

        tail = pl.ds(bw, BL - bw)
        home = pl.ds(j * BL + bw, BL - bw)
        pltpu.make_async_copy(kb.at[a, tail], ko.at[home], wsem.at[0]).start()
        pltpu.make_async_copy(vb.at[a, tail], vo.at[home], wsem.at[0]).start()
        pltpu.make_async_copy(ob.at[a], ao.at[j], osem.at[0]).start()
        return 2 * (BL - bw)

    def batch(_, c):
        def pick(j, n):
            hit = (st[DONE + j] == 0) & (tab[RDY + j] < r) & (n < A)
            sel[jnp.where(hit, n, A)] = j
            st[DONE + j] = jnp.where(hit, 1, st[DONE + j])
            return n + jnp.where(hit, 1, 0)

        n = lax.fori_loop(0, SL, pick, jnp.int32(0))

        def loads(a, _):
            load(a, sel[a])
            return 0

        lax.fori_loop(0, n, loads, 0)

        def computes(a, cnt):
            return cnt + compute(a, sel[a])

        cnt = lax.fori_loop(0, n, computes, jnp.int32(0))

        @pl.when(n > 0)
        def _():
            done = ko.at[pl.ds(0, cnt)]
            pltpu.make_async_copy(done, done, wsem.at[0]).wait()
            rows = ob.at[pl.ds(0, n)]
            pltpu.make_async_copy(rows, rows, osem.at[0]).wait()

        return c

    lax.fori_loop(0, batches, batch, 0)


SMEM = pl.BlockSpec(memory_space=pltpu.SMEM)
VMEM = pl.BlockSpec(memory_space=pltpu.VMEM)
ANY = pl.BlockSpec(memory_space=pl.ANY)
BLOCK = (128, 128)


def sds(shape, dtype=bf16):
    return jax.ShapeDtypeStruct(shape, dtype)


def dma(n):
    return pltpu.SemaphoreType.DMA((n,))


def buf(*lead):
    return pltpu.VMEM(lead + BLOCK, bf16)


def cost(us):
    return pl.CostEstimate(flops=int(us * 4e6), bytes_accessed=int(us * 2e6), transcendentals=0)


ST = sds((STATE,), i32)


def solution(mesh):
    group = mesh.shape['dp']
    ring = [0, 1, 3, 2]
    cw = [(ring[k] * 2 + c, ring[(k + 1) % 4] * 2 + c) for k in range(4) for c in range(2)]
    ccw = [(b, a) for a, b in cw]
    swap = [(d, d ^ 1) for d in range(group)]

    def local(query, k_cache, v_cache, cache_lens, dest_slot, k_new, v_new):
        kc = k_cache.reshape((SL * BL,) + BLOCK)
        vc = v_cache.reshape((SL * BL,) + BLOCK)
        lens_all = pl.pallas_call(
            lens_kernel, out_shape=sds((8, 1, 128), i32), in_specs=[VMEM], out_specs=VMEM,
            scratch_shapes=[pltpu.SemaphoreType.DMA, dma(8), dma(8)],
            compiler_params=pltpu.CompilerParams(collective_id=0, has_side_effects=True),
            name='lens')(jnp.pad(cache_lens, (0, 96)).reshape(1, 128))
        me = jnp.full((1,), lax.axis_index('dp'), i32)
        tab, lens_out = pl.pallas_call(
            plan_kernel, out_shape=(sds((TAB,), i32), sds((SL,), i32)), in_specs=[SMEM] * 3, out_specs=(SMEM, SMEM),
            scratch_shapes=[pltpu.SMEM((256,), i32), pltpu.SMEM((256,), i32)] + [pltpu.SMEM((16,), i32)] * 3,
            name='plan')(me, dest_slot, lens_all)

        def nothing(*refs):
            pass

        chunk, both, cross = sds((NB,) + BLOCK), sds((2, NB) + BLOCK), sds((2, NX) + BLOCK)
        cache, store = sds((SL * BL,) + BLOCK), sds((2 * SL * BL,) + BLOCK)
        ko, vo, ao, f0, f1, rc0, rc1, po0, po1, dxr = pl.pallas_call(
            nothing, out_shape=(cache, cache, sds((SL, 24, 128)), store, store, chunk, chunk, chunk, chunk, cross),
            out_specs=(ANY,) * 10, name='blank')()

        st = jnp.zeros((STATE,), i32)
        st, part0, part1, dxs = pl.pallas_call(
            open_kernel, out_shape=(ST, both, both, cross), in_specs=[SMEM, SMEM, ANY, ANY], out_specs=(SMEM, ANY, ANY, ANY),
            scratch_shapes=[buf(2, 2, NB), buf(2, NX), dma(3)], name='open')(tab, st, kc, vc)
        pre0 = lax.ppermute(part0, 'dp', swap)
        pre = lax.ppermute(part1, 'dp', swap)
        st, s0, s1, part = pl.pallas_call(
            open_merge_kernel, out_shape=(ST, chunk, chunk, both), in_specs=[SMEM, SMEM, ANY, ANY, ANY],
            out_specs=(SMEM, ANY, ANY, ANY), scratch_shapes=[buf(2, NB), buf(2, NB), dma(3)],
            name='open_merge')(tab, st, kc, vc, pre0)

        def attend(st, ko, vo, ao, batches):
            return pl.pallas_call(
                functools.partial(attn_kernel, batches),
                out_shape=(ST, cache, cache, sds((SL, 24, 128))),
                in_specs=[SMEM, SMEM, VMEM, VMEM, VMEM, ANY, ANY, ANY, ANY, ANY], out_specs=(SMEM, ANY, ANY, ANY),
                input_output_aliases={7: 1, 8: 2, 9: 3},
                scratch_shapes=[buf(A, BL), buf(A, BL), pltpu.VMEM((A, 24, 128), bf16), pltpu.SMEM((A + 1,), i32),
                                dma(A), dma(1), dma(1)],
                cost_estimate=cost(6), name='attend')(tab, st, query, k_new, v_new, kc, vc, ko, vo, ao)

        def one_round(tag, c):
            st, s0, s1, part, dxs, pre, rc0, rc1, po0, po1, dxr, f0, f1, ko, vo, ao = c
            nrc0 = lax.ppermute(s0, 'dp', cw)
            nrc1 = lax.ppermute(s1, 'dp', ccw)
            npre = lax.ppermute(part, 'dp', swap)
            npo0 = lax.ppermute(rc0, 'dp', swap)
            npo1 = lax.ppermute(rc1, 'dp', swap)
            ndxr = lax.ppermute(dxs, 'dp', swap)
            st, s0, s1, part, dxs, f0, f1, ko, vo = pl.pallas_call(
                round_kernel, out_shape=(ST, chunk, chunk, both, cross, store, store, cache, cache),
                in_specs=[SMEM, SMEM] + [ANY] * 12, out_specs=(SMEM,) + (ANY,) * 8,
                input_output_aliases={10: 5, 11: 6, 12: 7, 13: 8},
                scratch_shapes=[buf(2, NB)] * 4 + [buf(2, NX)] * 2 + [dma(10)],
                cost_estimate=cost(10), name='round')(tab, st, kc, vc, pre, rc0, rc1, po0, po1, dxr, f0, f1, ko, vo)
            st, ko, vo, ao = attend(st, ko, vo, ao, 1)
            if tag == 'ra':
                s0, s1, npo0, npo1 = lax.optimization_barrier((s0, s1, npo0, npo1))
            return st, s0, s1, part, dxs, npre, nrc0, nrc1, npo0, npo1, ndxr, f0, f1, ko, vo, ao

        rounds = tab[ROUNDS]

        def body(c):
            return (c[0] + 2,) + one_round('rb', one_round('ra', c[1:]))

        c = lax.while_loop(lambda c: c[0] < rounds, body,
                       (jnp.int32(0), st, s0, s1, part, dxs, pre, rc0, rc1, po0, po1, dxr, f0, f1, ko, vo, ao))
        _, st, _, _, _, _, _, rc0, rc1, po0, po1, dxr, _, _, ko, vo, ao = c

        def close(last, st, ko, vo, *ins):
            n = len(ins)
            extra = [] if last else [buf(2, NB), buf(2, NX)]
            return pl.pallas_call(
                functools.partial(close_kernel, last), out_shape=(ST, cache, cache),
                in_specs=[SMEM, SMEM] + [ANY] * (n + 2), out_specs=(SMEM, ANY, ANY),
                input_output_aliases={n + 2: 1, n + 3: 2},
                scratch_shapes=[buf(2, NB)] + extra + [dma(6)],
                name='close_last' if last else 'close')(tab, st, *ins, ko, vo)

        lpo0 = lax.ppermute(rc0, 'dp', swap)
        lpo1 = lax.ppermute(rc1, 'dp', swap)
        st, ko, vo = close(False, st, ko, vo, rc0, rc1, po0, po1, dxr)
        st, ko, vo = close(True, st, ko, vo, lpo0, lpo1)
        st, ko, vo, ao = attend(st, ko, vo, ao, SL // A)
        return ao, ko.reshape(k_cache.shape), vo.reshape(v_cache.shape), lens_out

    row_spec = P('dp')
    return jax.shard_map(local, mesh=mesh, in_specs=(row_spec, row_spec, row_spec, row_spec, P(), row_spec, row_spec),
                         out_specs=(row_spec, row_spec, row_spec, row_spec), check_vma=False)
```

profile of v0, /device:TPU:0, one launch (start us, length us, event | category | flops | bytes accessed | tf_op | source)
XLA Modules:
  0.0 840.9 jit_solution(2097760805949831852)
XLA Ops:
  1.8 7.8 lens.1.len_ref
  9.6 23.4 %plan.1 = (s32[1760]{0:T(1024)S(1)}, s32[32]{0:T(128)}) custom-call(s32[1]{0:T(128)} %bitcast.me_ref, s32[256]{0:T(256)} %dest_ref.1, s32[8,1,128]{2,1,0:T(1,128)} %lens.1.len_ref), custom_call_target="tpu_custom_call" | custom-call | tf_op jit(solution)/shard_map/plan/pallas_call | solution.py:570
  33.5 5.8 open.1
  45.1 6.0 open_merge.1
  51.1 774.6 %while.40 = (s32[]{:T(128)}, s32[64]{0:T(128)S(1)}, bf16[32,128,128]{2,1,0:T(8,128)(2,1)}, bf16[32,128,128]{2,1,0:T(8,128)(2,1)}, bf16[2,32,128,128]{3,2,1,0:T(8...) while((s32[]{:T(128)}, s32[64]{0:T(128)S(1)}, ...), condition=%wide.region_1.2_spmd, body=%wide.region_0.1_spmd.sunk | while | flops 128000000 | bytes 145789712 | solution.py:629
  54.2 22.7 %collective-permute-done.2.rc1 = bf16[32,128,128]{2,1,0:T(8,128)(2,1)} collective-permute-done((bf16[32,128,128]{2,1,0:T(8,128)(2,1)}, bf16[32,128,128]{2,1,0:T(8,128)(2,1)}, u32[]{:S(2)}, u32[]{:S(2)}) %collective-permute-start.2) | collective-permute-done | bytes 1048608 | tf_op jit(solution)/shard_map/while/body/ppermute | solution.py:608
  78.4 8.0 round.2
  90.7 6.4 attend.4
  101.0 10.0 %round.3 = (s32[64]{0:T(128)}, bf16[32,128,128]{2,1,0:T(8,128)(2,1)}, bf16[32,128,128]{2,1,0:T(8,128)(2,1)}, bf16[2,32,128,128]{3,2,1,0:T(8,128)(2,1)}, bf16[2,2...) custom-call(s32[1760]{0:T(1024)S(1)} %get-tuple-element.554.tab, ...), custom_call_target="tpu_custom_call", output_to_operand_aliasing={{5}: (10, {}), {6}: (11, {}), {7}: (12, {}), {8}: (13, {})} | custom-call | flops 40000000 | bytes 20000000 | tf_op jit(solution)/shard_map/while/body/round/pallas_call | solution.py:613
  115.8 4.4 collective-permute-start.2
  121.7 23.3 %collective-permute-done.2.rc1 = bf16[32,128,128]{2,1,0:T(8,128)(2,1)} collective-permute-done((bf16[32,128,128]{2,1,0:T(8,128)(2,1)}, bf16[32,128,128]{2,1,0:T(8,128)(2,1)}, u32[]{:S(2)}, u32[]{:S(2)}) %collective-permute-start.2) | collective-permute-done | bytes 1048608 | tf_op jit(solution)/shard_map/while/body/ppermute | solution.py:608
  146.7 9.6 %round.2 = (s32[64]{0:T(128)}, bf16[32,128,128]{2,1,0:T(8,128)(2,1)}, bf16[32,128,128]{2,1,0:T(8,128)(2,1)}, bf16[2,32,128,128]{3,2,1,0:T(8,128)(2,1)}, bf16[2,2...) custom-call(s32[1760]{0:T(1024)S(1)} %get-tuple-element.554.tab, ...), custom_call_target="tpu_custom_call", output_to_operand_aliasing={{5}: (10, {}), {6}: (11, {}), {7}: (12, {}), {8}: (13, {})} | custom-call | flops 40000000 | bytes 20000000 | tf_op jit(solution)/shard_map/while/body/round/pallas_call | solution.py:613
  160.3 5.0 attend.4
  169.2 10.1 %round.3 = (s32[64]{0:T(128)}, bf16[32,128,128]{2,1,0:T(8,128)(2,1)}, bf16[32,128,128]{2,1,0:T(8,128)(2,1)}, bf16[2,32,128,128]{3,2,1,0:T(8,128)(2,1)}, bf16[2,2...) custom-call(s32[1760]{0:T(1024)S(1)} %get-tuple-element.554.tab, ...), custom_call_target="tpu_custom_call", output_to_operand_aliasing={{5}: (10, {}), {6}: (11, {}), {7}: (12, {}), {8}: (13, {})} | custom-call | flops 40000000 | bytes 20000000 | tf_op jit(solution)/shard_map/while/body/round/pallas_call | solution.py:613
  179.3 5.1 attend.5
  187.9 22.1 %collective-permute-done.2.rc1 = bf16[32,128,128]{2,1,0:T(8,128)(2,1)} collective-permute-done((bf16[32,128,128]{2,1,0:T(8,128)(2,1)}, bf16[32,128,128]{2,1,0:T(8,128)(2,1)}, u32[]{:S(2)}, u32[]{:S(2)}) %collective-permute-start.2) | collective-permute-done | bytes 1048608 | tf_op jit(solution)/shard_map/while/body/ppermute | solution.py:608
  212.9 9.6 %round.2 = (s32[64]{0:T(128)}, bf16[32,128,128]{2,1,0:T(8,128)(2,1)}, bf16[32,128,128]{2,1,0:T(8,128)(2,1)}, bf16[2,32,128,128]{3,2,1,0:T(8,128)(2,1)}, bf16[2,2...) custom-call(s32[1760]{0:T(1024)S(1)} %get-tuple-element.554.tab, ...), custom_call_target="tpu_custom_call", output_to_operand_aliasing={{5}: (10, {}), {6}: (11, {}), {7}: (12, {}), {8}: (13, {})} | custom-call | flops 40000000 | bytes 20000000 | tf_op jit(solution)/shard_map/while/body/round/pallas_call | solution.py:613
  225.4 5.0 attend.4
  234.3 10.0 %round.3 = (s32[64]{0:T(128)}, bf16[32,128,128]{2,1,0:T(8,128)(2,1)}, bf16[32,128,128]{2,1,0:T(8,128)(2,1)}, bf16[2,32,128,128]{3,2,1,0:T(8,128)(2,1)}, bf16[2,2...) custom-call(s32[1760]{0:T(1024)S(1)} %get-tuple-element.554.tab, ...), custom_call_target="tpu_custom_call", output_to_operand_aliasing={{5}: (10, {}), {6}: (11, {}), {7}: (12, {}), {8}: (13, {})} | custom-call | flops 40000000 | bytes 20000000 | tf_op jit(solution)/shard_map/while/body/round/pallas_call | solution.py:613
  244.3 5.4 attend.5
  254.1 22.1 %collective-permute-done.2.rc1 = bf16[32,128,128]{2,1,0:T(8,128)(2,1)} collective-permute-done((bf16[32,128,128]{2,1,0:T(8,128)(2,1)}, bf16[32,128,128]{2,1,0:T(8,128)(2,1)}, u32[]{:S(2)}, u32[]{:S(2)}) %collective-permute-start.2) | collective-permute-done | bytes 1048608 | tf_op jit(solution)/shard_map/while/body/ppermute | solution.py:608
  278.0 9.4 %round.2 = (s32[64]{0:T(128)}, bf16[32,128,128]{2,1,0:T(8,128)(2,1)}, bf16[32,128,128]{2,1,0:T(8,128)(2,1)}, bf16[2,32,128,128]{3,2,1,0:T(8,128)(2,1)}, bf16[2,2...) custom-call(s32[1760]{0:T(1024)S(1)} %get-tuple-element.554.tab, ...), custom_call_target="tpu_custom_call", output_to_operand_aliasing={{5}: (10, {}), {6}: (11, {}), {7}: (12, {}), {8}: (13, {})} | custom-call | flops 40000000 | bytes 20000000 | tf_op jit(solution)/shard_map/while/body/round/pallas_call | solution.py:613
  290.3 5.4 attend.4
  299.5 8.8 %round.3 = (s32[64]{0:T(128)}, bf16[32,128,128]{2,1,0:T(8,128)(2,1)}, bf16[32,128,128]{2,1,0:T(8,128)(2,1)}, bf16[2,32,128,128]{3,2,1,0:T(8,128)(2,1)}, bf16[2,2...) custom-call(s32[1760]{0:T(1024)S(1)} %get-tuple-element.554.tab, ...), custom_call_target="tpu_custom_call", output_to_operand_aliasing={{5}: (10, {}), {6}: (11, {}), {7}: (12, {}), {8}: (13, {})} | custom-call | flops 40000000 | bytes 20000000 | tf_op jit(solution)/shard_map/while/body/round/pallas_call | solution.py:613
  308.4 5.2 attend.5
  319.0 22.1 %collective-permute-done.2.rc1 = bf16[32,128,128]{2,1,0:T(8,128)(2,1)} collective-permute-done((bf16[32,128,128]{2,1,0:T(8,128)(2,1)}, bf16[32,128,128]{2,1,0:T(8,128)(2,1)}, u32[]{:S(2)}, u32[]{:S(2)}) %collective-permute-start.2) | collective-permute-done | bytes 1048608 | tf_op jit(solution)/shard_map/while/body/ppermute | solution.py:608
  341.6 8.8 %round.2 = (s32[64]{0:T(128)}, bf16[32,128,128]{2,1,0:T(8,128)(2,1)}, bf16[32,128,128]{2,1,0:T(8,128)(2,1)}, bf16[2,32,128,128]{3,2,1,0:T(8,128)(2,1)}, bf16[2,2...) custom-call(s32[1760]{0:T(1024)S(1)} %get-tuple-element.554.tab, ...), custom_call_target="tpu_custom_call", output_to_operand_aliasing={{5}: (10, {}), {6}: (11, {}), {7}: (12, {}), {8}: (13, {})} | custom-call | flops 40000000 | bytes 20000000 | tf_op jit(solution)/shard_map/while/body/round/pallas_call | solution.py:613
  353.7 5.0 attend.4
  362.5 8.5 %round.3 = (s32[64]{0:T(128)}, bf16[32,128,128]{2,1,0:T(8,128)(2,1)}, bf16[32,128,128]{2,1,0:T(8,128)(2,1)}, bf16[2,32,128,128]{3,2,1,0:T(8,128)(2,1)}, bf16[2,2...) custom-call(s32[1760]{0:T(1024)S(1)} %get-tuple-element.554.tab, ...), custom_call_target="tpu_custom_call", output_to_operand_aliasing={{5}: (10, {}), {6}: (11, {}), {7}: (12, {}), {8}: (13, {})} | custom-call | flops 40000000 | bytes 20000000 | tf_op jit(solution)/shard_map/while/body/round/pallas_call | solution.py:613
  371.1 7.3 attend.5
  382.0 22.1 %collective-permute-done.2.rc1 = bf16[32,128,128]{2,1,0:T(8,128)(2,1)} collective-permute-done((bf16[32,128,128]{2,1,0:T(8,128)(2,1)}, bf16[32,128,128]{2,1,0:T(8,128)(2,1)}, u32[]{:S(2)}, u32[]{:S(2)}) %collective-permute-start.2) | collective-permute-done | bytes 1048608 | tf_op jit(solution)/shard_map/while/body/ppermute | solution.py:608
  404.6 8.1 round.2
  417.7 5.3 attend.4
  426.8 8.6 %round.3 = (s32[64]{0:T(128)}, bf16[32,128,128]{2,1,0:T(8,128)(2,1)}, bf16[32,128,128]{2,1,0:T(8,128)(2,1)}, bf16[2,32,128,128]{3,2,1,0:T(8,128)(2,1)}, bf16[2,2...) custom-call(s32[1760]{0:T(1024)S(1)} %get-tuple-element.554.tab, ...), custom_call_target="tpu_custom_call", output_to_operand_aliasing={{5}: (10, {}), {6}: (11, {}), {7}: (12, {}), {8}: (13, {})} | custom-call | flops 40000000 | bytes 20000000 | tf_op jit(solution)/shard_map/while/body/round/pallas_call | solution.py:613
  445.5 23.4 %collective-permute-done.2.rc1 = bf16[32,128,128]{2,1,0:T(8,128)(2,1)} collective-permute-done((bf16[32,128,128]{2,1,0:T(8,128)(2,1)}, bf16[32,128,128]{2,1,0:T(8,128)(2,1)}, u32[]{:S(2)}, u32[]{:S(2)}) %collective-permute-start.2) | collective-permute-done | bytes 1048608 | tf_op jit(solution)/shard_map/while/body/ppermute | solution.py:608
  469.4 8.2 round.2
  481.1 6.0 attend.4
  490.9 8.3 round.3
  510.3 22.1 %collective-permute-done.2.rc1 = bf16[32,128,128]{2,1,0:T(8,128)(2,1)} collective-permute-done((bf16[32,128,128]{2,1,0:T(8,128)(2,1)}, bf16[32,128,128]{2,1,0:T(8,128)(2,1)}, u32[]{:S(2)}, u32[]{:S(2)}) %collective-permute-start.2) | collective-permute-done | bytes 1048608 | tf_op jit(solution)/shard_map/while/body/ppermute | solution.py:608
  534.6 8.7 %round.2 = (s32[64]{0:T(128)}, bf16[32,128,128]{2,1,0:T(8,128)(2,1)}, bf16[32,128,128]{2,1,0:T(8,128)(2,1)}, bf16[2,32,128,128]{3,2,1,0:T(8,128)(2,1)}, bf16[2,2...) custom-call(s32[1760]{0:T(1024)S(1)} %get-tuple-element.554.tab, ...), custom_call_target="tpu_custom_call", output_to_operand_aliasing={{5}: (10, {}), {6}: (11, {}), {7}: (12, {}), {8}: (13, {})} | custom-call | flops 40000000 | bytes 20000000 | tf_op jit(solution)/shard_map/while/body/round/pallas_call | solution.py:613
  546.6 6.2 attend.4
  556.6 8.8 %round.3 = (s32[64]{0:T(128)}, bf16[32,128,128]{2,1,0:T(8,128)(2,1)}, bf16[32,128,128]{2,1,0:T(8,128)(2,1)}, bf16[2,32,128,128]{3,2,1,0:T(8,128)(2,1)}, bf16[2,2...) custom-call(s32[1760]{0:T(1024)S(1)} %get-tuple-element.554.tab, ...), custom_call_target="tpu_custom_call", output_to_operand_aliasing={{5}: (10, {}), {6}: (11, {}), {7}: (12, {}), {8}: (13, {})} | custom-call | flops 40000000 | bytes 20000000 | tf_op jit(solution)/shard_map/while/body/round/pallas_call | solution.py:613
  565.5 6.4 attend.5
  575.1 23.1 %collective-permute-done.2.rc1 = bf16[32,128,128]{2,1,0:T(8,128)(2,1)} collective-permute-done((bf16[32,128,128]{2,1,0:T(8,128)(2,1)}, bf16[32,128,128]{2,1,0:T(8,128)(2,1)}, u32[]{:S(2)}, u32[]{:S(2)}) %collective-permute-start.2) | collective-permute-done | bytes 1048608 | tf_op jit(solution)/shard_map/while/body/ppermute | solution.py:608
  598.7 8.7 %round.2 = (s32[64]{0:T(128)}, bf16[32,128,128]{2,1,0:T(8,128)(2,1)}, bf16[32,128,128]{2,1,0:T(8,128)(2,1)}, bf16[2,32,128,128]{3,2,1,0:T(8,128)(2,1)}, bf16[2,2...) custom-call(s32[1760]{0:T(1024)S(1)} %get-tuple-element.554.tab, ...), custom_call_target="tpu_custom_call", output_to_operand_aliasing={{5}: (10, {}), {6}: (11, {}), {7}: (12, {}), {8}: (13, {})} | custom-call | flops 40000000 | bytes 20000000 | tf_op jit(solution)/shard_map/while/body/round/pallas_call | solution.py:613
  611.7 4.8 attend.4
  620.3 8.9 %round.3 = (s32[64]{0:T(128)}, bf16[32,128,128]{2,1,0:T(8,128)(2,1)}, bf16[32,128,128]{2,1,0:T(8,128)(2,1)}, bf16[2,32,128,128]{3,2,1,0:T(8,128)(2,1)}, bf16[2,2...) custom-call(s32[1760]{0:T(1024)S(1)} %get-tuple-element.554.tab, ...), custom_call_target="tpu_custom_call", output_to_operand_aliasing={{5}: (10, {}), {6}: (11, {}), {7}: (12, {}), {8}: (13, {})} | custom-call | flops 40000000 | bytes 20000000 | tf_op jit(solution)/shard_map/while/body/round/pallas_call | solution.py:613
  629.3 6.1 attend.5
  639.0 22.2 %collective-permute-done.2.rc1 = bf16[32,128,128]{2,1,0:T(8,128)(2,1)} collective-permute-done((bf16[32,128,128]{2,1,0:T(8,128)(2,1)}, bf16[32,128,128]{2,1,0:T(8,128)(2,1)}, u32[]{:S(2)}, u32[]{:S(2)}) %collective-permute-start.2) | collective-permute-done | bytes 1048608 | tf_op jit(solution)/shard_map/while/body/ppermute | solution.py:608
  663.3 8.5 %round.2 = (s32[64]{0:T(128)}, bf16[32,128,128]{2,1,0:T(8,128)(2,1)}, bf16[32,128,128]{2,1,0:T(8,128)(2,1)}, bf16[2,32,128,128]{3,2,1,0:T(8,128)(2,1)}, bf16[2,2...) custom-call(s32[1760]{0:T(1024)S(1)} %get-tuple-element.554.tab, ...), custom_call_target="tpu_custom_call", output_to_operand_aliasing={{5}: (10, {}), {6}: (11, {}), {7}: (12, {}), {8}: (13, {})} | custom-call | flops 40000000 | bytes 20000000 | tf_op jit(solution)/shard_map/while/body/round/pallas_call | solution.py:613
  675.7 5.0 attend.4
  684.5 9.0 %round.3 = (s32[64]{0:T(128)}, bf16[32,128,128]{2,1,0:T(8,128)(2,1)}, bf16[32,128,128]{2,1,0:T(8,128)(2,1)}, bf16[2,32,128,128]{3,2,1,0:T(8,128)(2,1)}, bf16[2,2...) custom-call(s32[1760]{0:T(1024)S(1)} %get-tuple-element.554.tab, ...), custom_call_target="tpu_custom_call", output_to_operand_aliasing={{5}: (10, {}), {6}: (11, {}), {7}: (12, {}), {8}: (13, {})} | custom-call | flops 40000000 | bytes 20000000 | tf_op jit(solution)/shard_map/while/body/round/pallas_call | solution.py:613
  693.6 6.1 attend.5
  703.6 22.3 %collective-permute-done.2.rc1 = bf16[32,128,128]{2,1,0:T(8,128)(2,1)} collective-permute-done((bf16[32,128,128]{2,1,0:T(8,128)(2,1)}, bf16[32,128,128]{2,1,0:T(8,128)(2,1)}, u32[]{:S(2)}, u32[]{:S(2)}) %collective-permute-start.2) | collective-permute-done | bytes 1048608 | tf_op jit(solution)/shard_map/while/body/ppermute | solution.py:608
  726.4 8.9 %round.2 = (s32[64]{0:T(128)}, bf16[32,128,128]{2,1,0:T(8,128)(2,1)}, bf16[32,128,128]{2,1,0:T(8,128)(2,1)}, bf16[2,32,128,128]{3,2,1,0:T(8,128)(2,1)}, bf16[2,2...) custom-call(s32[1760]{0:T(1024)S(1)} %get-tuple-element.554.tab, ...), custom_call_target="tpu_custom_call", output_to_operand_aliasing={{5}: (10, {}), {6}: (11, {}), {7}: (12, {}), {8}: (13, {})} | custom-call | flops 40000000 | bytes 20000000 | tf_op jit(solution)/shard_map/while/body/round/pallas_call | solution.py:613
  738.3 6.1 attend.4
  748.2 8.5 %round.3 = (s32[64]{0:T(128)}, bf16[32,128,128]{2,1,0:T(8,128)(2,1)}, bf16[32,128,128]{2,1,0:T(8,128)(2,1)}, bf16[2,32,128,128]{3,2,1,0:T(8,128)(2,1)}, bf16[2,2...) custom-call(s32[1760]{0:T(1024)S(1)} %get-tuple-element.554.tab, ...), custom_call_target="tpu_custom_call", output_to_operand_aliasing={{5}: (10, {}), {6}: (11, {}), {7}: (12, {}), {8}: (13, {})} | custom-call | flops 40000000 | bytes 20000000 | tf_op jit(solution)/shard_map/while/body/round/pallas_call | solution.py:613
  756.8 6.0 attend.5
  766.9 22.1 %collective-permute-done.2.rc1 = bf16[32,128,128]{2,1,0:T(8,128)(2,1)} collective-permute-done((bf16[32,128,128]{2,1,0:T(8,128)(2,1)}, bf16[32,128,128]{2,1,0:T(8,128)(2,1)}, u32[]{:S(2)}, u32[]{:S(2)}) %collective-permute-start.2) | collective-permute-done | bytes 1048608 | tf_op jit(solution)/shard_map/while/body/ppermute | solution.py:608
  789.6 6.8 round.2
  799.9 6.1 attend.4
  809.8 7.1 round.3
  816.8 5.2 attend.5
  834.7 5.5 attend.3
  (388 shorter events, 179.4 us)
Async XLA Ops:
  53.7 33.3 %collective-permute-start.5 = (bf16[2,24,128,128]{3,2,1,0:T(8,128)(2,1)}, bf16[2,24,128,128]{3,2,1,0:T(8,128)(2,1)}, u32[]{:S(2)}, u32[]{:S(2)}) collective-permute-start(bf16[2,24,128,128]{3,2,1,0:T(8,128)(2,1)} %get-tuple-element.516), channel_id=1, source_target_pairs={{0,1},{1,0},{2,3},{3,2},{4,5},{5,4},{6,7},{7,6}} | collective-permute-start | bytes 4718600 | tf_op jit(solution)/shard_map/while/body/ppermute | solution.py:612
  53.7 32.7 %collective-permute-start.4 = (bf16[32,128,128]{2,1,0:T(8,128)(2,1)}, bf16[32,128,128]{2,1,0:T(8,128)(2,1)}, u32[]{:S(2)}, u32[]{:S(2)}) collective-permute-start(bf16[32,128,128]{2,1,0:T(8,128)(2,1)} %get-tuple-element.519.rc1), channel_id=1, source_target_pairs={{0,1},{1,0},{2,3},{3,2},{4,5},{5,4},{6,7},{7,6}} | collective-permute-start | bytes 3145736 | tf_op jit(solution)/shard_map/while/body/ppermute | solution.py:611
  54.2 32.7 %collective-permute-start.3 = (bf16[32,128,128]{2,1,0:T(8,128)(2,1)}, bf16[32,128,128]{2,1,0:T(8,128)(2,1)}, u32[]{:S(2)}, u32[]{:S(2)}) collective-permute-start(bf16[32,128,128]{2,1,0:T(8,128)(2,1)} %get-tuple-element.518.rc0), channel_id=1, source_target_pairs={{0,1},{1,0},{2,3},{3,2},{4,5},{5,4},{6,7},{7,6}} | collective-permute-start | bytes 3145736 | tf_op jit(solution)/shard_map/while/body/ppermute | solution.py:610
  86.9 28.3 %collective-permute-start.6 = (bf16[2,32,128,128]{3,2,1,0:T(8,128)(2,1)}, bf16[2,32,128,128]{3,2,1,0:T(8,128)(2,1)}, u32[]{:S(2)}, u32[]{:S(2)}) collective-permute-start(bf16[2,32,128,128]{3,2,1,0:T(8,128)(2,1)} %get-tuple-element.477), channel_id=1, source_target_pairs={{0,1},{1,0},{2,3},{3,2},{4,5},{5,4},{6,7},{7,6}} | collective-permute-start | bytes 6291464 | tf_op jit(solution)/shard_map/while/body/ppermute | solution.py:609
  87.0 26.5 %collective-permute-start.11 = (bf16[2,24,128,128]{3,2,1,0:T(8,128)(2,1)}, bf16[2,24,128,128]{3,2,1,0:T(8,128)(2,1)}, u32[]{:S(2)}, u32[]{:S(2)}) collective-permute-start(bf16[2,24,128,128]{3,2,1,0:T(8,128)(2,1)} %get-tuple-element.480), channel_id=1, source_target_pairs={{0,1},{1,0},{2,3},{3,2},{4,5},{5,4},{6,7},{7,6}} | collective-permute-start | bytes 4718600 | tf_op jit(solution)/shard_map/while/body/ppermute | solution.py:612
  115.8 29.3 %collective-permute-start.2 = (bf16[32,128,128]{2,1,0:T(8,128)(2,1)}, bf16[32,128,128]{2,1,0:T(8,128)(2,1)}, u32[]{:S(2)}, u32[]{:S(2)}) collective-permute-start(bf16[32,128,128]{2,1,0:T(8,128)(2,1)} %get-tuple-element.514), channel_id=1, source_target_pairs={{2,0},{3,1},{6,2},{7,3},{4,6},{5,7},{0,4},{1,5}} | collective-permute-start | bytes 3145736 | tf_op jit(solution)/shard_map/while/body/ppermute | solution.py:608
  121.2 35.6 %collective-permute-start.5 = (bf16[2,24,128,128]{3,2,1,0:T(8,128)(2,1)}, bf16[2,24,128,128]{3,2,1,0:T(8,128)(2,1)}, u32[]{:S(2)}, u32[]{:S(2)}) collective-permute-start(bf16[2,24,128,128]{3,2,1,0:T(8,128)(2,1)} %get-tuple-element.516), channel_id=1, source_target_pairs={{0,1},{1,0},{2,3},{3,2},{4,5},{5,4},{6,7},{7,6}} | collective-permute-start | bytes 4718600 | tf_op jit(solution)/shard_map/while/body/ppermute | solution.py:612
  121.2 35.1 %collective-permute-start.4 = (bf16[32,128,128]{2,1,0:T(8,128)(2,1)}, bf16[32,128,128]{2,1,0:T(8,128)(2,1)}, u32[]{:S(2)}, u32[]{:S(2)}) collective-permute-start(bf16[32,128,128]{2,1,0:T(8,128)(2,1)} %get-tuple-element.519.rc1), channel_id=1, source_target_pairs={{0,1},{1,0},{2,3},{3,2},{4,5},{5,4},{6,7},{7,6}} | collective-permute-start | bytes 3145736 | tf_op jit(solution)/shard_map/while/body/ppermute | solution.py:611
  121.7 34.6 %collective-permute-start.3 = (bf16[32,128,128]{2,1,0:T(8,128)(2,1)}, bf16[32,128,128]{2,1,0:T(8,128)(2,1)}, u32[]{:S(2)}, u32[]{:S(2)}) collective-permute-start(bf16[32,128,128]{2,1,0:T(8,128)(2,1)} %get-tuple-element.518.rc0), channel_id=1, source_target_pairs={{0,1},{1,0},{2,3},{3,2},{4,5},{5,4},{6,7},{7,6}} | collective-permute-start | bytes 3145736 | tf_op jit(solution)/shard_map/while/body/ppermute | solution.py:610
  156.3 28.4 %collective-permute-start.6 = (bf16[2,32,128,128]{3,2,1,0:T(8,128)(2,1)}, bf16[2,32,128,128]{3,2,1,0:T(8,128)(2,1)}, u32[]{:S(2)}, u32[]{:S(2)}) collective-permute-start(bf16[2,32,128,128]{3,2,1,0:T(8,128)(2,1)} %get-tuple-element.477), channel_id=1, source_target_pairs={{0,1},{1,0},{2,3},{3,2},{4,5},{5,4},{6,7},{7,6}} | collective-permute-start | bytes 6291464 | tf_op jit(solution)/shard_map/while/body/ppermute | solution.py:609
  156.8 27.6 %collective-permute-start.11 = (bf16[2,24,128,128]{3,2,1,0:T(8,128)(2,1)}, bf16[2,24,128,128]{3,2,1,0:T(8,128)(2,1)}, u32[]{:S(2)}, u32[]{:S(2)}) collective-permute-start(bf16[2,24,128,128]{3,2,1,0:T(8,128)(2,1)} %get-tuple-element.480), channel_id=1, source_target_pairs={{0,1},{1,0},{2,3},{3,2},{4,5},{5,4},{6,7},{7,6}} | collective-permute-start | bytes 4718600 | tf_op jit(solution)/shard_map/while/body/ppermute | solution.py:612
  156.9 27.5 %collective-permute-start.7 = (bf16[32,128,128]{2,1,0:T(8,128)(2,1)}, bf16[32,128,128]{2,1,0:T(8,128)(2,1)}, u32[]{:S(2)}, u32[]{:S(2)}) collective-permute-start(bf16[32,128,128]{2,1,0:T(8,128)(2,1)} %get-tuple-element.478), channel_id=1, source_target_pairs={{0,2},{1,3},{2,6},{3,7},{6,4},{7,5},{4,0},{5,1}} | collective-permute-start | bytes 3145736 | tf_op jit(solution)/shard_map/while/body/ppermute | solution.py:607
  187.3 35.7 %collective-permute-start.5 = (bf16[2,24,128,128]{3,2,1,0:T(8,128)(2,1)}, bf16[2,24,128,128]{3,2,1,0:T(8,128)(2,1)}, u32[]{:S(2)}, u32[]{:S(2)}) collective-permute-start(bf16[2,24,128,128]{3,2,1,0:T(8,128)(2,1)} %get-tuple-element.516), channel_id=1, source_target_pairs={{0,1},{1,0},{2,3},{3,2},{4,5},{5,4},{6,7},{7,6}} | collective-permute-start | bytes 4718600 | tf_op jit(solution)/shard_map/while/body/ppermute | solution.py:612
  187.3 35.2 %collective-permute-start.4 = (bf16[32,128,128]{2,1,0:T(8,128)(2,1)}, bf16[32,128,128]{2,1,0:T(8,128)(2,1)}, u32[]{:S(2)}, u32[]{:S(2)}) collective-permute-start(bf16[32,128,128]{2,1,0:T(8,128)(2,1)} %get-tuple-element.519.rc1), channel_id=1, source_target_pairs={{0,1},{1,0},{2,3},{3,2},{4,5},{5,4},{6,7},{7,6}} | collective-permute-start | bytes 3145736 | tf_op jit(solution)/shard_map/while/body/ppermute | solution.py:611
  187.9 34.7 %collective-permute-start.3 = (bf16[32,128,128]{2,1,0:T(8,128)(2,1)}, bf16[32,128,128]{2,1,0:T(8,128)(2,1)}, u32[]{:S(2)}, u32[]{:S(2)}) collective-permute-start(bf16[32,128,128]{2,1,0:T(8,128)(2,1)} %get-tuple-element.518.rc0), channel_id=1, source_target_pairs={{0,1},{1,0},{2,3},{3,2},{4,5},{5,4},{6,7},{7,6}} | collective-permute-start | bytes 3145736 | tf_op jit(solution)/shard_map/while/body/ppermute | solution.py:610
  222.6 28.4 %collective-permute-start.6 = (bf16[2,32,128,128]{3,2,1,0:T(8,128)(2,1)}, bf16[2,32,128,128]{3,2,1,0:T(8,128)(2,1)}, u32[]{:S(2)}, u32[]{:S(2)}) collective-permute-start(bf16[2,32,128,128]{3,2,1,0:T(8,128)(2,1)} %get-tuple-element.477), channel_id=1, source_target_pairs={{0,1},{1,0},{2,3},{3,2},{4,5},{5,4},{6,7},{7,6}} | collective-permute-start | bytes 6291464 | tf_op jit(solution)/shard_map/while/body/ppermute | solution.py:609
  223.1 26.7 %collective-permute-start.11 = (bf16[2,24,128,128]{3,2,1,0:T(8,128)(2,1)}, bf16[2,24,128,128]{3,2,1,0:T(8,128)(2,1)}, u32[]{:S(2)}, u32[]{:S(2)}) collective-permute-start(bf16[2,24,128,128]{3,2,1,0:T(8,128)(2,1)} %get-tuple-element.480), channel_id=1, source_target_pairs={{0,1},{1,0},{2,3},{3,2},{4,5},{5,4},{6,7},{7,6}} | collective-permute-start | bytes 4718600 | tf_op jit(solution)/shard_map/while/body/ppermute | solution.py:612
  223.1 26.7 %collective-permute-start.7 = (bf16[32,128,128]{2,1,0:T(8,128)(2,1)}, bf16[32,128,128]{2,1,0:T(8,128)(2,1)}, u32[]{:S(2)}, u32[]{:S(2)}) collective-permute-start(bf16[32,128,128]{2,1,0:T(8,128)(2,1)} %get-tuple-element.478), channel_id=1, source_target_pairs={{0,2},{1,3},{2,6},{3,7},{6,4},{7,5},{4,0},{5,1}} | collective-permute-start | bytes 3145736 | tf_op jit(solution)/shard_map/while/body/ppermute | solution.py:607
  253.6 34.4 %collective-permute-start.5 = (bf16[2,24,128,128]{3,2,1,0:T(8,128)(2,1)}, bf16[2,24,128,128]{3,2,1,0:T(8,128)(2,1)}, u32[]{:S(2)}, u32[]{:S(2)}) collective-permute-start(bf16[2,24,128,128]{3,2,1,0:T(8,128)(2,1)} %get-tuple-element.516), channel_id=1, source_target_pairs={{0,1},{1,0},{2,3},{3,2},{4,5},{5,4},{6,7},{7,6}} | collective-permute-start | bytes 4718600 | tf_op jit(solution)/shard_map/while/body/ppermute | solution.py:612
  253.6 33.8 %collective-permute-start.4 = (bf16[32,128,128]{2,1,0:T(8,128)(2,1)}, bf16[32,128,128]{2,1,0:T(8,128)(2,1)}, u32[]{:S(2)}, u32[]{:S(2)}) collective-permute-start(bf16[32,128,128]{2,1,0:T(8,128)(2,1)} %get-tuple-element.519.rc1), channel_id=1, source_target_pairs={{0,1},{1,0},{2,3},{3,2},{4,5},{5,4},{6,7},{7,6}} | collective-permute-start | bytes 3145736 | tf_op jit(solution)/shard_map/while/body/ppermute | solution.py:611
  254.1 33.4 %collective-permute-start.3 = (bf16[32,128,128]{2,1,0:T(8,128)(2,1)}, bf16[32,128,128]{2,1,0:T(8,128)(2,1)}, u32[]{:S(2)}, u32[]{:S(2)}) collective-permute-start(bf16[32,128,128]{2,1,0:T(8,128)(2,1)} %get-tuple-element.518.rc0), channel_id=1, source_target_pairs={{0,1},{1,0},{2,3},{3,2},{4,5},{5,4},{6,7},{7,6}} | collective-permute-start | bytes 3145736 | tf_op jit(solution)/shard_map/while/body/ppermute | solution.py:610
  287.5 28.4 %collective-permute-start.6 = (bf16[2,32,128,128]{3,2,1,0:T(8,128)(2,1)}, bf16[2,32,128,128]{3,2,1,0:T(8,128)(2,1)}, u32[]{:S(2)}, u32[]{:S(2)}) collective-permute-start(bf16[2,32,128,128]{3,2,1,0:T(8,128)(2,1)} %get-tuple-element.477), channel_id=1, source_target_pairs={{0,1},{1,0},{2,3},{3,2},{4,5},{5,4},{6,7},{7,6}} | collective-permute-start | bytes 6291464 | tf_op jit(solution)/shard_map/while/body/ppermute | solution.py:609
  318.5 32.5 %collective-permute-start.5 = (bf16[2,24,128,128]{3,2,1,0:T(8,128)(2,1)}, bf16[2,24,128,128]{3,2,1,0:T(8,128)(2,1)}, u32[]{:S(2)}, u32[]{:S(2)}) collective-permute-start(bf16[2,24,128,128]{3,2,1,0:T(8,128)(2,1)} %get-tuple-element.516), channel_id=1, source_target_pairs={{0,1},{1,0},{2,3},{3,2},{4,5},{5,4},{6,7},{7,6}} | collective-permute-start | bytes 4718600 | tf_op jit(solution)/shard_map/while/body/ppermute | solution.py:612
  318.5 31.9 %collective-permute-start.4 = (bf16[32,128,128]{2,1,0:T(8,128)(2,1)}, bf16[32,128,128]{2,1,0:T(8,128)(2,1)}, u32[]{:S(2)}, u32[]{:S(2)}) collective-permute-start(bf16[32,128,128]{2,1,0:T(8,128)(2,1)} %get-tuple-element.519.rc1), channel_id=1, source_target_pairs={{0,1},{1,0},{2,3},{3,2},{4,5},{5,4},{6,7},{7,6}} | collective-permute-start | bytes 3145736 | tf_op jit(solution)/shard_map/while/body/ppermute | solution.py:611
  319.0 31.6 %collective-permute-start.3 = (bf16[32,128,128]{2,1,0:T(8,128)(2,1)}, bf16[32,128,128]{2,1,0:T(8,128)(2,1)}, u32[]{:S(2)}, u32[]{:S(2)}) collective-permute-start(bf16[32,128,128]{2,1,0:T(8,128)(2,1)} %get-tuple-element.518.rc0), channel_id=1, source_target_pairs={{0,1},{1,0},{2,3},{3,2},{4,5},{5,4},{6,7},{7,6}} | collective-permute-start | bytes 3145736 | tf_op jit(solution)/shard_map/while/body/ppermute | solution.py:610
  350.6 28.3 %collective-permute-start.6 = (bf16[2,32,128,128]{3,2,1,0:T(8,128)(2,1)}, bf16[2,32,128,128]{3,2,1,0:T(8,128)(2,1)}, u32[]{:S(2)}, u32[]{:S(2)}) collective-permute-start(bf16[2,32,128,128]{3,2,1,0:T(8,128)(2,1)} %get-tuple-element.477), channel_id=1, source_target_pairs={{0,1},{1,0},{2,3},{3,2},{4,5},{5,4},{6,7},{7,6}} | collective-permute-start | bytes 6291464 | tf_op jit(solution)/shard_map/while/body/ppermute | solution.py:609
  351.0 27.4 %collective-permute-start.11 = (bf16[2,24,128,128]{3,2,1,0:T(8,128)(2,1)}, bf16[2,24,128,128]{3,2,1,0:T(8,128)(2,1)}, u32[]{:S(2)}, u32[]{:S(2)}) collective-permute-start(bf16[2,24,128,128]{3,2,1,0:T(8,128)(2,1)} %get-tuple-element.480), channel_id=1, source_target_pairs={{0,1},{1,0},{2,3},{3,2},{4,5},{5,4},{6,7},{7,6}} | collective-permute-start | bytes 4718600 | tf_op jit(solution)/shard_map/while/body/ppermute | solution.py:612
  351.1 27.3 %collective-permute-start.7 = (bf16[32,128,128]{2,1,0:T(8,128)(2,1)}, bf16[32,128,128]{2,1,0:T(8,128)(2,1)}, u32[]{:S(2)}, u32[]{:S(2)}) collective-permute-start(bf16[32,128,128]{2,1,0:T(8,128)(2,1)} %get-tuple-element.478), channel_id=1, source_target_pairs={{0,2},{1,3},{2,6},{3,7},{6,4},{7,5},{4,0},{5,1}} | collective-permute-start | bytes 3145736 | tf_op jit(solution)/shard_map/while/body/ppermute | solution.py:607
  381.5 32.4 %collective-permute-start.5 = (bf16[2,24,128,128]{3,2,1,0:T(8,128)(2,1)}, bf16[2,24,128,128]{3,2,1,0:T(8,128)(2,1)}, u32[]{:S(2)}, u32[]{:S(2)}) collective-permute-start(bf16[2,24,128,128]{3,2,1,0:T(8,128)(2,1)} %get-tuple-element.516), channel_id=1, source_target_pairs={{0,1},{1,0},{2,3},{3,2},{4,5},{5,4},{6,7},{7,6}} | collective-permute-start | bytes 4718600 | tf_op jit(solution)/shard_map/while/body/ppermute | solution.py:612
  381.5 31.3 %collective-permute-start.4 = (bf16[32,128,128]{2,1,0:T(8,128)(2,1)}, bf16[32,128,128]{2,1,0:T(8,128)(2,1)}, u32[]{:S(2)}, u32[]{:S(2)}) collective-permute-start(bf16[32,128,128]{2,1,0:T(8,128)(2,1)} %get-tuple-element.519.rc1), channel_id=1, source_target_pairs={{0,1},{1,0},{2,3},{3,2},{4,5},{5,4},{6,7},{7,6}} | collective-permute-start | bytes 3145736 | tf_op jit(solution)/shard_map/while/body/ppermute | solution.py:611
  382.0 31.8 %collective-permute-start.3 = (bf16[32,128,128]{2,1,0:T(8,128)(2,1)}, bf16[32,128,128]{2,1,0:T(8,128)(2,1)}, u32[]{:S(2)}, u32[]{:S(2)}) collective-permute-start(bf16[32,128,128]{2,1,0:T(8,128)(2,1)} %get-tuple-element.518.rc0), channel_id=1, source_target_pairs={{0,1},{1,0},{2,3},{3,2},{4,5},{5,4},{6,7},{7,6}} | collective-permute-start | bytes 3145736 | tf_op jit(solution)/shard_map/while/body/ppermute | solution.py:610
  413.8 28.3 %collective-permute-start.6 = (bf16[2,32,128,128]{3,2,1,0:T(8,128)(2,1)}, bf16[2,32,128,128]{3,2,1,0:T(8,128)(2,1)}, u32[]{:S(2)}, u32[]{:S(2)}) collective-permute-start(bf16[2,32,128,128]{3,2,1,0:T(8,128)(2,1)} %get-tuple-element.477), channel_id=1, source_target_pairs={{0,1},{1,0},{2,3},{3,2},{4,5},{5,4},{6,7},{7,6}} | collective-permute-start | bytes 6291464 | tf_op jit(solution)/shard_map/while/body/ppermute | solution.py:609
  444.7 33.8 %collective-permute-start.5 = (bf16[2,24,128,128]{3,2,1,0:T(8,128)(2,1)}, bf16[2,24,128,128]{3,2,1,0:T(8,128)(2,1)}, u32[]{:S(2)}, u32[]{:S(2)}) collective-permute-start(bf16[2,24,128,128]{3,2,1,0:T(8,128)(2,1)} %get-tuple-element.516), channel_id=1, source_target_pairs={{0,1},{1,0},{2,3},{3,2},{4,5},{5,4},{6,7},{7,6}} | collective-permute-start | bytes 4718600 | tf_op jit(solution)/shard_map/while/body/ppermute | solution.py:612
  445.0 32.6 %collective-permute-start.4 = (bf16[32,128,128]{2,1,0:T(8,128)(2,1)}, bf16[32,128,128]{2,1,0:T(8,128)(2,1)}, u32[]{:S(2)}, u32[]{:S(2)}) collective-permute-start(bf16[32,128,128]{2,1,0:T(8,128)(2,1)} %get-tuple-element.519.rc1), channel_id=1, source_target_pairs={{0,1},{1,0},{2,3},{3,2},{4,5},{5,4},{6,7},{7,6}} | collective-permute-start | bytes 3145736 | tf_op jit(solution)/shard_map/while/body/ppermute | solution.py:611
  445.2 33.3 %collective-permute-start.3 = (bf16[32,128,128]{2,1,0:T(8,128)(2,1)}, bf16[32,128,128]{2,1,0:T(8,128)(2,1)}, u32[]{:S(2)}, u32[]{:S(2)}) collective-permute-start(bf16[32,128,128]{2,1,0:T(8,128)(2,1)} %get-tuple-element.518.rc0), channel_id=1, source_target_pairs={{0,1},{1,0},{2,3},{3,2},{4,5},{5,4},{6,7},{7,6}} | collective-permute-start | bytes 3145736 | tf_op jit(solution)/shard_map/while/body/ppermute | solution.py:610
  478.5 28.3 %collective-permute-start.6 = (bf16[2,32,128,128]{3,2,1,0:T(8,128)(2,1)}, bf16[2,32,128,128]{3,2,1,0:T(8,128)(2,1)}, u32[]{:S(2)}, u32[]{:S(2)}) collective-permute-start(bf16[2,32,128,128]{3,2,1,0:T(8,128)(2,1)} %get-tuple-element.477), channel_id=1, source_target_pairs={{0,1},{1,0},{2,3},{3,2},{4,5},{5,4},{6,7},{7,6}} | collective-permute-start | bytes 6291464 | tf_op jit(solution)/shard_map/while/body/ppermute | solution.py:609
  509.7 34.1 %collective-permute-start.5 = (bf16[2,24,128,128]{3,2,1,0:T(8,128)(2,1)}, bf16[2,24,128,128]{3,2,1,0:T(8,128)(2,1)}, u32[]{:S(2)}, u32[]{:S(2)}) collective-permute-start(bf16[2,24,128,128]{3,2,1,0:T(8,128)(2,1)} %get-tuple-element.516), channel_id=1, source_target_pairs={{0,1},{1,0},{2,3},{3,2},{4,5},{5,4},{6,7},{7,6}} | collective-permute-start | bytes 4718600 | tf_op jit(solution)/shard_map/while/body/ppermute | solution.py:612
  509.7 33.5 %collective-permute-start.4 = (bf16[32,128,128]{2,1,0:T(8,128)(2,1)}, bf16[32,128,128]{2,1,0:T(8,128)(2,1)}, u32[]{:S(2)}, u32[]{:S(2)}) collective-permute-start(bf16[32,128,128]{2,1,0:T(8,128)(2,1)} %get-tuple-element.519.rc1), channel_id=1, source_target_pairs={{0,1},{1,0},{2,3},{3,2},{4,5},{5,4},{6,7},{7,6}} | collective-permute-start | bytes 3145736 | tf_op jit(solution)/shard_map/while/body/ppermute | solution.py:611
  510.3 33.1 %collective-permute-start.3 = (bf16[32,128,128]{2,1,0:T(8,128)(2,1)}, bf16[32,128,128]{2,1,0:T(8,128)(2,1)}, u32[]{:S(2)}, u32[]{:S(2)}) collective-permute-start(bf16[32,128,128]{2,1,0:T(8,128)(2,1)} %get-tuple-element.518.rc0), channel_id=1, source_target_pairs={{0,1},{1,0},{2,3},{3,2},{4,5},{5,4},{6,7},{7,6}} | collective-permute-start | bytes 3145736 | tf_op jit(solution)/shard_map/while/body/ppermute | solution.py:610
  543.4 28.6 %collective-permute-start.6 = (bf16[2,32,128,128]{3,2,1,0:T(8,128)(2,1)}, bf16[2,32,128,128]{3,2,1,0:T(8,128)(2,1)}, u32[]{:S(2)}, u32[]{:S(2)}) collective-permute-start(bf16[2,32,128,128]{3,2,1,0:T(8,128)(2,1)} %get-tuple-element.477), channel_id=1, source_target_pairs={{0,1},{1,0},{2,3},{3,2},{4,5},{5,4},{6,7},{7,6}} | collective-permute-start | bytes 6291464 | tf_op jit(solution)/shard_map/while/body/ppermute | solution.py:609
  543.8 28.1 %collective-permute-start.11 = (bf16[2,24,128,128]{3,2,1,0:T(8,128)(2,1)}, bf16[2,24,128,128]{3,2,1,0:T(8,128)(2,1)}, u32[]{:S(2)}, u32[]{:S(2)}) collective-permute-start(bf16[2,24,128,128]{3,2,1,0:T(8,128)(2,1)} %get-tuple-element.480), channel_id=1, source_target_pairs={{0,1},{1,0},{2,3},{3,2},{4,5},{5,4},{6,7},{7,6}} | collective-permute-start | bytes 4718600 | tf_op jit(solution)/shard_map/while/body/ppermute | solution.py:612
  543.9 28.0 %collective-permute-start.7 = (bf16[32,128,128]{2,1,0:T(8,128)(2,1)}, bf16[32,128,128]{2,1,0:T(8,128)(2,1)}, u32[]{:S(2)}, u32[]{:S(2)}) collective-permute-start(bf16[32,128,128]{2,1,0:T(8,128)(2,1)} %get-tuple-element.478), channel_id=1, source_target_pairs={{0,2},{1,3},{2,6},{3,7},{6,4},{7,5},{4,0},{5,1}} | collective-permute-start | bytes 3145736 | tf_op jit(solution)/shard_map/while/body/ppermute | solution.py:607
  574.6 33.3 %collective-permute-start.5 = (bf16[2,24,128,128]{3,2,1,0:T(8,128)(2,1)}, bf16[2,24,128,128]{3,2,1,0:T(8,128)(2,1)}, u32[]{:S(2)}, u32[]{:S(2)}) collective-permute-start(bf16[2,24,128,128]{3,2,1,0:T(8,128)(2,1)} %get-tuple-element.516), channel_id=1, source_target_pairs={{0,1},{1,0},{2,3},{3,2},{4,5},{5,4},{6,7},{7,6}} | collective-permute-start | bytes 4718600 | tf_op jit(solution)/shard_map/while/body/ppermute | solution.py:612
  574.6 32.8 %collective-permute-start.4 = (bf16[32,128,128]{2,1,0:T(8,128)(2,1)}, bf16[32,128,128]{2,1,0:T(8,128)(2,1)}, u32[]{:S(2)}, u32[]{:S(2)}) collective-permute-start(bf16[32,128,128]{2,1,0:T(8,128)(2,1)} %get-tuple-element.519.rc1), channel_id=1, source_target_pairs={{0,1},{1,0},{2,3},{3,2},{4,5},{5,4},{6,7},{7,6}} | collective-permute-start | bytes 3145736 | tf_op jit(solution)/shard_map/while/body/ppermute | solution.py:611
  575.1 32.3 %collective-permute-start.3 = (bf16[32,128,128]{2,1,0:T(8,128)(2,1)}, bf16[32,128,128]{2,1,0:T(8,128)(2,1)}, u32[]{:S(2)}, u32[]{:S(2)}) collective-permute-start(bf16[32,128,128]{2,1,0:T(8,128)(2,1)} %get-tuple-element.518.rc0), channel_id=1, source_target_pairs={{0,1},{1,0},{2,3},{3,2},{4,5},{5,4},{6,7},{7,6}} | collective-permute-start | bytes 3145736 | tf_op jit(solution)/shard_map/while/body/ppermute | solution.py:610
  607.4 28.4 %collective-permute-start.6 = (bf16[2,32,128,128]{3,2,1,0:T(8,128)(2,1)}, bf16[2,32,128,128]{3,2,1,0:T(8,128)(2,1)}, u32[]{:S(2)}, u32[]{:S(2)}) collective-permute-start(bf16[2,32,128,128]{3,2,1,0:T(8,128)(2,1)} %get-tuple-element.477), channel_id=1, source_target_pairs={{0,1},{1,0},{2,3},{3,2},{4,5},{5,4},{6,7},{7,6}} | collective-permute-start | bytes 6291464 | tf_op jit(solution)/shard_map/while/body/ppermute | solution.py:609
  607.9 27.5 %collective-permute-start.11 = (bf16[2,24,128,128]{3,2,1,0:T(8,128)(2,1)}, bf16[2,24,128,128]{3,2,1,0:T(8,128)(2,1)}, u32[]{:S(2)}, u32[]{:S(2)}) collective-permute-start(bf16[2,24,128,128]{3,2,1,0:T(8,128)(2,1)} %get-tuple-element.480), channel_id=1, source_target_pairs={{0,1},{1,0},{2,3},{3,2},{4,5},{5,4},{6,7},{7,6}} | collective-permute-start | bytes 4718600 | tf_op jit(solution)/shard_map/while/body/ppermute | solution.py:612
  608.0 27.5 %collective-permute-start.7 = (bf16[32,128,128]{2,1,0:T(8,128)(2,1)}, bf16[32,128,128]{2,1,0:T(8,128)(2,1)}, u32[]{:S(2)}, u32[]{:S(2)}) collective-permute-start(bf16[32,128,128]{2,1,0:T(8,128)(2,1)} %get-tuple-element.478), channel_id=1, source_target_pairs={{0,2},{1,3},{2,6},{3,7},{6,4},{7,5},{4,0},{5,1}} | collective-permute-start | bytes 3145736 | tf_op jit(solution)/shard_map/while/body/ppermute | solution.py:607
  638.5 34.0 %collective-permute-start.5 = (bf16[2,24,128,128]{3,2,1,0:T(8,128)(2,1)}, bf16[2,24,128,128]{3,2,1,0:T(8,128)(2,1)}, u32[]{:S(2)}, u32[]{:S(2)}) collective-permute-start(bf16[2,24,128,128]{3,2,1,0:T(8,128)(2,1)} %get-tuple-element.516), channel_id=1, source_target_pairs={{0,1},{1,0},{2,3},{3,2},{4,5},{5,4},{6,7},{7,6}} | collective-permute-start | bytes 4718600 | tf_op jit(solution)/shard_map/while/body/ppermute | solution.py:612
  638.5 33.4 %collective-permute-start.4 = (bf16[32,128,128]{2,1,0:T(8,128)(2,1)}, bf16[32,128,128]{2,1,0:T(8,128)(2,1)}, u32[]{:S(2)}, u32[]{:S(2)}) collective-permute-start(bf16[32,128,128]{2,1,0:T(8,128)(2,1)} %get-tuple-element.519.rc1), channel_id=1, source_target_pairs={{0,1},{1,0},{2,3},{3,2},{4,5},{5,4},{6,7},{7,6}} | collective-permute-start | bytes 3145736 | tf_op jit(solution)/shard_map/while/body/ppermute | solution.py:611
  639.0 33.3 %collective-permute-start.3 = (bf16[32,128,128]{2,1,0:T(8,128)(2,1)}, bf16[32,128,128]{2,1,0:T(8,128)(2,1)}, u32[]{:S(2)}, u32[]{:S(2)}) collective-permute-start(bf16[32,128,128]{2,1,0:T(8,128)(2,1)} %get-tuple-element.518.rc0), channel_id=1, source_target_pairs={{0,1},{1,0},{2,3},{3,2},{4,5},{5,4},{6,7},{7,6}} | collective-permute-start | bytes 3145736 | tf_op jit(solution)/shard_map/while/body/ppermute | solution.py:610
  672.2 28.3 %collective-permute-start.6 = (bf16[2,32,128,128]{3,2,1,0:T(8,128)(2,1)}, bf16[2,32,128,128]{3,2,1,0:T(8,128)(2,1)}, u32[]{:S(2)}, u32[]{:S(2)}) collective-permute-start(bf16[2,32,128,128]{3,2,1,0:T(8,128)(2,1)} %get-tuple-element.477), channel_id=1, source_target_pairs={{0,1},{1,0},{2,3},{3,2},{4,5},{5,4},{6,7},{7,6}} | collective-permute-start | bytes 6291464 | tf_op jit(solution)/shard_map/while/body/ppermute | solution.py:609
  672.5 27.2 %collective-permute-start.11 = (bf16[2,24,128,128]{3,2,1,0:T(8,128)(2,1)}, bf16[2,24,128,128]{3,2,1,0:T(8,128)(2,1)}, u32[]{:S(2)}, u32[]{:S(2)}) collective-permute-start(bf16[2,24,128,128]{3,2,1,0:T(8,128)(2,1)} %get-tuple-element.480), channel_id=1, source_target_pairs={{0,1},{1,0},{2,3},{3,2},{4,5},{5,4},{6,7},{7,6}} | collective-permute-start | bytes 4718600 | tf_op jit(solution)/shard_map/while/body/ppermute | solution.py:612
  672.7 26.9 %collective-permute-start.7 = (bf16[32,128,128]{2,1,0:T(8,128)(2,1)}, bf16[32,128,128]{2,1,0:T(8,128)(2,1)}, u32[]{:S(2)}, u32[]{:S(2)}) collective-permute-start(bf16[32,128,128]{2,1,0:T(8,128)(2,1)} %get-tuple-element.478), channel_id=1, source_target_pairs={{0,2},{1,3},{2,6},{3,7},{6,4},{7,5},{4,0},{5,1}} | collective-permute-start | bytes 3145736 | tf_op jit(solution)/shard_map/while/body/ppermute | solution.py:607
  703.1 32.8 %collective-permute-start.5 = (bf16[2,24,128,128]{3,2,1,0:T(8,128)(2,1)}, bf16[2,24,128,128]{3,2,1,0:T(8,128)(2,1)}, u32[]{:S(2)}, u32[]{:S(2)}) collective-permute-start(bf16[2,24,128,128]{3,2,1,0:T(8,128)(2,1)} %get-tuple-element.516), channel_id=1, source_target_pairs={{0,1},{1,0},{2,3},{3,2},{4,5},{5,4},{6,7},{7,6}} | collective-permute-start | bytes 4718600 | tf_op jit(solution)/shard_map/while/body/ppermute | solution.py:612
  703.1 32.2 %collective-permute-start.4 = (bf16[32,128,128]{2,1,0:T(8,128)(2,1)}, bf16[32,128,128]{2,1,0:T(8,128)(2,1)}, u32[]{:S(2)}, u32[]{:S(2)}) collective-permute-start(bf16[32,128,128]{2,1,0:T(8,128)(2,1)} %get-tuple-element.519.rc1), channel_id=1, source_target_pairs={{0,1},{1,0},{2,3},{3,2},{4,5},{5,4},{6,7},{7,6}} | collective-permute-start | bytes 3145736 | tf_op jit(solution)/shard_map/while/body/ppermute | solution.py:611
  703.6 31.8 %collective-permute-start.3 = (bf16[32,128,128]{2,1,0:T(8,128)(2,1)}, bf16[32,128,128]{2,1,0:T(8,128)(2,1)}, u32[]{:S(2)}, u32[]{:S(2)}) collective-permute-start(bf16[32,128,128]{2,1,0:T(8,128)(2,1)} %get-tuple-element.518.rc0), channel_id=1, source_target_pairs={{0,1},{1,0},{2,3},{3,2},{4,5},{5,4},{6,7},{7,6}} | collective-permute-start | bytes 3145736 | tf_op jit(solution)/shard_map/while/body/ppermute | solution.py:610
  735.4 28.4 %collective-permute-start.6 = (bf16[2,32,128,128]{3,2,1,0:T(8,128)(2,1)}, bf16[2,32,128,128]{3,2,1,0:T(8,128)(2,1)}, u32[]{:S(2)}, u32[]{:S(2)}) collective-permute-start(bf16[2,32,128,128]{3,2,1,0:T(8,128)(2,1)} %get-tuple-element.477), channel_id=1, source_target_pairs={{0,1},{1,0},{2,3},{3,2},{4,5},{5,4},{6,7},{7,6}} | collective-permute-start | bytes 6291464 | tf_op jit(solution)/shard_map/while/body/ppermute | solution.py:609
  735.9 26.9 %collective-permute-start.11 = (bf16[2,24,128,128]{3,2,1,0:T(8,128)(2,1)}, bf16[2,24,128,128]{3,2,1,0:T(8,128)(2,1)}, u32[]{:S(2)}, u32[]{:S(2)}) collective-permute-start(bf16[2,24,128,128]{3,2,1,0:T(8,128)(2,1)} %get-tuple-element.480), channel_id=1, source_target_pairs={{0,1},{1,0},{2,3},{3,2},{4,5},{5,4},{6,7},{7,6}} | collective-permute-start | bytes 4718600 | tf_op jit(solution)/shard_map/while/body/ppermute | solution.py:612
  736.0 26.9 %collective-permute-start.7 = (bf16[32,128,128]{2,1,0:T(8,128)(2,1)}, bf16[32,128,128]{2,1,0:T(8,128)(2,1)}, u32[]{:S(2)}, u32[]{:S(2)}) collective-permute-start(bf16[32,128,128]{2,1,0:T(8,128)(2,1)} %get-tuple-element.478), channel_id=1, source_target_pairs={{0,2},{1,3},{2,6},{3,7},{6,4},{7,5},{4,0},{5,1}} | collective-permute-start | bytes 3145736 | tf_op jit(solution)/shard_map/while/body/ppermute | solution.py:607
  766.4 30.5 %collective-permute-start.5 = (bf16[2,24,128,128]{3,2,1,0:T(8,128)(2,1)}, bf16[2,24,128,128]{3,2,1,0:T(8,128)(2,1)}, u32[]{:S(2)}, u32[]{:S(2)}) collective-permute-start(bf16[2,24,128,128]{3,2,1,0:T(8,128)(2,1)} %get-tuple-element.516), channel_id=1, source_target_pairs={{0,1},{1,0},{2,3},{3,2},{4,5},{5,4},{6,7},{7,6}} | collective-permute-start | bytes 4718600 | tf_op jit(solution)/shard_map/while/body/ppermute | solution.py:612
  766.4 29.9 %collective-permute-start.4 = (bf16[32,128,128]{2,1,0:T(8,128)(2,1)}, bf16[32,128,128]{2,1,0:T(8,128)(2,1)}, u32[]{:S(2)}, u32[]{:S(2)}) collective-permute-start(bf16[32,128,128]{2,1,0:T(8,128)(2,1)} %get-tuple-element.519.rc1), channel_id=1, source_target_pairs={{0,1},{1,0},{2,3},{3,2},{4,5},{5,4},{6,7},{7,6}} | collective-permute-start | bytes 3145736 | tf_op jit(solution)/shard_map/while/body/ppermute | solution.py:611
  766.9 29.9 %collective-permute-start.3 = (bf16[32,128,128]{2,1,0:T(8,128)(2,1)}, bf16[32,128,128]{2,1,0:T(8,128)(2,1)}, u32[]{:S(2)}, u32[]{:S(2)}) collective-permute-start(bf16[32,128,128]{2,1,0:T(8,128)(2,1)} %get-tuple-element.518.rc0), channel_id=1, source_target_pairs={{0,1},{1,0},{2,3},{3,2},{4,5},{5,4},{6,7},{7,6}} | collective-permute-start | bytes 3145736 | tf_op jit(solution)/shard_map/while/body/ppermute | solution.py:610
  796.8 28.3 %collective-permute-start.6 = (bf16[2,32,128,128]{3,2,1,0:T(8,128)(2,1)}, bf16[2,32,128,128]{3,2,1,0:T(8,128)(2,1)}, u32[]{:S(2)}, u32[]{:S(2)}) collective-permute-start(bf16[2,32,128,128]{3,2,1,0:T(8,128)(2,1)} %get-tuple-element.477), channel_id=1, source_target_pairs={{0,1},{1,0},{2,3},{3,2},{4,5},{5,4},{6,7},{7,6}} | collective-permute-start | bytes 6291464 | tf_op jit(solution)/shard_map/while/body/ppermute | solution.py:609
  (126 other events, 1734.1 us)
where the time goes:
time: 846 us; the launch traced here: 841 us
  Pallas kernels  393 us (46%)
  waiting for transfers between devices  319 us (38%)
  starting transfers between devices  68.7 us (8%)
  local copies, waits for them, and re-layouts  50.8 us (6%)
  loops' own time  8.7 us (1%)
    ppermute x24, waiting for transfers between devices, one_round(): nrc1 = lax.ppermute(s1, 'dp', ccw)  284 us
    pallas_call x24, Pallas kernels, one_round(): pl.pallas_call(round_kernel, out_shape=(ST, chunk, chunk, both, cross, st...  210 us
    pallas_call x25, Pallas kernels, attend(): pl.pallas_call(functools.partial(attn_kernel, batches), out_shape=(ST, ca...  132 us
    while x84, local copies, waits for them, and re-layouts  45.5 us
    pallas_call x1, Pallas kernels, local(): pl.pallas_call(plan_kernel, out_shape=(sds((TAB,), i32), sds((SL,), i32))...  23.4 us
    ppermute x24, starting transfers between devices, one_round(): nrc1 = lax.ppermute(s1, 'dp', ccw)  23 us
    ppermute x24, starting transfers between devices, one_round(): nrc0 = lax.ppermute(s0, 'dp', cw)  22.1 us
    ppermute x24, waiting for transfers between devices, one_round(): npo0 = lax.ppermute(rc0, 'dp', swap)  17 us
  transfers between devices with their start and end apart: 148, of which 49 were waited for; matrix products, arithmetic and copies ran while one was open for 4% of the time, Pallas kernels for 41%

commit v1 on v0

v1 whole, which is shorter than its diff:
```python
import functools

import jax
import jax.numpy as jnp
from jax import lax
from jax.experimental import pallas as pl
from jax.experimental.pallas import tpu as pltpu
from jax.sharding import PartitionSpec as P


BP, SHIFT = 8, 3
SIZES = (64, 58, 52)
NX = 32
A = 4
SL = 32
BL = 64
WIDE = 272
S0, S1, R0, R1, XS, XR, FREE = range(7)
RDY, RDX, MLEN, SRC, ROUNDS = range(FREE * WIDE, FREE * WIDE + 200, 40)
CORE, PICK, DUMP = ROUNDS + 1, ROUNDS + 2, ROUNDS + 4
TAB = ROUNDS + 8
FWD, NONE = 2, 3
HALF = 1 << 16
FLOPS = 4000000
LOW = HALF - 1
U_PART, U_MERGE, U_OWN, U_POST, U_XS, U_XR = 0, 2, 4, 6, 8, 9
STEP, DONE, STATE = 24, 32, 64
END = HALF * HALF // 4
bf16 = jnp.bfloat16
f32 = jnp.float32
i32 = jnp.int32


def gray(c):
    return c ^ (c >> 1)


def lens_kernel(x, o, bsem, ssem, rsem):
    me = lax.axis_index('dp')
    barrier = pltpu.get_barrier_semaphore()
    for k in range(1, 8):
        pl.semaphore_signal(barrier, inc=1, device_id=(lax.rem(me + k, 8),), device_id_type=pl.DeviceIdType.MESH)
    pl.semaphore_wait(barrier, 7)
    here = pltpu.make_async_copy(x, o.at[me], bsem)
    here.start()
    sends = []
    for k in range(1, 8):
        c = pltpu.make_async_remote_copy(src_ref=x, dst_ref=o.at[me], send_sem=ssem.at[k], recv_sem=rsem.at[k],
                                         device_id=(lax.rem(me + k, 8),), device_id_type=pl.DeviceIdType.MESH)
        c.start()
        sends.append(c)
    here.wait()
    for c in sends:
        c.wait()


def plan_kernel(me_ref, dest_ref, len_ref, tab, lens_out, nbv, kindv, todo, load, hop, swap, addr, at):
    me = me_ref[0]
    zero = me * 0
    for i in range(9):
        for ref in (load, hop, swap):
            ref[i] = zero
    tab[CORE] = me & 1
    for j in range(SL):
        tab[RDY + j] = zero
        tab[RDX + j] = zero

    def first(i, n):
        size = len_ref[i >> 5, 0, i & 31]
        d = dest_ref[i]
        nb = (size + (BP - 1)) >> SHIFT
        ra = gray(i >> 6)
        delta = (gray(d >> 6) - ra) & 3
        nbv[i] = nb
        kindv[i] = delta
        slot = jnp.where(delta == 1, ra, jnp.where(delta == 3, 4 + ra, 8))
        load[slot] = load[slot] + nb + HALF
        todo[n] = i
        cross = (delta == 0) & ((i >> 5) != (d >> 5))
        xslot = jnp.where(cross, i >> 5, 8)
        swap[xslot] = swap[xslot] + nb
        mine = jnp.where((d >> 5) == me, d & 31, SL)
        tab[MLEN + mine] = size
        tab[SRC + mine] = jnp.where((i >> 5) == me, i & 31, -1)
        return n + jnp.where(delta == 2, 1, 0)

    far = lax.fori_loop(0, 8 * SL, first, zero, unroll=4)

    def lens(j, c):
        lens_out[j] = tab[MLEN + j] + 1
        return c

    lax.fori_loop(0, SL, lens, 0, unroll=8)

    def choose(n, c):
        i = todo[n]
        nb = nbv[i]
        ra = gray(i >> 6)
        a1, a2, b1, b2 = ra, (ra + 1) & 3, 4 + ra, 4 + ((ra - 1) & 3)
        la1, la2, lb1, lb2 = load[a1] & LOW, load[a2] & LOW, load[b1] & LOW, load[b2] & LOW
        la, lb = jnp.maximum(la1, la2), jnp.maximum(lb1, lb2)
        cw = (la < lb) | ((la == lb) & (la1 + la2 <= lb1 + lb2))
        x1, x2 = jnp.where(cw, a1, b1), jnp.where(cw, a2, b2)
        load[x1] = load[x1] + nb + HALF
        load[x2] = load[x2] + nb + HALF
        hop[x1] = hop[x1] + nb + HALF
        kindv[i] = jnp.where(cw, 2, 4)
        return c

    lax.fori_loop(0, far, choose, 0)

    def link(d, x, size):
        fwd = hop[4 * d + ((x - 1 + 2 * d) & 3)]
        own = load[4 * d + x] - fwd
        start = jnp.where(fwd > 0, jnp.maximum(own & LOW, 2 * size), own & LOW)
        return own, fwd, start

    cross = zero
    for d in range(8):
        cross = jnp.maximum(cross, (swap[d] + NX - 1) // NX)
    best, pick, turns, chunk = zero + END, zero, zero, zero
    for o, size in enumerate(SIZES):
        longest = zero
        for d in range(2):
            for x in range(4):
                _, fwd, start = link(d, x, size)
                longest = jnp.maximum(longest, start + (fwd & LOW))
        rounds = (jnp.maximum((longest + size - 1) // size, cross) + 1) & -2
        price = rounds * (size + BP // 2)
        better = price < best
        best, pick, turns, chunk = [jnp.where(better, n, o) for n, o in (
            (price, best), (o, pick), (rounds, turns), (size, chunk))]
    tab[ROUNDS] = turns
    tab[PICK] = pick

    x0 = gray(me >> 1)
    left, right, opposite = (x0 - 1) & 3, (x0 + 1) & 3, (x0 + 2) & 3
    for lid, d, x in ((S0, 0, x0), (S1, 1, x0), (R0, 0, left), (R1, 1, right)):
        own, fwd, start = link(d, x, chunk)
        near = hop[4 * d + x]
        base = lid * WIDE
        pad = base + 2 * (own >> 16)
        last = pad + 2 + 2 * (fwd >> 16)
        tab[pad] = start - (own & LOW)
        tab[last] = zero + END
        for a in (pad, last):
            tab[a + 1] = zero + NONE * HALF
        for k, (where, pos) in enumerate(((base, 0), (base + 2 * (near >> 16), near & LOW), (pad + 2, start))):
            addr[3 * lid + k] = zero + where
            at[3 * lid + k] = zero + pos
    addr[12] = zero + DUMP
    at[12] = zero

    def append(seg, hit, nb, code):
        seg = jnp.where(hit, seg, 12)
        a, p = addr[seg], at[seg]
        tab[a] = nb
        tab[a + 1] = code
        addr[seg] = a + jnp.where(hit, 2, 0)
        at[seg] = p + nb
        return p + nb

    def source(s, c):
        i = (me >> 1) * 2 * SL + s
        kind = kindv[i]
        seg = jnp.where(kind < 3, 2 - kind, 7 - kind)
        append(seg, kind > 0, nbv[i], ((s >> 5) << 16) + (s & 31) * BL)
        return c

    lax.fori_loop(0, 2 * SL, source, 0, unroll=4)

    def arrive(seg, hit, i):
        dst = dest_ref[i]
        end = append(seg, hit, nbv[i], (((dst >> 5) & 1) << 16) + (dst & 31) * BL)
        mine = hit & ((dst >> 5) == me)
        tab[RDY + jnp.where(mine, dst & 31, SL)] = end

    for d, x in ((0, left), (1, right)):
        def upstream(s, c):
            i = gray(x) * 2 * SL + s
            kind = kindv[i]
            hit = kind == 2 + 2 * d
            code = FWD * HALF + at[6 + 3 * d]
            append(6 + 3 * d, hit, nbv[i], code)
            append(2 + 3 * d, hit, nbv[i], code)
            arrive(7 + 3 * d, kind == 1 + 2 * d, i)
            return c

        lax.fori_loop(0, 2 * SL, upstream, 0, unroll=2)

    def across(s, c):
        i = gray(opposite) * 2 * SL + s
        kind = kindv[i]
        arrive(jnp.where(kind == 2, 8, 11), (kind == FWD) | (kind == 4), i)
        return c

    lax.fori_loop(0, 2 * SL, across, 0, unroll=2)

    for lid, sender, receiver in ((XS, me, me ^ 1), (XR, me ^ 1, me)):
        def cross_list(s, c):
            a, pos = c
            i = sender * SL + s
            nb = nbv[i]
            dst = dest_ref[i]
            hit = (dst >> 5) == receiver
            tab[a] = nb
            tab[a + 1] = (s if lid == XS else dst & 31) * BL
            pos = pos + jnp.where(hit, nb, 0)
            if lid == XR:
                tab[RDX + jnp.where(hit, dst & 31, SL)] = pos
            return a + jnp.where(hit, 2, 0), pos

        a, _ = lax.fori_loop(0, SL, cross_list, (zero + lid * WIDE, zero), unroll=2)
        tab[a] = zero + END
        tab[a + 1] = zero + NONE * HALF


class Mover:
    def __init__(self, tab, st_in, st, size):
        self.tab, self.st, self.size = tab, st, size
        self.core = tab[CORE]

        def cp(i, _):
            st[i] = st_in[i]
            return 0

        lax.fori_loop(0, STATE, cp, 0)

    def walk(self, lid, use, n, fn):
        tab, st = self.tab, self.st
        base = lid * WIDE

        def body(c):
            p, item, off, cnt = c
            width = tab[base + 2 * item]
            code = tab[base + 2 * item + 1]
            take = jnp.minimum(n - p, width - off)
            cnt = cnt + fn(p, take, code >> 16, (code & LOW) + off)
            off = off + take
            adv = off >= width
            return p + take, jnp.where(adv, item + 1, item), jnp.where(adv, 0, off), cnt

        c0 = (jnp.int32(0), st[2 * use], st[2 * use + 1], jnp.int32(0))
        _, item, off, cnt = lax.while_loop(lambda c: c[0] < n, body, c0)
        st[2 * use] = item
        st[2 * use + 1] = off
        return cnt

    @staticmethod
    def drain(cnt, ref, sem):
        @pl.when(cnt > 0)
        def _():
            part = ref.at[pl.ds(0, cnt)]
            pltpu.make_async_copy(part, part, sem).wait()

    def partial(self, d, kc, vc, buf, sem):
        core = self.core

        def fn(p, take, kind, idx):
            mine = kind == core

            @pl.when(mine & (core == 0))
            def _():
                pltpu.make_async_copy(vc.at[pl.ds(idx, take)], buf.at[d, pl.ds(p, take)], sem).start()

            @pl.when(mine & (core == 1))
            def _():
                pltpu.make_async_copy(kc.at[pl.ds(idx, take)], buf.at[d, pl.ds(p, take)], sem).start()

            return jnp.where(mine, take, 0)

        return self.walk(S0 + d, U_PART + d, self.size, fn)

    def merge(self, d, kc, vc, pre, fwd, buf, sem):
        core = self.core

        def fn(p, take, kind, idx):
            mine = kind == core

            @pl.when(mine & (core == 0))
            def _():
                pltpu.make_async_copy(kc.at[pl.ds(idx, take)], buf.at[d, pl.ds(p, take)], sem).start()

            @pl.when(mine & (core == 1))
            def _():
                pltpu.make_async_copy(vc.at[pl.ds(idx, take)], buf.at[d, pl.ds(p, take)], sem).start()

            @pl.when(kind == 1 - core)
            def _():
                pltpu.make_async_copy(pre.at[d, pl.ds(p, take)], buf.at[d, pl.ds(p, take)], sem).start()

            if fwd is not None:
                @pl.when(kind == FWD)
                def _():
                    pltpu.make_async_copy(fwd.at[pl.ds(idx, take)], buf.at[d, pl.ds(p, take)], sem).start()
            return jnp.where(kind < NONE, take, 0)

        return self.walk(S0 + d, U_MERGE + d, self.size, fn)

    def cross_send(self, kc, vc, buf, sem):
        def fn(p, take, kind, idx):
            @pl.when(kind == 0)
            def _():
                pltpu.make_async_copy(kc.at[pl.ds(idx, take)], buf.at[0, pl.ds(p, take)], sem).start()
                pltpu.make_async_copy(vc.at[pl.ds(idx, take)], buf.at[1, pl.ds(p, take)], sem).start()

            return jnp.where(kind == 0, 2 * take, 0)

        return self.walk(XS, U_XS, NX, fn)

    def cross_recv(self, n, ko, vo, buf, sem):
        def fn(p, take, kind, idx):
            @pl.when(kind == 0)
            def _():
                pltpu.make_async_copy(buf.at[0, pl.ds(p, take)], ko.at[pl.ds(idx, take)], sem).start()
                pltpu.make_async_copy(buf.at[1, pl.ds(p, take)], vo.at[pl.ds(idx, take)], sem).start()

            return jnp.where(kind == 0, 2 * take, 0)

        return self.walk(XR, U_XR, n, fn)

    def unpack(self, d, use, n, flip, ko, vo, fwd, buf, sem):
        core = self.core
        plane = 1 - core if flip else core

        def fn(p, take, kind, idx):
            mine = kind == core

            @pl.when(mine & (plane == 0))
            def _():
                pltpu.make_async_copy(buf.at[d, pl.ds(p, take)], ko.at[pl.ds(idx, take)], sem).start()

            @pl.when(mine & (plane == 1))
            def _():
                pltpu.make_async_copy(buf.at[d, pl.ds(p, take)], vo.at[pl.ds(idx, take)], sem).start()

            cnt = jnp.where(mine, take, 0)
            if fwd is not None:
                @pl.when(kind == FWD)
                def _():
                    pltpu.make_async_copy(buf.at[d, pl.ds(p, take)], fwd.at[pl.ds(idx, take)], sem).start()

                cnt = cnt + jnp.where(kind == FWD, take, 0)
            return cnt

        return self.walk(R0 + d, use + d, n, fn)


def open_kernel(NB, tab, st_in, kc, vc, st, part0, part1, dxs, vpart, vdx, sem):
    mv = Mover(tab, st_in, st, NB)
    outs = [pltpu.make_async_copy(vpart.at[0], part0, sem.at[0]),
            pltpu.make_async_copy(vpart.at[1], part1, sem.at[1]),
            pltpu.make_async_copy(vdx, dxs, sem.at[2])]
    cnt = [mv.partial(0, kc, vc, vpart.at[c], sem.at[c]) + mv.partial(1, kc, vc, vpart.at[c], sem.at[c]) for c in range(2)]
    cnt.append(mv.cross_send(kc, vc, vdx, sem.at[2]))
    for c in range(3):
        mv.drain(cnt[c], kc, sem.at[c])
        outs[c].start()
    for c in outs:
        c.wait()


def open_merge_kernel(NB, tab, st_in, kc, vc, pre, st, send0, send1, part, vsend, vpart, sem):
    mv = Mover(tab, st_in, st, NB)
    c0 = mv.merge(0, kc, vc, pre, None, vsend, sem.at[0])
    c1 = mv.merge(1, kc, vc, pre, None, vsend, sem.at[1])
    c2 = mv.partial(0, kc, vc, vpart, sem.at[2]) + mv.partial(1, kc, vc, vpart, sem.at[2])
    mv.drain(c0, kc, sem.at[0])
    mv.drain(c1, kc, sem.at[1])
    mv.drain(c2, kc, sem.at[2])
    outs = [pltpu.make_async_copy(vsend.at[0], send0, sem.at[0]),
            pltpu.make_async_copy(vsend.at[1], send1, sem.at[1]),
            pltpu.make_async_copy(vpart, part, sem.at[2])]
    for c in outs:
        c.start()
    for c in outs:
        c.wait()


def round_kernel(NB, tab, st_in, kc, vc, pre, rc0, rc1, po0, po1, dxr, f0i, f1i, koi, voi,
                 st, send0, send1, part, dxs, f0, f1, ko, vo,
                 vsend, vpart, vrecv, vpost, vdxs, vdxr, sem):
    mv = Mover(tab, st_in, st, NB)
    r = st_in[STEP]
    st[STEP] = r + 1
    ins = [pltpu.make_async_copy(rc0, vrecv.at[0], sem.at[0]),
           pltpu.make_async_copy(rc1, vrecv.at[1], sem.at[1]),
           pltpu.make_async_copy(po0, vpost.at[0], sem.at[2]),
           pltpu.make_async_copy(po1, vpost.at[1], sem.at[3]),
           pltpu.make_async_copy(dxr, vdxr, sem.at[4])]
    for c in ins:
        c.start()
    n1 = jnp.where(r >= 1, NB, 0)
    n2 = jnp.where(r >= 2, NB, 0)
    nx = jnp.where(r >= 1, NX, 0)
    cp = mv.partial(0, kc, vc, vpart, sem.at[5]) + mv.partial(1, kc, vc, vpart, sem.at[5])
    cx = mv.cross_send(kc, vc, vdxs, sem.at[6])
    ins[0].wait()
    o0 = mv.unpack(0, U_OWN, n1, False, ko, vo, f0, vrecv, sem.at[7])
    ins[1].wait()
    o1 = mv.unpack(1, U_OWN, n1, False, ko, vo, f1, vrecv, sem.at[7])
    mv.drain(o0 + o1, kc, sem.at[7])
    c0 = mv.merge(0, kc, vc, pre, f0, vsend, sem.at[8])
    c1 = mv.merge(1, kc, vc, pre, f1, vsend, sem.at[9])
    ins[2].wait()
    ins[3].wait()
    o2 = mv.unpack(0, U_POST, n2, True, ko, vo, None, vpost, sem.at[7])
    o3 = mv.unpack(1, U_POST, n2, True, ko, vo, None, vpost, sem.at[7])
    ins[4].wait()
    o4 = mv.cross_recv(nx, ko, vo, vdxr, sem.at[7])
    mv.drain(cp, kc, sem.at[5])
    mv.drain(cx, kc, sem.at[6])
    mv.drain(c0, kc, sem.at[8])
    mv.drain(c1, kc, sem.at[9])
    outs = [pltpu.make_async_copy(vsend.at[0], send0, sem.at[0]),
            pltpu.make_async_copy(vsend.at[1], send1, sem.at[1]),
            pltpu.make_async_copy(vpart, part, sem.at[2]),
            pltpu.make_async_copy(vdxs, dxs, sem.at[3])]
    for c in outs:
        c.start()
    mv.drain(o2 + o3 + o4, kc, sem.at[7])
    for c in outs:
        c.wait()


def close_kernel(NB, last, tab, st_in, *refs):
    if last:
        (po0, po1, koi, voi, st, ko, vo, vpost, sem) = refs
    else:
        (rc0, rc1, po0, po1, dxr, koi, voi, st, ko, vo, vpost, vrecv, vdxr, sem) = refs
    mv = Mover(tab, st_in, st, NB)
    r = st_in[STEP]
    st[STEP] = r + 1
    ins = [pltpu.make_async_copy(po0, vpost.at[0], sem.at[0]),
           pltpu.make_async_copy(po1, vpost.at[1], sem.at[1])]
    if not last:
        ins += [pltpu.make_async_copy(rc0, vrecv.at[0], sem.at[2]),
                pltpu.make_async_copy(rc1, vrecv.at[1], sem.at[3]),
                pltpu.make_async_copy(dxr, vdxr, sem.at[4])]
    for c in ins:
        c.start()
    n1 = jnp.where(r >= 1, NB, 0)
    n2 = jnp.where(r >= 2, NB, 0)
    nx = jnp.where(r >= 1, NX, 0)
    for c in ins:
        c.wait()
    cnt = mv.unpack(0, U_POST, n2, True, ko, vo, None, vpost, sem.at[5])
    cnt += mv.unpack(1, U_POST, n2, True, ko, vo, None, vpost, sem.at[5])
    if not last:
        cnt += mv.unpack(0, U_OWN, n1, False, ko, vo, None, vrecv, sem.at[5])
        cnt += mv.unpack(1, U_OWN, n1, False, ko, vo, None, vrecv, sem.at[5])
        cnt += mv.cross_recv(nx, ko, vo, vdxr, sem.at[5])
    mv.drain(cnt, ko, sem.at[5])


def attn_kernel(NB, batches, tab, st_in, q, kn, vn, kc, vc, koi, voi, aoi, st, ko, vo, ao,
                kb, vb, ob, sel, lsem, wsem, osem):
    def cp(i, _):
        st[i] = st_in[i]
        return 0

    lax.fori_loop(0, STATE, cp, 0)
    link_end = jnp.maximum((st_in[STEP] - 2) * NB, 0)
    swap_end = jnp.maximum((st_in[STEP] - 1) * NX, 0)

    def load(a, j):
        s = tab[SRC + j]

        @pl.when(s >= 0)
        def _():
            pltpu.make_async_copy(kc.at[pl.ds(s * BL, BL)], kb.at[a], lsem.at[a]).start()
            pltpu.make_async_copy(vc.at[pl.ds(s * BL, BL)], vb.at[a], lsem.at[a]).start()

        @pl.when(s < 0)
        def _():
            pltpu.make_async_copy(ko.at[pl.ds(j * BL, BL)], kb.at[a], lsem.at[a]).start()
            pltpu.make_async_copy(vo.at[pl.ds(j * BL, BL)], vb.at[a], lsem.at[a]).start()

    def compute(a, j):
        pltpu.make_async_copy(kb.at[a], kb.at[a], lsem.at[a]).wait()
        pltpu.make_async_copy(vb.at[a], vb.at[a], lsem.at[a]).wait()
        m = tab[MLEN + j]
        s = tab[SRC + j]
        b0 = m >> SHIFT
        row = lax.broadcasted_iota(i32, BLOCK, 0) >> 3
        for buf, new in ((kb, kn), (vb, vn)):
            x = buf[a, b0].astype(f32)
            fresh = jnp.concatenate([new[j].astype(f32)] * BP, axis=0)
            t = b0 * BP + row
            buf[a, b0] = jnp.where(t < m, x, jnp.where(t == m, fresh, 0.0)).astype(bf16)

        def wipe(b, _):
            kb[a, b] = jnp.zeros(BLOCK, bf16)
            vb[a, b] = jnp.zeros(BLOCK, bf16)
            return 0

        lax.fori_loop(b0 + 1, BL, wipe, 0)
        kf = kb[a].reshape(-1, 128)
        vf = vb[a].reshape(-1, 128)
        sc = lax.dot_general(q[j], kf, (((1,), (1,)), ((), ())), preferred_element_type=f32) * (128 ** -0.5)
        col = lax.broadcasted_iota(i32, sc.shape, 1)
        head = lax.broadcasted_iota(i32, sc.shape, 0) // 3
        ok = ((col & 7) == head) & ((col >> 3) <= m)
        sc = jnp.where(ok, sc, -1e30)
        top = jnp.max(sc, axis=1, keepdims=True)
        w = jnp.exp(sc - top)
        tot = jnp.sum(w, axis=1, keepdims=True)
        acc = lax.dot_general(w.astype(bf16), vf, (((1,), (0,)), ((), ())), preferred_element_type=f32)
        ob[a] = (acc / tot).astype(bf16)
        bw = jnp.where(s >= 0, 0, b0)

        tail = pl.ds(bw, BL - bw)
        home = pl.ds(j * BL + bw, BL - bw)
        pltpu.make_async_copy(kb.at[a, tail], ko.at[home], wsem.at[0]).start()
        pltpu.make_async_copy(vb.at[a, tail], vo.at[home], wsem.at[0]).start()
        pltpu.make_async_copy(ob.at[a], ao.at[j], osem.at[0]).start()
        return 2 * (BL - bw)

    def batch(_, c):
        def pick(j, n):
            hit = (st[DONE + j] == 0) & (tab[RDY + j] <= link_end) & (tab[RDX + j] <= swap_end) & (n < A)
            sel[jnp.where(hit, n, A)] = j
            st[DONE + j] = jnp.where(hit, 1, st[DONE + j])
            return n + jnp.where(hit, 1, 0)

        n = lax.fori_loop(0, SL, pick, jnp.int32(0))

        def loads(a, _):
            load(a, sel[a])
            return 0

        lax.fori_loop(0, n, loads, 0)

        def computes(a, cnt):
            return cnt + compute(a, sel[a])

        cnt = lax.fori_loop(0, n, computes, jnp.int32(0))

        @pl.when(n > 0)
        def _():
            done = ko.at[pl.ds(0, cnt)]
            pltpu.make_async_copy(done, done, wsem.at[0]).wait()
            rows = ob.at[pl.ds(0, n)]
            pltpu.make_async_copy(rows, rows, osem.at[0]).wait()

        return c

    lax.fori_loop(0, batches, batch, 0)


SMEM = pl.BlockSpec(memory_space=pltpu.SMEM)
VMEM = pl.BlockSpec(memory_space=pltpu.VMEM)
ANY = pl.BlockSpec(memory_space=pl.ANY)
BLOCK = (8 * BP, 128)


def sds(shape, dtype=bf16):
    return jax.ShapeDtypeStruct(shape, dtype)


def dma(n):
    return pltpu.SemaphoreType.DMA((n,))


def buf(*lead):
    return pltpu.VMEM(lead + BLOCK, bf16)


def cost(us):
    return pl.CostEstimate(flops=us * FLOPS, bytes_accessed=us * FLOPS, transcendentals=0)


ST = sds((STATE,), i32)


def solution(mesh):
    group = mesh.shape['dp']
    ring = [0, 1, 3, 2]
    cw = [(ring[k] * 2 + c, ring[(k + 1) % 4] * 2 + c) for k in range(4) for c in range(2)]
    ccw = [(b, a) for a, b in cw]
    swap = [(d, d ^ 1) for d in range(group)]

    def local(query, k_cache, v_cache, cache_lens, dest_slot, k_new, v_new):
        kc = k_cache.reshape((SL * BL,) + BLOCK)
        vc = v_cache.reshape((SL * BL,) + BLOCK)
        lens_all = pl.pallas_call(
            lens_kernel, out_shape=sds((8, 1, SL), i32), in_specs=[VMEM], out_specs=VMEM,
            scratch_shapes=[pltpu.SemaphoreType.DMA, dma(8), dma(8)],
            compiler_params=pltpu.CompilerParams(collective_id=0, has_side_effects=True),
            name='lens')(cache_lens.reshape(1, SL))
        me = jnp.full((1,), lax.axis_index('dp'), i32)
        tab, lens_out = pl.pallas_call(
            plan_kernel, out_shape=(sds((TAB,), i32), sds((SL,), i32)), in_specs=[SMEM] * 3, out_specs=(SMEM, SMEM),
            scratch_shapes=[pltpu.SMEM((8 * SL + 1,), i32)] * 3 + [pltpu.SMEM((16,), i32)] * 5,
            name='plan')(me, dest_slot, lens_all)

        def run(NB):
            def nothing(*refs):
                pass

            chunk, both, cross = sds((NB,) + BLOCK), sds((2, NB) + BLOCK), sds((2, NX) + BLOCK)
            cache, store = sds((SL * BL,) + BLOCK), sds((2 * SL * BL,) + BLOCK)
            ko, vo, ao, f0, f1, rc0, rc1, po0, po1, dxr = pl.pallas_call(
                nothing, out_shape=(cache, cache, sds((SL, 24, 128)), store, store, chunk, chunk, chunk, chunk, cross),
                out_specs=(ANY,) * 10, name='blank')()

            st = jnp.zeros((STATE,), i32)
            st, part0, part1, dxs = pl.pallas_call(
                functools.partial(open_kernel, NB), out_shape=(ST, both, both, cross), in_specs=[SMEM, SMEM, ANY, ANY], out_specs=(SMEM, ANY, ANY, ANY),
                scratch_shapes=[buf(2, 2, NB), buf(2, NX), dma(3)], name='open')(tab, st, kc, vc)
            pre0 = lax.ppermute(part0, 'dp', swap)
            pre = lax.ppermute(part1, 'dp', swap)
            st, s0, s1, part = pl.pallas_call(
                functools.partial(open_merge_kernel, NB), out_shape=(ST, chunk, chunk, both), in_specs=[SMEM, SMEM, ANY, ANY, ANY],
                out_specs=(SMEM, ANY, ANY, ANY), scratch_shapes=[buf(2, NB), buf(2, NB), dma(3)],
                name='open_merge')(tab, st, kc, vc, pre0)

            def attend(st, ko, vo, ao, batches):
                return pl.pallas_call(
                    functools.partial(attn_kernel, NB, batches),
                    out_shape=(ST, cache, cache, sds((SL, 24, 128))),
                    in_specs=[SMEM, SMEM, VMEM, VMEM, VMEM, ANY, ANY, ANY, ANY, ANY], out_specs=(SMEM, ANY, ANY, ANY),
                    input_output_aliases={7: 1, 8: 2, 9: 3},
                    scratch_shapes=[buf(A, BL), buf(A, BL), pltpu.VMEM((A, 24, 128), bf16), pltpu.SMEM((A + 1,), i32),
                                    dma(A), dma(1), dma(1)],
                    cost_estimate=cost(6), name='attend')(tab, st, query, k_new, v_new, kc, vc, ko, vo, ao)

            def one_round(tag, c):
                st, s0, s1, part, dxs, pre, rc0, rc1, po0, po1, dxr, f0, f1, ko, vo, ao = c
                nrc0 = lax.ppermute(s0, 'dp', cw)
                nrc1 = lax.ppermute(s1, 'dp', ccw)
                npre = lax.ppermute(part, 'dp', swap)
                npo0 = lax.ppermute(rc0, 'dp', swap)
                npo1 = lax.ppermute(rc1, 'dp', swap)
                ndxr = lax.ppermute(dxs, 'dp', swap)
                st, s0, s1, part, dxs, f0, f1, ko, vo = pl.pallas_call(
                    functools.partial(round_kernel, NB), out_shape=(ST, chunk, chunk, both, cross, store, store, cache, cache),
                    in_specs=[SMEM, SMEM] + [ANY] * 12, out_specs=(SMEM,) + (ANY,) * 8,
                    input_output_aliases={10: 5, 11: 6, 12: 7, 13: 8},
                    scratch_shapes=[buf(2, NB)] * 4 + [buf(2, NX)] * 2 + [dma(10)],
                    cost_estimate=cost(10), name='round')(tab, st, kc, vc, pre, rc0, rc1, po0, po1, dxr, f0, f1, ko, vo)
                st, ko, vo, ao = attend(st, ko, vo, ao, 1)
                if tag == 'ra':
                    s0, s1, npo0, npo1 = lax.optimization_barrier((s0, s1, npo0, npo1))
                return st, s0, s1, part, dxs, npre, nrc0, nrc1, npo0, npo1, ndxr, f0, f1, ko, vo, ao

            rounds = tab[ROUNDS]

            def body(c):
                return (c[0] + 2,) + one_round('rb', one_round('ra', c[1:]))

            c = lax.while_loop(lambda c: c[0] < rounds, body,
                           (jnp.int32(0), st, s0, s1, part, dxs, pre, rc0, rc1, po0, po1, dxr, f0, f1, ko, vo, ao))
            _, st, _, _, _, _, _, rc0, rc1, po0, po1, dxr, _, _, ko, vo, ao = c

            def close(last, st, ko, vo, *ins):
                n = len(ins)
                extra = [] if last else [buf(2, NB), buf(2, NX)]
                return pl.pallas_call(
                    functools.partial(close_kernel, NB, last), out_shape=(ST, cache, cache),
                    in_specs=[SMEM, SMEM] + [ANY] * (n + 2), out_specs=(SMEM, ANY, ANY),
                    input_output_aliases={n + 2: 1, n + 3: 2},
                    scratch_shapes=[buf(2, NB)] + extra + [dma(6)],
                    name='close_last' if last else 'close')(tab, st, *ins, ko, vo)

            lpo0 = lax.ppermute(rc0, 'dp', swap)
            lpo1 = lax.ppermute(rc1, 'dp', swap)
            st, ko, vo = close(False, st, ko, vo, rc0, rc1, po0, po1, dxr)
            st, ko, vo = close(True, st, ko, vo, lpo0, lpo1)
            st, ko, vo, ao = attend(st, ko, vo, ao, SL // A)
            return ao, ko, vo

        ao, ko, vo = lax.switch(tab[PICK], [functools.partial(run, size) for size in SIZES])
        return ao, ko.reshape(k_cache.shape), vo.reshape(v_cache.shape), lens_out

    row_spec = P('dp')
    return jax.shard_map(local, mesh=mesh, in_specs=(row_spec, row_spec, row_spec, row_spec, P(), row_spec, row_spec),
                         out_specs=(row_spec, row_spec, row_spec, row_spec), check_vma=False)
```

time: 846 us -> 860 us (1.017)
  waiting for transfers between devices: 319 us -> 282 us
  starting transfers between devices: 68.7 us -> 101 us
  Pallas kernels: 393 us -> 407 us
    ppermute x24 -> x28, waiting for transfers between devices: 284 us -> 249 us  [one_round(): nrc1 = lax.ppermute(s1, 'dp', ccw)]
    pallas_call x55 -> x63, Pallas kernels: 370 us -> 395 us  [the longest x28 220 us: one_round(): pl.pallas_call(functools.partial(round_kernel, NB), out_shape=(ST, chunk,...]
    pallas_call x1, Pallas kernels: 23.4 us -> 12.3 us  [local(): pl.pallas_call(plan_kernel, out_shape=(sds((TAB,), i32), sds((SL,), i32))...]
    ppermute x24 -> x28, starting transfers between devices: 23 us -> 34 us  [one_round(): nrc1 = lax.ppermute(s1, 'dp', ccw)]
    ppermute x24 -> x28, starting transfers between devices: 22.1 us -> 31.8 us  [one_round(): nrc0 = lax.ppermute(s0, 'dp', cw)]
    while x84 -> x98, local copies, waits for them, and re-layouts: 45.5 us -> 46.7 us
  transfers between devices with their start and end apart: 148 -> 172, of which waited for: 49 -> 41; matrix products, arithmetic and copies ran while one was open for 4% -> 4% of each run, Pallas kernels for 41% -> 43%
where the time goes in v1:
time: 860 us; the launch traced here: 854 us
  Pallas kernels  407 us (47%)
  waiting for transfers between devices  282 us (33%)
  starting transfers between devices  101 us (12%)
  local copies, waits for them, and re-layouts  50.7 us (6%)
  loops' own time  12 us (1%)
    ppermute x28, waiting for transfers between devices, one_round(): nrc1 = lax.ppermute(s1, 'dp', ccw)  249 us
    pallas_call x28, Pallas kernels, one_round(): pl.pallas_call(functools.partial(round_kernel, NB), out_shape=(ST, chunk,...  220 us
    pallas_call x29, Pallas kernels, attend(): pl.pallas_call(functools.partial(attn_kernel, NB, batches), out_shape=(ST...  148 us
    while x98, local copies, waits for them, and re-layouts  46.7 us
    ppermute x28, starting transfers between devices, one_round(): nrc1 = lax.ppermute(s1, 'dp', ccw)  34 us
    ppermute x28, starting transfers between devices, one_round(): nrc0 = lax.ppermute(s0, 'dp', cw)  31.8 us
  transfers between devices with their start and end apart: 172, of which 41 were waited for; matrix products, arithmetic and copies ran while one was open for 4% of the time, Pallas kernels for 43%

profile of v1, /device:TPU:0, one launch (start us, length us, event | category | flops | bytes accessed | tf_op | source)
XLA Modules:
  0.0 854.0 jit_solution(12805778580179790798)
XLA Ops:
  0.6 7.8 lens.1.len_ref
  8.4 12.3 %plan.1 = (s32[1800]{0:T(1024)S(1)}, s32[32]{0:T(128)}) custom-call(s32[1]{0:T(128)} %bitcast.3.me_ref, s32[256]{0:T(256)} %dest_ref.1, s32[8,1,32]{2,1,0:T(1,128)} %lens.1.len_ref), custom_call_target="tpu_custom_call" | custom-call | tf_op jit(solution)/shard_map/plan/pallas_call | solution.py:592
  22.0 832.1 %conditional.1 = (bf16[32,24,128]{2,1,0:T(8,128)(2,1)}, bf16[2048,64,128]{2,1,0:T(8,128)(2,1)}, bf16[2048,64,128]{2,1,0:T(8,128)(2,1)}) conditional(s32[]{:T(128)} %bitcast.5, (s32[1800]{0:T(1024)S(1)}, bf16[2048,64,128]{2,1,0:T(8,128)(2,1)}, bf16[2048,64,128]{2,1,0:T(8,128)(2,1)}, bf16[32,24,128]{2,1,0:T(8,128)(2,1)}, ...), branch_computations={%region_0.0_spmd, %region_3.0_spmd, %region_6.0_spmd} | conditional | flops 152000000 | bytes 272849984 | solution.py:673
  32.8 5.5 open_merge.5
  38.3 798.0 %while.119 = (s32[]{:T(128)}, s32[64]{0:T(128)S(1)}, bf16[52,64,128]{2,1,0:T(8,128)(2,1)}, bf16[52,64,128]{2,1,0:T(8,128)(2,1)}, bf16[2,52,64,128]{3,2,1,0:T(8,1...) while((s32[]{:T(128)}, s32[64]{0:T(128)S(1)}, ...), condition=%wide.region_8.0_spmd, body=%wide.region_7.0_spmd.sunk | while | flops 128000000 | bytes 192619248 | solution.py:652
  41.6 18.7 %collective-permute-done.2.rc1 = bf16[52,64,128]{2,1,0:T(8,128)(2,1)} collective-permute-done((bf16[52,64,128]{2,1,0:T(8,128)(2,1)}, bf16[52,64,128]{2,1,0:T(8,128)(2,1)}, u32[]{:S(2)}, u32[]{:S(2)}) %collective-permute-start.2) | collective-permute-done | bytes 852000 | tf_op jit(solution)/shard_map/cond/branch_2_fun/while/body/ppermute | solution.py:631
  61.5 7.1 round.6
  72.2 6.7 attend.12
  82.3 8.4 round.7
  102.6 18.8 %collective-permute-done.2.rc1 = bf16[52,64,128]{2,1,0:T(8,128)(2,1)} collective-permute-done((bf16[52,64,128]{2,1,0:T(8,128)(2,1)}, bf16[52,64,128]{2,1,0:T(8,128)(2,1)}, u32[]{:S(2)}, u32[]{:S(2)}) %collective-permute-start.2) | collective-permute-done | bytes 852000 | tf_op jit(solution)/shard_map/cond/branch_2_fun/while/body/ppermute | solution.py:631
  123.2 8.1 round.6
  144.2 8.7 %round.7 = (s32[64]{0:T(128)}, bf16[52,64,128]{2,1,0:T(8,128)(2,1)}, bf16[52,64,128]{2,1,0:T(8,128)(2,1)}, bf16[2,52,64,128]{3,2,1,0:T(8,128)(2,1)}, bf16[2,32,6...) custom-call(s32[1800]{0:T(1024)S(1)} %get-tuple-element.1462.tab, ...), custom_call_target="tpu_custom_call", output_to_operand_aliasing={{5}: (10, {}), {6}: (11, {}), {7}: (12, {}), {8}: (13, {})} | custom-call | flops 40000000 | bytes 40000000 | tf_op jit(solution)/shard_map/cond/branch_2_fun/while/body/round/pallas_call | solution.py:636
  160.0 16.8 %collective-permute-done.2.rc1 = bf16[52,64,128]{2,1,0:T(8,128)(2,1)} collective-permute-done((bf16[52,64,128]{2,1,0:T(8,128)(2,1)}, bf16[52,64,128]{2,1,0:T(8,128)(2,1)}, u32[]{:S(2)}, u32[]{:S(2)}) %collective-permute-start.2) | collective-permute-done | bytes 852000 | tf_op jit(solution)/shard_map/cond/branch_2_fun/while/body/ppermute | solution.py:631
  179.6 8.1 round.6
  199.0 8.7 %round.7 = (s32[64]{0:T(128)}, bf16[52,64,128]{2,1,0:T(8,128)(2,1)}, bf16[52,64,128]{2,1,0:T(8,128)(2,1)}, bf16[2,52,64,128]{3,2,1,0:T(8,128)(2,1)}, bf16[2,32,6...) custom-call(s32[1800]{0:T(1024)S(1)} %get-tuple-element.1462.tab, ...), custom_call_target="tpu_custom_call", output_to_operand_aliasing={{5}: (10, {}), {6}: (11, {}), {7}: (12, {}), {8}: (13, {})} | custom-call | flops 40000000 | bytes 40000000 | tf_op jit(solution)/shard_map/cond/branch_2_fun/while/body/round/pallas_call | solution.py:636
  216.9 18.0 %collective-permute-done.2.rc1 = bf16[52,64,128]{2,1,0:T(8,128)(2,1)} collective-permute-done((bf16[52,64,128]{2,1,0:T(8,128)(2,1)}, bf16[52,64,128]{2,1,0:T(8,128)(2,1)}, u32[]{:S(2)}, u32[]{:S(2)}) %collective-permute-start.2) | collective-permute-done | bytes 852000 | tf_op jit(solution)/shard_map/cond/branch_2_fun/while/body/ppermute | solution.py:631
  235.4 8.1 round.6
  256.4 8.7 %round.7 = (s32[64]{0:T(128)}, bf16[52,64,128]{2,1,0:T(8,128)(2,1)}, bf16[52,64,128]{2,1,0:T(8,128)(2,1)}, bf16[2,52,64,128]{3,2,1,0:T(8,128)(2,1)}, bf16[2,32,6...) custom-call(s32[1800]{0:T(1024)S(1)} %get-tuple-element.1462.tab, ...), custom_call_target="tpu_custom_call", output_to_operand_aliasing={{5}: (10, {}), {6}: (11, {}), {7}: (12, {}), {8}: (13, {})} | custom-call | flops 40000000 | bytes 40000000 | tf_op jit(solution)/shard_map/cond/branch_2_fun/while/body/round/pallas_call | solution.py:636
  265.2 5.8 attend.13
  274.3 19.2 %collective-permute-done.2.rc1 = bf16[52,64,128]{2,1,0:T(8,128)(2,1)} collective-permute-done((bf16[52,64,128]{2,1,0:T(8,128)(2,1)}, bf16[52,64,128]{2,1,0:T(8,128)(2,1)}, u32[]{:S(2)}, u32[]{:S(2)}) %collective-permute-start.2) | collective-permute-done | bytes 852000 | tf_op jit(solution)/shard_map/cond/branch_2_fun/while/body/ppermute | solution.py:631
  293.9 7.9 round.6
  305.7 5.5 attend.12
  314.6 8.8 %round.7 = (s32[64]{0:T(128)}, bf16[52,64,128]{2,1,0:T(8,128)(2,1)}, bf16[52,64,128]{2,1,0:T(8,128)(2,1)}, bf16[2,52,64,128]{3,2,1,0:T(8,128)(2,1)}, bf16[2,32,6...) custom-call(s32[1800]{0:T(1024)S(1)} %get-tuple-element.1462.tab, ...), custom_call_target="tpu_custom_call", output_to_operand_aliasing={{5}: (10, {}), {6}: (11, {}), {7}: (12, {}), {8}: (13, {})} | custom-call | flops 40000000 | bytes 40000000 | tf_op jit(solution)/shard_map/cond/branch_2_fun/while/body/round/pallas_call | solution.py:636
  331.5 18.1 %collective-permute-done.2.rc1 = bf16[52,64,128]{2,1,0:T(8,128)(2,1)} collective-permute-done((bf16[52,64,128]{2,1,0:T(8,128)(2,1)}, bf16[52,64,128]{2,1,0:T(8,128)(2,1)}, u32[]{:S(2)}, u32[]{:S(2)}) %collective-permute-start.2) | collective-permute-done | bytes 852000 | tf_op jit(solution)/shard_map/cond/branch_2_fun/while/body/ppermute | solution.py:631
  350.1 8.0 round.6
  362.2 7.4 attend.12
  373.0 7.0 round.7
  380.0 7.5 attend.13
  390.8 14.8 %collective-permute-done.2.rc1 = bf16[52,64,128]{2,1,0:T(8,128)(2,1)} collective-permute-done((bf16[52,64,128]{2,1,0:T(8,128)(2,1)}, bf16[52,64,128]{2,1,0:T(8,128)(2,1)}, u32[]{:S(2)}, u32[]{:S(2)}) %collective-permute-start.2) | collective-permute-done | bytes 852000 | tf_op jit(solution)/shard_map/cond/branch_2_fun/while/body/ppermute | solution.py:631
  407.7 7.3 round.6
  424.5 7.9 round.7
  446.8 14.9 %collective-permute-done.2.rc1 = bf16[52,64,128]{2,1,0:T(8,128)(2,1)} collective-permute-done((bf16[52,64,128]{2,1,0:T(8,128)(2,1)}, bf16[52,64,128]{2,1,0:T(8,128)(2,1)}, u32[]{:S(2)}, u32[]{:S(2)}) %collective-permute-start.2) | collective-permute-done | bytes 852000 | tf_op jit(solution)/shard_map/cond/branch_2_fun/while/body/ppermute | solution.py:631
  465.1 7.1 round.6
  475.8 6.1 attend.12
  485.3 7.6 round.7
  501.6 18.7 %collective-permute-done.2.rc1 = bf16[52,64,128]{2,1,0:T(8,128)(2,1)} collective-permute-done((bf16[52,64,128]{2,1,0:T(8,128)(2,1)}, bf16[52,64,128]{2,1,0:T(8,128)(2,1)}, u32[]{:S(2)}, u32[]{:S(2)}) %collective-permute-start.2) | collective-permute-done | bytes 852000 | tf_op jit(solution)/shard_map/cond/branch_2_fun/while/body/ppermute | solution.py:631
  521.7 7.4 round.6
  538.7 8.1 round.7
  546.8 6.7 attend.13
  554.4 6.1 collective-permute-start.2
  561.1 16.6 %collective-permute-done.2.rc1 = bf16[52,64,128]{2,1,0:T(8,128)(2,1)} collective-permute-done((bf16[52,64,128]{2,1,0:T(8,128)(2,1)}, bf16[52,64,128]{2,1,0:T(8,128)(2,1)}, u32[]{:S(2)}, u32[]{:S(2)}) %collective-permute-start.2) | collective-permute-done | bytes 852000 | tf_op jit(solution)/shard_map/cond/branch_2_fun/while/body/ppermute | solution.py:631
  579.8 7.7 round.6
  591.0 6.6 attend.12
  600.9 8.1 round.7
  609.0 5.5 attend.13
  617.8 18.8 %collective-permute-done.2.rc1 = bf16[52,64,128]{2,1,0:T(8,128)(2,1)} collective-permute-done((bf16[52,64,128]{2,1,0:T(8,128)(2,1)}, bf16[52,64,128]{2,1,0:T(8,128)(2,1)}, u32[]{:S(2)}, u32[]{:S(2)}) %collective-permute-start.2) | collective-permute-done | bytes 852000 | tf_op jit(solution)/shard_map/cond/branch_2_fun/while/body/ppermute | solution.py:631
  637.1 7.9 round.6
  647.6 6.3 attend.12
  657.2 8.1 round.7
  665.3 5.6 attend.13
  674.2 17.4 %collective-permute-done.2.rc1 = bf16[52,64,128]{2,1,0:T(8,128)(2,1)} collective-permute-done((bf16[52,64,128]{2,1,0:T(8,128)(2,1)}, bf16[52,64,128]{2,1,0:T(8,128)(2,1)}, u32[]{:S(2)}, u32[]{:S(2)}) %collective-permute-start.2) | collective-permute-done | bytes 852000 | tf_op jit(solution)/shard_map/cond/branch_2_fun/while/body/ppermute | solution.py:631
  694.5 7.7 round.6
  713.8 8.2 round.7
  722.0 5.5 attend.13
  731.5 17.2 %collective-permute-done.2.rc1 = bf16[52,64,128]{2,1,0:T(8,128)(2,1)} collective-permute-done((bf16[52,64,128]{2,1,0:T(8,128)(2,1)}, bf16[52,64,128]{2,1,0:T(8,128)(2,1)}, u32[]{:S(2)}, u32[]{:S(2)}) %collective-permute-start.2) | collective-permute-done | bytes 852000 | tf_op jit(solution)/shard_map/cond/branch_2_fun/while/body/ppermute | solution.py:631
  749.3 8.0 round.6
  759.9 6.3 attend.12
  769.5 8.2 round.7
  777.7 6.4 attend.13
  787.5 15.9 %collective-permute-done.2.rc1 = bf16[52,64,128]{2,1,0:T(8,128)(2,1)} collective-permute-done((bf16[52,64,128]{2,1,0:T(8,128)(2,1)}, bf16[52,64,128]{2,1,0:T(8,128)(2,1)}, u32[]{:S(2)}, u32[]{:S(2)}) %collective-permute-start.2) | collective-permute-done | bytes 852000 | tf_op jit(solution)/shard_map/cond/branch_2_fun/while/body/ppermute | solution.py:631
  804.0 7.2 round.6
  823.6 6.2 round.7
  829.8 5.7 attend.13
  845.7 8.4 attend.11
  (459 shorter events, 242.6 us)
Async XLA Ops:
  41.0 27.5 %collective-permute-start.4 = (bf16[52,64,128]{2,1,0:T(8,128)(2,1)}, bf16[52,64,128]{2,1,0:T(8,128)(2,1)}, u32[]{:S(2)}, u32[]{:S(2)}) collective-permute-start(bf16[52,64,128]{2,1,0:T(8,128)(2,1)} %get-tuple-element.1427.rc1), channel_id=1, source_target_pairs={{0,1},{1,0},{2,3},{3,2},{4,5},{5,4},{6,7},{7,6}} | collective-permute-start | bytes 2555912 | tf_op jit(solution)/shard_map/cond/branch_2_fun/while/body/ppermute | solution.py:634
  41.0 27.8 %collective-permute-start.3 = (bf16[52,64,128]{2,1,0:T(8,128)(2,1)}, bf16[52,64,128]{2,1,0:T(8,128)(2,1)}, u32[]{:S(2)}, u32[]{:S(2)}) collective-permute-start(bf16[52,64,128]{2,1,0:T(8,128)(2,1)} %get-tuple-element.1426.rc0), channel_id=1, source_target_pairs={{0,1},{1,0},{2,3},{3,2},{4,5},{5,4},{6,7},{7,6}} | collective-permute-start | bytes 2555912 | tf_op jit(solution)/shard_map/cond/branch_2_fun/while/body/ppermute | solution.py:633
  41.6 27.5 %collective-permute-start.5 = (bf16[2,32,64,128]{3,2,1,0:T(8,128)(2,1)}, bf16[2,32,64,128]{3,2,1,0:T(8,128)(2,1)}, u32[]{:S(2)}, u32[]{:S(2)}) collective-permute-start(bf16[2,32,64,128]{3,2,1,0:T(8,128)(2,1)} %get-tuple-element.1424), channel_id=1, source_target_pairs={{0,1},{1,0},{2,3},{3,2},{4,5},{5,4},{6,7},{7,6}} | collective-permute-start | bytes 3145736 | tf_op jit(solution)/shard_map/cond/branch_2_fun/while/body/ppermute | solution.py:635
  68.9 24.4 %collective-permute-start.6 = (bf16[2,52,64,128]{3,2,1,0:T(8,128)(2,1)}, bf16[2,52,64,128]{3,2,1,0:T(8,128)(2,1)}, u32[]{:S(2)}, u32[]{:S(2)}) collective-permute-start(bf16[2,52,64,128]{3,2,1,0:T(8,128)(2,1)} %get-tuple-element.1277), channel_id=1, source_target_pairs={{0,1},{1,0},{2,3},{3,2},{4,5},{5,4},{6,7},{7,6}} | collective-permute-start | bytes 5111816 | tf_op jit(solution)/shard_map/cond/branch_2_fun/while/body/ppermute | solution.py:632
  94.0 27.4 %collective-permute-start.2 = (bf16[52,64,128]{2,1,0:T(8,128)(2,1)}, bf16[52,64,128]{2,1,0:T(8,128)(2,1)}, u32[]{:S(2)}, u32[]{:S(2)}) collective-permute-start(bf16[52,64,128]{2,1,0:T(8,128)(2,1)} %get-tuple-element.1422), channel_id=1, source_target_pairs={{2,0},{3,1},{6,2},{7,3},{4,6},{5,7},{0,4},{1,5}} | collective-permute-start | bytes 2555912 | tf_op jit(solution)/shard_map/cond/branch_2_fun/while/body/ppermute | solution.py:631
  97.1 25.4 %collective-permute-start.1 = (bf16[52,64,128]{2,1,0:T(8,128)(2,1)}, bf16[52,64,128]{2,1,0:T(8,128)(2,1)}, u32[]{:S(2)}, u32[]{:S(2)}) collective-permute-start(bf16[52,64,128]{2,1,0:T(8,128)(2,1)} %get-tuple-element.1421), channel_id=1, source_target_pairs={{0,2},{1,3},{2,6},{3,7},{6,4},{7,5},{4,0},{5,1}} | collective-permute-start | bytes 2555912 | tf_op jit(solution)/shard_map/cond/branch_2_fun/while/body/ppermute | solution.py:630
  101.5 29.8 %collective-permute-start.4 = (bf16[52,64,128]{2,1,0:T(8,128)(2,1)}, bf16[52,64,128]{2,1,0:T(8,128)(2,1)}, u32[]{:S(2)}, u32[]{:S(2)}) collective-permute-start(bf16[52,64,128]{2,1,0:T(8,128)(2,1)} %get-tuple-element.1427.rc1), channel_id=1, source_target_pairs={{0,1},{1,0},{2,3},{3,2},{4,5},{5,4},{6,7},{7,6}} | collective-permute-start | bytes 2555912 | tf_op jit(solution)/shard_map/cond/branch_2_fun/while/body/ppermute | solution.py:634
  102.1 29.3 %collective-permute-start.3 = (bf16[52,64,128]{2,1,0:T(8,128)(2,1)}, bf16[52,64,128]{2,1,0:T(8,128)(2,1)}, u32[]{:S(2)}, u32[]{:S(2)}) collective-permute-start(bf16[52,64,128]{2,1,0:T(8,128)(2,1)} %get-tuple-element.1426.rc0), channel_id=1, source_target_pairs={{0,1},{1,0},{2,3},{3,2},{4,5},{5,4},{6,7},{7,6}} | collective-permute-start | bytes 2555912 | tf_op jit(solution)/shard_map/cond/branch_2_fun/while/body/ppermute | solution.py:633
  102.1 29.8 %collective-permute-start.5 = (bf16[2,32,64,128]{3,2,1,0:T(8,128)(2,1)}, bf16[2,32,64,128]{3,2,1,0:T(8,128)(2,1)}, u32[]{:S(2)}, u32[]{:S(2)}) collective-permute-start(bf16[2,32,64,128]{3,2,1,0:T(8,128)(2,1)} %get-tuple-element.1424), channel_id=1, source_target_pairs={{0,1},{1,0},{2,3},{3,2},{4,5},{5,4},{6,7},{7,6}} | collective-permute-start | bytes 3145736 | tf_op jit(solution)/shard_map/cond/branch_2_fun/while/body/ppermute | solution.py:635
  158.2 29.5 %collective-permute-start.4 = (bf16[52,64,128]{2,1,0:T(8,128)(2,1)}, bf16[52,64,128]{2,1,0:T(8,128)(2,1)}, u32[]{:S(2)}, u32[]{:S(2)}) collective-permute-start(bf16[52,64,128]{2,1,0:T(8,128)(2,1)} %get-tuple-element.1427.rc1), channel_id=1, source_target_pairs={{0,1},{1,0},{2,3},{3,2},{4,5},{5,4},{6,7},{7,6}} | collective-permute-start | bytes 2555912 | tf_op jit(solution)/shard_map/cond/branch_2_fun/while/body/ppermute | solution.py:634
  159.4 28.3 %collective-permute-start.3 = (bf16[52,64,128]{2,1,0:T(8,128)(2,1)}, bf16[52,64,128]{2,1,0:T(8,128)(2,1)}, u32[]{:S(2)}, u32[]{:S(2)}) collective-permute-start(bf16[52,64,128]{2,1,0:T(8,128)(2,1)} %get-tuple-element.1426.rc0), channel_id=1, source_target_pairs={{0,1},{1,0},{2,3},{3,2},{4,5},{5,4},{6,7},{7,6}} | collective-permute-start | bytes 2555912 | tf_op jit(solution)/shard_map/cond/branch_2_fun/while/body/ppermute | solution.py:633
  159.4 28.8 %collective-permute-start.5 = (bf16[2,32,64,128]{3,2,1,0:T(8,128)(2,1)}, bf16[2,32,64,128]{3,2,1,0:T(8,128)(2,1)}, u32[]{:S(2)}, u32[]{:S(2)}) collective-permute-start(bf16[2,32,64,128]{3,2,1,0:T(8,128)(2,1)} %get-tuple-element.1424), channel_id=1, source_target_pairs={{0,1},{1,0},{2,3},{3,2},{4,5},{5,4},{6,7},{7,6}} | collective-permute-start | bytes 3145736 | tf_op jit(solution)/shard_map/cond/branch_2_fun/while/body/ppermute | solution.py:635
  215.4 28.1 %collective-permute-start.4 = (bf16[52,64,128]{2,1,0:T(8,128)(2,1)}, bf16[52,64,128]{2,1,0:T(8,128)(2,1)}, u32[]{:S(2)}, u32[]{:S(2)}) collective-permute-start(bf16[52,64,128]{2,1,0:T(8,128)(2,1)} %get-tuple-element.1427.rc1), channel_id=1, source_target_pairs={{0,1},{1,0},{2,3},{3,2},{4,5},{5,4},{6,7},{7,6}} | collective-permute-start | bytes 2555912 | tf_op jit(solution)/shard_map/cond/branch_2_fun/while/body/ppermute | solution.py:634
  216.4 27.3 %collective-permute-start.3 = (bf16[52,64,128]{2,1,0:T(8,128)(2,1)}, bf16[52,64,128]{2,1,0:T(8,128)(2,1)}, u32[]{:S(2)}, u32[]{:S(2)}) collective-permute-start(bf16[52,64,128]{2,1,0:T(8,128)(2,1)} %get-tuple-element.1426.rc0), channel_id=1, source_target_pairs={{0,1},{1,0},{2,3},{3,2},{4,5},{5,4},{6,7},{7,6}} | collective-permute-start | bytes 2555912 | tf_op jit(solution)/shard_map/cond/branch_2_fun/while/body/ppermute | solution.py:633
  216.4 27.7 %collective-permute-start.5 = (bf16[2,32,64,128]{3,2,1,0:T(8,128)(2,1)}, bf16[2,32,64,128]{3,2,1,0:T(8,128)(2,1)}, u32[]{:S(2)}, u32[]{:S(2)}) collective-permute-start(bf16[2,32,64,128]{3,2,1,0:T(8,128)(2,1)} %get-tuple-element.1424), channel_id=1, source_target_pairs={{0,1},{1,0},{2,3},{3,2},{4,5},{5,4},{6,7},{7,6}} | collective-permute-start | bytes 3145736 | tf_op jit(solution)/shard_map/cond/branch_2_fun/while/body/ppermute | solution.py:635
  243.7 27.3 %collective-permute-start.6 = (bf16[2,52,64,128]{3,2,1,0:T(8,128)(2,1)}, bf16[2,52,64,128]{3,2,1,0:T(8,128)(2,1)}, u32[]{:S(2)}, u32[]{:S(2)}) collective-permute-start(bf16[2,52,64,128]{3,2,1,0:T(8,128)(2,1)} %get-tuple-element.1277), channel_id=1, source_target_pairs={{0,1},{1,0},{2,3},{3,2},{4,5},{5,4},{6,7},{7,6}} | collective-permute-start | bytes 5111816 | tf_op jit(solution)/shard_map/cond/branch_2_fun/while/body/ppermute | solution.py:632
  244.1 26.9 %collective-permute-start.11 = (bf16[2,32,64,128]{3,2,1,0:T(8,128)(2,1)}, bf16[2,32,64,128]{3,2,1,0:T(8,128)(2,1)}, u32[]{:S(2)}, u32[]{:S(2)}) collective-permute-start(bf16[2,32,64,128]{3,2,1,0:T(8,128)(2,1)} %get-tuple-element.1280), channel_id=1, source_target_pairs={{0,1},{1,0},{2,3},{3,2},{4,5},{5,4},{6,7},{7,6}} | collective-permute-start | bytes 3145736 | tf_op jit(solution)/shard_map/cond/branch_2_fun/while/body/ppermute | solution.py:635
  244.2 26.8 %collective-permute-start.7 = (bf16[52,64,128]{2,1,0:T(8,128)(2,1)}, bf16[52,64,128]{2,1,0:T(8,128)(2,1)}, u32[]{:S(2)}, u32[]{:S(2)}) collective-permute-start(bf16[52,64,128]{2,1,0:T(8,128)(2,1)} %get-tuple-element.1278), channel_id=1, source_target_pairs={{0,2},{1,3},{2,6},{3,7},{6,4},{7,5},{4,0},{5,1}} | collective-permute-start | bytes 2555912 | tf_op jit(solution)/shard_map/cond/branch_2_fun/while/body/ppermute | solution.py:630
  273.8 28.1 %collective-permute-start.4 = (bf16[52,64,128]{2,1,0:T(8,128)(2,1)}, bf16[52,64,128]{2,1,0:T(8,128)(2,1)}, u32[]{:S(2)}, u32[]{:S(2)}) collective-permute-start(bf16[52,64,128]{2,1,0:T(8,128)(2,1)} %get-tuple-element.1427.rc1), channel_id=1, source_target_pairs={{0,1},{1,0},{2,3},{3,2},{4,5},{5,4},{6,7},{7,6}} | collective-permute-start | bytes 2555912 | tf_op jit(solution)/shard_map/cond/branch_2_fun/while/body/ppermute | solution.py:634
  273.8 28.2 %collective-permute-start.3 = (bf16[52,64,128]{2,1,0:T(8,128)(2,1)}, bf16[52,64,128]{2,1,0:T(8,128)(2,1)}, u32[]{:S(2)}, u32[]{:S(2)}) collective-permute-start(bf16[52,64,128]{2,1,0:T(8,128)(2,1)} %get-tuple-element.1426.rc0), channel_id=1, source_target_pairs={{0,1},{1,0},{2,3},{3,2},{4,5},{5,4},{6,7},{7,6}} | collective-permute-start | bytes 2555912 | tf_op jit(solution)/shard_map/cond/branch_2_fun/while/body/ppermute | solution.py:633
  274.3 28.2 %collective-permute-start.5 = (bf16[2,32,64,128]{3,2,1,0:T(8,128)(2,1)}, bf16[2,32,64,128]{3,2,1,0:T(8,128)(2,1)}, u32[]{:S(2)}, u32[]{:S(2)}) collective-permute-start(bf16[2,32,64,128]{3,2,1,0:T(8,128)(2,1)} %get-tuple-element.1424), channel_id=1, source_target_pairs={{0,1},{1,0},{2,3},{3,2},{4,5},{5,4},{6,7},{7,6}} | collective-permute-start | bytes 3145736 | tf_op jit(solution)/shard_map/cond/branch_2_fun/while/body/ppermute | solution.py:635
  331.0 27.2 %collective-permute-start.4 = (bf16[52,64,128]{2,1,0:T(8,128)(2,1)}, bf16[52,64,128]{2,1,0:T(8,128)(2,1)}, u32[]{:S(2)}, u32[]{:S(2)}) collective-permute-start(bf16[52,64,128]{2,1,0:T(8,128)(2,1)} %get-tuple-element.1427.rc1), channel_id=1, source_target_pairs={{0,1},{1,0},{2,3},{3,2},{4,5},{5,4},{6,7},{7,6}} | collective-permute-start | bytes 2555912 | tf_op jit(solution)/shard_map/cond/branch_2_fun/while/body/ppermute | solution.py:634
  331.0 27.2 %collective-permute-start.3 = (bf16[52,64,128]{2,1,0:T(8,128)(2,1)}, bf16[52,64,128]{2,1,0:T(8,128)(2,1)}, u32[]{:S(2)}, u32[]{:S(2)}) collective-permute-start(bf16[52,64,128]{2,1,0:T(8,128)(2,1)} %get-tuple-element.1426.rc0), channel_id=1, source_target_pairs={{0,1},{1,0},{2,3},{3,2},{4,5},{5,4},{6,7},{7,6}} | collective-permute-start | bytes 2555912 | tf_op jit(solution)/shard_map/cond/branch_2_fun/while/body/ppermute | solution.py:633
  331.5 27.2 %collective-permute-start.5 = (bf16[2,32,64,128]{3,2,1,0:T(8,128)(2,1)}, bf16[2,32,64,128]{3,2,1,0:T(8,128)(2,1)}, u32[]{:S(2)}, u32[]{:S(2)}) collective-permute-start(bf16[2,32,64,128]{3,2,1,0:T(8,128)(2,1)} %get-tuple-element.1424), channel_id=1, source_target_pairs={{0,1},{1,0},{2,3},{3,2},{4,5},{5,4},{6,7},{7,6}} | collective-permute-start | bytes 3145736 | tf_op jit(solution)/shard_map/cond/branch_2_fun/while/body/ppermute | solution.py:635
  358.2 29.3 %collective-permute-start.6 = (bf16[2,52,64,128]{3,2,1,0:T(8,128)(2,1)}, bf16[2,52,64,128]{3,2,1,0:T(8,128)(2,1)}, u32[]{:S(2)}, u32[]{:S(2)}) collective-permute-start(bf16[2,52,64,128]{3,2,1,0:T(8,128)(2,1)} %get-tuple-element.1277), channel_id=1, source_target_pairs={{0,1},{1,0},{2,3},{3,2},{4,5},{5,4},{6,7},{7,6}} | collective-permute-start | bytes 5111816 | tf_op jit(solution)/shard_map/cond/branch_2_fun/while/body/ppermute | solution.py:632
  358.7 28.7 %collective-permute-start.11 = (bf16[2,32,64,128]{3,2,1,0:T(8,128)(2,1)}, bf16[2,32,64,128]{3,2,1,0:T(8,128)(2,1)}, u32[]{:S(2)}, u32[]{:S(2)}) collective-permute-start(bf16[2,32,64,128]{3,2,1,0:T(8,128)(2,1)} %get-tuple-element.1280), channel_id=1, source_target_pairs={{0,1},{1,0},{2,3},{3,2},{4,5},{5,4},{6,7},{7,6}} | collective-permute-start | bytes 3145736 | tf_op jit(solution)/shard_map/cond/branch_2_fun/while/body/ppermute | solution.py:635
  358.7 28.7 %collective-permute-start.7 = (bf16[52,64,128]{2,1,0:T(8,128)(2,1)}, bf16[52,64,128]{2,1,0:T(8,128)(2,1)}, u32[]{:S(2)}, u32[]{:S(2)}) collective-permute-start(bf16[52,64,128]{2,1,0:T(8,128)(2,1)} %get-tuple-element.1278), channel_id=1, source_target_pairs={{0,2},{1,3},{2,6},{3,7},{6,4},{7,5},{4,0},{5,1}} | collective-permute-start | bytes 2555912 | tf_op jit(solution)/shard_map/cond/branch_2_fun/while/body/ppermute | solution.py:630
  360.8 26.7 %collective-permute-start.8 = (bf16[52,64,128]{2,1,0:T(8,128)(2,1)}, bf16[52,64,128]{2,1,0:T(8,128)(2,1)}, u32[]{:S(2)}, u32[]{:S(2)}) collective-permute-start(bf16[52,64,128]{2,1,0:T(8,128)(2,1)} %get-tuple-element.1279), channel_id=1, source_target_pairs={{2,0},{3,1},{6,2},{7,3},{4,6},{5,7},{0,4},{1,5}} | collective-permute-start | bytes 2555912 | tf_op jit(solution)/shard_map/cond/branch_2_fun/while/body/ppermute | solution.py:631
  390.2 24.8 %collective-permute-start.4 = (bf16[52,64,128]{2,1,0:T(8,128)(2,1)}, bf16[52,64,128]{2,1,0:T(8,128)(2,1)}, u32[]{:S(2)}, u32[]{:S(2)}) collective-permute-start(bf16[52,64,128]{2,1,0:T(8,128)(2,1)} %get-tuple-element.1427.rc1), channel_id=1, source_target_pairs={{0,1},{1,0},{2,3},{3,2},{4,5},{5,4},{6,7},{7,6}} | collective-permute-start | bytes 2555912 | tf_op jit(solution)/shard_map/cond/branch_2_fun/while/body/ppermute | solution.py:634
  390.2 26.1 %collective-permute-start.3 = (bf16[52,64,128]{2,1,0:T(8,128)(2,1)}, bf16[52,64,128]{2,1,0:T(8,128)(2,1)}, u32[]{:S(2)}, u32[]{:S(2)}) collective-permute-start(bf16[52,64,128]{2,1,0:T(8,128)(2,1)} %get-tuple-element.1426.rc0), channel_id=1, source_target_pairs={{0,1},{1,0},{2,3},{3,2},{4,5},{5,4},{6,7},{7,6}} | collective-permute-start | bytes 2555912 | tf_op jit(solution)/shard_map/cond/branch_2_fun/while/body/ppermute | solution.py:633
  390.7 25.6 %collective-permute-start.5 = (bf16[2,32,64,128]{3,2,1,0:T(8,128)(2,1)}, bf16[2,32,64,128]{3,2,1,0:T(8,128)(2,1)}, u32[]{:S(2)}, u32[]{:S(2)}) collective-permute-start(bf16[2,32,64,128]{3,2,1,0:T(8,128)(2,1)} %get-tuple-element.1424), channel_id=1, source_target_pairs={{0,1},{1,0},{2,3},{3,2},{4,5},{5,4},{6,7},{7,6}} | collective-permute-start | bytes 3145736 | tf_op jit(solution)/shard_map/cond/branch_2_fun/while/body/ppermute | solution.py:635
  443.1 29.0 %collective-permute-start.4 = (bf16[52,64,128]{2,1,0:T(8,128)(2,1)}, bf16[52,64,128]{2,1,0:T(8,128)(2,1)}, u32[]{:S(2)}, u32[]{:S(2)}) collective-permute-start(bf16[52,64,128]{2,1,0:T(8,128)(2,1)} %get-tuple-element.1427.rc1), channel_id=1, source_target_pairs={{0,1},{1,0},{2,3},{3,2},{4,5},{5,4},{6,7},{7,6}} | collective-permute-start | bytes 2555912 | tf_op jit(solution)/shard_map/cond/branch_2_fun/while/body/ppermute | solution.py:634
  446.3 26.6 %collective-permute-start.3 = (bf16[52,64,128]{2,1,0:T(8,128)(2,1)}, bf16[52,64,128]{2,1,0:T(8,128)(2,1)}, u32[]{:S(2)}, u32[]{:S(2)}) collective-permute-start(bf16[52,64,128]{2,1,0:T(8,128)(2,1)} %get-tuple-element.1426.rc0), channel_id=1, source_target_pairs={{0,1},{1,0},{2,3},{3,2},{4,5},{5,4},{6,7},{7,6}} | collective-permute-start | bytes 2555912 | tf_op jit(solution)/shard_map/cond/branch_2_fun/while/body/ppermute | solution.py:633
  446.3 26.6 %collective-permute-start.5 = (bf16[2,32,64,128]{3,2,1,0:T(8,128)(2,1)}, bf16[2,32,64,128]{3,2,1,0:T(8,128)(2,1)}, u32[]{:S(2)}, u32[]{:S(2)}) collective-permute-start(bf16[2,32,64,128]{3,2,1,0:T(8,128)(2,1)} %get-tuple-element.1424), channel_id=1, source_target_pairs={{0,1},{1,0},{2,3},{3,2},{4,5},{5,4},{6,7},{7,6}} | collective-permute-start | bytes 3145736 | tf_op jit(solution)/shard_map/cond/branch_2_fun/while/body/ppermute | solution.py:635
  500.5 28.7 %collective-permute-start.4 = (bf16[52,64,128]{2,1,0:T(8,128)(2,1)}, bf16[52,64,128]{2,1,0:T(8,128)(2,1)}, u32[]{:S(2)}, u32[]{:S(2)}) collective-permute-start(bf16[52,64,128]{2,1,0:T(8,128)(2,1)} %get-tuple-element.1427.rc1), channel_id=1, source_target_pairs={{0,1},{1,0},{2,3},{3,2},{4,5},{5,4},{6,7},{7,6}} | collective-permute-start | bytes 2555912 | tf_op jit(solution)/shard_map/cond/branch_2_fun/while/body/ppermute | solution.py:634
  501.1 28.9 %collective-permute-start.3 = (bf16[52,64,128]{2,1,0:T(8,128)(2,1)}, bf16[52,64,128]{2,1,0:T(8,128)(2,1)}, u32[]{:S(2)}, u32[]{:S(2)}) collective-permute-start(bf16[52,64,128]{2,1,0:T(8,128)(2,1)} %get-tuple-element.1426.rc0), channel_id=1, source_target_pairs={{0,1},{1,0},{2,3},{3,2},{4,5},{5,4},{6,7},{7,6}} | collective-permute-start | bytes 2555912 | tf_op jit(solution)/shard_map/cond/branch_2_fun/while/body/ppermute | solution.py:633
  501.1 28.9 %collective-permute-start.5 = (bf16[2,32,64,128]{3,2,1,0:T(8,128)(2,1)}, bf16[2,32,64,128]{3,2,1,0:T(8,128)(2,1)}, u32[]{:S(2)}, u32[]{:S(2)}) collective-permute-start(bf16[2,32,64,128]{3,2,1,0:T(8,128)(2,1)} %get-tuple-element.1424), channel_id=1, source_target_pairs={{0,1},{1,0},{2,3},{3,2},{4,5},{5,4},{6,7},{7,6}} | collective-permute-start | bytes 3145736 | tf_op jit(solution)/shard_map/cond/branch_2_fun/while/body/ppermute | solution.py:635
  560.5 27.0 %collective-permute-start.4 = (bf16[52,64,128]{2,1,0:T(8,128)(2,1)}, bf16[52,64,128]{2,1,0:T(8,128)(2,1)}, u32[]{:S(2)}, u32[]{:S(2)}) collective-permute-start(bf16[52,64,128]{2,1,0:T(8,128)(2,1)} %get-tuple-element.1427.rc1), channel_id=1, source_target_pairs={{0,1},{1,0},{2,3},{3,2},{4,5},{5,4},{6,7},{7,6}} | collective-permute-start | bytes 2555912 | tf_op jit(solution)/shard_map/cond/branch_2_fun/while/body/ppermute | solution.py:634
  560.5 27.3 %collective-permute-start.3 = (bf16[52,64,128]{2,1,0:T(8,128)(2,1)}, bf16[52,64,128]{2,1,0:T(8,128)(2,1)}, u32[]{:S(2)}, u32[]{:S(2)}) collective-permute-start(bf16[52,64,128]{2,1,0:T(8,128)(2,1)} %get-tuple-element.1426.rc0), channel_id=1, source_target_pairs={{0,1},{1,0},{2,3},{3,2},{4,5},{5,4},{6,7},{7,6}} | collective-permute-start | bytes 2555912 | tf_op jit(solution)/shard_map/cond/branch_2_fun/while/body/ppermute | solution.py:633
  561.1 27.0 %collective-permute-start.5 = (bf16[2,32,64,128]{3,2,1,0:T(8,128)(2,1)}, bf16[2,32,64,128]{3,2,1,0:T(8,128)(2,1)}, u32[]{:S(2)}, u32[]{:S(2)}) collective-permute-start(bf16[2,32,64,128]{3,2,1,0:T(8,128)(2,1)} %get-tuple-element.1424), channel_id=1, source_target_pairs={{0,1},{1,0},{2,3},{3,2},{4,5},{5,4},{6,7},{7,6}} | collective-permute-start | bytes 3145736 | tf_op jit(solution)/shard_map/cond/branch_2_fun/while/body/ppermute | solution.py:635
  587.9 26.6 %collective-permute-start.6 = (bf16[2,52,64,128]{3,2,1,0:T(8,128)(2,1)}, bf16[2,52,64,128]{3,2,1,0:T(8,128)(2,1)}, u32[]{:S(2)}, u32[]{:S(2)}) collective-permute-start(bf16[2,52,64,128]{3,2,1,0:T(8,128)(2,1)} %get-tuple-element.1277), channel_id=1, source_target_pairs={{0,1},{1,0},{2,3},{3,2},{4,5},{5,4},{6,7},{7,6}} | collective-permute-start | bytes 5111816 | tf_op jit(solution)/shard_map/cond/branch_2_fun/while/body/ppermute | solution.py:632
  588.1 26.4 %collective-permute-start.11 = (bf16[2,32,64,128]{3,2,1,0:T(8,128)(2,1)}, bf16[2,32,64,128]{3,2,1,0:T(8,128)(2,1)}, u32[]{:S(2)}, u32[]{:S(2)}) collective-permute-start(bf16[2,32,64,128]{3,2,1,0:T(8,128)(2,1)} %get-tuple-element.1280), channel_id=1, source_target_pairs={{0,1},{1,0},{2,3},{3,2},{4,5},{5,4},{6,7},{7,6}} | collective-permute-start | bytes 3145736 | tf_op jit(solution)/shard_map/cond/branch_2_fun/while/body/ppermute | solution.py:635
  588.4 26.1 %collective-permute-start.7 = (bf16[52,64,128]{2,1,0:T(8,128)(2,1)}, bf16[52,64,128]{2,1,0:T(8,128)(2,1)}, u32[]{:S(2)}, u32[]{:S(2)}) collective-permute-start(bf16[52,64,128]{2,1,0:T(8,128)(2,1)} %get-tuple-element.1278), channel_id=1, source_target_pairs={{0,2},{1,3},{2,6},{3,7},{6,4},{7,5},{4,0},{5,1}} | collective-permute-start | bytes 2555912 | tf_op jit(solution)/shard_map/cond/branch_2_fun/while/body/ppermute | solution.py:630
  590.2 24.3 %collective-permute-start.8 = (bf16[52,64,128]{2,1,0:T(8,128)(2,1)}, bf16[52,64,128]{2,1,0:T(8,128)(2,1)}, u32[]{:S(2)}, u32[]{:S(2)}) collective-permute-start(bf16[52,64,128]{2,1,0:T(8,128)(2,1)} %get-tuple-element.1279), channel_id=1, source_target_pairs={{2,0},{3,1},{6,2},{7,3},{4,6},{5,7},{0,4},{1,5}} | collective-permute-start | bytes 2555912 | tf_op jit(solution)/shard_map/cond/branch_2_fun/while/body/ppermute | solution.py:631
  617.3 27.7 %collective-permute-start.4 = (bf16[52,64,128]{2,1,0:T(8,128)(2,1)}, bf16[52,64,128]{2,1,0:T(8,128)(2,1)}, u32[]{:S(2)}, u32[]{:S(2)}) collective-permute-start(bf16[52,64,128]{2,1,0:T(8,128)(2,1)} %get-tuple-element.1427.rc1), channel_id=1, source_target_pairs={{0,1},{1,0},{2,3},{3,2},{4,5},{5,4},{6,7},{7,6}} | collective-permute-start | bytes 2555912 | tf_op jit(solution)/shard_map/cond/branch_2_fun/while/body/ppermute | solution.py:634
  617.3 27.7 %collective-permute-start.3 = (bf16[52,64,128]{2,1,0:T(8,128)(2,1)}, bf16[52,64,128]{2,1,0:T(8,128)(2,1)}, u32[]{:S(2)}, u32[]{:S(2)}) collective-permute-start(bf16[52,64,128]{2,1,0:T(8,128)(2,1)} %get-tuple-element.1426.rc0), channel_id=1, source_target_pairs={{0,1},{1,0},{2,3},{3,2},{4,5},{5,4},{6,7},{7,6}} | collective-permute-start | bytes 2555912 | tf_op jit(solution)/shard_map/cond/branch_2_fun/while/body/ppermute | solution.py:633
  617.8 27.7 %collective-permute-start.5 = (bf16[2,32,64,128]{3,2,1,0:T(8,128)(2,1)}, bf16[2,32,64,128]{3,2,1,0:T(8,128)(2,1)}, u32[]{:S(2)}, u32[]{:S(2)}) collective-permute-start(bf16[2,32,64,128]{3,2,1,0:T(8,128)(2,1)} %get-tuple-element.1424), channel_id=1, source_target_pairs={{0,1},{1,0},{2,3},{3,2},{4,5},{5,4},{6,7},{7,6}} | collective-permute-start | bytes 3145736 | tf_op jit(solution)/shard_map/cond/branch_2_fun/while/body/ppermute | solution.py:635
  645.0 25.9 %collective-permute-start.6 = (bf16[2,52,64,128]{3,2,1,0:T(8,128)(2,1)}, bf16[2,52,64,128]{3,2,1,0:T(8,128)(2,1)}, u32[]{:S(2)}, u32[]{:S(2)}) collective-permute-start(bf16[2,52,64,128]{3,2,1,0:T(8,128)(2,1)} %get-tuple-element.1277), channel_id=1, source_target_pairs={{0,1},{1,0},{2,3},{3,2},{4,5},{5,4},{6,7},{7,6}} | collective-permute-start | bytes 5111816 | tf_op jit(solution)/shard_map/cond/branch_2_fun/while/body/ppermute | solution.py:632
  645.5 25.4 %collective-permute-start.11 = (bf16[2,32,64,128]{3,2,1,0:T(8,128)(2,1)}, bf16[2,32,64,128]{3,2,1,0:T(8,128)(2,1)}, u32[]{:S(2)}, u32[]{:S(2)}) collective-permute-start(bf16[2,32,64,128]{3,2,1,0:T(8,128)(2,1)} %get-tuple-element.1280), channel_id=1, source_target_pairs={{0,1},{1,0},{2,3},{3,2},{4,5},{5,4},{6,7},{7,6}} | collective-permute-start | bytes 3145736 | tf_op jit(solution)/shard_map/cond/branch_2_fun/while/body/ppermute | solution.py:635
  645.6 25.4 %collective-permute-start.7 = (bf16[52,64,128]{2,1,0:T(8,128)(2,1)}, bf16[52,64,128]{2,1,0:T(8,128)(2,1)}, u32[]{:S(2)}, u32[]{:S(2)}) collective-permute-start(bf16[52,64,128]{2,1,0:T(8,128)(2,1)} %get-tuple-element.1278), channel_id=1, source_target_pairs={{0,2},{1,3},{2,6},{3,7},{6,4},{7,5},{4,0},{5,1}} | collective-permute-start | bytes 2555912 | tf_op jit(solution)/shard_map/cond/branch_2_fun/while/body/ppermute | solution.py:630
  673.7 28.5 %collective-permute-start.4 = (bf16[52,64,128]{2,1,0:T(8,128)(2,1)}, bf16[52,64,128]{2,1,0:T(8,128)(2,1)}, u32[]{:S(2)}, u32[]{:S(2)}) collective-permute-start(bf16[52,64,128]{2,1,0:T(8,128)(2,1)} %get-tuple-element.1427.rc1), channel_id=1, source_target_pairs={{0,1},{1,0},{2,3},{3,2},{4,5},{5,4},{6,7},{7,6}} | collective-permute-start | bytes 2555912 | tf_op jit(solution)/shard_map/cond/branch_2_fun/while/body/ppermute | solution.py:634
  673.7 28.8 %collective-permute-start.3 = (bf16[52,64,128]{2,1,0:T(8,128)(2,1)}, bf16[52,64,128]{2,1,0:T(8,128)(2,1)}, u32[]{:S(2)}, u32[]{:S(2)}) collective-permute-start(bf16[52,64,128]{2,1,0:T(8,128)(2,1)} %get-tuple-element.1426.rc0), channel_id=1, source_target_pairs={{0,1},{1,0},{2,3},{3,2},{4,5},{5,4},{6,7},{7,6}} | collective-permute-start | bytes 2555912 | tf_op jit(solution)/shard_map/cond/branch_2_fun/while/body/ppermute | solution.py:633
  674.2 28.5 %collective-permute-start.5 = (bf16[2,32,64,128]{3,2,1,0:T(8,128)(2,1)}, bf16[2,32,64,128]{3,2,1,0:T(8,128)(2,1)}, u32[]{:S(2)}, u32[]{:S(2)}) collective-permute-start(bf16[2,32,64,128]{3,2,1,0:T(8,128)(2,1)} %get-tuple-element.1424), channel_id=1, source_target_pairs={{0,1},{1,0},{2,3},{3,2},{4,5},{5,4},{6,7},{7,6}} | collective-permute-start | bytes 3145736 | tf_op jit(solution)/shard_map/cond/branch_2_fun/while/body/ppermute | solution.py:635
  702.5 25.0 %collective-permute-start.6 = (bf16[2,52,64,128]{3,2,1,0:T(8,128)(2,1)}, bf16[2,52,64,128]{3,2,1,0:T(8,128)(2,1)}, u32[]{:S(2)}, u32[]{:S(2)}) collective-permute-start(bf16[2,52,64,128]{3,2,1,0:T(8,128)(2,1)} %get-tuple-element.1277), channel_id=1, source_target_pairs={{0,1},{1,0},{2,3},{3,2},{4,5},{5,4},{6,7},{7,6}} | collective-permute-start | bytes 5111816 | tf_op jit(solution)/shard_map/cond/branch_2_fun/while/body/ppermute | solution.py:632
  702.7 24.8 %collective-permute-start.11 = (bf16[2,32,64,128]{3,2,1,0:T(8,128)(2,1)}, bf16[2,32,64,128]{3,2,1,0:T(8,128)(2,1)}, u32[]{:S(2)}, u32[]{:S(2)}) collective-permute-start(bf16[2,32,64,128]{3,2,1,0:T(8,128)(2,1)} %get-tuple-element.1280), channel_id=1, source_target_pairs={{0,1},{1,0},{2,3},{3,2},{4,5},{5,4},{6,7},{7,6}} | collective-permute-start | bytes 3145736 | tf_op jit(solution)/shard_map/cond/branch_2_fun/while/body/ppermute | solution.py:635
  703.0 24.5 %collective-permute-start.7 = (bf16[52,64,128]{2,1,0:T(8,128)(2,1)}, bf16[52,64,128]{2,1,0:T(8,128)(2,1)}, u32[]{:S(2)}, u32[]{:S(2)}) collective-permute-start(bf16[52,64,128]{2,1,0:T(8,128)(2,1)} %get-tuple-element.1278), channel_id=1, source_target_pairs={{0,2},{1,3},{2,6},{3,7},{6,4},{7,5},{4,0},{5,1}} | collective-permute-start | bytes 2555912 | tf_op jit(solution)/shard_map/cond/branch_2_fun/while/body/ppermute | solution.py:630
  731.0 26.3 %collective-permute-start.4 = (bf16[52,64,128]{2,1,0:T(8,128)(2,1)}, bf16[52,64,128]{2,1,0:T(8,128)(2,1)}, u32[]{:S(2)}, u32[]{:S(2)}) collective-permute-start(bf16[52,64,128]{2,1,0:T(8,128)(2,1)} %get-tuple-element.1427.rc1), channel_id=1, source_target_pairs={{0,1},{1,0},{2,3},{3,2},{4,5},{5,4},{6,7},{7,6}} | collective-permute-start | bytes 2555912 | tf_op jit(solution)/shard_map/cond/branch_2_fun/while/body/ppermute | solution.py:634
  731.0 26.3 %collective-permute-start.3 = (bf16[52,64,128]{2,1,0:T(8,128)(2,1)}, bf16[52,64,128]{2,1,0:T(8,128)(2,1)}, u32[]{:S(2)}, u32[]{:S(2)}) collective-permute-start(bf16[52,64,128]{2,1,0:T(8,128)(2,1)} %get-tuple-element.1426.rc0), channel_id=1, source_target_pairs={{0,1},{1,0},{2,3},{3,2},{4,5},{5,4},{6,7},{7,6}} | collective-permute-start | bytes 2555912 | tf_op jit(solution)/shard_map/cond/branch_2_fun/while/body/ppermute | solution.py:633
  731.5 26.3 %collective-permute-start.5 = (bf16[2,32,64,128]{3,2,1,0:T(8,128)(2,1)}, bf16[2,32,64,128]{3,2,1,0:T(8,128)(2,1)}, u32[]{:S(2)}, u32[]{:S(2)}) collective-permute-start(bf16[2,32,64,128]{3,2,1,0:T(8,128)(2,1)} %get-tuple-element.1424), channel_id=1, source_target_pairs={{0,1},{1,0},{2,3},{3,2},{4,5},{5,4},{6,7},{7,6}} | collective-permute-start | bytes 3145736 | tf_op jit(solution)/shard_map/cond/branch_2_fun/while/body/ppermute | solution.py:635
  757.4 26.9 %collective-permute-start.6 = (bf16[2,52,64,128]{3,2,1,0:T(8,128)(2,1)}, bf16[2,52,64,128]{3,2,1,0:T(8,128)(2,1)}, u32[]{:S(2)}, u32[]{:S(2)}) collective-permute-start(bf16[2,52,64,128]{3,2,1,0:T(8,128)(2,1)} %get-tuple-element.1277), channel_id=1, source_target_pairs={{0,1},{1,0},{2,3},{3,2},{4,5},{5,4},{6,7},{7,6}} | collective-permute-start | bytes 5111816 | tf_op jit(solution)/shard_map/cond/branch_2_fun/while/body/ppermute | solution.py:632
  757.8 26.3 %collective-permute-start.11 = (bf16[2,32,64,128]{3,2,1,0:T(8,128)(2,1)}, bf16[2,32,64,128]{3,2,1,0:T(8,128)(2,1)}, u32[]{:S(2)}, u32[]{:S(2)}) collective-permute-start(bf16[2,32,64,128]{3,2,1,0:T(8,128)(2,1)} %get-tuple-element.1280), channel_id=1, source_target_pairs={{0,1},{1,0},{2,3},{3,2},{4,5},{5,4},{6,7},{7,6}} | collective-permute-start | bytes 3145736 | tf_op jit(solution)/shard_map/cond/branch_2_fun/while/body/ppermute | solution.py:635
  757.9 26.3 %collective-permute-start.7 = (bf16[52,64,128]{2,1,0:T(8,128)(2,1)}, bf16[52,64,128]{2,1,0:T(8,128)(2,1)}, u32[]{:S(2)}, u32[]{:S(2)}) collective-permute-start(bf16[52,64,128]{2,1,0:T(8,128)(2,1)} %get-tuple-element.1278), channel_id=1, source_target_pairs={{0,2},{1,3},{2,6},{3,7},{6,4},{7,5},{4,0},{5,1}} | collective-permute-start | bytes 2555912 | tf_op jit(solution)/shard_map/cond/branch_2_fun/while/body/ppermute | solution.py:630
  787.0 24.8 %collective-permute-start.3 = (bf16[52,64,128]{2,1,0:T(8,128)(2,1)}, bf16[52,64,128]{2,1,0:T(8,128)(2,1)}, u32[]{:S(2)}, u32[]{:S(2)}) collective-permute-start(bf16[52,64,128]{2,1,0:T(8,128)(2,1)} %get-tuple-element.1426.rc0), channel_id=1, source_target_pairs={{0,1},{1,0},{2,3},{3,2},{4,5},{5,4},{6,7},{7,6}} | collective-permute-start | bytes 2555912 | tf_op jit(solution)/shard_map/cond/branch_2_fun/while/body/ppermute | solution.py:633
  787.5 24.3 %collective-permute-start.5 = (bf16[2,32,64,128]{3,2,1,0:T(8,128)(2,1)}, bf16[2,32,64,128]{3,2,1,0:T(8,128)(2,1)}, u32[]{:S(2)}, u32[]{:S(2)}) collective-permute-start(bf16[2,32,64,128]{3,2,1,0:T(8,128)(2,1)} %get-tuple-element.1424), channel_id=1, source_target_pairs={{0,1},{1,0},{2,3},{3,2},{4,5},{5,4},{6,7},{7,6}} | collective-permute-start | bytes 3145736 | tf_op jit(solution)/shard_map/cond/branch_2_fun/while/body/ppermute | solution.py:635
  (156 other events, 2032.8 us)

commit v2 on v1

--- a/solution.py
+++ b/solution.py
@@ -9,17 +9,20 @@
 
 
 BP, SHIFT = 8, 3
-SIZES = (64, 58, 52)
+SIZES = (66, 60, 54, 48)
 NX = 32
 A = 4
 SL = 32
 BL = 64
-WIDE = 272
+WIDE = 400
 S0, S1, R0, R1, XS, XR, FREE = range(7)
 RDY, RDX, MLEN, SRC, ROUNDS = range(FREE * WIDE, FREE * WIDE + 200, 40)
 CORE, PICK, DUMP = ROUNDS + 1, ROUNDS + 2, ROUNDS + 4
 TAB = ROUNDS + 8
 FWD, NONE = 2, 3
+TURN = 4
+SEGS = 6
+IDLE = 4 * SEGS
 HALF = 1 << 16
 FLOPS = 4000000
 LOW = HALF - 1
@@ -54,37 +57,41 @@
         c.wait()
 
 
-def plan_kernel(me_ref, dest_ref, len_ref, tab, lens_out, nbv, kindv, todo, load, hop, swap, addr, at):
+def plan_kernel(me_ref, dest_ref, len_ref, tab, lens_out, nbv, kindv, todo, near, load, one, two, three, swap, addr, at):
     me = me_ref[0]
-    zero = me * 0
+    zero = me - me
     for i in range(9):
-        for ref in (load, hop, swap):
+        for ref in (load, one, two, three, swap):
             ref[i] = zero
     tab[CORE] = me & 1
     for j in range(SL):
         tab[RDY + j] = zero
         tab[RDX + j] = zero
 
-    def first(i, n):
+    def first(i, c):
         size = len_ref[i >> 5, 0, i & 31]
         d = dest_ref[i]
         nb = (size + (BP - 1)) >> SHIFT
         ra = gray(i >> 6)
         delta = (gray(d >> 6) - ra) & 3
         nbv[i] = nb
-        kindv[i] = delta
-        slot = jnp.where(delta == 1, ra, jnp.where(delta == 3, 4 + ra, 8))
-        load[slot] = load[slot] + nb + HALF
-        todo[n] = i
+        beside = (delta & 1) == 1
+        ccw = delta == 3
+        kindv[i] = jnp.where(beside, jnp.where(ccw, 4, 1), 0)
+        slot = jnp.where(beside, jnp.where(ccw, 4, 0) + ra, 8)
+        one[slot] = one[slot] + nb + HALF
+        load[slot] = load[slot] + nb
+        todo[c[0]] = i
+        near[c[1]] = i
         cross = (delta == 0) & ((i >> 5) != (d >> 5))
         xslot = jnp.where(cross, i >> 5, 8)
         swap[xslot] = swap[xslot] + nb
         mine = jnp.where((d >> 5) == me, d & 31, SL)
         tab[MLEN + mine] = size
         tab[SRC + mine] = jnp.where((i >> 5) == me, i & 31, -1)
-        return n + jnp.where(delta == 2, 1, 0)
-
-    far = lax.fori_loop(0, 8 * SL, first, zero, unroll=4)
+        return c[0] + jnp.where(delta == 2, 1, 0), c[1] + jnp.where(beside, 1, 0)
+
+    far, side = lax.fori_loop(0, 8 * SL, first, (zero, zero), unroll=4)
 
     def lens(j, c):
         lens_out[j] = tab[MLEN + j] + 1
@@ -92,28 +99,86 @@
 
     lax.fori_loop(0, SL, lens, 0, unroll=8)
 
+    def hops(x):
+        return (x, (x + 1) & 3, (x + 2) & 3), (4 + x, 4 + ((x - 1) & 3), 4 + ((x + 2) & 3))
+
     def choose(n, c):
         i = todo[n]
         nb = nbv[i]
-        ra = gray(i >> 6)
-        a1, a2, b1, b2 = ra, (ra + 1) & 3, 4 + ra, 4 + ((ra - 1) & 3)
-        la1, la2, lb1, lb2 = load[a1] & LOW, load[a2] & LOW, load[b1] & LOW, load[b2] & LOW
+        (a1, a2, _), (b1, b2, _) = hops(gray(i >> 6))
+        la1, la2, lb1, lb2 = load[a1], load[a2], load[b1], load[b2]
         la, lb = jnp.maximum(la1, la2), jnp.maximum(lb1, lb2)
         cw = (la < lb) | ((la == lb) & (la1 + la2 <= lb1 + lb2))
         x1, x2 = jnp.where(cw, a1, b1), jnp.where(cw, a2, b2)
-        load[x1] = load[x1] + nb + HALF
-        load[x2] = load[x2] + nb + HALF
-        hop[x1] = hop[x1] + nb + HALF
-        kindv[i] = jnp.where(cw, 2, 4)
+        load[x1] = load[x1] + nb
+        load[x2] = load[x2] + nb
+        two[x1] = two[x1] + nb + HALF
+        kindv[i] = jnp.where(cw, 2, 5)
         return c
 
     lax.fori_loop(0, far, choose, 0)
 
+    def detour(n, c):
+        i = near[n]
+        nb = nbv[i]
+        cws, ccws = hops(gray(i >> 6))
+        cw = kindv[i] == 1
+        a = jnp.where(cw, cws[0], ccws[0])
+        b = [jnp.where(cw, y, x) for x, y in zip(cws, ccws)]
+        lb = [load[x] for x in b]
+        la = load[a]
+        top = functools.reduce(jnp.maximum, [load[x] for x in range(8)])
+
+        @pl.when((la - nb >= functools.reduce(jnp.maximum, lb) + nb) & (la * 10 >= top * 9))
+        def _():
+            load[a] = la - nb
+            one[a] = one[a] - nb - HALF
+            for x, l in zip(b, lb):
+                load[x] = l + nb
+            three[b[0]] = three[b[0]] + nb + HALF
+            kindv[i] = jnp.where(cw, 6, 3)
+
+        return c
+
+    lax.fori_loop(0, side, detour, 0)
+
+    def again(n, c):
+        i = todo[n]
+        nb = nbv[i]
+        cws, ccws = hops(gray(i >> 6))
+        cw = kindv[i] == 2
+        a = [jnp.where(cw, x, y) for x, y in zip(cws[:2], ccws)]
+        b = [jnp.where(cw, y, x) for x, y in zip(cws[:2], ccws)]
+        la, lb = [load[x] for x in a], [load[x] for x in b]
+
+        @pl.when(jnp.maximum(*lb) + nb < jnp.maximum(*la))
+        def _():
+            for x, l in zip(a + b, [l - nb for l in la] + [l + nb for l in lb]):
+                load[x] = l
+            two[a[0]] = two[a[0]] - nb - HALF
+            two[b[0]] = two[b[0]] + nb + HALF
+            kindv[i] = jnp.where(cw, 5, 2)
+
+        return c
+
+    lax.fori_loop(0, far, again, 0)
+
+    def back(d, x, n):
+        return 4 * d + ((x + (2 * d - 1) * n) & 3)
+
+    def own_of(d, x):
+        x = back(d, x, 0)
+        return one[x] + two[x] + three[x]
+
     def link(d, x, size):
-        fwd = hop[4 * d + ((x - 1 + 2 * d) & 3)]
-        own = load[4 * d + x] - fwd
-        start = jnp.where(fwd > 0, jnp.maximum(own & LOW, 2 * size), own & LOW)
-        return own, fwd, start
+        up, up2 = back(d, x, 1), back(d, x, 2)
+        own = own_of(d, x)
+        fwd, fwd2 = two[up] + three[up], three[up2]
+        start = jnp.maximum(own & LOW, jnp.where(fwd > 0, 2 * size, 0))
+        own_up = own_of(d, up & 3)
+        start_up = jnp.maximum(own_up & LOW, jnp.where(two[up2] + three[up2] > 0, 2 * size, 0))
+        start2 = jnp.maximum(start + (fwd & LOW), jnp.where(fwd2 > 0, start_up + 2 * size, 0))
+        return own, fwd, fwd2, start, start_up, start2
 
     cross = zero
     for d in range(8):
@@ -123,36 +188,44 @@
         longest = zero
         for d in range(2):
             for x in range(4):
-                _, fwd, start = link(d, x, size)
-                longest = jnp.maximum(longest, start + (fwd & LOW))
-        rounds = (jnp.maximum((longest + size - 1) // size, cross) + 1) & -2
-        price = rounds * (size + BP // 2)
+                _, _, fwd2, _, _, start2 = link(d, x, size)
+                longest = jnp.maximum(longest, start2 + (fwd2 & LOW))
+        trips = (jnp.maximum((longest + size - 1) // size, cross) + TURN - 1) // TURN
+        price = trips * (TURN * size + 12)
         better = price < best
         best, pick, turns, chunk = [jnp.where(better, n, o) for n, o in (
-            (price, best), (o, pick), (rounds, turns), (size, chunk))]
+            (price, best), (o, pick), (trips * TURN, turns), (size, chunk))]
     tab[ROUNDS] = turns
     tab[PICK] = pick
 
     x0 = gray(me >> 1)
     left, right, opposite = (x0 - 1) & 3, (x0 + 1) & 3, (x0 + 2) & 3
+    shift = []
     for lid, d, x in ((S0, 0, x0), (S1, 1, x0), (R0, 0, left), (R1, 1, right)):
-        own, fwd, start = link(d, x, chunk)
-        near = hop[4 * d + x]
-        base = lid * WIDE
+        own, fwd, fwd2, start, _, start2 = link(d, x, chunk)
+        here, up = back(d, x, 0), back(d, x, 1)
+        base = zero + lid * WIDE
+        wide = 2 * (three[here] >> 16)
         pad = base + 2 * (own >> 16)
-        last = pad + 2 + 2 * (fwd >> 16)
+        pad2 = pad + 2 + 2 * (fwd >> 16)
         tab[pad] = start - (own & LOW)
+        tab[pad2] = start2 - start - (fwd & LOW)
+        last = pad2 + 2 + 2 * (fwd2 >> 16)
         tab[last] = zero + END
-        for a in (pad, last):
+        for a in (pad, pad2, last):
             tab[a + 1] = zero + NONE * HALF
-        for k, (where, pos) in enumerate(((base, 0), (base + 2 * (near >> 16), near & LOW), (pad + 2, start))):
-            addr[3 * lid + k] = zero + where
-            at[3 * lid + k] = zero + pos
-    addr[12] = zero + DUMP
-    at[12] = zero
+        hop3, hop2 = three[here], two[here]
+        segs = ((base, zero), (base + wide, hop3 & LOW), (base + wide + 2 * (hop2 >> 16), (hop3 + hop2) & LOW),
+                (pad + 2, start), (pad + 2 + 2 * (three[up] >> 16), start + (three[up] & LOW)), (pad2 + 2, start2))
+        for k, (where, pos) in enumerate(segs):
+            addr[SEGS * lid + k] = where
+            at[SEGS * lid + k] = pos
+        shift.append(((hop3 + hop2) & LOW) - start)
+    addr[IDLE] = zero + DUMP
+    at[IDLE] = zero
 
     def append(seg, hit, nb, code):
-        seg = jnp.where(hit, seg, 12)
+        seg = jnp.where(hit, seg, IDLE)
         a, p = addr[seg], at[seg]
         tab[a] = nb
         tab[a + 1] = code
@@ -163,35 +236,41 @@
     def source(s, c):
         i = (me >> 1) * 2 * SL + s
         kind = kindv[i]
-        seg = jnp.where(kind < 3, 2 - kind, 7 - kind)
+        seg = jnp.where(kind > 3, SEGS + 6, 3) - kind
         append(seg, kind > 0, nbv[i], ((s >> 5) << 16) + (s & 31) * BL)
         return c
 
     lax.fori_loop(0, 2 * SL, source, 0, unroll=4)
 
-    def arrive(seg, hit, i):
+    def visit(i, hit, seg, goes_on, seg_on, ahead):
+        nb = nbv[i]
         dst = dest_ref[i]
-        end = append(seg, hit, nbv[i], (((dst >> 5) & 1) << 16) + (dst & 31) * BL)
-        mine = hit & ((dst >> 5) == me)
+        code = jnp.where(goes_on, FWD * HALF + at[seg] + ahead, (((dst >> 5) & 1) << 16) + (dst & 31) * BL)
+        end = append(seg, hit, nb, code)
+        append(seg_on, goes_on, nb, code)
+        mine = hit & ((dst >> 5) == me) & jnp.logical_not(goes_on)
         tab[RDY + jnp.where(mine, dst & 31, SL)] = end
 
     for d, x in ((0, left), (1, right)):
-        def upstream(s, c):
+        def beside(s, c):
             i = gray(x) * 2 * SL + s
             kind = kindv[i]
-            hit = kind == 2 + 2 * d
-            code = FWD * HALF + at[6 + 3 * d]
-            append(6 + 3 * d, hit, nbv[i], code)
-            append(2 + 3 * d, hit, nbv[i], code)
-            arrive(7 + 3 * d, kind == 1 + 2 * d, i)
+            h = kind - 3 * d
+            along = (h > 0) & (h <= 3)
+            about = kind == 6 - 3 * d
+            seg = jnp.where(along, SEGS * (R0 + d) + 3 - h, SEGS * (R1 - d) + 5)
+            visit(i, along | about, seg, along & (h > 1), SEGS * d + 6 - h, 0)
             return c
 
-        lax.fori_loop(0, 2 * SL, upstream, 0, unroll=2)
+        lax.fori_loop(0, 2 * SL, beside, 0, unroll=2)
 
     def across(s, c):
         i = gray(opposite) * 2 * SL + s
         kind = kindv[i]
-        arrive(jnp.where(kind == 2, 8, 11), (kind == FWD) | (kind == 4), i)
+        d = jnp.where(kind > 3, 1, 0)
+        h = kind - 3 * d
+        seg = SEGS * (R0 + d) + jnp.where(h == 3, 3, 4)
+        visit(i, h > 1, seg, h == 3, SEGS * d + 5, jnp.where(d == 0, shift[R0], shift[R1]))
         return c
 
     lax.fori_loop(0, 2 * SL, across, 0, unroll=2)
@@ -346,111 +425,97 @@
         return self.walk(R0 + d, use + d, n, fn)
 
 
-def open_kernel(NB, tab, st_in, kc, vc, st, part0, part1, dxs, vpart, vdx, sem):
+def copies(pairs, sems):
+    made = [pltpu.make_async_copy(src, dst, sem) for (src, dst), sem in zip(pairs, sems)]
+    for c in made:
+        c.start()
+    return made
+
+
+def halves(ref):
+    return [ref.at[d] for d in range(2)]
+
+
+def finish(made):
+    for c in made:
+        c.wait()
+
+
+def open_kernel(NB, tab, st_in, kc, vc, st, part, vpart, sem):
     mv = Mover(tab, st_in, st, NB)
-    outs = [pltpu.make_async_copy(vpart.at[0], part0, sem.at[0]),
-            pltpu.make_async_copy(vpart.at[1], part1, sem.at[1]),
-            pltpu.make_async_copy(vdx, dxs, sem.at[2])]
-    cnt = [mv.partial(0, kc, vc, vpart.at[c], sem.at[c]) + mv.partial(1, kc, vc, vpart.at[c], sem.at[c]) for c in range(2)]
-    cnt.append(mv.cross_send(kc, vc, vdx, sem.at[2]))
-    for c in range(3):
-        mv.drain(cnt[c], kc, sem.at[c])
-        outs[c].start()
-    for c in outs:
-        c.wait()
-
-
-def open_merge_kernel(NB, tab, st_in, kc, vc, pre, st, send0, send1, part, vsend, vpart, sem):
+    mv.drain(sum(mv.partial(d, kc, vc, vpart, sem) for d in range(2)), kc, sem)
+    finish(copies([(vpart, part)], [sem]))
+
+
+def open_more_kernel(NB, tab, st_in, kc, vc, st, part1, part2, dxs, vpart, vdx, *sems):
     mv = Mover(tab, st_in, st, NB)
-    c0 = mv.merge(0, kc, vc, pre, None, vsend, sem.at[0])
-    c1 = mv.merge(1, kc, vc, pre, None, vsend, sem.at[1])
-    c2 = mv.partial(0, kc, vc, vpart, sem.at[2]) + mv.partial(1, kc, vc, vpart, sem.at[2])
-    mv.drain(c0, kc, sem.at[0])
-    mv.drain(c1, kc, sem.at[1])
-    mv.drain(c2, kc, sem.at[2])
-    outs = [pltpu.make_async_copy(vsend.at[0], send0, sem.at[0]),
-            pltpu.make_async_copy(vsend.at[1], send1, sem.at[1]),
-            pltpu.make_async_copy(vpart, part, sem.at[2])]
-    for c in outs:
-        c.start()
-    for c in outs:
-        c.wait()
+    cnt = [sum(mv.partial(d, kc, vc, buf, sem) for d in range(2)) for buf, sem in zip(halves(vpart), sems)]
+    cnt.append(mv.cross_send(kc, vc, vdx, sems[-1]))
+    made = []
+    for n, sem, pair in zip(cnt, sems, zip(halves(vpart) + [vdx], (part1, part2, dxs))):
+        mv.drain(n, kc, sem)
+        made += copies([pair], [sem])
+    finish(made)
+
+
+def open_merge_kernel(NB, tab, st_in, kc, vc, pre, st, send0, send1, vsend, *sems):
+    mv = Mover(tab, st_in, st, NB)
+    cnt = [mv.merge(d, kc, vc, pre, None, vsend, sem) for d, sem in enumerate(sems)]
+    made = []
+    for n, sem, pair in zip(cnt, sems, zip(halves(vsend), (send0, send1))):
+        mv.drain(n, kc, sem)
+        made += copies([pair], [sem])
+    finish(made)
 
 
 def round_kernel(NB, tab, st_in, kc, vc, pre, rc0, rc1, po0, po1, dxr, f0i, f1i, koi, voi,
                  st, send0, send1, part, dxs, f0, f1, ko, vo,
-                 vsend, vpart, vrecv, vpost, vdxs, vdxr, sem):
+                 vsend, vpart, vrecv, vpost, vdxs, vdxr, *sems):
     mv = Mover(tab, st_in, st, NB)
+    part_sem, cross_sem, out_sem, post_sem, *sems = sems
     r = st_in[STEP]
     st[STEP] = r + 1
-    ins = [pltpu.make_async_copy(rc0, vrecv.at[0], sem.at[0]),
-           pltpu.make_async_copy(rc1, vrecv.at[1], sem.at[1]),
-           pltpu.make_async_copy(po0, vpost.at[0], sem.at[2]),
-           pltpu.make_async_copy(po1, vpost.at[1], sem.at[3]),
-           pltpu.make_async_copy(dxr, vdxr, sem.at[4])]
-    for c in ins:
-        c.start()
-    n1 = jnp.where(r >= 1, NB, 0)
-    n2 = jnp.where(r >= 2, NB, 0)
-    nx = jnp.where(r >= 1, NX, 0)
-    cp = mv.partial(0, kc, vc, vpart, sem.at[5]) + mv.partial(1, kc, vc, vpart, sem.at[5])
-    cx = mv.cross_send(kc, vc, vdxs, sem.at[6])
-    ins[0].wait()
-    o0 = mv.unpack(0, U_OWN, n1, False, ko, vo, f0, vrecv, sem.at[7])
-    ins[1].wait()
-    o1 = mv.unpack(1, U_OWN, n1, False, ko, vo, f1, vrecv, sem.at[7])
-    mv.drain(o0 + o1, kc, sem.at[7])
-    c0 = mv.merge(0, kc, vc, pre, f0, vsend, sem.at[8])
-    c1 = mv.merge(1, kc, vc, pre, f1, vsend, sem.at[9])
-    ins[2].wait()
-    ins[3].wait()
-    o2 = mv.unpack(0, U_POST, n2, True, ko, vo, None, vpost, sem.at[7])
-    o3 = mv.unpack(1, U_POST, n2, True, ko, vo, None, vpost, sem.at[7])
-    ins[4].wait()
-    o4 = mv.cross_recv(nx, ko, vo, vdxr, sem.at[7])
-    mv.drain(cp, kc, sem.at[5])
-    mv.drain(cx, kc, sem.at[6])
-    mv.drain(c0, kc, sem.at[8])
-    mv.drain(c1, kc, sem.at[9])
-    outs = [pltpu.make_async_copy(vsend.at[0], send0, sem.at[0]),
-            pltpu.make_async_copy(vsend.at[1], send1, sem.at[1]),
-            pltpu.make_async_copy(vpart, part, sem.at[2]),
-            pltpu.make_async_copy(vdxs, dxs, sem.at[3])]
-    for c in outs:
-        c.start()
-    mv.drain(o2 + o3 + o4, kc, sem.at[7])
-    for c in outs:
-        c.wait()
+    ins = copies(zip([rc0, rc1, po0, po1, dxr], halves(vrecv) + halves(vpost) + [vdxr]), sems)
+    n1, n2, nx = [jnp.where(r >= back, n, 0) for back, n in ((1, NB), (2, NB), (1, NX))]
+    cp = sum(mv.partial(d, kc, vc, vpart, part_sem) for d in range(2))
+    cx = mv.cross_send(kc, vc, vdxs, cross_sem)
+    fwd = (f0, f1)
+    cnt = []
+    for d in range(2):
+        ins[d].wait()
+        cnt.append(mv.unpack(d, U_OWN, n1, False, ko, vo, fwd[d], vrecv, out_sem))
+    mv.drain(sum(cnt), kc, out_sem)
+    merged = [mv.merge(d, kc, vc, pre, fwd[d], vsend, sem) for d, sem in enumerate(sems[:2])]
+    finish(ins[2:])
+    cnt = sum(mv.unpack(d, U_POST, n2, True, ko, vo, None, vpost, post_sem) for d in range(2))
+    cnt += mv.cross_recv(nx, ko, vo, vdxr, post_sem)
+    outs = []
+    for n, sem, pair in zip(merged + [cp, cx], sems[:2] + [part_sem, cross_sem],
+                            zip(halves(vsend) + [vpart, vdxs], (send0, send1, part, dxs))):
+        mv.drain(n, kc, sem)
+        outs += copies([pair], [sem])
+    mv.drain(cnt, kc, post_sem)
+    finish(outs)
 
 
 def close_kernel(NB, last, tab, st_in, *refs):
     if last:
-        (po0, po1, koi, voi, st, ko, vo, vpost, sem) = refs
+        (po0, po1, koi, voi, st, ko, vo, vpost, *sems) = refs
+        pairs = zip((po0, po1), halves(vpost))
     else:
-        (rc0, rc1, po0, po1, dxr, koi, voi, st, ko, vo, vpost, vrecv, vdxr, sem) = refs
+        (rc0, rc1, po0, po1, dxr, koi, voi, st, ko, vo, vpost, vrecv, vdxr, *sems) = refs
+        pairs = zip((po0, po1, rc0, rc1, dxr), halves(vpost) + halves(vrecv) + [vdxr])
     mv = Mover(tab, st_in, st, NB)
+    sem = sems[-1]
     r = st_in[STEP]
     st[STEP] = r + 1
-    ins = [pltpu.make_async_copy(po0, vpost.at[0], sem.at[0]),
-           pltpu.make_async_copy(po1, vpost.at[1], sem.at[1])]
+    finish(copies(pairs, sems))
+    n1, n2, nx = [jnp.where(r >= back, n, 0) for back, n in ((1, NB), (2, NB), (1, NX))]
+    cnt = sum(mv.unpack(d, U_POST, n2, True, ko, vo, None, vpost, sem) for d in range(2))
     if not last:
-        ins += [pltpu.make_async_copy(rc0, vrecv.at[0], sem.at[2]),
-                pltpu.make_async_copy(rc1, vrecv.at[1], sem.at[3]),
-                pltpu.make_async_copy(dxr, vdxr, sem.at[4])]
-    for c in ins:
-        c.start()
-    n1 = jnp.where(r >= 1, NB, 0)
-    n2 = jnp.where(r >= 2, NB, 0)
-    nx = jnp.where(r >= 1, NX, 0)
-    for c in ins:
-        c.wait()
-    cnt = mv.unpack(0, U_POST, n2, True, ko, vo, None, vpost, sem.at[5])
-    cnt += mv.unpack(1, U_POST, n2, True, ko, vo, None, vpost, sem.at[5])
-    if not last:
-        cnt += mv.unpack(0, U_OWN, n1, False, ko, vo, None, vrecv, sem.at[5])
-        cnt += mv.unpack(1, U_OWN, n1, False, ko, vo, None, vrecv, sem.at[5])
-        cnt += mv.cross_recv(nx, ko, vo, vdxr, sem.at[5])
-    mv.drain(cnt, ko, sem.at[5])
+        cnt += sum(mv.unpack(d, U_OWN, n1, False, ko, vo, None, vrecv, sem) for d in range(2))
+        cnt += mv.cross_recv(nx, ko, vo, vdxr, sem)
+    mv.drain(cnt, ko, sem)
 
 
 def attn_kernel(NB, batches, tab, st_in, q, kn, vn, kc, vc, koi, voi, aoi, st, ko, vo, ao,
@@ -571,6 +636,8 @@
 
 
 ST = sds((STATE,), i32)
+DMA = [pltpu.SemaphoreType.DMA]
+TAGS = ('ra', 'rb', 'rc', 'rd')
 
 
 def solution(mesh):
@@ -591,7 +658,7 @@
         me = jnp.full((1,), lax.axis_index('dp'), i32)
         tab, lens_out = pl.pallas_call(
             plan_kernel, out_shape=(sds((TAB,), i32), sds((SL,), i32)), in_specs=[SMEM] * 3, out_specs=(SMEM, SMEM),
-            scratch_shapes=[pltpu.SMEM((8 * SL + 1,), i32)] * 3 + [pltpu.SMEM((16,), i32)] * 5,
+            scratch_shapes=[pltpu.SMEM((8 * SL + 1,), i32)] * 4 + [pltpu.SMEM((IDLE + 1,), i32)] * 7,
             name='plan')(me, dest_slot, lens_all)
 
         def run(NB):
@@ -599,21 +666,27 @@
                 pass
 
             chunk, both, cross = sds((NB,) + BLOCK), sds((2, NB) + BLOCK), sds((2, NX) + BLOCK)
-            cache, store = sds((SL * BL,) + BLOCK), sds((2 * SL * BL,) + BLOCK)
+            cache, store = sds((SL * BL,) + BLOCK), sds((4 * SL * BL,) + BLOCK)
             ko, vo, ao, f0, f1, rc0, rc1, po0, po1, dxr = pl.pallas_call(
                 nothing, out_shape=(cache, cache, sds((SL, 24, 128)), store, store, chunk, chunk, chunk, chunk, cross),
                 out_specs=(ANY,) * 10, name='blank')()
 
             st = jnp.zeros((STATE,), i32)
-            st, part0, part1, dxs = pl.pallas_call(
-                functools.partial(open_kernel, NB), out_shape=(ST, both, both, cross), in_specs=[SMEM, SMEM, ANY, ANY], out_specs=(SMEM, ANY, ANY, ANY),
-                scratch_shapes=[buf(2, 2, NB), buf(2, NX), dma(3)], name='open')(tab, st, kc, vc)
-            pre0 = lax.ppermute(part0, 'dp', swap)
-            pre = lax.ppermute(part1, 'dp', swap)
-            st, s0, s1, part = pl.pallas_call(
-                functools.partial(open_merge_kernel, NB), out_shape=(ST, chunk, chunk, both), in_specs=[SMEM, SMEM, ANY, ANY, ANY],
-                out_specs=(SMEM, ANY, ANY, ANY), scratch_shapes=[buf(2, NB), buf(2, NB), dma(3)],
-                name='open_merge')(tab, st, kc, vc, pre0)
+            caches = [SMEM, SMEM, ANY, ANY]
+            st, part = pl.pallas_call(
+                functools.partial(open_kernel, NB), out_shape=(ST, both), in_specs=caches, out_specs=(SMEM, ANY),
+                scratch_shapes=[buf(2, NB)] + DMA, name='open')(tab, st, kc, vc)
+            pre = lax.ppermute(part, 'dp', swap)
+            st, part1, part, dxs = pl.pallas_call(
+                functools.partial(open_more_kernel, NB), out_shape=(ST, both, both, cross), in_specs=caches,
+                out_specs=(SMEM,) + (ANY,) * 3, scratch_shapes=[buf(2, 2, NB), buf(2, NX)] + DMA * 3,
+                name='open_more')(tab, st, kc, vc)
+            pre1 = lax.ppermute(part1, 'dp', swap)
+            st, s0, s1 = pl.pallas_call(
+                functools.partial(open_merge_kernel, NB), out_shape=(ST, chunk, chunk), in_specs=caches + [VMEM],
+                out_specs=(SMEM, ANY, ANY), scratch_shapes=[buf(2, NB)] + DMA * 2,
+                name='open_merge')(tab, st, kc, vc, pre)
+            pre = pre1
 
             def attend(st, ko, vo, ao, batches):
                 return pl.pallas_call(
@@ -635,19 +708,19 @@
                 ndxr = lax.ppermute(dxs, 'dp', swap)
                 st, s0, s1, part, dxs, f0, f1, ko, vo = pl.pallas_call(
                     functools.partial(round_kernel, NB), out_shape=(ST, chunk, chunk, both, cross, store, store, cache, cache),
-                    in_specs=[SMEM, SMEM] + [ANY] * 12, out_specs=(SMEM,) + (ANY,) * 8,
+                    in_specs=caches + [VMEM] + [ANY] * 9, out_specs=(SMEM,) + (ANY,) * 8,
                     input_output_aliases={10: 5, 11: 6, 12: 7, 13: 8},
-                    scratch_shapes=[buf(2, NB)] * 4 + [buf(2, NX)] * 2 + [dma(10)],
+                    scratch_shapes=[buf(2, NB)] * 4 + [buf(2, NX)] * 2 + DMA * 9,
                     cost_estimate=cost(10), name='round')(tab, st, kc, vc, pre, rc0, rc1, po0, po1, dxr, f0, f1, ko, vo)
                 st, ko, vo, ao = attend(st, ko, vo, ao, 1)
-                if tag == 'ra':
+                if tag != TAGS[-1]:
                     s0, s1, npo0, npo1 = lax.optimization_barrier((s0, s1, npo0, npo1))
                 return st, s0, s1, part, dxs, npre, nrc0, nrc1, npo0, npo1, ndxr, f0, f1, ko, vo, ao
 
             rounds = tab[ROUNDS]
 
             def body(c):
-                return (c[0] + 2,) + one_round('rb', one_round('ra', c[1:]))
+                return (c[0] + TURN,) + functools.reduce(lambda c, tag: one_round(tag, c), TAGS, c[1:])
 
             c = lax.while_loop(lambda c: c[0] < rounds, body,
                            (jnp.int32(0), st, s0, s1, part, dxs, pre, rc0, rc1, po0, po1, dxr, f0, f1, ko, vo, ao))
@@ -658,9 +731,9 @@
                 extra = [] if last else [buf(2, NB), buf(2, NX)]
                 return pl.pallas_call(
                     functools.partial(close_kernel, NB, last), out_shape=(ST, cache, cache),
-                    in_specs=[SMEM, SMEM] + [ANY] * (n + 2), out_specs=(SMEM, ANY, ANY),
+                    in_specs=[SMEM, SMEM] + [VMEM if last else ANY] * n + [ANY] * 2, out_specs=(SMEM, ANY, ANY),
                     input_output_aliases={n + 2: 1, n + 3: 2},
-                    scratch_shapes=[buf(2, NB)] + extra + [dma(6)],
+                    scratch_shapes=[buf(2, NB)] + extra + DMA * 6,
                     name='close_last' if last else 'close')(tab, st, *ins, ko, vo)
 
             lpo0 = lax.ppermute(rc0, 'dp', swap)

time: 860 us -> 854 us (level)
  waiting for transfers between devices: 282 us -> 358 us
  local copies, waits for them, and re-layouts: 50.7 us -> 4.36 us
  starting transfers between devices: 101 us -> 77.1 us
    ppermute x28 -> x24, waiting for transfers between devices: 15 us -> 86.7 us  [one_round(): nrc0 = lax.ppermute(s0, 'dp', cw)]
    while x98 -> x48, local copies, waits for them, and re-layouts: 46.7 us -> 0.1 us
    ppermute x28 -> x24, waiting for transfers between devices: 249 us -> 271 us  [one_round(): nrc1 = lax.ppermute(s1, 'dp', ccw)]
    ppermute x28 -> x24, starting transfers between devices: 31.8 us -> 12.1 us  [one_round(): nrc0 = lax.ppermute(s0, 'dp', cw)]
    ppermute x28 -> x24, waiting for transfers between devices: 14.9 us -> 0.06 us  [one_round(): npo0 = lax.ppermute(rc0, 'dp', swap)]
    pallas_call x29 -> x25, Pallas kernels: 148 us -> 136 us  [attend(): pl.pallas_call(functools.partial(attn_kernel, NB, batches), out_shape=(ST...]
    ppermute x28 -> x24, starting transfers between devices: 5.71 us -> 15.1 us  [one_round(): ndxr = lax.ppermute(dxs, 'dp', swap)]
    pallas_call x28 -> x24, Pallas kernels: 220 us -> 217 us  [one_round(): pl.pallas_call(functools.partial(round_kernel, NB), out_shape=(ST, chunk,...]
  transfers between devices with their start and end apart: 172 -> 148, of which waited for: 41 -> 41; matrix products, arithmetic and copies ran while one was open for 4% -> 0% of each run, Pallas kernels for 43% -> 42%
where the time goes in v2:
time: 854 us; the launch traced here: 850 us
  Pallas kernels  403 us (47%)
  waiting for transfers between devices  358 us (42%)
  starting transfers between devices  77.1 us (9%)
    ppermute x24, waiting for transfers between devices, one_round(): nrc1 = lax.ppermute(s1, 'dp', ccw)  271 us
    pallas_call x24, Pallas kernels, one_round(): pl.pallas_call(functools.partial(round_kernel, NB), out_shape=(ST, chunk,...  217 us
    pallas_call x25, Pallas kernels, attend(): pl.pallas_call(functools.partial(attn_kernel, NB, batches), out_shape=(ST...  136 us
    ppermute x24, waiting for transfers between devices, one_round(): nrc0 = lax.ppermute(s0, 'dp', cw)  86.7 us
    ppermute x24, starting transfers between devices, one_round(): nrc1 = lax.ppermute(s1, 'dp', ccw)  34.7 us
    pallas_call x1, Pallas kernels, local(): pl.pallas_call(plan_kernel, out_shape=(sds((TAB,), i32), sds((SL,), i32))...  19.2 us
  transfers between devices with their start and end apart: 148, of which 41 were waited for; matrix products, arithmetic and copies ran while one was open for 0% of the time, Pallas kernels for 42%

profile of v2, /device:TPU:0, one launch (start us, length us, event | category | flops | bytes accessed | tf_op | source)
XLA Modules:
  0.0 850.2 jit_solution(7053583745827250312)
XLA Ops:
  0.6 7.8 lens.1.len_ref
  8.4 19.2 %plan.1 = (s32[2568]{0:T(1024)S(1)}, s32[32]{0:T(128)}) custom-call(s32[1]{0:T(128)} %bitcast.4.me_ref, s32[256]{0:T(256)} %dest_ref.1, s32[8,1,32]{2,1,0:T(1,128)} %lens.1.len_ref), custom_call_target="tpu_custom_call" | custom-call | tf_op jit(solution)/shard_map/plan/pallas_call | solution.py:659
  28.9 821.1 %conditional.1 = (bf16[32,24,128]{2,1,0:T(8,128)(2,1)}, bf16[2048,64,128]{2,1,0:T(8,128)(2,1)}, bf16[2048,64,128]{2,1,0:T(8,128)(2,1)}) conditional(s32[]{:T(128)} %bitcast.6, (s32[2568]{0:T(1024)S(1)}, bf16[2048,64,128]{2,1,0:T(8,128)(2,1)}, bf16[2048,64,128]{2,1,0:T(8,128)(2,1)}, bf16[32,24,128]{2,1,0:T(8,128)(2,1)}, ...), branch_computations={%region_0.0_spmd, %region_3.0_spmd, %region_6.0_spmd, %region_9.0_... | conditional | flops 280000000 | bytes 474906112 | solution.py:746
  46.8 783.8 %while.157 = (s32[]{:T(128)}, s32[64]{0:T(128)S(1)}, bf16[60,64,128]{2,1,0:T(8,128)(2,1)}, bf16[60,64,128]{2,1,0:T(8,128)(2,1)}, bf16[2,60,64,128]{3,2,1,0:T(8,1...) while((s32[]{:T(128)}, s32[64]{0:T(128)S(1)}, ...), condition=%wide.region_5.0_spmd, body=%wide.region_4.0_spmd.sunk | while | flops 256000000 | bytes 387597440 | solution.py:725
  50.2 21.0 %collective-permute-done.58.rc1 = bf16[60,64,128]{2,1,0:T(8,128)(2,1)} collective-permute-done((bf16[60,64,128]{2,1,0:T(8,128)(2,1)}, bf16[60,64,128]{2,1,0:T(8,128)(2,1)}, u32[]{:S(2)}, u32[]{:S(2)}) %collective-permute-start.58) | collective-permute-done | bytes 983072 | tf_op jit(solution)/shard_map/cond/branch_1_fun/while/body/ppermute | solution.py:704
  72.7 8.8 %round.24 = (s32[64]{0:T(128)}, bf16[60,64,128]{2,1,0:T(8,128)(2,1)}, bf16[60,64,128]{2,1,0:T(8,128)(2,1)}, bf16[2,60,64,128]{3,2,1,0:T(8,128)(2,1)}, bf16[2,32,...) custom-call(s32[2568]{0:T(1024)S(1)} %get-tuple-element.2484.tab, ...), custom_call_target="tpu_custom_call", output_to_operand_aliasing={{5}: (10, {}), {6}: (11, {}), {7}: (12, {}), {8}: (13, {})} | custom-call | flops 40000000 | bytes 40000000 | tf_op jit(solution)/shard_map/cond/branch_1_fun/while/body/round/pallas_call | solution.py:709
  84.1 6.8 attend.32
  90.9 9.5 %round.25 = (s32[64]{0:T(128)}, bf16[60,64,128]{2,1,0:T(8,128)(2,1)}, bf16[60,64,128]{2,1,0:T(8,128)(2,1)}, bf16[2,60,64,128]{3,2,1,0:T(8,128)(2,1)}, bf16[2,32,...) custom-call(s32[2568]{0:T(1024)S(1)} %get-tuple-element.2484.tab, ...), custom_call_target="tpu_custom_call", output_to_operand_aliasing={{5}: (10, {}), {6}: (11, {}), {7}: (12, {}), {8}: (13, {})} | custom-call | flops 40000000 | bytes 40000000 | tf_op jit(solution)/shard_map/cond/branch_1_fun/while/body/round/pallas_call | solution.py:709
  115.0 9.3 %round.26 = (s32[64]{0:T(128)}, bf16[60,64,128]{2,1,0:T(8,128)(2,1)}, bf16[60,64,128]{2,1,0:T(8,128)(2,1)}, bf16[2,60,64,128]{3,2,1,0:T(8,128)(2,1)}, bf16[2,32,...) custom-call(s32[2568]{0:T(1024)S(1)} %get-tuple-element.2484.tab, ...), custom_call_target="tpu_custom_call", output_to_operand_aliasing={{5}: (10, {}), {6}: (11, {}), {7}: (12, {}), {8}: (13, {})} | custom-call | flops 40000000 | bytes 40000000 | tf_op jit(solution)/shard_map/cond/branch_1_fun/while/body/round/pallas_call | solution.py:709
  128.6 23.5 %collective-permute-done.70.rc1 = bf16[60,64,128]{2,1,0:T(8,128)(2,1)} collective-permute-done((bf16[60,64,128]{2,1,0:T(8,128)(2,1)}, bf16[60,64,128]{2,1,0:T(8,128)(2,1)}, u32[]{:S(2)}, u32[]{:S(2)}) %collective-permute-start.70) | collective-permute-done | bytes 983072 | tf_op jit(solution)/shard_map/cond/branch_1_fun/while/body/ppermute | solution.py:704
  154.6 5.4 attend.34
  160.1 9.5 %round.27 = (s32[64]{0:T(128)}, bf16[60,64,128]{2,1,0:T(8,128)(2,1)}, bf16[60,64,128]{2,1,0:T(8,128)(2,1)}, bf16[2,60,64,128]{3,2,1,0:T(8,128)(2,1)}, bf16[2,32,...) custom-call(s32[2568]{0:T(1024)S(1)} %get-tuple-element.2484.tab, ...), custom_call_target="tpu_custom_call", output_to_operand_aliasing={{5}: (10, {}), {6}: (11, {}), {7}: (12, {}), {8}: (13, {})} | custom-call | flops 40000000 | bytes 40000000 | tf_op jit(solution)/shard_map/cond/branch_1_fun/while/body/round/pallas_call | solution.py:709
  180.1 20.6 %collective-permute-done.58.rc1 = bf16[60,64,128]{2,1,0:T(8,128)(2,1)} collective-permute-done((bf16[60,64,128]{2,1,0:T(8,128)(2,1)}, bf16[60,64,128]{2,1,0:T(8,128)(2,1)}, u32[]{:S(2)}, u32[]{:S(2)}) %collective-permute-start.58) | collective-permute-done | bytes 983072 | tf_op jit(solution)/shard_map/cond/branch_1_fun/while/body/ppermute | solution.py:704
  204.1 9.5 %round.24 = (s32[64]{0:T(128)}, bf16[60,64,128]{2,1,0:T(8,128)(2,1)}, bf16[60,64,128]{2,1,0:T(8,128)(2,1)}, bf16[2,60,64,128]{3,2,1,0:T(8,128)(2,1)}, bf16[2,32,...) custom-call(s32[2568]{0:T(1024)S(1)} %get-tuple-element.2484.tab, ...), custom_call_target="tpu_custom_call", output_to_operand_aliasing={{5}: (10, {}), {6}: (11, {}), {7}: (12, {}), {8}: (13, {})} | custom-call | flops 40000000 | bytes 40000000 | tf_op jit(solution)/shard_map/cond/branch_1_fun/while/body/round/pallas_call | solution.py:709
  216.2 5.3 attend.32
  221.6 9.6 %round.25 = (s32[64]{0:T(128)}, bf16[60,64,128]{2,1,0:T(8,128)(2,1)}, bf16[60,64,128]{2,1,0:T(8,128)(2,1)}, bf16[2,60,64,128]{3,2,1,0:T(8,128)(2,1)}, bf16[2,32,...) custom-call(s32[2568]{0:T(1024)S(1)} %get-tuple-element.2484.tab, ...), custom_call_target="tpu_custom_call", output_to_operand_aliasing={{5}: (10, {}), {6}: (11, {}), {7}: (12, {}), {8}: (13, {})} | custom-call | flops 40000000 | bytes 40000000 | tf_op jit(solution)/shard_map/cond/branch_1_fun/while/body/round/pallas_call | solution.py:709
  231.2 7.9 collective-permute-done.63.rc0
  245.8 9.6 %round.26 = (s32[64]{0:T(128)}, bf16[60,64,128]{2,1,0:T(8,128)(2,1)}, bf16[60,64,128]{2,1,0:T(8,128)(2,1)}, bf16[2,60,64,128]{3,2,1,0:T(8,128)(2,1)}, bf16[2,32,...) custom-call(s32[2568]{0:T(1024)S(1)} %get-tuple-element.2484.tab, ...), custom_call_target="tpu_custom_call", output_to_operand_aliasing={{5}: (10, {}), {6}: (11, {}), {7}: (12, {}), {8}: (13, {})} | custom-call | flops 40000000 | bytes 40000000 | tf_op jit(solution)/shard_map/cond/branch_1_fun/while/body/round/pallas_call | solution.py:709
  260.7 23.5 %collective-permute-done.70.rc1 = bf16[60,64,128]{2,1,0:T(8,128)(2,1)} collective-permute-done((bf16[60,64,128]{2,1,0:T(8,128)(2,1)}, bf16[60,64,128]{2,1,0:T(8,128)(2,1)}, u32[]{:S(2)}, u32[]{:S(2)}) %collective-permute-start.70) | collective-permute-done | bytes 983072 | tf_op jit(solution)/shard_map/cond/branch_1_fun/while/body/ppermute | solution.py:704
  286.8 5.3 attend.34
  292.1 9.3 %round.27 = (s32[64]{0:T(128)}, bf16[60,64,128]{2,1,0:T(8,128)(2,1)}, bf16[60,64,128]{2,1,0:T(8,128)(2,1)}, bf16[2,60,64,128]{3,2,1,0:T(8,128)(2,1)}, bf16[2,32,...) custom-call(s32[2568]{0:T(1024)S(1)} %get-tuple-element.2484.tab, ...), custom_call_target="tpu_custom_call", output_to_operand_aliasing={{5}: (10, {}), {6}: (11, {}), {7}: (12, {}), {8}: (13, {})} | custom-call | flops 40000000 | bytes 40000000 | tf_op jit(solution)/shard_map/cond/branch_1_fun/while/body/round/pallas_call | solution.py:709
  301.4 5.8 attend.35
  312.2 20.6 %collective-permute-done.58.rc1 = bf16[60,64,128]{2,1,0:T(8,128)(2,1)} collective-permute-done((bf16[60,64,128]{2,1,0:T(8,128)(2,1)}, bf16[60,64,128]{2,1,0:T(8,128)(2,1)}, u32[]{:S(2)}, u32[]{:S(2)}) %collective-permute-start.58) | collective-permute-done | bytes 983072 | tf_op jit(solution)/shard_map/cond/branch_1_fun/while/body/ppermute | solution.py:704
  334.3 9.8 %round.24 = (s32[64]{0:T(128)}, bf16[60,64,128]{2,1,0:T(8,128)(2,1)}, bf16[60,64,128]{2,1,0:T(8,128)(2,1)}, bf16[2,60,64,128]{3,2,1,0:T(8,128)(2,1)}, bf16[2,32,...) custom-call(s32[2568]{0:T(1024)S(1)} %get-tuple-element.2484.tab, ...), custom_call_target="tpu_custom_call", output_to_operand_aliasing={{5}: (10, {}), {6}: (11, {}), {7}: (12, {}), {8}: (13, {})} | custom-call | flops 40000000 | bytes 40000000 | tf_op jit(solution)/shard_map/cond/branch_1_fun/while/body/round/pallas_call | solution.py:709
  346.8 6.5 attend.32
  353.3 8.9 %round.25 = (s32[64]{0:T(128)}, bf16[60,64,128]{2,1,0:T(8,128)(2,1)}, bf16[60,64,128]{2,1,0:T(8,128)(2,1)}, bf16[2,60,64,128]{3,2,1,0:T(8,128)(2,1)}, bf16[2,32,...) custom-call(s32[2568]{0:T(1024)S(1)} %get-tuple-element.2484.tab, ...), custom_call_target="tpu_custom_call", output_to_operand_aliasing={{5}: (10, {}), {6}: (11, {}), {7}: (12, {}), {8}: (13, {})} | custom-call | flops 40000000 | bytes 40000000 | tf_op jit(solution)/shard_map/cond/branch_1_fun/while/body/round/pallas_call | solution.py:709
  362.2 7.5 collective-permute-done.63.rc0
  370.2 6.5 attend.33
  376.8 9.1 %round.26 = (s32[64]{0:T(128)}, bf16[60,64,128]{2,1,0:T(8,128)(2,1)}, bf16[60,64,128]{2,1,0:T(8,128)(2,1)}, bf16[2,60,64,128]{3,2,1,0:T(8,128)(2,1)}, bf16[2,32,...) custom-call(s32[2568]{0:T(1024)S(1)} %get-tuple-element.2484.tab, ...), custom_call_target="tpu_custom_call", output_to_operand_aliasing={{5}: (10, {}), {6}: (11, {}), {7}: (12, {}), {8}: (13, {})} | custom-call | flops 40000000 | bytes 40000000 | tf_op jit(solution)/shard_map/cond/branch_1_fun/while/body/round/pallas_call | solution.py:709
  391.0 23.8 %collective-permute-done.70.rc1 = bf16[60,64,128]{2,1,0:T(8,128)(2,1)} collective-permute-done((bf16[60,64,128]{2,1,0:T(8,128)(2,1)}, bf16[60,64,128]{2,1,0:T(8,128)(2,1)}, u32[]{:S(2)}, u32[]{:S(2)}) %collective-permute-start.70) | collective-permute-done | bytes 983072 | tf_op jit(solution)/shard_map/cond/branch_1_fun/while/body/ppermute | solution.py:704
  417.3 7.4 attend.34
  424.7 8.4 round.27
  442.8 20.6 %collective-permute-done.58.rc1 = bf16[60,64,128]{2,1,0:T(8,128)(2,1)} collective-permute-done((bf16[60,64,128]{2,1,0:T(8,128)(2,1)}, bf16[60,64,128]{2,1,0:T(8,128)(2,1)}, u32[]{:S(2)}, u32[]{:S(2)}) %collective-permute-start.58) | collective-permute-done | bytes 983072 | tf_op jit(solution)/shard_map/cond/branch_1_fun/while/body/ppermute | solution.py:704
  464.8 8.2 round.24
  477.3 5.3 attend.32
  482.7 8.7 %round.25 = (s32[64]{0:T(128)}, bf16[60,64,128]{2,1,0:T(8,128)(2,1)}, bf16[60,64,128]{2,1,0:T(8,128)(2,1)}, bf16[2,60,64,128]{3,2,1,0:T(8,128)(2,1)}, bf16[2,32,...) custom-call(s32[2568]{0:T(1024)S(1)} %get-tuple-element.2484.tab, ...), custom_call_target="tpu_custom_call", output_to_operand_aliasing={{5}: (10, {}), {6}: (11, {}), {7}: (12, {}), {8}: (13, {})} | custom-call | flops 40000000 | bytes 40000000 | tf_op jit(solution)/shard_map/cond/branch_1_fun/while/body/round/pallas_call | solution.py:709
  491.4 8.8 %collective-permute-done.63.rc0 = bf16[60,64,128]{2,1,0:T(8,128)(2,1)} collective-permute-done((bf16[60,64,128]{2,1,0:T(8,128)(2,1)}, bf16[60,64,128]{2,1,0:T(8,128)(2,1)}, u32[]{:S(2)}, u32[]{:S(2)}) %collective-permute-start.63) | collective-permute-done | bytes 983072 | tf_op jit(solution)/shard_map/cond/branch_1_fun/while/body/ppermute | solution.py:703
  500.8 5.3 attend.33
  507.7 8.3 round.26
  521.5 23.4 %collective-permute-done.70.rc1 = bf16[60,64,128]{2,1,0:T(8,128)(2,1)} collective-permute-done((bf16[60,64,128]{2,1,0:T(8,128)(2,1)}, bf16[60,64,128]{2,1,0:T(8,128)(2,1)}, u32[]{:S(2)}, u32[]{:S(2)}) %collective-permute-start.70) | collective-permute-done | bytes 983072 | tf_op jit(solution)/shard_map/cond/branch_1_fun/while/body/ppermute | solution.py:704
  549.8 8.5 %round.27 = (s32[64]{0:T(128)}, bf16[60,64,128]{2,1,0:T(8,128)(2,1)}, bf16[60,64,128]{2,1,0:T(8,128)(2,1)}, bf16[2,60,64,128]{3,2,1,0:T(8,128)(2,1)}, bf16[2,32,...) custom-call(s32[2568]{0:T(1024)S(1)} %get-tuple-element.2484.tab, ...), custom_call_target="tpu_custom_call", output_to_operand_aliasing={{5}: (10, {}), {6}: (11, {}), {7}: (12, {}), {8}: (13, {})} | custom-call | flops 40000000 | bytes 40000000 | tf_op jit(solution)/shard_map/cond/branch_1_fun/while/body/round/pallas_call | solution.py:709
  558.4 6.8 attend.35
  573.0 20.6 %collective-permute-done.58.rc1 = bf16[60,64,128]{2,1,0:T(8,128)(2,1)} collective-permute-done((bf16[60,64,128]{2,1,0:T(8,128)(2,1)}, bf16[60,64,128]{2,1,0:T(8,128)(2,1)}, u32[]{:S(2)}, u32[]{:S(2)}) %collective-permute-start.58) | collective-permute-done | bytes 983072 | tf_op jit(solution)/shard_map/cond/branch_1_fun/while/body/ppermute | solution.py:704
  595.0 9.1 %round.24 = (s32[64]{0:T(128)}, bf16[60,64,128]{2,1,0:T(8,128)(2,1)}, bf16[60,64,128]{2,1,0:T(8,128)(2,1)}, bf16[2,60,64,128]{3,2,1,0:T(8,128)(2,1)}, bf16[2,32,...) custom-call(s32[2568]{0:T(1024)S(1)} %get-tuple-element.2484.tab, ...), custom_call_target="tpu_custom_call", output_to_operand_aliasing={{5}: (10, {}), {6}: (11, {}), {7}: (12, {}), {8}: (13, {})} | custom-call | flops 40000000 | bytes 40000000 | tf_op jit(solution)/shard_map/cond/branch_1_fun/while/body/round/pallas_call | solution.py:709
  607.1 6.6 attend.32
  613.7 9.3 %round.25 = (s32[64]{0:T(128)}, bf16[60,64,128]{2,1,0:T(8,128)(2,1)}, bf16[60,64,128]{2,1,0:T(8,128)(2,1)}, bf16[2,60,64,128]{3,2,1,0:T(8,128)(2,1)}, bf16[2,32,...) custom-call(s32[2568]{0:T(1024)S(1)} %get-tuple-element.2484.tab, ...), custom_call_target="tpu_custom_call", output_to_operand_aliasing={{5}: (10, {}), {6}: (11, {}), {7}: (12, {}), {8}: (13, {})} | custom-call | flops 40000000 | bytes 40000000 | tf_op jit(solution)/shard_map/cond/branch_1_fun/while/body/round/pallas_call | solution.py:709
  623.1 6.9 collective-permute-done.63.rc0
  636.4 9.1 %round.26 = (s32[64]{0:T(128)}, bf16[60,64,128]{2,1,0:T(8,128)(2,1)}, bf16[60,64,128]{2,1,0:T(8,128)(2,1)}, bf16[2,60,64,128]{3,2,1,0:T(8,128)(2,1)}, bf16[2,32,...) custom-call(s32[2568]{0:T(1024)S(1)} %get-tuple-element.2484.tab, ...), custom_call_target="tpu_custom_call", output_to_operand_aliasing={{5}: (10, {}), {6}: (11, {}), {7}: (12, {}), {8}: (13, {})} | custom-call | flops 40000000 | bytes 40000000 | tf_op jit(solution)/shard_map/cond/branch_1_fun/while/body/round/pallas_call | solution.py:709
  652.0 22.7 %collective-permute-done.70.rc1 = bf16[60,64,128]{2,1,0:T(8,128)(2,1)} collective-permute-done((bf16[60,64,128]{2,1,0:T(8,128)(2,1)}, bf16[60,64,128]{2,1,0:T(8,128)(2,1)}, u32[]{:S(2)}, u32[]{:S(2)}) %collective-permute-start.70) | collective-permute-done | bytes 983072 | tf_op jit(solution)/shard_map/cond/branch_1_fun/while/body/ppermute | solution.py:704
  677.2 6.4 attend.34
  683.6 9.0 %round.27 = (s32[64]{0:T(128)}, bf16[60,64,128]{2,1,0:T(8,128)(2,1)}, bf16[60,64,128]{2,1,0:T(8,128)(2,1)}, bf16[2,60,64,128]{3,2,1,0:T(8,128)(2,1)}, bf16[2,32,...) custom-call(s32[2568]{0:T(1024)S(1)} %get-tuple-element.2484.tab, ...), custom_call_target="tpu_custom_call", output_to_operand_aliasing={{5}: (10, {}), {6}: (11, {}), {7}: (12, {}), {8}: (13, {})} | custom-call | flops 40000000 | bytes 40000000 | tf_op jit(solution)/shard_map/cond/branch_1_fun/while/body/round/pallas_call | solution.py:709
  692.6 6.5 attend.35
  703.4 20.6 %collective-permute-done.58.rc1 = bf16[60,64,128]{2,1,0:T(8,128)(2,1)} collective-permute-done((bf16[60,64,128]{2,1,0:T(8,128)(2,1)}, bf16[60,64,128]{2,1,0:T(8,128)(2,1)}, u32[]{:S(2)}, u32[]{:S(2)}) %collective-permute-start.58) | collective-permute-done | bytes 983072 | tf_op jit(solution)/shard_map/cond/branch_1_fun/while/body/ppermute | solution.py:704
  724.8 9.5 %round.24 = (s32[64]{0:T(128)}, bf16[60,64,128]{2,1,0:T(8,128)(2,1)}, bf16[60,64,128]{2,1,0:T(8,128)(2,1)}, bf16[2,60,64,128]{3,2,1,0:T(8,128)(2,1)}, bf16[2,32,...) custom-call(s32[2568]{0:T(1024)S(1)} %get-tuple-element.2484.tab, ...), custom_call_target="tpu_custom_call", output_to_operand_aliasing={{5}: (10, {}), {6}: (11, {}), {7}: (12, {}), {8}: (13, {})} | custom-call | flops 40000000 | bytes 40000000 | tf_op jit(solution)/shard_map/cond/branch_1_fun/while/body/round/pallas_call | solution.py:709
  736.9 5.3 attend.32
  742.3 9.5 %round.25 = (s32[64]{0:T(128)}, bf16[60,64,128]{2,1,0:T(8,128)(2,1)}, bf16[60,64,128]{2,1,0:T(8,128)(2,1)}, bf16[2,60,64,128]{3,2,1,0:T(8,128)(2,1)}, bf16[2,32,...) custom-call(s32[2568]{0:T(1024)S(1)} %get-tuple-element.2484.tab, ...), custom_call_target="tpu_custom_call", output_to_operand_aliasing={{5}: (10, {}), {6}: (11, {}), {7}: (12, {}), {8}: (13, {})} | custom-call | flops 40000000 | bytes 40000000 | tf_op jit(solution)/shard_map/cond/branch_1_fun/while/body/round/pallas_call | solution.py:709
  754.2 5.6 collective-permute-done.63.rc0
  760.4 6.3 attend.33
  766.7 8.8 %round.26 = (s32[64]{0:T(128)}, bf16[60,64,128]{2,1,0:T(8,128)(2,1)}, bf16[60,64,128]{2,1,0:T(8,128)(2,1)}, bf16[2,60,64,128]{3,2,1,0:T(8,128)(2,1)}, bf16[2,32,...) custom-call(s32[2568]{0:T(1024)S(1)} %get-tuple-element.2484.tab, ...), custom_call_target="tpu_custom_call", output_to_operand_aliasing={{5}: (10, {}), {6}: (11, {}), {7}: (12, {}), {8}: (13, {})} | custom-call | flops 40000000 | bytes 40000000 | tf_op jit(solution)/shard_map/cond/branch_1_fun/while/body/round/pallas_call | solution.py:709
  782.2 22.7 %collective-permute-done.70.rc1 = bf16[60,64,128]{2,1,0:T(8,128)(2,1)} collective-permute-done((bf16[60,64,128]{2,1,0:T(8,128)(2,1)}, bf16[60,64,128]{2,1,0:T(8,128)(2,1)}, u32[]{:S(2)}, u32[]{:S(2)}) %collective-permute-start.70) | collective-permute-done | bytes 983072 | tf_op jit(solution)/shard_map/cond/branch_1_fun/while/body/ppermute | solution.py:704
  807.4 6.3 attend.34
  813.7 7.8 round.27
  821.6 5.6 attend.35
  840.4 9.4 %attend.21 = (s32[64]{0:T(128)}, bf16[2048,64,128]{2,1,0:T(8,128)(2,1)}, bf16[2048,64,128]{2,1,0:T(8,128)(2,1)}, bf16[32,24,128]{2,1,0:T(8,128)(2,1)}) custom-call(s32[2568]{0:T(1024)S(1)} %get-tuple-element.2599, s32[64]{0:T(128)} %get-tuple-element.691.st_in, ...), custom_call_target="tpu_custom_call", output_to_operand_aliasing={{1}: (7, {}), {2}: (8, {}), {3}: (9, {})} | custom-call | flops 24000000 | bytes 24000000 | tf_op jit(solution)/shard_map/cond/branch_1_fun/attend/pallas_call | solution.py:692
  (354 shorter events, 179.2 us)
Async XLA Ops:
  49.7 32.7 %collective-permute-start.56 = (bf16[2,60,64,128]{3,2,1,0:T(8,128)(2,1)}, bf16[2,60,64,128]{3,2,1,0:T(8,128)(2,1)S(1)}, u32[]{:S(2)}, u32[]{:S(2)}) collective-permute-start(bf16[2,60,64,128]{3,2,1,0:T(8,128)(2,1)} %get-tuple-element.2445), channel_id=1, source_target_pairs={{0,1},{1,0},{2,3},{3,2},{4,5},{5,4},{6,7},{7,6}} | collective-permute-start | bytes 5898248 | tf_op jit(solution)/shard_map/cond/branch_1_fun/while/body/ppermute | solution.py:705
  49.7 32.4 %collective-permute-start.61 = (bf16[2,32,64,128]{3,2,1,0:T(8,128)(2,1)}, bf16[2,32,64,128]{3,2,1,0:T(8,128)(2,1)}, u32[]{:S(2)}, u32[]{:S(2)}) collective-permute-start(bf16[2,32,64,128]{3,2,1,0:T(8,128)(2,1)} %get-tuple-element.2446), channel_id=1, source_target_pairs={{0,1},{1,0},{2,3},{3,2},{4,5},{5,4},{6,7},{7,6}} | collective-permute-start | bytes 3145736 | tf_op jit(solution)/shard_map/cond/branch_1_fun/while/body/ppermute | solution.py:708
  50.2 31.3 %collective-permute-start.60 = (bf16[60,64,128]{2,1,0:T(8,128)(2,1)}, bf16[60,64,128]{2,1,0:T(8,128)(2,1)}, u32[]{:S(2)}, u32[]{:S(2)}) collective-permute-start(bf16[60,64,128]{2,1,0:T(8,128)(2,1)} %get-tuple-element.2449.rc1), channel_id=1, source_target_pairs={{0,1},{1,0},{2,3},{3,2},{4,5},{5,4},{6,7},{7,6}} | collective-permute-start | bytes 2949128 | tf_op jit(solution)/shard_map/cond/branch_1_fun/while/body/ppermute | solution.py:707
  81.5 28.4 %collective-permute-start.62 = (bf16[2,60,64,128]{3,2,1,0:T(8,128)(2,1)}, bf16[2,60,64,128]{3,2,1,0:T(8,128)(2,1)}, u32[]{:S(2)}, u32[]{:S(2)}) collective-permute-start(bf16[2,60,64,128]{3,2,1,0:T(8,128)(2,1)} %get-tuple-element.2131), channel_id=1, source_target_pairs={{0,1},{1,0},{2,3},{3,2},{4,5},{5,4},{6,7},{7,6}} | collective-permute-start | bytes 5898248 | tf_op jit(solution)/shard_map/cond/branch_1_fun/while/body/ppermute | solution.py:705
  82.0 25.0 %collective-permute-start.67 = (bf16[2,32,64,128]{3,2,1,0:T(8,128)(2,1)}, bf16[2,32,64,128]{3,2,1,0:T(8,128)(2,1)}, u32[]{:S(2)}, u32[]{:S(2)}) collective-permute-start(bf16[2,32,64,128]{3,2,1,0:T(8,128)(2,1)} %get-tuple-element.2138), channel_id=1, source_target_pairs={{0,1},{1,0},{2,3},{3,2},{4,5},{5,4},{6,7},{7,6}} | collective-permute-start | bytes 3145736 | tf_op jit(solution)/shard_map/cond/branch_1_fun/while/body/ppermute | solution.py:708
  82.3 25.2 %collective-permute-start.64 = (bf16[60,64,128]{2,1,0:T(8,128)(2,1)}, bf16[60,64,128]{2,1,0:T(8,128)(2,1)}, u32[]{:S(2)}, u32[]{:S(2)}) collective-permute-start(bf16[60,64,128]{2,1,0:T(8,128)(2,1)} %get-tuple-element.2133), channel_id=1, source_target_pairs={{2,0},{3,1},{6,2},{7,3},{4,6},{5,7},{0,4},{1,5}} | collective-permute-start | bytes 2949128 | tf_op jit(solution)/shard_map/cond/branch_1_fun/while/body/ppermute | solution.py:704
  100.5 27.1 %collective-permute-start.69 = (bf16[60,64,128]{2,1,0:T(8,128)(2,1)}, bf16[60,64,128]{2,1,0:T(8,128)(2,1)}, u32[]{:S(2)}, u32[]{:S(2)}) collective-permute-start(bf16[60,64,128]{2,1,0:T(8,128)(2,1)} %get-tuple-element.2149), channel_id=1, source_target_pairs={{0,2},{1,3},{2,6},{3,7},{6,4},{7,5},{4,0},{5,1}} | collective-permute-start | bytes 2949128 | tf_op jit(solution)/shard_map/cond/branch_1_fun/while/body/ppermute | solution.py:703
  107.0 45.9 %collective-permute-start.68 = (bf16[2,60,64,128]{3,2,1,0:T(8,128)(2,1)}, bf16[2,60,64,128]{3,2,1,0:T(8,128)(2,1)}, u32[]{:S(2)}, u32[]{:S(2)}) collective-permute-start(bf16[2,60,64,128]{3,2,1,0:T(8,128)(2,1)} %get-tuple-element.2148), channel_id=1, source_target_pairs={{0,1},{1,0},{2,3},{3,2},{4,5},{5,4},{6,7},{7,6}} | collective-permute-start | bytes 5898248 | tf_op jit(solution)/shard_map/cond/branch_1_fun/while/body/ppermute | solution.py:705
  109.9 42.5 %collective-permute-start.73 = (bf16[2,32,64,128]{3,2,1,0:T(8,128)(2,1)}, bf16[2,32,64,128]{3,2,1,0:T(8,128)(2,1)S(1)}, u32[]{:S(2)}, u32[]{:S(2)}) collective-permute-start(bf16[2,32,64,128]{3,2,1,0:T(8,128)(2,1)} %get-tuple-element.2155), channel_id=1, source_target_pairs={{0,1},{1,0},{2,3},{3,2},{4,5},{5,4},{6,7},{7,6}} | collective-permute-start | bytes 3145736 | tf_op jit(solution)/shard_map/cond/branch_1_fun/while/body/ppermute | solution.py:708
  128.4 48.5 %collective-permute-start.74 = (bf16[2,60,64,128]{3,2,1,0:T(8,128)(2,1)}, bf16[2,60,64,128]{3,2,1,0:T(8,128)(2,1)}, u32[]{:S(2)}, u32[]{:S(2)}) collective-permute-start(bf16[2,60,64,128]{3,2,1,0:T(8,128)(2,1)} %get-tuple-element.2169), channel_id=1, source_target_pairs={{0,1},{1,0},{2,3},{3,2},{4,5},{5,4},{6,7},{7,6}} | collective-permute-start | bytes 5898248 | tf_op jit(solution)/shard_map/cond/branch_1_fun/while/body/ppermute | solution.py:705
  179.6 34.6 %collective-permute-start.56 = (bf16[2,60,64,128]{3,2,1,0:T(8,128)(2,1)}, bf16[2,60,64,128]{3,2,1,0:T(8,128)(2,1)S(1)}, u32[]{:S(2)}, u32[]{:S(2)}) collective-permute-start(bf16[2,60,64,128]{3,2,1,0:T(8,128)(2,1)} %get-tuple-element.2445), channel_id=1, source_target_pairs={{0,1},{1,0},{2,3},{3,2},{4,5},{5,4},{6,7},{7,6}} | collective-permute-start | bytes 5898248 | tf_op jit(solution)/shard_map/cond/branch_1_fun/while/body/ppermute | solution.py:705
  179.6 34.5 %collective-permute-start.61 = (bf16[2,32,64,128]{3,2,1,0:T(8,128)(2,1)}, bf16[2,32,64,128]{3,2,1,0:T(8,128)(2,1)}, u32[]{:S(2)}, u32[]{:S(2)}) collective-permute-start(bf16[2,32,64,128]{3,2,1,0:T(8,128)(2,1)} %get-tuple-element.2446), channel_id=1, source_target_pairs={{0,1},{1,0},{2,3},{3,2},{4,5},{5,4},{6,7},{7,6}} | collective-permute-start | bytes 3145736 | tf_op jit(solution)/shard_map/cond/branch_1_fun/while/body/ppermute | solution.py:708
  180.1 33.5 %collective-permute-start.60 = (bf16[60,64,128]{2,1,0:T(8,128)(2,1)}, bf16[60,64,128]{2,1,0:T(8,128)(2,1)}, u32[]{:S(2)}, u32[]{:S(2)}) collective-permute-start(bf16[60,64,128]{2,1,0:T(8,128)(2,1)} %get-tuple-element.2449.rc1), channel_id=1, source_target_pairs={{0,1},{1,0},{2,3},{3,2},{4,5},{5,4},{6,7},{7,6}} | collective-permute-start | bytes 2949128 | tf_op jit(solution)/shard_map/cond/branch_1_fun/while/body/ppermute | solution.py:707
  213.6 28.4 %collective-permute-start.62 = (bf16[2,60,64,128]{3,2,1,0:T(8,128)(2,1)}, bf16[2,60,64,128]{3,2,1,0:T(8,128)(2,1)}, u32[]{:S(2)}, u32[]{:S(2)}) collective-permute-start(bf16[2,60,64,128]{3,2,1,0:T(8,128)(2,1)} %get-tuple-element.2131), channel_id=1, source_target_pairs={{0,1},{1,0},{2,3},{3,2},{4,5},{5,4},{6,7},{7,6}} | collective-permute-start | bytes 5898248 | tf_op jit(solution)/shard_map/cond/branch_1_fun/while/body/ppermute | solution.py:705
  214.2 25.0 %collective-permute-start.67 = (bf16[2,32,64,128]{3,2,1,0:T(8,128)(2,1)}, bf16[2,32,64,128]{3,2,1,0:T(8,128)(2,1)}, u32[]{:S(2)}, u32[]{:S(2)}) collective-permute-start(bf16[2,32,64,128]{3,2,1,0:T(8,128)(2,1)} %get-tuple-element.2138), channel_id=1, source_target_pairs={{0,1},{1,0},{2,3},{3,2},{4,5},{5,4},{6,7},{7,6}} | collective-permute-start | bytes 3145736 | tf_op jit(solution)/shard_map/cond/branch_1_fun/while/body/ppermute | solution.py:708
  214.2 24.9 %collective-permute-start.63 = (bf16[60,64,128]{2,1,0:T(8,128)(2,1)}, bf16[60,64,128]{2,1,0:T(8,128)(2,1)}, u32[]{:S(2)}, u32[]{:S(2)}) collective-permute-start(bf16[60,64,128]{2,1,0:T(8,128)(2,1)} %get-tuple-element.2132), channel_id=1, source_target_pairs={{0,2},{1,3},{2,6},{3,7},{6,4},{7,5},{4,0},{5,1}} | collective-permute-start | bytes 2949128 | tf_op jit(solution)/shard_map/cond/branch_1_fun/while/body/ppermute | solution.py:703
  214.2 25.4 %collective-permute-start.64 = (bf16[60,64,128]{2,1,0:T(8,128)(2,1)}, bf16[60,64,128]{2,1,0:T(8,128)(2,1)}, u32[]{:S(2)}, u32[]{:S(2)}) collective-permute-start(bf16[60,64,128]{2,1,0:T(8,128)(2,1)} %get-tuple-element.2133), channel_id=1, source_target_pairs={{2,0},{3,1},{6,2},{7,3},{4,6},{5,7},{0,4},{1,5}} | collective-permute-start | bytes 2949128 | tf_op jit(solution)/shard_map/cond/branch_1_fun/while/body/ppermute | solution.py:704
  231.2 28.5 %collective-permute-start.69 = (bf16[60,64,128]{2,1,0:T(8,128)(2,1)}, bf16[60,64,128]{2,1,0:T(8,128)(2,1)}, u32[]{:S(2)}, u32[]{:S(2)}) collective-permute-start(bf16[60,64,128]{2,1,0:T(8,128)(2,1)} %get-tuple-element.2149), channel_id=1, source_target_pairs={{0,2},{1,3},{2,6},{3,7},{6,4},{7,5},{4,0},{5,1}} | collective-permute-start | bytes 2949128 | tf_op jit(solution)/shard_map/cond/branch_1_fun/while/body/ppermute | solution.py:703
  239.2 45.9 %collective-permute-start.68 = (bf16[2,60,64,128]{3,2,1,0:T(8,128)(2,1)}, bf16[2,60,64,128]{3,2,1,0:T(8,128)(2,1)}, u32[]{:S(2)}, u32[]{:S(2)}) collective-permute-start(bf16[2,60,64,128]{3,2,1,0:T(8,128)(2,1)} %get-tuple-element.2148), channel_id=1, source_target_pairs={{0,1},{1,0},{2,3},{3,2},{4,5},{5,4},{6,7},{7,6}} | collective-permute-start | bytes 5898248 | tf_op jit(solution)/shard_map/cond/branch_1_fun/while/body/ppermute | solution.py:705
  242.0 42.5 %collective-permute-start.73 = (bf16[2,32,64,128]{3,2,1,0:T(8,128)(2,1)}, bf16[2,32,64,128]{3,2,1,0:T(8,128)(2,1)S(1)}, u32[]{:S(2)}, u32[]{:S(2)}) collective-permute-start(bf16[2,32,64,128]{3,2,1,0:T(8,128)(2,1)} %get-tuple-element.2155), channel_id=1, source_target_pairs={{0,1},{1,0},{2,3},{3,2},{4,5},{5,4},{6,7},{7,6}} | collective-permute-start | bytes 3145736 | tf_op jit(solution)/shard_map/cond/branch_1_fun/while/body/ppermute | solution.py:708
  260.5 48.5 %collective-permute-start.74 = (bf16[2,60,64,128]{3,2,1,0:T(8,128)(2,1)}, bf16[2,60,64,128]{3,2,1,0:T(8,128)(2,1)}, u32[]{:S(2)}, u32[]{:S(2)}) collective-permute-start(bf16[2,60,64,128]{3,2,1,0:T(8,128)(2,1)} %get-tuple-element.2169), channel_id=1, source_target_pairs={{0,1},{1,0},{2,3},{3,2},{4,5},{5,4},{6,7},{7,6}} | collective-permute-start | bytes 5898248 | tf_op jit(solution)/shard_map/cond/branch_1_fun/while/body/ppermute | solution.py:705
  311.7 33.0 %collective-permute-start.56 = (bf16[2,60,64,128]{3,2,1,0:T(8,128)(2,1)}, bf16[2,60,64,128]{3,2,1,0:T(8,128)(2,1)S(1)}, u32[]{:S(2)}, u32[]{:S(2)}) collective-permute-start(bf16[2,60,64,128]{3,2,1,0:T(8,128)(2,1)} %get-tuple-element.2445), channel_id=1, source_target_pairs={{0,1},{1,0},{2,3},{3,2},{4,5},{5,4},{6,7},{7,6}} | collective-permute-start | bytes 5898248 | tf_op jit(solution)/shard_map/cond/branch_1_fun/while/body/ppermute | solution.py:705
  311.7 32.9 %collective-permute-start.61 = (bf16[2,32,64,128]{3,2,1,0:T(8,128)(2,1)}, bf16[2,32,64,128]{3,2,1,0:T(8,128)(2,1)}, u32[]{:S(2)}, u32[]{:S(2)}) collective-permute-start(bf16[2,32,64,128]{3,2,1,0:T(8,128)(2,1)} %get-tuple-element.2446), channel_id=1, source_target_pairs={{0,1},{1,0},{2,3},{3,2},{4,5},{5,4},{6,7},{7,6}} | collective-permute-start | bytes 3145736 | tf_op jit(solution)/shard_map/cond/branch_1_fun/while/body/ppermute | solution.py:708
  312.2 31.9 %collective-permute-start.60 = (bf16[60,64,128]{2,1,0:T(8,128)(2,1)}, bf16[60,64,128]{2,1,0:T(8,128)(2,1)}, u32[]{:S(2)}, u32[]{:S(2)}) collective-permute-start(bf16[60,64,128]{2,1,0:T(8,128)(2,1)} %get-tuple-element.2449.rc1), channel_id=1, source_target_pairs={{0,1},{1,0},{2,3},{3,2},{4,5},{5,4},{6,7},{7,6}} | collective-permute-start | bytes 2949128 | tf_op jit(solution)/shard_map/cond/branch_1_fun/while/body/ppermute | solution.py:707
  344.1 32.6 %collective-permute-start.62 = (bf16[2,60,64,128]{3,2,1,0:T(8,128)(2,1)}, bf16[2,60,64,128]{3,2,1,0:T(8,128)(2,1)}, u32[]{:S(2)}, u32[]{:S(2)}) collective-permute-start(bf16[2,60,64,128]{3,2,1,0:T(8,128)(2,1)} %get-tuple-element.2131), channel_id=1, source_target_pairs={{0,1},{1,0},{2,3},{3,2},{4,5},{5,4},{6,7},{7,6}} | collective-permute-start | bytes 5898248 | tf_op jit(solution)/shard_map/cond/branch_1_fun/while/body/ppermute | solution.py:705
  344.7 25.0 %collective-permute-start.67 = (bf16[2,32,64,128]{3,2,1,0:T(8,128)(2,1)}, bf16[2,32,64,128]{3,2,1,0:T(8,128)(2,1)}, u32[]{:S(2)}, u32[]{:S(2)}) collective-permute-start(bf16[2,32,64,128]{3,2,1,0:T(8,128)(2,1)} %get-tuple-element.2138), channel_id=1, source_target_pairs={{0,1},{1,0},{2,3},{3,2},{4,5},{5,4},{6,7},{7,6}} | collective-permute-start | bytes 3145736 | tf_op jit(solution)/shard_map/cond/branch_1_fun/while/body/ppermute | solution.py:708
  344.7 24.9 %collective-permute-start.63 = (bf16[60,64,128]{2,1,0:T(8,128)(2,1)}, bf16[60,64,128]{2,1,0:T(8,128)(2,1)}, u32[]{:S(2)}, u32[]{:S(2)}) collective-permute-start(bf16[60,64,128]{2,1,0:T(8,128)(2,1)} %get-tuple-element.2132), channel_id=1, source_target_pairs={{0,2},{1,3},{2,6},{3,7},{6,4},{7,5},{4,0},{5,1}} | collective-permute-start | bytes 2949128 | tf_op jit(solution)/shard_map/cond/branch_1_fun/while/body/ppermute | solution.py:703
  344.7 25.4 %collective-permute-start.64 = (bf16[60,64,128]{2,1,0:T(8,128)(2,1)}, bf16[60,64,128]{2,1,0:T(8,128)(2,1)}, u32[]{:S(2)}, u32[]{:S(2)}) collective-permute-start(bf16[60,64,128]{2,1,0:T(8,128)(2,1)} %get-tuple-element.2133), channel_id=1, source_target_pairs={{2,0},{3,1},{6,2},{7,3},{4,6},{5,7},{0,4},{1,5}} | collective-permute-start | bytes 2949128 | tf_op jit(solution)/shard_map/cond/branch_1_fun/while/body/ppermute | solution.py:704
  362.2 28.1 %collective-permute-start.69 = (bf16[60,64,128]{2,1,0:T(8,128)(2,1)}, bf16[60,64,128]{2,1,0:T(8,128)(2,1)}, u32[]{:S(2)}, u32[]{:S(2)}) collective-permute-start(bf16[60,64,128]{2,1,0:T(8,128)(2,1)} %get-tuple-element.2149), channel_id=1, source_target_pairs={{0,2},{1,3},{2,6},{3,7},{6,4},{7,5},{4,0},{5,1}} | collective-permute-start | bytes 2949128 | tf_op jit(solution)/shard_map/cond/branch_1_fun/while/body/ppermute | solution.py:703
  369.7 45.9 %collective-permute-start.68 = (bf16[2,60,64,128]{3,2,1,0:T(8,128)(2,1)}, bf16[2,60,64,128]{3,2,1,0:T(8,128)(2,1)}, u32[]{:S(2)}, u32[]{:S(2)}) collective-permute-start(bf16[2,60,64,128]{3,2,1,0:T(8,128)(2,1)} %get-tuple-element.2148), channel_id=1, source_target_pairs={{0,1},{1,0},{2,3},{3,2},{4,5},{5,4},{6,7},{7,6}} | collective-permute-start | bytes 5898248 | tf_op jit(solution)/shard_map/cond/branch_1_fun/while/body/ppermute | solution.py:705
  376.8 38.2 %collective-permute-start.73 = (bf16[2,32,64,128]{3,2,1,0:T(8,128)(2,1)}, bf16[2,32,64,128]{3,2,1,0:T(8,128)(2,1)S(1)}, u32[]{:S(2)}, u32[]{:S(2)}) collective-permute-start(bf16[2,32,64,128]{3,2,1,0:T(8,128)(2,1)} %get-tuple-element.2155), channel_id=1, source_target_pairs={{0,1},{1,0},{2,3},{3,2},{4,5},{5,4},{6,7},{7,6}} | collective-permute-start | bytes 3145736 | tf_op jit(solution)/shard_map/cond/branch_1_fun/while/body/ppermute | solution.py:708
  390.7 48.8 %collective-permute-start.74 = (bf16[2,60,64,128]{3,2,1,0:T(8,128)(2,1)}, bf16[2,60,64,128]{3,2,1,0:T(8,128)(2,1)}, u32[]{:S(2)}, u32[]{:S(2)}) collective-permute-start(bf16[2,60,64,128]{3,2,1,0:T(8,128)(2,1)} %get-tuple-element.2169), channel_id=1, source_target_pairs={{0,1},{1,0},{2,3},{3,2},{4,5},{5,4},{6,7},{7,6}} | collective-permute-start | bytes 5898248 | tf_op jit(solution)/shard_map/cond/branch_1_fun/while/body/ppermute | solution.py:705
  442.2 33.1 %collective-permute-start.56 = (bf16[2,60,64,128]{3,2,1,0:T(8,128)(2,1)}, bf16[2,60,64,128]{3,2,1,0:T(8,128)(2,1)S(1)}, u32[]{:S(2)}, u32[]{:S(2)}) collective-permute-start(bf16[2,60,64,128]{3,2,1,0:T(8,128)(2,1)} %get-tuple-element.2445), channel_id=1, source_target_pairs={{0,1},{1,0},{2,3},{3,2},{4,5},{5,4},{6,7},{7,6}} | collective-permute-start | bytes 5898248 | tf_op jit(solution)/shard_map/cond/branch_1_fun/while/body/ppermute | solution.py:705
  442.2 32.6 %collective-permute-start.61 = (bf16[2,32,64,128]{3,2,1,0:T(8,128)(2,1)}, bf16[2,32,64,128]{3,2,1,0:T(8,128)(2,1)}, u32[]{:S(2)}, u32[]{:S(2)}) collective-permute-start(bf16[2,32,64,128]{3,2,1,0:T(8,128)(2,1)} %get-tuple-element.2446), channel_id=1, source_target_pairs={{0,1},{1,0},{2,3},{3,2},{4,5},{5,4},{6,7},{7,6}} | collective-permute-start | bytes 3145736 | tf_op jit(solution)/shard_map/cond/branch_1_fun/while/body/ppermute | solution.py:708
  442.8 30.3 %collective-permute-start.60 = (bf16[60,64,128]{2,1,0:T(8,128)(2,1)}, bf16[60,64,128]{2,1,0:T(8,128)(2,1)}, u32[]{:S(2)}, u32[]{:S(2)}) collective-permute-start(bf16[60,64,128]{2,1,0:T(8,128)(2,1)} %get-tuple-element.2449.rc1), channel_id=1, source_target_pairs={{0,1},{1,0},{2,3},{3,2},{4,5},{5,4},{6,7},{7,6}} | collective-permute-start | bytes 2949128 | tf_op jit(solution)/shard_map/cond/branch_1_fun/while/body/ppermute | solution.py:707
  473.1 33.1 %collective-permute-start.62 = (bf16[2,60,64,128]{3,2,1,0:T(8,128)(2,1)}, bf16[2,60,64,128]{3,2,1,0:T(8,128)(2,1)}, u32[]{:S(2)}, u32[]{:S(2)}) collective-permute-start(bf16[2,60,64,128]{3,2,1,0:T(8,128)(2,1)} %get-tuple-element.2131), channel_id=1, source_target_pairs={{0,1},{1,0},{2,3},{3,2},{4,5},{5,4},{6,7},{7,6}} | collective-permute-start | bytes 5898248 | tf_op jit(solution)/shard_map/cond/branch_1_fun/while/body/ppermute | solution.py:705
  474.8 25.4 %collective-permute-start.67 = (bf16[2,32,64,128]{3,2,1,0:T(8,128)(2,1)}, bf16[2,32,64,128]{3,2,1,0:T(8,128)(2,1)}, u32[]{:S(2)}, u32[]{:S(2)}) collective-permute-start(bf16[2,32,64,128]{3,2,1,0:T(8,128)(2,1)} %get-tuple-element.2138), channel_id=1, source_target_pairs={{0,1},{1,0},{2,3},{3,2},{4,5},{5,4},{6,7},{7,6}} | collective-permute-start | bytes 3145736 | tf_op jit(solution)/shard_map/cond/branch_1_fun/while/body/ppermute | solution.py:708
  475.3 24.9 %collective-permute-start.63 = (bf16[60,64,128]{2,1,0:T(8,128)(2,1)}, bf16[60,64,128]{2,1,0:T(8,128)(2,1)}, u32[]{:S(2)}, u32[]{:S(2)}) collective-permute-start(bf16[60,64,128]{2,1,0:T(8,128)(2,1)} %get-tuple-element.2132), channel_id=1, source_target_pairs={{0,2},{1,3},{2,6},{3,7},{6,4},{7,5},{4,0},{5,1}} | collective-permute-start | bytes 2949128 | tf_op jit(solution)/shard_map/cond/branch_1_fun/while/body/ppermute | solution.py:703
  475.3 25.4 %collective-permute-start.64 = (bf16[60,64,128]{2,1,0:T(8,128)(2,1)}, bf16[60,64,128]{2,1,0:T(8,128)(2,1)}, u32[]{:S(2)}, u32[]{:S(2)}) collective-permute-start(bf16[60,64,128]{2,1,0:T(8,128)(2,1)} %get-tuple-element.2133), channel_id=1, source_target_pairs={{2,0},{3,1},{6,2},{7,3},{4,6},{5,7},{0,4},{1,5}} | collective-permute-start | bytes 2949128 | tf_op jit(solution)/shard_map/cond/branch_1_fun/while/body/ppermute | solution.py:704
  491.4 29.0 %collective-permute-start.69 = (bf16[60,64,128]{2,1,0:T(8,128)(2,1)}, bf16[60,64,128]{2,1,0:T(8,128)(2,1)}, u32[]{:S(2)}, u32[]{:S(2)}) collective-permute-start(bf16[60,64,128]{2,1,0:T(8,128)(2,1)} %get-tuple-element.2149), channel_id=1, source_target_pairs={{0,2},{1,3},{2,6},{3,7},{6,4},{7,5},{4,0},{5,1}} | collective-permute-start | bytes 2949128 | tf_op jit(solution)/shard_map/cond/branch_1_fun/while/body/ppermute | solution.py:703
  500.3 45.5 %collective-permute-start.68 = (bf16[2,60,64,128]{3,2,1,0:T(8,128)(2,1)}, bf16[2,60,64,128]{3,2,1,0:T(8,128)(2,1)}, u32[]{:S(2)}, u32[]{:S(2)}) collective-permute-start(bf16[2,60,64,128]{3,2,1,0:T(8,128)(2,1)} %get-tuple-element.2148), channel_id=1, source_target_pairs={{0,1},{1,0},{2,3},{3,2},{4,5},{5,4},{6,7},{7,6}} | collective-permute-start | bytes 5898248 | tf_op jit(solution)/shard_map/cond/branch_1_fun/while/body/ppermute | solution.py:705
  506.2 39.1 %collective-permute-start.73 = (bf16[2,32,64,128]{3,2,1,0:T(8,128)(2,1)}, bf16[2,32,64,128]{3,2,1,0:T(8,128)(2,1)S(1)}, u32[]{:S(2)}, u32[]{:S(2)}) collective-permute-start(bf16[2,32,64,128]{3,2,1,0:T(8,128)(2,1)} %get-tuple-element.2155), channel_id=1, source_target_pairs={{0,1},{1,0},{2,3},{3,2},{4,5},{5,4},{6,7},{7,6}} | collective-permute-start | bytes 3145736 | tf_op jit(solution)/shard_map/cond/branch_1_fun/while/body/ppermute | solution.py:708
  521.3 48.5 %collective-permute-start.74 = (bf16[2,60,64,128]{3,2,1,0:T(8,128)(2,1)}, bf16[2,60,64,128]{3,2,1,0:T(8,128)(2,1)}, u32[]{:S(2)}, u32[]{:S(2)}) collective-permute-start(bf16[2,60,64,128]{3,2,1,0:T(8,128)(2,1)} %get-tuple-element.2169), channel_id=1, source_target_pairs={{0,1},{1,0},{2,3},{3,2},{4,5},{5,4},{6,7},{7,6}} | collective-permute-start | bytes 5898248 | tf_op jit(solution)/shard_map/cond/branch_1_fun/while/body/ppermute | solution.py:705
  572.5 33.5 %collective-permute-start.56 = (bf16[2,60,64,128]{3,2,1,0:T(8,128)(2,1)}, bf16[2,60,64,128]{3,2,1,0:T(8,128)(2,1)S(1)}, u32[]{:S(2)}, u32[]{:S(2)}) collective-permute-start(bf16[2,60,64,128]{3,2,1,0:T(8,128)(2,1)} %get-tuple-element.2445), channel_id=1, source_target_pairs={{0,1},{1,0},{2,3},{3,2},{4,5},{5,4},{6,7},{7,6}} | collective-permute-start | bytes 5898248 | tf_op jit(solution)/shard_map/cond/branch_1_fun/while/body/ppermute | solution.py:705
  572.5 32.1 %collective-permute-start.61 = (bf16[2,32,64,128]{3,2,1,0:T(8,128)(2,1)}, bf16[2,32,64,128]{3,2,1,0:T(8,128)(2,1)}, u32[]{:S(2)}, u32[]{:S(2)}) collective-permute-start(bf16[2,32,64,128]{3,2,1,0:T(8,128)(2,1)} %get-tuple-element.2446), channel_id=1, source_target_pairs={{0,1},{1,0},{2,3},{3,2},{4,5},{5,4},{6,7},{7,6}} | collective-permute-start | bytes 3145736 | tf_op jit(solution)/shard_map/cond/branch_1_fun/while/body/ppermute | solution.py:708
  573.0 31.0 %collective-permute-start.60 = (bf16[60,64,128]{2,1,0:T(8,128)(2,1)}, bf16[60,64,128]{2,1,0:T(8,128)(2,1)}, u32[]{:S(2)}, u32[]{:S(2)}) collective-permute-start(bf16[60,64,128]{2,1,0:T(8,128)(2,1)} %get-tuple-element.2449.rc1), channel_id=1, source_target_pairs={{0,1},{1,0},{2,3},{3,2},{4,5},{5,4},{6,7},{7,6}} | collective-permute-start | bytes 2949128 | tf_op jit(solution)/shard_map/cond/branch_1_fun/while/body/ppermute | solution.py:707
  604.1 31.8 %collective-permute-start.62 = (bf16[2,60,64,128]{3,2,1,0:T(8,128)(2,1)}, bf16[2,60,64,128]{3,2,1,0:T(8,128)(2,1)}, u32[]{:S(2)}, u32[]{:S(2)}) collective-permute-start(bf16[2,60,64,128]{3,2,1,0:T(8,128)(2,1)} %get-tuple-element.2131), channel_id=1, source_target_pairs={{0,1},{1,0},{2,3},{3,2},{4,5},{5,4},{6,7},{7,6}} | collective-permute-start | bytes 5898248 | tf_op jit(solution)/shard_map/cond/branch_1_fun/while/body/ppermute | solution.py:705
  604.6 25.4 %collective-permute-start.67 = (bf16[2,32,64,128]{3,2,1,0:T(8,128)(2,1)}, bf16[2,32,64,128]{3,2,1,0:T(8,128)(2,1)}, u32[]{:S(2)}, u32[]{:S(2)}) collective-permute-start(bf16[2,32,64,128]{3,2,1,0:T(8,128)(2,1)} %get-tuple-element.2138), channel_id=1, source_target_pairs={{0,1},{1,0},{2,3},{3,2},{4,5},{5,4},{6,7},{7,6}} | collective-permute-start | bytes 3145736 | tf_op jit(solution)/shard_map/cond/branch_1_fun/while/body/ppermute | solution.py:708
  623.0 27.1 %collective-permute-start.69 = (bf16[60,64,128]{2,1,0:T(8,128)(2,1)}, bf16[60,64,128]{2,1,0:T(8,128)(2,1)}, u32[]{:S(2)}, u32[]{:S(2)}) collective-permute-start(bf16[60,64,128]{2,1,0:T(8,128)(2,1)} %get-tuple-element.2149), channel_id=1, source_target_pairs={{0,2},{1,3},{2,6},{3,7},{6,4},{7,5},{4,0},{5,1}} | collective-permute-start | bytes 2949128 | tf_op jit(solution)/shard_map/cond/branch_1_fun/while/body/ppermute | solution.py:703
  630.0 46.1 %collective-permute-start.68 = (bf16[2,60,64,128]{3,2,1,0:T(8,128)(2,1)}, bf16[2,60,64,128]{3,2,1,0:T(8,128)(2,1)}, u32[]{:S(2)}, u32[]{:S(2)}) collective-permute-start(bf16[2,60,64,128]{3,2,1,0:T(8,128)(2,1)} %get-tuple-element.2148), channel_id=1, source_target_pairs={{0,1},{1,0},{2,3},{3,2},{4,5},{5,4},{6,7},{7,6}} | collective-permute-start | bytes 5898248 | tf_op jit(solution)/shard_map/cond/branch_1_fun/while/body/ppermute | solution.py:705
  635.9 39.8 %collective-permute-start.73 = (bf16[2,32,64,128]{3,2,1,0:T(8,128)(2,1)}, bf16[2,32,64,128]{3,2,1,0:T(8,128)(2,1)S(1)}, u32[]{:S(2)}, u32[]{:S(2)}) collective-permute-start(bf16[2,32,64,128]{3,2,1,0:T(8,128)(2,1)} %get-tuple-element.2155), channel_id=1, source_target_pairs={{0,1},{1,0},{2,3},{3,2},{4,5},{5,4},{6,7},{7,6}} | collective-permute-start | bytes 3145736 | tf_op jit(solution)/shard_map/cond/branch_1_fun/while/body/ppermute | solution.py:708
  650.2 25.5 %collective-permute-start.79 = (bf16[2,32,64,128]{3,2,1,0:T(8,128)(2,1)}, bf16[2,32,64,128]{3,2,1,0:T(8,128)(2,1)S(1)}, u32[]{:S(2)}, u32[]{:S(2)}) collective-permute-start(bf16[2,32,64,128]{3,2,1,0:T(8,128)(2,1)} %get-tuple-element.2172), channel_id=1, source_target_pairs={{0,1},{1,0},{2,3},{3,2},{4,5},{5,4},{6,7},{7,6}} | collective-permute-start | bytes 3145736 | tf_op jit(solution)/shard_map/cond/branch_1_fun/while/body/ppermute | solution.py:708
  651.8 48.4 %collective-permute-start.74 = (bf16[2,60,64,128]{3,2,1,0:T(8,128)(2,1)}, bf16[2,60,64,128]{3,2,1,0:T(8,128)(2,1)}, u32[]{:S(2)}, u32[]{:S(2)}) collective-permute-start(bf16[2,60,64,128]{3,2,1,0:T(8,128)(2,1)} %get-tuple-element.2169), channel_id=1, source_target_pairs={{0,1},{1,0},{2,3},{3,2},{4,5},{5,4},{6,7},{7,6}} | collective-permute-start | bytes 5898248 | tf_op jit(solution)/shard_map/cond/branch_1_fun/while/body/ppermute | solution.py:705
  702.9 33.0 %collective-permute-start.56 = (bf16[2,60,64,128]{3,2,1,0:T(8,128)(2,1)}, bf16[2,60,64,128]{3,2,1,0:T(8,128)(2,1)S(1)}, u32[]{:S(2)}, u32[]{:S(2)}) collective-permute-start(bf16[2,60,64,128]{3,2,1,0:T(8,128)(2,1)} %get-tuple-element.2445), channel_id=1, source_target_pairs={{0,1},{1,0},{2,3},{3,2},{4,5},{5,4},{6,7},{7,6}} | collective-permute-start | bytes 5898248 | tf_op jit(solution)/shard_map/cond/branch_1_fun/while/body/ppermute | solution.py:705
  702.9 32.0 %collective-permute-start.61 = (bf16[2,32,64,128]{3,2,1,0:T(8,128)(2,1)}, bf16[2,32,64,128]{3,2,1,0:T(8,128)(2,1)}, u32[]{:S(2)}, u32[]{:S(2)}) collective-permute-start(bf16[2,32,64,128]{3,2,1,0:T(8,128)(2,1)} %get-tuple-element.2446), channel_id=1, source_target_pairs={{0,1},{1,0},{2,3},{3,2},{4,5},{5,4},{6,7},{7,6}} | collective-permute-start | bytes 3145736 | tf_op jit(solution)/shard_map/cond/branch_1_fun/while/body/ppermute | solution.py:708
  703.4 30.9 %collective-permute-start.60 = (bf16[60,64,128]{2,1,0:T(8,128)(2,1)}, bf16[60,64,128]{2,1,0:T(8,128)(2,1)}, u32[]{:S(2)}, u32[]{:S(2)}) collective-permute-start(bf16[60,64,128]{2,1,0:T(8,128)(2,1)} %get-tuple-element.2449.rc1), channel_id=1, source_target_pairs={{0,1},{1,0},{2,3},{3,2},{4,5},{5,4},{6,7},{7,6}} | collective-permute-start | bytes 2949128 | tf_op jit(solution)/shard_map/cond/branch_1_fun/while/body/ppermute | solution.py:707
  734.3 32.4 %collective-permute-start.62 = (bf16[2,60,64,128]{3,2,1,0:T(8,128)(2,1)}, bf16[2,60,64,128]{3,2,1,0:T(8,128)(2,1)}, u32[]{:S(2)}, u32[]{:S(2)}) collective-permute-start(bf16[2,60,64,128]{3,2,1,0:T(8,128)(2,1)} %get-tuple-element.2131), channel_id=1, source_target_pairs={{0,1},{1,0},{2,3},{3,2},{4,5},{5,4},{6,7},{7,6}} | collective-permute-start | bytes 5898248 | tf_op jit(solution)/shard_map/cond/branch_1_fun/while/body/ppermute | solution.py:705
  734.8 25.0 %collective-permute-start.67 = (bf16[2,32,64,128]{3,2,1,0:T(8,128)(2,1)}, bf16[2,32,64,128]{3,2,1,0:T(8,128)(2,1)}, u32[]{:S(2)}, u32[]{:S(2)}) collective-permute-start(bf16[2,32,64,128]{3,2,1,0:T(8,128)(2,1)} %get-tuple-element.2138), channel_id=1, source_target_pairs={{0,1},{1,0},{2,3},{3,2},{4,5},{5,4},{6,7},{7,6}} | collective-permute-start | bytes 3145736 | tf_op jit(solution)/shard_map/cond/branch_1_fun/while/body/ppermute | solution.py:708
  734.9 24.9 %collective-permute-start.63 = (bf16[60,64,128]{2,1,0:T(8,128)(2,1)}, bf16[60,64,128]{2,1,0:T(8,128)(2,1)}, u32[]{:S(2)}, u32[]{:S(2)}) collective-permute-start(bf16[60,64,128]{2,1,0:T(8,128)(2,1)} %get-tuple-element.2132), channel_id=1, source_target_pairs={{0,2},{1,3},{2,6},{3,7},{6,4},{7,5},{4,0},{5,1}} | collective-permute-start | bytes 2949128 | tf_op jit(solution)/shard_map/cond/branch_1_fun/while/body/ppermute | solution.py:703
  751.8 28.6 %collective-permute-start.69 = (bf16[60,64,128]{2,1,0:T(8,128)(2,1)}, bf16[60,64,128]{2,1,0:T(8,128)(2,1)}, u32[]{:S(2)}, u32[]{:S(2)}) collective-permute-start(bf16[60,64,128]{2,1,0:T(8,128)(2,1)} %get-tuple-element.2149), channel_id=1, source_target_pairs={{0,2},{1,3},{2,6},{3,7},{6,4},{7,5},{4,0},{5,1}} | collective-permute-start | bytes 2949128 | tf_op jit(solution)/shard_map/cond/branch_1_fun/while/body/ppermute | solution.py:703
  759.8 46.2 %collective-permute-start.68 = (bf16[2,60,64,128]{3,2,1,0:T(8,128)(2,1)}, bf16[2,60,64,128]{3,2,1,0:T(8,128)(2,1)}, u32[]{:S(2)}, u32[]{:S(2)}) collective-permute-start(bf16[2,60,64,128]{3,2,1,0:T(8,128)(2,1)} %get-tuple-element.2148), channel_id=1, source_target_pairs={{0,1},{1,0},{2,3},{3,2},{4,5},{5,4},{6,7},{7,6}} | collective-permute-start | bytes 5898248 | tf_op jit(solution)/shard_map/cond/branch_1_fun/while/body/ppermute | solution.py:705
  766.7 38.8 %collective-permute-start.73 = (bf16[2,32,64,128]{3,2,1,0:T(8,128)(2,1)}, bf16[2,32,64,128]{3,2,1,0:T(8,128)(2,1)S(1)}, u32[]{:S(2)}, u32[]{:S(2)}) collective-permute-start(bf16[2,32,64,128]{3,2,1,0:T(8,128)(2,1)} %get-tuple-element.2155), channel_id=1, source_target_pairs={{0,1},{1,0},{2,3},{3,2},{4,5},{5,4},{6,7},{7,6}} | collective-permute-start | bytes 3145736 | tf_op jit(solution)/shard_map/cond/branch_1_fun/while/body/ppermute | solution.py:708
  780.4 25.1 %collective-permute-start.79 = (bf16[2,32,64,128]{3,2,1,0:T(8,128)(2,1)}, bf16[2,32,64,128]{3,2,1,0:T(8,128)(2,1)S(1)}, u32[]{:S(2)}, u32[]{:S(2)}) collective-permute-start(bf16[2,32,64,128]{3,2,1,0:T(8,128)(2,1)} %get-tuple-element.2172), channel_id=1, source_target_pairs={{0,1},{1,0},{2,3},{3,2},{4,5},{5,4},{6,7},{7,6}} | collective-permute-start | bytes 3145736 | tf_op jit(solution)/shard_map/cond/branch_1_fun/while/body/ppermute | solution.py:708
  782.0 48.0 %collective-permute-start.74 = (bf16[2,60,64,128]{3,2,1,0:T(8,128)(2,1)}, bf16[2,60,64,128]{3,2,1,0:T(8,128)(2,1)}, u32[]{:S(2)}, u32[]{:S(2)}) collective-permute-start(bf16[2,60,64,128]{3,2,1,0:T(8,128)(2,1)} %get-tuple-element.2169), channel_id=1, source_target_pairs={{0,1},{1,0},{2,3},{3,2},{4,5},{5,4},{6,7},{7,6}} | collective-permute-start | bytes 5898248 | tf_op jit(solution)/shard_map/cond/branch_1_fun/while/body/ppermute | solution.py:705
  (114 other events, 1879.7 us)

commit v3 on v2

--- a/solution.py
+++ b/solution.py
@@ -17,7 +17,7 @@
 WIDE = 400
 S0, S1, R0, R1, XS, XR, FREE = range(7)
 RDY, RDX, MLEN, SRC, ROUNDS = range(FREE * WIDE, FREE * WIDE + 200, 40)
-CORE, PICK, DUMP = ROUNDS + 1, ROUNDS + 2, ROUNDS + 4
+CORE, PICK, SHARE, DUMP = range(ROUNDS + 1, ROUNDS + 5)
 TAB = ROUNDS + 8
 FWD, NONE = 2, 3
 TURN = 4
@@ -197,6 +197,7 @@
             (price, best), (o, pick), (trips * TURN, turns), (size, chunk))]
     tab[ROUNDS] = turns
     tab[PICK] = pick
+    tab[SHARE] = jnp.minimum(SL // jnp.maximum(turns - TURN, 1) + 1, A)
 
     x0 = gray(me >> 1)
     left, right, opposite = (x0 - 1) & 3, (x0 + 1) & 3, (x0 + 2) & 3
@@ -340,11 +341,11 @@
 
             @pl.when(mine & (core == 0))
             def _():
-                pltpu.make_async_copy(vc.at[pl.ds(idx, take)], buf.at[d, pl.ds(p, take)], sem).start()
+                pltpu.make_async_copy(vc.at[pl.ds(idx, take)], buf.at[pl.ds(p, take)], sem).start()
 
             @pl.when(mine & (core == 1))
             def _():
-                pltpu.make_async_copy(kc.at[pl.ds(idx, take)], buf.at[d, pl.ds(p, take)], sem).start()
+                pltpu.make_async_copy(kc.at[pl.ds(idx, take)], buf.at[pl.ds(p, take)], sem).start()
 
             return jnp.where(mine, take, 0)
 
@@ -358,20 +359,20 @@
 
             @pl.when(mine & (core == 0))
             def _():
-                pltpu.make_async_copy(kc.at[pl.ds(idx, take)], buf.at[d, pl.ds(p, take)], sem).start()
+                pltpu.make_async_copy(kc.at[pl.ds(idx, take)], buf.at[pl.ds(p, take)], sem).start()
 
             @pl.when(mine & (core == 1))
             def _():
-                pltpu.make_async_copy(vc.at[pl.ds(idx, take)], buf.at[d, pl.ds(p, take)], sem).start()
+                pltpu.make_async_copy(vc.at[pl.ds(idx, take)], buf.at[pl.ds(p, take)], sem).start()
 
             @pl.when(kind == 1 - core)
             def _():
-                pltpu.make_async_copy(pre.at[d, pl.ds(p, take)], buf.at[d, pl.ds(p, take)], sem).start()
+                pltpu.make_async_copy(pre.at[d, pl.ds(p, take)], buf.at[pl.ds(p, take)], sem).start()
 
             if fwd is not None:
                 @pl.when(kind == FWD)
                 def _():
-                    pltpu.make_async_copy(fwd.at[pl.ds(idx, take)], buf.at[d, pl.ds(p, take)], sem).start()
+                    pltpu.make_async_copy(fwd.at[pl.ds(idx, take)], buf.at[pl.ds(p, take)], sem).start()
             return jnp.where(kind < NONE, take, 0)
 
         return self.walk(S0 + d, U_MERGE + d, self.size, fn)
@@ -407,17 +408,17 @@
 
             @pl.when(mine & (plane == 0))
             def _():
-                pltpu.make_async_copy(buf.at[d, pl.ds(p, take)], ko.at[pl.ds(idx, take)], sem).start()
+                pltpu.make_async_copy(buf.at[pl.ds(p, take)], ko.at[pl.ds(idx, take)], sem).start()
 
             @pl.when(mine & (plane == 1))
             def _():
-                pltpu.make_async_copy(buf.at[d, pl.ds(p, take)], vo.at[pl.ds(idx, take)], sem).start()
+                pltpu.make_async_copy(buf.at[pl.ds(p, take)], vo.at[pl.ds(idx, take)], sem).start()
 
             cnt = jnp.where(mine, take, 0)
             if fwd is not None:
                 @pl.when(kind == FWD)
                 def _():
-                    pltpu.make_async_copy(buf.at[d, pl.ds(p, take)], fwd.at[pl.ds(idx, take)], sem).start()
+                    pltpu.make_async_copy(buf.at[pl.ds(p, take)], fwd.at[pl.ds(idx, take)], sem).start()
 
                 cnt = cnt + jnp.where(kind == FWD, take, 0)
             return cnt
@@ -425,96 +426,55 @@
         return self.walk(R0 + d, use + d, n, fn)
 
 
-def copies(pairs, sems):
-    made = [pltpu.make_async_copy(src, dst, sem) for (src, dst), sem in zip(pairs, sems)]
-    for c in made:
-        c.start()
-    return made
-
-
-def halves(ref):
-    return [ref.at[d] for d in range(2)]
-
-
-def finish(made):
-    for c in made:
-        c.wait()
-
-
-def open_kernel(NB, tab, st_in, kc, vc, st, part, vpart, sem):
+def open_kernel(NB, tab, st_in, kc, vc, st, part, sem):
     mv = Mover(tab, st_in, st, NB)
-    mv.drain(sum(mv.partial(d, kc, vc, vpart, sem) for d in range(2)), kc, sem)
-    finish(copies([(vpart, part)], [sem]))
-
-
-def open_more_kernel(NB, tab, st_in, kc, vc, st, part1, part2, dxs, vpart, vdx, *sems):
+    mv.drain(sum(mv.partial(d, kc, vc, part.at[d], sem) for d in range(2)), kc, sem)
+
+
+def open_more_kernel(NB, tab, st_in, kc, vc, st, part1, part2, dxs, sem):
     mv = Mover(tab, st_in, st, NB)
-    cnt = [sum(mv.partial(d, kc, vc, buf, sem) for d in range(2)) for buf, sem in zip(halves(vpart), sems)]
-    cnt.append(mv.cross_send(kc, vc, vdx, sems[-1]))
-    made = []
-    for n, sem, pair in zip(cnt, sems, zip(halves(vpart) + [vdx], (part1, part2, dxs))):
-        mv.drain(n, kc, sem)
-        made += copies([pair], [sem])
-    finish(made)
-
-
-def open_merge_kernel(NB, tab, st_in, kc, vc, pre, st, send0, send1, vsend, *sems):
+    cnt = sum(mv.partial(d, kc, vc, part.at[d], sem) for part in (part1, part2) for d in range(2))
+    mv.drain(cnt + mv.cross_send(kc, vc, dxs, sem), kc, sem)
+
+
+def open_merge_kernel(NB, tab, st_in, kc, vc, pre, st, send0, send1, sem):
     mv = Mover(tab, st_in, st, NB)
-    cnt = [mv.merge(d, kc, vc, pre, None, vsend, sem) for d, sem in enumerate(sems)]
-    made = []
-    for n, sem, pair in zip(cnt, sems, zip(halves(vsend), (send0, send1))):
-        mv.drain(n, kc, sem)
-        made += copies([pair], [sem])
-    finish(made)
+    mv.drain(sum(mv.merge(d, kc, vc, pre, None, buf, sem) for d, buf in enumerate((send0, send1))), kc, sem)
+
+
+def stages(r, NB):
+    return [jnp.where(r >= back, n, 0) for back, n in ((1, NB), (2, NB), (1, NX))]
 
 
 def round_kernel(NB, tab, st_in, kc, vc, pre, rc0, rc1, po0, po1, dxr, f0i, f1i, koi, voi,
-                 st, send0, send1, part, dxs, f0, f1, ko, vo,
-                 vsend, vpart, vrecv, vpost, vdxs, vdxr, *sems):
+                 st, send0, send1, part, dxs, f0, f1, ko, vo, in_sem, out_sem, post_sem):
     mv = Mover(tab, st_in, st, NB)
-    part_sem, cross_sem, out_sem, post_sem, *sems = sems
     r = st_in[STEP]
     st[STEP] = r + 1
-    ins = copies(zip([rc0, rc1, po0, po1, dxr], halves(vrecv) + halves(vpost) + [vdxr]), sems)
-    n1, n2, nx = [jnp.where(r >= back, n, 0) for back, n in ((1, NB), (2, NB), (1, NX))]
-    cp = sum(mv.partial(d, kc, vc, vpart, part_sem) for d in range(2))
-    cx = mv.cross_send(kc, vc, vdxs, cross_sem)
-    fwd = (f0, f1)
-    cnt = []
-    for d in range(2):
-        ins[d].wait()
-        cnt.append(mv.unpack(d, U_OWN, n1, False, ko, vo, fwd[d], vrecv, out_sem))
-    mv.drain(sum(cnt), kc, out_sem)
-    merged = [mv.merge(d, kc, vc, pre, fwd[d], vsend, sem) for d, sem in enumerate(sems[:2])]
-    finish(ins[2:])
-    cnt = sum(mv.unpack(d, U_POST, n2, True, ko, vo, None, vpost, post_sem) for d in range(2))
-    cnt += mv.cross_recv(nx, ko, vo, vdxr, post_sem)
-    outs = []
-    for n, sem, pair in zip(merged + [cp, cx], sems[:2] + [part_sem, cross_sem],
-                            zip(halves(vsend) + [vpart, vdxs], (send0, send1, part, dxs))):
-        mv.drain(n, kc, sem)
-        outs += copies([pair], [sem])
-    mv.drain(cnt, kc, post_sem)
-    finish(outs)
+    n1, n2, nx = stages(r, NB)
+    links = ((0, rc0, po0, f0, send0), (1, rc1, po1, f1, send1))
+    mv.drain(sum(mv.unpack(d, U_OWN, n1, False, ko, vo, fwd, rc, out_sem) for d, rc, _, fwd, _ in links), kc, out_sem)
+    cnt = sum(mv.merge(d, kc, vc, pre, fwd, send, in_sem) for d, _, _, fwd, send in links)
+    late = sum(mv.unpack(d, U_POST, n2, True, ko, vo, None, po, post_sem) for d, _, po, _, _ in links)
+    cnt += sum(mv.partial(d, kc, vc, part.at[d], in_sem) for d in range(2)) + mv.cross_send(kc, vc, dxs, in_sem)
+    late += mv.cross_recv(nx, ko, vo, dxr, post_sem)
+    mv.drain(cnt, kc, in_sem)
+    mv.drain(late, kc, post_sem)
 
 
 def close_kernel(NB, last, tab, st_in, *refs):
     if last:
-        (po0, po1, koi, voi, st, ko, vo, vpost, *sems) = refs
-        pairs = zip((po0, po1), halves(vpost))
+        (po0, po1, koi, voi, st, ko, vo, sem) = refs
     else:
-        (rc0, rc1, po0, po1, dxr, koi, voi, st, ko, vo, vpost, vrecv, vdxr, *sems) = refs
-        pairs = zip((po0, po1, rc0, rc1, dxr), halves(vpost) + halves(vrecv) + [vdxr])
+        (rc0, rc1, po0, po1, dxr, koi, voi, st, ko, vo, sem) = refs
     mv = Mover(tab, st_in, st, NB)
-    sem = sems[-1]
     r = st_in[STEP]
     st[STEP] = r + 1
-    finish(copies(pairs, sems))
-    n1, n2, nx = [jnp.where(r >= back, n, 0) for back, n in ((1, NB), (2, NB), (1, NX))]
-    cnt = sum(mv.unpack(d, U_POST, n2, True, ko, vo, None, vpost, sem) for d in range(2))
+    n1, n2, nx = stages(r, NB)
+    cnt = sum(mv.unpack(d, U_POST, n2, True, ko, vo, None, po, sem) for d, po in enumerate((po0, po1)))
     if not last:
-        cnt += sum(mv.unpack(d, U_OWN, n1, False, ko, vo, None, vrecv, sem) for d in range(2))
-        cnt += mv.cross_recv(nx, ko, vo, vdxr, sem)
+        cnt += sum(mv.unpack(d, U_OWN, n1, False, ko, vo, None, rc, sem) for d, rc in enumerate((rc0, rc1)))
+        cnt += mv.cross_recv(nx, ko, vo, dxr, sem)
     mv.drain(cnt, ko, sem)
 
 
@@ -581,9 +541,11 @@
         pltpu.make_async_copy(ob.at[a], ao.at[j], osem.at[0]).start()
         return 2 * (BL - bw)
 
+    share = tab[SHARE] if batches == 1 else A
+
     def batch(_, c):
         def pick(j, n):
-            hit = (st[DONE + j] == 0) & (tab[RDY + j] <= link_end) & (tab[RDX + j] <= swap_end) & (n < A)
+            hit = (st[DONE + j] == 0) & (tab[RDY + j] <= link_end) & (tab[RDX + j] <= swap_end) & (n < share)
             sel[jnp.where(hit, n, A)] = j
             st[DONE + j] = jnp.where(hit, 1, st[DONE + j])
             return n + jnp.where(hit, 1, 0)
@@ -674,17 +636,17 @@
             st = jnp.zeros((STATE,), i32)
             caches = [SMEM, SMEM, ANY, ANY]
             st, part = pl.pallas_call(
-                functools.partial(open_kernel, NB), out_shape=(ST, both), in_specs=caches, out_specs=(SMEM, ANY),
-                scratch_shapes=[buf(2, NB)] + DMA, name='open')(tab, st, kc, vc)
+                functools.partial(open_kernel, NB), out_shape=(ST, both), in_specs=caches, out_specs=(SMEM, VMEM),
+                scratch_shapes=DMA, name='open')(tab, st, kc, vc)
             pre = lax.ppermute(part, 'dp', swap)
             st, part1, part, dxs = pl.pallas_call(
                 functools.partial(open_more_kernel, NB), out_shape=(ST, both, both, cross), in_specs=caches,
-                out_specs=(SMEM,) + (ANY,) * 3, scratch_shapes=[buf(2, 2, NB), buf(2, NX)] + DMA * 3,
+                out_specs=(SMEM,) + (VMEM,) * 3, scratch_shapes=DMA,
                 name='open_more')(tab, st, kc, vc)
             pre1 = lax.ppermute(part1, 'dp', swap)
             st, s0, s1 = pl.pallas_call(
                 functools.partial(open_merge_kernel, NB), out_shape=(ST, chunk, chunk), in_specs=caches + [VMEM],
-                out_specs=(SMEM, ANY, ANY), scratch_shapes=[buf(2, NB)] + DMA * 2,
+                out_specs=(SMEM, VMEM, VMEM), scratch_shapes=DMA,
                 name='open_merge')(tab, st, kc, vc, pre)
             pre = pre1
 
@@ -708,9 +670,9 @@
                 ndxr = lax.ppermute(dxs, 'dp', swap)
                 st, s0, s1, part, dxs, f0, f1, ko, vo = pl.pallas_call(
                     functools.partial(round_kernel, NB), out_shape=(ST, chunk, chunk, both, cross, store, store, cache, cache),
-                    in_specs=caches + [VMEM] + [ANY] * 9, out_specs=(SMEM,) + (ANY,) * 8,
+                    in_specs=caches + [VMEM] * 6 + [ANY] * 4, out_specs=(SMEM,) + (VMEM,) * 4 + (ANY,) * 4,
                     input_output_aliases={10: 5, 11: 6, 12: 7, 13: 8},
-                    scratch_shapes=[buf(2, NB)] * 4 + [buf(2, NX)] * 2 + DMA * 9,
+                    scratch_shapes=DMA * 3,
                     cost_estimate=cost(10), name='round')(tab, st, kc, vc, pre, rc0, rc1, po0, po1, dxr, f0, f1, ko, vo)
                 st, ko, vo, ao = attend(st, ko, vo, ao, 1)
                 if tag != TAGS[-1]:
@@ -728,12 +690,11 @@
 
             def close(last, st, ko, vo, *ins):
                 n = len(ins)
-                extra = [] if last else [buf(2, NB), buf(2, NX)]
                 return pl.pallas_call(
                     functools.partial(close_kernel, NB, last), out_shape=(ST, cache, cache),
-                    in_specs=[SMEM, SMEM] + [VMEM if last else ANY] * n + [ANY] * 2, out_specs=(SMEM, ANY, ANY),
+                    in_specs=[SMEM, SMEM] + [VMEM] * n + [ANY] * 2, out_specs=(SMEM, ANY, ANY),
                     input_output_aliases={n + 2: 1, n + 3: 2},
-                    scratch_shapes=[buf(2, NB)] + extra + DMA * 6,
+                    scratch_shapes=DMA,
                     name='close_last' if last else 'close')(tab, st, *ins, ko, vo)
 
             lpo0 = lax.ppermute(rc0, 'dp', swap)

time: 854 us -> 850 us (level)
  no operation moved by 1% of the time
where the time goes in v3:
time: 850 us; the launch traced here: 844 us
  Pallas kernels  400 us (47%)
  waiting for transfers between devices  357 us (42%)
  starting transfers between devices  74.6 us (9%)
    ppermute x24, waiting for transfers between devices, one_round(): nrc1 = lax.ppermute(s1, 'dp', ccw)  272 us
    pallas_call x24, Pallas kernels, one_round(): pl.pallas_call(functools.partial(round_kernel, NB), out_shape=(ST, chunk,...  214 us
    pallas_call x25, Pallas kernels, attend(): pl.pallas_call(functools.partial(attn_kernel, NB, batches), out_shape=(ST...  139 us
    ppermute x24, waiting for transfers between devices, one_round(): nrc0 = lax.ppermute(s0, 'dp', cw)  85.3 us
    ppermute x24, starting transfers between devices, one_round(): nrc1 = lax.ppermute(s1, 'dp', ccw)  33.3 us
    pallas_call x1, Pallas kernels, local(): pl.pallas_call(plan_kernel, out_shape=(sds((TAB,), i32), sds((SL,), i32))...  19.2 us
  transfers between devices with their start and end apart: 148, of which 41 were waited for; matrix products, arithmetic and copies ran while one was open for 0% of the time, Pallas kernels for 42%

profile of v3, /device:TPU:0, one launch (start us, length us, event | category | flops | bytes accessed | tf_op | source)
XLA Modules:
  0.0 844.1 jit_solution(3734982262976170159)
XLA Ops:
  0.6 7.8 lens.1.len_ref
  8.4 19.2 %plan.1 = (s32[2568]{0:T(1024)S(1)}, s32[32]{0:T(128)}) custom-call(s32[1]{0:T(128)} %bitcast.4.me_ref, s32[256]{0:T(256)} %dest_ref.1, s32[8,1,32]{2,1,0:T(1,128)} %lens.1.len_ref), custom_call_target="tpu_custom_call" | custom-call | tf_op jit(solution)/shard_map/plan/pallas_call | solution.py:621
  28.9 815.1 %conditional.1 = (bf16[32,24,128]{2,1,0:T(8,128)(2,1)}, bf16[2048,64,128]{2,1,0:T(8,128)(2,1)}, bf16[2048,64,128]{2,1,0:T(8,128)(2,1)}) conditional(s32[]{:T(128)} %bitcast.6, (s32[2568]{0:T(1024)S(1)}, bf16[2048,64,128]{2,1,0:T(8,128)(2,1)}, bf16[2048,64,128]{2,1,0:T(8,128)(2,1)}, bf16[32,24,128]{2,1,0:T(8,128)(2,1)}, ...), branch_computations={%region_0.0_spmd, %region_3.0_spmd, %region_6.0_spmd, %region_9.0_... | conditional | flops 280000000 | bytes 474906112 | solution.py:707
  33.5 5.5 open_more.5
  46.1 780.0 %while.157 = (s32[]{:T(128)}, s32[64]{0:T(128)S(1)}, bf16[60,64,128]{2,1,0:T(8,128)(2,1)}, bf16[60,64,128]{2,1,0:T(8,128)(2,1)}, bf16[2,60,64,128]{3,2,1,0:T(8,1...) while((s32[]{:T(128)}, s32[64]{0:T(128)S(1)}, ...), condition=%wide.region_5.0_spmd, body=%wide.region_4.0_spmd.sunk | while | flops 256000000 | bytes 387597440 | solution.py:687
  49.4 21.0 %collective-permute-done.58.rc1 = bf16[60,64,128]{2,1,0:T(8,128)(2,1)} collective-permute-done((bf16[60,64,128]{2,1,0:T(8,128)(2,1)}, bf16[60,64,128]{2,1,0:T(8,128)(2,1)}, u32[]{:S(2)}, u32[]{:S(2)}) %collective-permute-start.58) | collective-permute-done | bytes 983072 | tf_op jit(solution)/shard_map/cond/branch_1_fun/while/body/ppermute | solution.py:666
  71.8 8.0 round.24
  82.4 6.8 attend.32
  89.2 9.9 %round.25 = (s32[64]{0:T(128)}, bf16[60,64,128]{2,1,0:T(8,128)(2,1)}, bf16[60,64,128]{2,1,0:T(8,128)(2,1)}, bf16[2,60,64,128]{3,2,1,0:T(8,128)(2,1)}, bf16[2,32,...) custom-call(s32[2568]{0:T(1024)S(1)} %get-tuple-element.2484.tab, ...), custom_call_target="tpu_custom_call", output_to_operand_aliasing={{5}: (10, {}), {6}: (11, {}), {7}: (12, {}), {8}: (13, {})} | custom-call | flops 40000000 | bytes 40000000 | tf_op jit(solution)/shard_map/cond/branch_1_fun/while/body/round/pallas_call | solution.py:671
  99.3 6.0 collective-permute-done.63.rc0
  113.3 9.8 %round.26 = (s32[64]{0:T(128)}, bf16[60,64,128]{2,1,0:T(8,128)(2,1)}, bf16[60,64,128]{2,1,0:T(8,128)(2,1)}, bf16[2,60,64,128]{3,2,1,0:T(8,128)(2,1)}, bf16[2,32,...) custom-call(s32[2568]{0:T(1024)S(1)} %get-tuple-element.2484.tab, ...), custom_call_target="tpu_custom_call", output_to_operand_aliasing={{5}: (10, {}), {6}: (11, {}), {7}: (12, {}), {8}: (13, {})} | custom-call | flops 40000000 | bytes 40000000 | tf_op jit(solution)/shard_map/cond/branch_1_fun/while/body/round/pallas_call | solution.py:671
  127.4 23.0 %collective-permute-done.70.rc1 = bf16[60,64,128]{2,1,0:T(8,128)(2,1)} collective-permute-done((bf16[60,64,128]{2,1,0:T(8,128)(2,1)}, bf16[60,64,128]{2,1,0:T(8,128)(2,1)}, u32[]{:S(2)}, u32[]{:S(2)}) %collective-permute-start.70) | collective-permute-done | bytes 983072 | tf_op jit(solution)/shard_map/cond/branch_1_fun/while/body/ppermute | solution.py:666
  152.9 5.4 attend.34
  158.3 9.9 %round.27 = (s32[64]{0:T(128)}, bf16[60,64,128]{2,1,0:T(8,128)(2,1)}, bf16[60,64,128]{2,1,0:T(8,128)(2,1)}, bf16[2,60,64,128]{3,2,1,0:T(8,128)(2,1)}, bf16[2,32,...) custom-call(s32[2568]{0:T(1024)S(1)} %get-tuple-element.2484.tab, ...), custom_call_target="tpu_custom_call", output_to_operand_aliasing={{5}: (10, {}), {6}: (11, {}), {7}: (12, {}), {8}: (13, {})} | custom-call | flops 40000000 | bytes 40000000 | tf_op jit(solution)/shard_map/cond/branch_1_fun/while/body/round/pallas_call | solution.py:671
  178.7 21.3 %collective-permute-done.58.rc1 = bf16[60,64,128]{2,1,0:T(8,128)(2,1)} collective-permute-done((bf16[60,64,128]{2,1,0:T(8,128)(2,1)}, bf16[60,64,128]{2,1,0:T(8,128)(2,1)}, u32[]{:S(2)}, u32[]{:S(2)}) %collective-permute-start.58) | collective-permute-done | bytes 983072 | tf_op jit(solution)/shard_map/cond/branch_1_fun/while/body/ppermute | solution.py:666
  201.3 9.6 %round.24 = (s32[64]{0:T(128)}, bf16[60,64,128]{2,1,0:T(8,128)(2,1)}, bf16[60,64,128]{2,1,0:T(8,128)(2,1)}, bf16[2,60,64,128]{3,2,1,0:T(8,128)(2,1)}, bf16[2,32,...) custom-call(s32[2568]{0:T(1024)S(1)} %get-tuple-element.2484.tab, ...), custom_call_target="tpu_custom_call", output_to_operand_aliasing={{5}: (10, {}), {6}: (11, {}), {7}: (12, {}), {8}: (13, {})} | custom-call | flops 40000000 | bytes 40000000 | tf_op jit(solution)/shard_map/cond/branch_1_fun/while/body/round/pallas_call | solution.py:671
  219.4 9.9 %round.25 = (s32[64]{0:T(128)}, bf16[60,64,128]{2,1,0:T(8,128)(2,1)}, bf16[60,64,128]{2,1,0:T(8,128)(2,1)}, bf16[2,60,64,128]{3,2,1,0:T(8,128)(2,1)}, bf16[2,32,...) custom-call(s32[2568]{0:T(1024)S(1)} %get-tuple-element.2484.tab, ...), custom_call_target="tpu_custom_call", output_to_operand_aliasing={{5}: (10, {}), {6}: (11, {}), {7}: (12, {}), {8}: (13, {})} | custom-call | flops 40000000 | bytes 40000000 | tf_op jit(solution)/shard_map/cond/branch_1_fun/while/body/round/pallas_call | solution.py:671
  229.4 7.6 collective-permute-done.63.rc0
  243.7 9.9 %round.26 = (s32[64]{0:T(128)}, bf16[60,64,128]{2,1,0:T(8,128)(2,1)}, bf16[60,64,128]{2,1,0:T(8,128)(2,1)}, bf16[2,60,64,128]{3,2,1,0:T(8,128)(2,1)}, bf16[2,32,...) custom-call(s32[2568]{0:T(1024)S(1)} %get-tuple-element.2484.tab, ...), custom_call_target="tpu_custom_call", output_to_operand_aliasing={{5}: (10, {}), {6}: (11, {}), {7}: (12, {}), {8}: (13, {})} | custom-call | flops 40000000 | bytes 40000000 | tf_op jit(solution)/shard_map/cond/branch_1_fun/while/body/round/pallas_call | solution.py:671
  258.3 23.3 %collective-permute-done.70.rc1 = bf16[60,64,128]{2,1,0:T(8,128)(2,1)} collective-permute-done((bf16[60,64,128]{2,1,0:T(8,128)(2,1)}, bf16[60,64,128]{2,1,0:T(8,128)(2,1)}, u32[]{:S(2)}, u32[]{:S(2)}) %collective-permute-start.70) | collective-permute-done | bytes 983072 | tf_op jit(solution)/shard_map/cond/branch_1_fun/while/body/ppermute | solution.py:666
  289.5 9.4 %round.27 = (s32[64]{0:T(128)}, bf16[60,64,128]{2,1,0:T(8,128)(2,1)}, bf16[60,64,128]{2,1,0:T(8,128)(2,1)}, bf16[2,60,64,128]{3,2,1,0:T(8,128)(2,1)}, bf16[2,32,...) custom-call(s32[2568]{0:T(1024)S(1)} %get-tuple-element.2484.tab, ...), custom_call_target="tpu_custom_call", output_to_operand_aliasing={{5}: (10, {}), {6}: (11, {}), {7}: (12, {}), {8}: (13, {})} | custom-call | flops 40000000 | bytes 40000000 | tf_op jit(solution)/shard_map/cond/branch_1_fun/while/body/round/pallas_call | solution.py:671
  298.9 5.8 attend.35
  309.6 20.6 %collective-permute-done.58.rc1 = bf16[60,64,128]{2,1,0:T(8,128)(2,1)} collective-permute-done((bf16[60,64,128]{2,1,0:T(8,128)(2,1)}, bf16[60,64,128]{2,1,0:T(8,128)(2,1)}, u32[]{:S(2)}, u32[]{:S(2)}) %collective-permute-start.58) | collective-permute-done | bytes 983072 | tf_op jit(solution)/shard_map/cond/branch_1_fun/while/body/ppermute | solution.py:666
  331.7 9.5 %round.24 = (s32[64]{0:T(128)}, bf16[60,64,128]{2,1,0:T(8,128)(2,1)}, bf16[60,64,128]{2,1,0:T(8,128)(2,1)}, bf16[2,60,64,128]{3,2,1,0:T(8,128)(2,1)}, bf16[2,32,...) custom-call(s32[2568]{0:T(1024)S(1)} %get-tuple-element.2484.tab, ...), custom_call_target="tpu_custom_call", output_to_operand_aliasing={{5}: (10, {}), {6}: (11, {}), {7}: (12, {}), {8}: (13, {})} | custom-call | flops 40000000 | bytes 40000000 | tf_op jit(solution)/shard_map/cond/branch_1_fun/while/body/round/pallas_call | solution.py:671
  343.9 6.5 attend.32
  350.4 9.3 %round.25 = (s32[64]{0:T(128)}, bf16[60,64,128]{2,1,0:T(8,128)(2,1)}, bf16[60,64,128]{2,1,0:T(8,128)(2,1)}, bf16[2,60,64,128]{3,2,1,0:T(8,128)(2,1)}, bf16[2,32,...) custom-call(s32[2568]{0:T(1024)S(1)} %get-tuple-element.2484.tab, ...), custom_call_target="tpu_custom_call", output_to_operand_aliasing={{5}: (10, {}), {6}: (11, {}), {7}: (12, {}), {8}: (13, {})} | custom-call | flops 40000000 | bytes 40000000 | tf_op jit(solution)/shard_map/cond/branch_1_fun/while/body/round/pallas_call | solution.py:671
  359.8 7.0 collective-permute-done.63.rc0
  367.4 6.5 attend.33
  374.0 8.6 %round.26 = (s32[64]{0:T(128)}, bf16[60,64,128]{2,1,0:T(8,128)(2,1)}, bf16[60,64,128]{2,1,0:T(8,128)(2,1)}, bf16[2,60,64,128]{3,2,1,0:T(8,128)(2,1)}, bf16[2,32,...) custom-call(s32[2568]{0:T(1024)S(1)} %get-tuple-element.2484.tab, ...), custom_call_target="tpu_custom_call", output_to_operand_aliasing={{5}: (10, {}), {6}: (11, {}), {7}: (12, {}), {8}: (13, {})} | custom-call | flops 40000000 | bytes 40000000 | tf_op jit(solution)/shard_map/cond/branch_1_fun/while/body/round/pallas_call | solution.py:671
  388.6 23.2 %collective-permute-done.70.rc1 = bf16[60,64,128]{2,1,0:T(8,128)(2,1)} collective-permute-done((bf16[60,64,128]{2,1,0:T(8,128)(2,1)}, bf16[60,64,128]{2,1,0:T(8,128)(2,1)}, u32[]{:S(2)}, u32[]{:S(2)}) %collective-permute-start.70) | collective-permute-done | bytes 983072 | tf_op jit(solution)/shard_map/cond/branch_1_fun/while/body/ppermute | solution.py:666
  414.4 6.6 attend.34
  421.0 8.4 round.27
  429.4 5.6 attend.35
  439.9 20.6 %collective-permute-done.58.rc1 = bf16[60,64,128]{2,1,0:T(8,128)(2,1)} collective-permute-done((bf16[60,64,128]{2,1,0:T(8,128)(2,1)}, bf16[60,64,128]{2,1,0:T(8,128)(2,1)}, u32[]{:S(2)}, u32[]{:S(2)}) %collective-permute-start.58) | collective-permute-done | bytes 983072 | tf_op jit(solution)/shard_map/cond/branch_1_fun/while/body/ppermute | solution.py:666
  462.0 8.0 round.24
  479.5 8.4 round.25
  488.8 8.3 collective-permute-done.63.rc0
  504.5 8.4 round.26
  518.1 23.6 %collective-permute-done.70.rc1 = bf16[60,64,128]{2,1,0:T(8,128)(2,1)} collective-permute-done((bf16[60,64,128]{2,1,0:T(8,128)(2,1)}, bf16[60,64,128]{2,1,0:T(8,128)(2,1)}, u32[]{:S(2)}, u32[]{:S(2)}) %collective-permute-start.70) | collective-permute-done | bytes 983072 | tf_op jit(solution)/shard_map/cond/branch_1_fun/while/body/ppermute | solution.py:666
  546.6 8.6 %round.27 = (s32[64]{0:T(128)}, bf16[60,64,128]{2,1,0:T(8,128)(2,1)}, bf16[60,64,128]{2,1,0:T(8,128)(2,1)}, bf16[2,60,64,128]{3,2,1,0:T(8,128)(2,1)}, bf16[2,32,...) custom-call(s32[2568]{0:T(1024)S(1)} %get-tuple-element.2484.tab, ...), custom_call_target="tpu_custom_call", output_to_operand_aliasing={{5}: (10, {}), {6}: (11, {}), {7}: (12, {}), {8}: (13, {})} | custom-call | flops 40000000 | bytes 40000000 | tf_op jit(solution)/shard_map/cond/branch_1_fun/while/body/round/pallas_call | solution.py:671
  555.2 6.8 attend.35
  569.7 20.6 %collective-permute-done.58.rc1 = bf16[60,64,128]{2,1,0:T(8,128)(2,1)} collective-permute-done((bf16[60,64,128]{2,1,0:T(8,128)(2,1)}, bf16[60,64,128]{2,1,0:T(8,128)(2,1)}, u32[]{:S(2)}, u32[]{:S(2)}) %collective-permute-start.58) | collective-permute-done | bytes 983072 | tf_op jit(solution)/shard_map/cond/branch_1_fun/while/body/ppermute | solution.py:666
  591.8 8.2 round.24
  602.8 6.6 attend.32
  609.4 8.8 %round.25 = (s32[64]{0:T(128)}, bf16[60,64,128]{2,1,0:T(8,128)(2,1)}, bf16[60,64,128]{2,1,0:T(8,128)(2,1)}, bf16[2,60,64,128]{3,2,1,0:T(8,128)(2,1)}, bf16[2,32,...) custom-call(s32[2568]{0:T(1024)S(1)} %get-tuple-element.2484.tab, ...), custom_call_target="tpu_custom_call", output_to_operand_aliasing={{5}: (10, {}), {6}: (11, {}), {7}: (12, {}), {8}: (13, {})} | custom-call | flops 40000000 | bytes 40000000 | tf_op jit(solution)/shard_map/cond/branch_1_fun/while/body/round/pallas_call | solution.py:671
  618.3 7.4 collective-permute-done.63.rc0
  632.1 8.7 %round.26 = (s32[64]{0:T(128)}, bf16[60,64,128]{2,1,0:T(8,128)(2,1)}, bf16[60,64,128]{2,1,0:T(8,128)(2,1)}, bf16[2,60,64,128]{3,2,1,0:T(8,128)(2,1)}, bf16[2,32,...) custom-call(s32[2568]{0:T(1024)S(1)} %get-tuple-element.2484.tab, ...), custom_call_target="tpu_custom_call", output_to_operand_aliasing={{5}: (10, {}), {6}: (11, {}), {7}: (12, {}), {8}: (13, {})} | custom-call | flops 40000000 | bytes 40000000 | tf_op jit(solution)/shard_map/cond/branch_1_fun/while/body/round/pallas_call | solution.py:671
  640.8 5.4 collective-permute-done.69.rc0
  648.1 22.6 %collective-permute-done.70.rc1 = bf16[60,64,128]{2,1,0:T(8,128)(2,1)} collective-permute-done((bf16[60,64,128]{2,1,0:T(8,128)(2,1)}, bf16[60,64,128]{2,1,0:T(8,128)(2,1)}, u32[]{:S(2)}, u32[]{:S(2)}) %collective-permute-start.70) | collective-permute-done | bytes 983072 | tf_op jit(solution)/shard_map/cond/branch_1_fun/while/body/ppermute | solution.py:666
  673.2 6.3 attend.34
  679.6 8.7 %round.27 = (s32[64]{0:T(128)}, bf16[60,64,128]{2,1,0:T(8,128)(2,1)}, bf16[60,64,128]{2,1,0:T(8,128)(2,1)}, bf16[2,60,64,128]{3,2,1,0:T(8,128)(2,1)}, bf16[2,32,...) custom-call(s32[2568]{0:T(1024)S(1)} %get-tuple-element.2484.tab, ...), custom_call_target="tpu_custom_call", output_to_operand_aliasing={{5}: (10, {}), {6}: (11, {}), {7}: (12, {}), {8}: (13, {})} | custom-call | flops 40000000 | bytes 40000000 | tf_op jit(solution)/shard_map/cond/branch_1_fun/while/body/round/pallas_call | solution.py:671
  688.4 6.5 attend.35
  699.7 20.6 %collective-permute-done.58.rc1 = bf16[60,64,128]{2,1,0:T(8,128)(2,1)} collective-permute-done((bf16[60,64,128]{2,1,0:T(8,128)(2,1)}, bf16[60,64,128]{2,1,0:T(8,128)(2,1)}, u32[]{:S(2)}, u32[]{:S(2)}) %collective-permute-start.58) | collective-permute-done | bytes 983072 | tf_op jit(solution)/shard_map/cond/branch_1_fun/while/body/ppermute | solution.py:666
  720.8 8.6 %round.24 = (s32[64]{0:T(128)}, bf16[60,64,128]{2,1,0:T(8,128)(2,1)}, bf16[60,64,128]{2,1,0:T(8,128)(2,1)}, bf16[2,60,64,128]{3,2,1,0:T(8,128)(2,1)}, bf16[2,32,...) custom-call(s32[2568]{0:T(1024)S(1)} %get-tuple-element.2484.tab, ...), custom_call_target="tpu_custom_call", output_to_operand_aliasing={{5}: (10, {}), {6}: (11, {}), {7}: (12, {}), {8}: (13, {})} | custom-call | flops 40000000 | bytes 40000000 | tf_op jit(solution)/shard_map/cond/branch_1_fun/while/body/round/pallas_call | solution.py:671
  732.1 5.3 attend.32
  737.4 9.0 %round.25 = (s32[64]{0:T(128)}, bf16[60,64,128]{2,1,0:T(8,128)(2,1)}, bf16[60,64,128]{2,1,0:T(8,128)(2,1)}, bf16[2,60,64,128]{3,2,1,0:T(8,128)(2,1)}, bf16[2,32,...) custom-call(s32[2568]{0:T(1024)S(1)} %get-tuple-element.2484.tab, ...), custom_call_target="tpu_custom_call", output_to_operand_aliasing={{5}: (10, {}), {6}: (11, {}), {7}: (12, {}), {8}: (13, {})} | custom-call | flops 40000000 | bytes 40000000 | tf_op jit(solution)/shard_map/cond/branch_1_fun/while/body/round/pallas_call | solution.py:671
  748.2 6.7 collective-permute-done.63.rc0
  755.5 6.3 attend.33
  761.9 8.4 round.26
  777.3 22.8 %collective-permute-done.70.rc1 = bf16[60,64,128]{2,1,0:T(8,128)(2,1)} collective-permute-done((bf16[60,64,128]{2,1,0:T(8,128)(2,1)}, bf16[60,64,128]{2,1,0:T(8,128)(2,1)}, u32[]{:S(2)}, u32[]{:S(2)}) %collective-permute-start.70) | collective-permute-done | bytes 983072 | tf_op jit(solution)/shard_map/cond/branch_1_fun/while/body/ppermute | solution.py:666
  802.6 6.3 attend.34
  808.9 7.6 round.27
  816.5 5.6 attend.35
  834.3 9.4 %attend.21 = (s32[64]{0:T(128)}, bf16[2048,64,128]{2,1,0:T(8,128)(2,1)}, bf16[2048,64,128]{2,1,0:T(8,128)(2,1)}, bf16[32,24,128]{2,1,0:T(8,128)(2,1)}) custom-call(s32[2568]{0:T(1024)S(1)} %get-tuple-element.2599, s32[64]{0:T(128)} %get-tuple-element.691.st_in, ...), custom_call_target="tpu_custom_call", output_to_operand_aliasing={{1}: (7, {}), {2}: (8, {}), {3}: (9, {})} | custom-call | flops 24000000 | bytes 24000000 | tf_op jit(solution)/shard_map/cond/branch_1_fun/attend/pallas_call | solution.py:654
  (354 shorter events, 176.2 us)
Async XLA Ops:
  48.9 32.1 %collective-permute-start.56 = (bf16[2,60,64,128]{3,2,1,0:T(8,128)(2,1)}, bf16[2,60,64,128]{3,2,1,0:T(8,128)(2,1)S(1)}, u32[]{:S(2)}, u32[]{:S(2)}) collective-permute-start(bf16[2,60,64,128]{3,2,1,0:T(8,128)(2,1)} %get-tuple-element.2445), channel_id=1, source_target_pairs={{0,1},{1,0},{2,3},{3,2},{4,5},{5,4},{6,7},{7,6}} | collective-permute-start | bytes 5898248 | tf_op jit(solution)/shard_map/cond/branch_1_fun/while/body/ppermute | solution.py:667
  48.9 31.4 %collective-permute-start.61 = (bf16[2,32,64,128]{3,2,1,0:T(8,128)(2,1)}, bf16[2,32,64,128]{3,2,1,0:T(8,128)(2,1)}, u32[]{:S(2)}, u32[]{:S(2)}) collective-permute-start(bf16[2,32,64,128]{3,2,1,0:T(8,128)(2,1)} %get-tuple-element.2446), channel_id=1, source_target_pairs={{0,1},{1,0},{2,3},{3,2},{4,5},{5,4},{6,7},{7,6}} | collective-permute-start | bytes 3145736 | tf_op jit(solution)/shard_map/cond/branch_1_fun/while/body/ppermute | solution.py:670
  49.4 30.3 %collective-permute-start.60 = (bf16[60,64,128]{2,1,0:T(8,128)(2,1)}, bf16[60,64,128]{2,1,0:T(8,128)(2,1)}, u32[]{:S(2)}, u32[]{:S(2)}) collective-permute-start(bf16[60,64,128]{2,1,0:T(8,128)(2,1)} %get-tuple-element.2449.rc1), channel_id=1, source_target_pairs={{0,1},{1,0},{2,3},{3,2},{4,5},{5,4},{6,7},{7,6}} | collective-permute-start | bytes 2949128 | tf_op jit(solution)/shard_map/cond/branch_1_fun/while/body/ppermute | solution.py:669
  79.8 28.4 %collective-permute-start.62 = (bf16[2,60,64,128]{3,2,1,0:T(8,128)(2,1)}, bf16[2,60,64,128]{3,2,1,0:T(8,128)(2,1)}, u32[]{:S(2)}, u32[]{:S(2)}) collective-permute-start(bf16[2,60,64,128]{3,2,1,0:T(8,128)(2,1)} %get-tuple-element.2131), channel_id=1, source_target_pairs={{0,1},{1,0},{2,3},{3,2},{4,5},{5,4},{6,7},{7,6}} | collective-permute-start | bytes 5898248 | tf_op jit(solution)/shard_map/cond/branch_1_fun/while/body/ppermute | solution.py:667
  80.3 25.0 %collective-permute-start.67 = (bf16[2,32,64,128]{3,2,1,0:T(8,128)(2,1)}, bf16[2,32,64,128]{3,2,1,0:T(8,128)(2,1)}, u32[]{:S(2)}, u32[]{:S(2)}) collective-permute-start(bf16[2,32,64,128]{3,2,1,0:T(8,128)(2,1)} %get-tuple-element.2138), channel_id=1, source_target_pairs={{0,1},{1,0},{2,3},{3,2},{4,5},{5,4},{6,7},{7,6}} | collective-permute-start | bytes 3145736 | tf_op jit(solution)/shard_map/cond/branch_1_fun/while/body/ppermute | solution.py:670
  80.3 24.9 %collective-permute-start.63 = (bf16[60,64,128]{2,1,0:T(8,128)(2,1)}, bf16[60,64,128]{2,1,0:T(8,128)(2,1)}, u32[]{:S(2)}, u32[]{:S(2)}) collective-permute-start(bf16[60,64,128]{2,1,0:T(8,128)(2,1)} %get-tuple-element.2132), channel_id=1, source_target_pairs={{0,2},{1,3},{2,6},{3,7},{6,4},{7,5},{4,0},{5,1}} | collective-permute-start | bytes 2949128 | tf_op jit(solution)/shard_map/cond/branch_1_fun/while/body/ppermute | solution.py:665
  99.1 26.7 %collective-permute-start.69 = (bf16[60,64,128]{2,1,0:T(8,128)(2,1)}, bf16[60,64,128]{2,1,0:T(8,128)(2,1)}, u32[]{:S(2)}, u32[]{:S(2)}) collective-permute-start(bf16[60,64,128]{2,1,0:T(8,128)(2,1)} %get-tuple-element.2149), channel_id=1, source_target_pairs={{0,2},{1,3},{2,6},{3,7},{6,4},{7,5},{4,0},{5,1}} | collective-permute-start | bytes 2949128 | tf_op jit(solution)/shard_map/cond/branch_1_fun/while/body/ppermute | solution.py:665
  105.3 46.2 %collective-permute-start.68 = (bf16[2,60,64,128]{3,2,1,0:T(8,128)(2,1)}, bf16[2,60,64,128]{3,2,1,0:T(8,128)(2,1)}, u32[]{:S(2)}, u32[]{:S(2)}) collective-permute-start(bf16[2,60,64,128]{3,2,1,0:T(8,128)(2,1)} %get-tuple-element.2148), channel_id=1, source_target_pairs={{0,1},{1,0},{2,3},{3,2},{4,5},{5,4},{6,7},{7,6}} | collective-permute-start | bytes 5898248 | tf_op jit(solution)/shard_map/cond/branch_1_fun/while/body/ppermute | solution.py:667
  108.2 42.8 %collective-permute-start.73 = (bf16[2,32,64,128]{3,2,1,0:T(8,128)(2,1)}, bf16[2,32,64,128]{3,2,1,0:T(8,128)(2,1)S(1)}, u32[]{:S(2)}, u32[]{:S(2)}) collective-permute-start(bf16[2,32,64,128]{3,2,1,0:T(8,128)(2,1)} %get-tuple-element.2155), channel_id=1, source_target_pairs={{0,1},{1,0},{2,3},{3,2},{4,5},{5,4},{6,7},{7,6}} | collective-permute-start | bytes 3145736 | tf_op jit(solution)/shard_map/cond/branch_1_fun/while/body/ppermute | solution.py:670
  125.9 25.1 %collective-permute-start.79 = (bf16[2,32,64,128]{3,2,1,0:T(8,128)(2,1)}, bf16[2,32,64,128]{3,2,1,0:T(8,128)(2,1)S(1)}, u32[]{:S(2)}, u32[]{:S(2)}) collective-permute-start(bf16[2,32,64,128]{3,2,1,0:T(8,128)(2,1)} %get-tuple-element.2172), channel_id=1, source_target_pairs={{0,1},{1,0},{2,3},{3,2},{4,5},{5,4},{6,7},{7,6}} | collective-permute-start | bytes 3145736 | tf_op jit(solution)/shard_map/cond/branch_1_fun/while/body/ppermute | solution.py:670
  127.1 48.4 %collective-permute-start.74 = (bf16[2,60,64,128]{3,2,1,0:T(8,128)(2,1)}, bf16[2,60,64,128]{3,2,1,0:T(8,128)(2,1)}, u32[]{:S(2)}, u32[]{:S(2)}) collective-permute-start(bf16[2,60,64,128]{3,2,1,0:T(8,128)(2,1)} %get-tuple-element.2169), channel_id=1, source_target_pairs={{0,1},{1,0},{2,3},{3,2},{4,5},{5,4},{6,7},{7,6}} | collective-permute-start | bytes 5898248 | tf_op jit(solution)/shard_map/cond/branch_1_fun/while/body/ppermute | solution.py:667
  178.2 33.9 %collective-permute-start.56 = (bf16[2,60,64,128]{3,2,1,0:T(8,128)(2,1)}, bf16[2,60,64,128]{3,2,1,0:T(8,128)(2,1)S(1)}, u32[]{:S(2)}, u32[]{:S(2)}) collective-permute-start(bf16[2,60,64,128]{3,2,1,0:T(8,128)(2,1)} %get-tuple-element.2445), channel_id=1, source_target_pairs={{0,1},{1,0},{2,3},{3,2},{4,5},{5,4},{6,7},{7,6}} | collective-permute-start | bytes 5898248 | tf_op jit(solution)/shard_map/cond/branch_1_fun/while/body/ppermute | solution.py:667
  178.2 33.4 %collective-permute-start.61 = (bf16[2,32,64,128]{3,2,1,0:T(8,128)(2,1)}, bf16[2,32,64,128]{3,2,1,0:T(8,128)(2,1)}, u32[]{:S(2)}, u32[]{:S(2)}) collective-permute-start(bf16[2,32,64,128]{3,2,1,0:T(8,128)(2,1)} %get-tuple-element.2446), channel_id=1, source_target_pairs={{0,1},{1,0},{2,3},{3,2},{4,5},{5,4},{6,7},{7,6}} | collective-permute-start | bytes 3145736 | tf_op jit(solution)/shard_map/cond/branch_1_fun/while/body/ppermute | solution.py:670
  178.7 32.2 %collective-permute-start.60 = (bf16[60,64,128]{2,1,0:T(8,128)(2,1)}, bf16[60,64,128]{2,1,0:T(8,128)(2,1)}, u32[]{:S(2)}, u32[]{:S(2)}) collective-permute-start(bf16[60,64,128]{2,1,0:T(8,128)(2,1)} %get-tuple-element.2449.rc1), channel_id=1, source_target_pairs={{0,1},{1,0},{2,3},{3,2},{4,5},{5,4},{6,7},{7,6}} | collective-permute-start | bytes 2949128 | tf_op jit(solution)/shard_map/cond/branch_1_fun/while/body/ppermute | solution.py:669
  210.9 28.9 %collective-permute-start.62 = (bf16[2,60,64,128]{3,2,1,0:T(8,128)(2,1)}, bf16[2,60,64,128]{3,2,1,0:T(8,128)(2,1)}, u32[]{:S(2)}, u32[]{:S(2)}) collective-permute-start(bf16[2,60,64,128]{3,2,1,0:T(8,128)(2,1)} %get-tuple-element.2131), channel_id=1, source_target_pairs={{0,1},{1,0},{2,3},{3,2},{4,5},{5,4},{6,7},{7,6}} | collective-permute-start | bytes 5898248 | tf_op jit(solution)/shard_map/cond/branch_1_fun/while/body/ppermute | solution.py:667
  211.6 25.4 %collective-permute-start.67 = (bf16[2,32,64,128]{3,2,1,0:T(8,128)(2,1)}, bf16[2,32,64,128]{3,2,1,0:T(8,128)(2,1)}, u32[]{:S(2)}, u32[]{:S(2)}) collective-permute-start(bf16[2,32,64,128]{3,2,1,0:T(8,128)(2,1)} %get-tuple-element.2138), channel_id=1, source_target_pairs={{0,1},{1,0},{2,3},{3,2},{4,5},{5,4},{6,7},{7,6}} | collective-permute-start | bytes 3145736 | tf_op jit(solution)/shard_map/cond/branch_1_fun/while/body/ppermute | solution.py:670
  212.0 24.9 %collective-permute-start.63 = (bf16[60,64,128]{2,1,0:T(8,128)(2,1)}, bf16[60,64,128]{2,1,0:T(8,128)(2,1)}, u32[]{:S(2)}, u32[]{:S(2)}) collective-permute-start(bf16[60,64,128]{2,1,0:T(8,128)(2,1)} %get-tuple-element.2132), channel_id=1, source_target_pairs={{0,2},{1,3},{2,6},{3,7},{6,4},{7,5},{4,0},{5,1}} | collective-permute-start | bytes 2949128 | tf_op jit(solution)/shard_map/cond/branch_1_fun/while/body/ppermute | solution.py:665
  212.1 25.4 %collective-permute-start.64 = (bf16[60,64,128]{2,1,0:T(8,128)(2,1)}, bf16[60,64,128]{2,1,0:T(8,128)(2,1)}, u32[]{:S(2)}, u32[]{:S(2)}) collective-permute-start(bf16[60,64,128]{2,1,0:T(8,128)(2,1)} %get-tuple-element.2133), channel_id=1, source_target_pairs={{2,0},{3,1},{6,2},{7,3},{4,6},{5,7},{0,4},{1,5}} | collective-permute-start | bytes 2949128 | tf_op jit(solution)/shard_map/cond/branch_1_fun/while/body/ppermute | solution.py:666
  229.3 27.8 %collective-permute-start.69 = (bf16[60,64,128]{2,1,0:T(8,128)(2,1)}, bf16[60,64,128]{2,1,0:T(8,128)(2,1)}, u32[]{:S(2)}, u32[]{:S(2)}) collective-permute-start(bf16[60,64,128]{2,1,0:T(8,128)(2,1)} %get-tuple-element.2149), channel_id=1, source_target_pairs={{0,2},{1,3},{2,6},{3,7},{6,4},{7,5},{4,0},{5,1}} | collective-permute-start | bytes 2949128 | tf_op jit(solution)/shard_map/cond/branch_1_fun/while/body/ppermute | solution.py:665
  237.0 45.4 %collective-permute-start.68 = (bf16[2,60,64,128]{3,2,1,0:T(8,128)(2,1)}, bf16[2,60,64,128]{3,2,1,0:T(8,128)(2,1)}, u32[]{:S(2)}, u32[]{:S(2)}) collective-permute-start(bf16[2,60,64,128]{3,2,1,0:T(8,128)(2,1)} %get-tuple-element.2148), channel_id=1, source_target_pairs={{0,1},{1,0},{2,3},{3,2},{4,5},{5,4},{6,7},{7,6}} | collective-permute-start | bytes 5898248 | tf_op jit(solution)/shard_map/cond/branch_1_fun/while/body/ppermute | solution.py:667
  239.9 42.0 %collective-permute-start.73 = (bf16[2,32,64,128]{3,2,1,0:T(8,128)(2,1)}, bf16[2,32,64,128]{3,2,1,0:T(8,128)(2,1)S(1)}, u32[]{:S(2)}, u32[]{:S(2)}) collective-permute-start(bf16[2,32,64,128]{3,2,1,0:T(8,128)(2,1)} %get-tuple-element.2155), channel_id=1, source_target_pairs={{0,1},{1,0},{2,3},{3,2},{4,5},{5,4},{6,7},{7,6}} | collective-permute-start | bytes 3145736 | tf_op jit(solution)/shard_map/cond/branch_1_fun/while/body/ppermute | solution.py:670
  258.1 48.4 %collective-permute-start.74 = (bf16[2,60,64,128]{3,2,1,0:T(8,128)(2,1)}, bf16[2,60,64,128]{3,2,1,0:T(8,128)(2,1)}, u32[]{:S(2)}, u32[]{:S(2)}) collective-permute-start(bf16[2,60,64,128]{3,2,1,0:T(8,128)(2,1)} %get-tuple-element.2169), channel_id=1, source_target_pairs={{0,1},{1,0},{2,3},{3,2},{4,5},{5,4},{6,7},{7,6}} | collective-permute-start | bytes 5898248 | tf_op jit(solution)/shard_map/cond/branch_1_fun/while/body/ppermute | solution.py:667
  309.1 32.8 %collective-permute-start.56 = (bf16[2,60,64,128]{3,2,1,0:T(8,128)(2,1)}, bf16[2,60,64,128]{3,2,1,0:T(8,128)(2,1)S(1)}, u32[]{:S(2)}, u32[]{:S(2)}) collective-permute-start(bf16[2,60,64,128]{3,2,1,0:T(8,128)(2,1)} %get-tuple-element.2445), channel_id=1, source_target_pairs={{0,1},{1,0},{2,3},{3,2},{4,5},{5,4},{6,7},{7,6}} | collective-permute-start | bytes 5898248 | tf_op jit(solution)/shard_map/cond/branch_1_fun/while/body/ppermute | solution.py:667
  309.1 32.7 %collective-permute-start.61 = (bf16[2,32,64,128]{3,2,1,0:T(8,128)(2,1)}, bf16[2,32,64,128]{3,2,1,0:T(8,128)(2,1)}, u32[]{:S(2)}, u32[]{:S(2)}) collective-permute-start(bf16[2,32,64,128]{3,2,1,0:T(8,128)(2,1)} %get-tuple-element.2446), channel_id=1, source_target_pairs={{0,1},{1,0},{2,3},{3,2},{4,5},{5,4},{6,7},{7,6}} | collective-permute-start | bytes 3145736 | tf_op jit(solution)/shard_map/cond/branch_1_fun/while/body/ppermute | solution.py:670
  309.6 31.6 %collective-permute-start.60 = (bf16[60,64,128]{2,1,0:T(8,128)(2,1)}, bf16[60,64,128]{2,1,0:T(8,128)(2,1)}, u32[]{:S(2)}, u32[]{:S(2)}) collective-permute-start(bf16[60,64,128]{2,1,0:T(8,128)(2,1)} %get-tuple-element.2449.rc1), channel_id=1, source_target_pairs={{0,1},{1,0},{2,3},{3,2},{4,5},{5,4},{6,7},{7,6}} | collective-permute-start | bytes 2949128 | tf_op jit(solution)/shard_map/cond/branch_1_fun/while/body/ppermute | solution.py:669
  341.3 32.6 %collective-permute-start.62 = (bf16[2,60,64,128]{3,2,1,0:T(8,128)(2,1)}, bf16[2,60,64,128]{3,2,1,0:T(8,128)(2,1)}, u32[]{:S(2)}, u32[]{:S(2)}) collective-permute-start(bf16[2,60,64,128]{3,2,1,0:T(8,128)(2,1)} %get-tuple-element.2131), channel_id=1, source_target_pairs={{0,1},{1,0},{2,3},{3,2},{4,5},{5,4},{6,7},{7,6}} | collective-permute-start | bytes 5898248 | tf_op jit(solution)/shard_map/cond/branch_1_fun/while/body/ppermute | solution.py:667
  341.8 25.0 %collective-permute-start.67 = (bf16[2,32,64,128]{3,2,1,0:T(8,128)(2,1)}, bf16[2,32,64,128]{3,2,1,0:T(8,128)(2,1)}, u32[]{:S(2)}, u32[]{:S(2)}) collective-permute-start(bf16[2,32,64,128]{3,2,1,0:T(8,128)(2,1)} %get-tuple-element.2138), channel_id=1, source_target_pairs={{0,1},{1,0},{2,3},{3,2},{4,5},{5,4},{6,7},{7,6}} | collective-permute-start | bytes 3145736 | tf_op jit(solution)/shard_map/cond/branch_1_fun/while/body/ppermute | solution.py:670
  341.9 25.4 %collective-permute-start.64 = (bf16[60,64,128]{2,1,0:T(8,128)(2,1)}, bf16[60,64,128]{2,1,0:T(8,128)(2,1)}, u32[]{:S(2)}, u32[]{:S(2)}) collective-permute-start(bf16[60,64,128]{2,1,0:T(8,128)(2,1)} %get-tuple-element.2133), channel_id=1, source_target_pairs={{2,0},{3,1},{6,2},{7,3},{4,6},{5,7},{0,4},{1,5}} | collective-permute-start | bytes 2949128 | tf_op jit(solution)/shard_map/cond/branch_1_fun/while/body/ppermute | solution.py:666
  359.8 27.6 %collective-permute-start.69 = (bf16[60,64,128]{2,1,0:T(8,128)(2,1)}, bf16[60,64,128]{2,1,0:T(8,128)(2,1)}, u32[]{:S(2)}, u32[]{:S(2)}) collective-permute-start(bf16[60,64,128]{2,1,0:T(8,128)(2,1)} %get-tuple-element.2149), channel_id=1, source_target_pairs={{0,2},{1,3},{2,6},{3,7},{6,4},{7,5},{4,0},{5,1}} | collective-permute-start | bytes 2949128 | tf_op jit(solution)/shard_map/cond/branch_1_fun/while/body/ppermute | solution.py:665
  366.8 45.9 %collective-permute-start.68 = (bf16[2,60,64,128]{3,2,1,0:T(8,128)(2,1)}, bf16[2,60,64,128]{3,2,1,0:T(8,128)(2,1)}, u32[]{:S(2)}, u32[]{:S(2)}) collective-permute-start(bf16[2,60,64,128]{3,2,1,0:T(8,128)(2,1)} %get-tuple-element.2148), channel_id=1, source_target_pairs={{0,1},{1,0},{2,3},{3,2},{4,5},{5,4},{6,7},{7,6}} | collective-permute-start | bytes 5898248 | tf_op jit(solution)/shard_map/cond/branch_1_fun/while/body/ppermute | solution.py:667
  373.9 38.2 %collective-permute-start.73 = (bf16[2,32,64,128]{3,2,1,0:T(8,128)(2,1)}, bf16[2,32,64,128]{3,2,1,0:T(8,128)(2,1)S(1)}, u32[]{:S(2)}, u32[]{:S(2)}) collective-permute-start(bf16[2,32,64,128]{3,2,1,0:T(8,128)(2,1)} %get-tuple-element.2155), channel_id=1, source_target_pairs={{0,1},{1,0},{2,3},{3,2},{4,5},{5,4},{6,7},{7,6}} | collective-permute-start | bytes 3145736 | tf_op jit(solution)/shard_map/cond/branch_1_fun/while/body/ppermute | solution.py:670
  388.4 48.3 %collective-permute-start.74 = (bf16[2,60,64,128]{3,2,1,0:T(8,128)(2,1)}, bf16[2,60,64,128]{3,2,1,0:T(8,128)(2,1)}, u32[]{:S(2)}, u32[]{:S(2)}) collective-permute-start(bf16[2,60,64,128]{3,2,1,0:T(8,128)(2,1)} %get-tuple-element.2169), channel_id=1, source_target_pairs={{0,1},{1,0},{2,3},{3,2},{4,5},{5,4},{6,7},{7,6}} | collective-permute-start | bytes 5898248 | tf_op jit(solution)/shard_map/cond/branch_1_fun/while/body/ppermute | solution.py:667
  439.4 32.8 %collective-permute-start.56 = (bf16[2,60,64,128]{3,2,1,0:T(8,128)(2,1)}, bf16[2,60,64,128]{3,2,1,0:T(8,128)(2,1)S(1)}, u32[]{:S(2)}, u32[]{:S(2)}) collective-permute-start(bf16[2,60,64,128]{3,2,1,0:T(8,128)(2,1)} %get-tuple-element.2445), channel_id=1, source_target_pairs={{0,1},{1,0},{2,3},{3,2},{4,5},{5,4},{6,7},{7,6}} | collective-permute-start | bytes 5898248 | tf_op jit(solution)/shard_map/cond/branch_1_fun/while/body/ppermute | solution.py:667
  439.4 32.3 %collective-permute-start.61 = (bf16[2,32,64,128]{3,2,1,0:T(8,128)(2,1)}, bf16[2,32,64,128]{3,2,1,0:T(8,128)(2,1)}, u32[]{:S(2)}, u32[]{:S(2)}) collective-permute-start(bf16[2,32,64,128]{3,2,1,0:T(8,128)(2,1)} %get-tuple-element.2446), channel_id=1, source_target_pairs={{0,1},{1,0},{2,3},{3,2},{4,5},{5,4},{6,7},{7,6}} | collective-permute-start | bytes 3145736 | tf_op jit(solution)/shard_map/cond/branch_1_fun/while/body/ppermute | solution.py:670
  439.9 30.0 %collective-permute-start.60 = (bf16[60,64,128]{2,1,0:T(8,128)(2,1)}, bf16[60,64,128]{2,1,0:T(8,128)(2,1)}, u32[]{:S(2)}, u32[]{:S(2)}) collective-permute-start(bf16[60,64,128]{2,1,0:T(8,128)(2,1)} %get-tuple-element.2449.rc1), channel_id=1, source_target_pairs={{0,1},{1,0},{2,3},{3,2},{4,5},{5,4},{6,7},{7,6}} | collective-permute-start | bytes 2949128 | tf_op jit(solution)/shard_map/cond/branch_1_fun/while/body/ppermute | solution.py:669
  470.0 33.0 %collective-permute-start.62 = (bf16[2,60,64,128]{3,2,1,0:T(8,128)(2,1)}, bf16[2,60,64,128]{3,2,1,0:T(8,128)(2,1)}, u32[]{:S(2)}, u32[]{:S(2)}) collective-permute-start(bf16[2,60,64,128]{3,2,1,0:T(8,128)(2,1)} %get-tuple-element.2131), channel_id=1, source_target_pairs={{0,1},{1,0},{2,3},{3,2},{4,5},{5,4},{6,7},{7,6}} | collective-permute-start | bytes 5898248 | tf_op jit(solution)/shard_map/cond/branch_1_fun/while/body/ppermute | solution.py:667
  471.7 25.4 %collective-permute-start.67 = (bf16[2,32,64,128]{3,2,1,0:T(8,128)(2,1)}, bf16[2,32,64,128]{3,2,1,0:T(8,128)(2,1)}, u32[]{:S(2)}, u32[]{:S(2)}) collective-permute-start(bf16[2,32,64,128]{3,2,1,0:T(8,128)(2,1)} %get-tuple-element.2138), channel_id=1, source_target_pairs={{0,1},{1,0},{2,3},{3,2},{4,5},{5,4},{6,7},{7,6}} | collective-permute-start | bytes 3145736 | tf_op jit(solution)/shard_map/cond/branch_1_fun/while/body/ppermute | solution.py:670
  472.1 24.9 %collective-permute-start.63 = (bf16[60,64,128]{2,1,0:T(8,128)(2,1)}, bf16[60,64,128]{2,1,0:T(8,128)(2,1)}, u32[]{:S(2)}, u32[]{:S(2)}) collective-permute-start(bf16[60,64,128]{2,1,0:T(8,128)(2,1)} %get-tuple-element.2132), channel_id=1, source_target_pairs={{0,2},{1,3},{2,6},{3,7},{6,4},{7,5},{4,0},{5,1}} | collective-permute-start | bytes 2949128 | tf_op jit(solution)/shard_map/cond/branch_1_fun/while/body/ppermute | solution.py:665
  472.2 25.4 %collective-permute-start.64 = (bf16[60,64,128]{2,1,0:T(8,128)(2,1)}, bf16[60,64,128]{2,1,0:T(8,128)(2,1)}, u32[]{:S(2)}, u32[]{:S(2)}) collective-permute-start(bf16[60,64,128]{2,1,0:T(8,128)(2,1)} %get-tuple-element.2133), channel_id=1, source_target_pairs={{2,0},{3,1},{6,2},{7,3},{4,6},{5,7},{0,4},{1,5}} | collective-permute-start | bytes 2949128 | tf_op jit(solution)/shard_map/cond/branch_1_fun/while/body/ppermute | solution.py:666
  487.9 29.3 %collective-permute-start.69 = (bf16[60,64,128]{2,1,0:T(8,128)(2,1)}, bf16[60,64,128]{2,1,0:T(8,128)(2,1)}, u32[]{:S(2)}, u32[]{:S(2)}) collective-permute-start(bf16[60,64,128]{2,1,0:T(8,128)(2,1)} %get-tuple-element.2149), channel_id=1, source_target_pairs={{0,2},{1,3},{2,6},{3,7},{6,4},{7,5},{4,0},{5,1}} | collective-permute-start | bytes 2949128 | tf_op jit(solution)/shard_map/cond/branch_1_fun/while/body/ppermute | solution.py:665
  497.1 45.4 %collective-permute-start.68 = (bf16[2,60,64,128]{3,2,1,0:T(8,128)(2,1)}, bf16[2,60,64,128]{3,2,1,0:T(8,128)(2,1)}, u32[]{:S(2)}, u32[]{:S(2)}) collective-permute-start(bf16[2,60,64,128]{3,2,1,0:T(8,128)(2,1)} %get-tuple-element.2148), channel_id=1, source_target_pairs={{0,1},{1,0},{2,3},{3,2},{4,5},{5,4},{6,7},{7,6}} | collective-permute-start | bytes 5898248 | tf_op jit(solution)/shard_map/cond/branch_1_fun/while/body/ppermute | solution.py:667
  503.0 39.0 %collective-permute-start.73 = (bf16[2,32,64,128]{3,2,1,0:T(8,128)(2,1)}, bf16[2,32,64,128]{3,2,1,0:T(8,128)(2,1)S(1)}, u32[]{:S(2)}, u32[]{:S(2)}) collective-permute-start(bf16[2,32,64,128]{3,2,1,0:T(8,128)(2,1)} %get-tuple-element.2155), channel_id=1, source_target_pairs={{0,1},{1,0},{2,3},{3,2},{4,5},{5,4},{6,7},{7,6}} | collective-permute-start | bytes 3145736 | tf_op jit(solution)/shard_map/cond/branch_1_fun/while/body/ppermute | solution.py:670
  517.9 48.6 %collective-permute-start.74 = (bf16[2,60,64,128]{3,2,1,0:T(8,128)(2,1)}, bf16[2,60,64,128]{3,2,1,0:T(8,128)(2,1)}, u32[]{:S(2)}, u32[]{:S(2)}) collective-permute-start(bf16[2,60,64,128]{3,2,1,0:T(8,128)(2,1)} %get-tuple-element.2169), channel_id=1, source_target_pairs={{0,1},{1,0},{2,3},{3,2},{4,5},{5,4},{6,7},{7,6}} | collective-permute-start | bytes 5898248 | tf_op jit(solution)/shard_map/cond/branch_1_fun/while/body/ppermute | solution.py:667
  569.2 33.1 %collective-permute-start.56 = (bf16[2,60,64,128]{3,2,1,0:T(8,128)(2,1)}, bf16[2,60,64,128]{3,2,1,0:T(8,128)(2,1)S(1)}, u32[]{:S(2)}, u32[]{:S(2)}) collective-permute-start(bf16[2,60,64,128]{3,2,1,0:T(8,128)(2,1)} %get-tuple-element.2445), channel_id=1, source_target_pairs={{0,1},{1,0},{2,3},{3,2},{4,5},{5,4},{6,7},{7,6}} | collective-permute-start | bytes 5898248 | tf_op jit(solution)/shard_map/cond/branch_1_fun/while/body/ppermute | solution.py:667
  569.2 31.4 %collective-permute-start.61 = (bf16[2,32,64,128]{3,2,1,0:T(8,128)(2,1)}, bf16[2,32,64,128]{3,2,1,0:T(8,128)(2,1)}, u32[]{:S(2)}, u32[]{:S(2)}) collective-permute-start(bf16[2,32,64,128]{3,2,1,0:T(8,128)(2,1)} %get-tuple-element.2446), channel_id=1, source_target_pairs={{0,1},{1,0},{2,3},{3,2},{4,5},{5,4},{6,7},{7,6}} | collective-permute-start | bytes 3145736 | tf_op jit(solution)/shard_map/cond/branch_1_fun/while/body/ppermute | solution.py:670
  569.7 30.3 %collective-permute-start.60 = (bf16[60,64,128]{2,1,0:T(8,128)(2,1)}, bf16[60,64,128]{2,1,0:T(8,128)(2,1)}, u32[]{:S(2)}, u32[]{:S(2)}) collective-permute-start(bf16[60,64,128]{2,1,0:T(8,128)(2,1)} %get-tuple-element.2449.rc1), channel_id=1, source_target_pairs={{0,1},{1,0},{2,3},{3,2},{4,5},{5,4},{6,7},{7,6}} | collective-permute-start | bytes 2949128 | tf_op jit(solution)/shard_map/cond/branch_1_fun/while/body/ppermute | solution.py:669
  600.1 31.4 %collective-permute-start.62 = (bf16[2,60,64,128]{3,2,1,0:T(8,128)(2,1)}, bf16[2,60,64,128]{3,2,1,0:T(8,128)(2,1)}, u32[]{:S(2)}, u32[]{:S(2)}) collective-permute-start(bf16[2,60,64,128]{3,2,1,0:T(8,128)(2,1)} %get-tuple-element.2131), channel_id=1, source_target_pairs={{0,1},{1,0},{2,3},{3,2},{4,5},{5,4},{6,7},{7,6}} | collective-permute-start | bytes 5898248 | tf_op jit(solution)/shard_map/cond/branch_1_fun/while/body/ppermute | solution.py:667
  600.6 25.1 %collective-permute-start.67 = (bf16[2,32,64,128]{3,2,1,0:T(8,128)(2,1)}, bf16[2,32,64,128]{3,2,1,0:T(8,128)(2,1)}, u32[]{:S(2)}, u32[]{:S(2)}) collective-permute-start(bf16[2,32,64,128]{3,2,1,0:T(8,128)(2,1)} %get-tuple-element.2138), channel_id=1, source_target_pairs={{0,1},{1,0},{2,3},{3,2},{4,5},{5,4},{6,7},{7,6}} | collective-permute-start | bytes 3145736 | tf_op jit(solution)/shard_map/cond/branch_1_fun/while/body/ppermute | solution.py:670
  600.7 24.9 %collective-permute-start.63 = (bf16[60,64,128]{2,1,0:T(8,128)(2,1)}, bf16[60,64,128]{2,1,0:T(8,128)(2,1)}, u32[]{:S(2)}, u32[]{:S(2)}) collective-permute-start(bf16[60,64,128]{2,1,0:T(8,128)(2,1)} %get-tuple-element.2132), channel_id=1, source_target_pairs={{0,2},{1,3},{2,6},{3,7},{6,4},{7,5},{4,0},{5,1}} | collective-permute-start | bytes 2949128 | tf_op jit(solution)/shard_map/cond/branch_1_fun/while/body/ppermute | solution.py:665
  618.2 27.9 %collective-permute-start.69 = (bf16[60,64,128]{2,1,0:T(8,128)(2,1)}, bf16[60,64,128]{2,1,0:T(8,128)(2,1)}, u32[]{:S(2)}, u32[]{:S(2)}) collective-permute-start(bf16[60,64,128]{2,1,0:T(8,128)(2,1)} %get-tuple-element.2149), channel_id=1, source_target_pairs={{0,2},{1,3},{2,6},{3,7},{6,4},{7,5},{4,0},{5,1}} | collective-permute-start | bytes 2949128 | tf_op jit(solution)/shard_map/cond/branch_1_fun/while/body/ppermute | solution.py:665
  625.7 46.8 %collective-permute-start.68 = (bf16[2,60,64,128]{3,2,1,0:T(8,128)(2,1)}, bf16[2,60,64,128]{3,2,1,0:T(8,128)(2,1)}, u32[]{:S(2)}, u32[]{:S(2)}) collective-permute-start(bf16[2,60,64,128]{3,2,1,0:T(8,128)(2,1)} %get-tuple-element.2148), channel_id=1, source_target_pairs={{0,1},{1,0},{2,3},{3,2},{4,5},{5,4},{6,7},{7,6}} | collective-permute-start | bytes 5898248 | tf_op jit(solution)/shard_map/cond/branch_1_fun/while/body/ppermute | solution.py:667
  631.5 40.4 %collective-permute-start.73 = (bf16[2,32,64,128]{3,2,1,0:T(8,128)(2,1)}, bf16[2,32,64,128]{3,2,1,0:T(8,128)(2,1)S(1)}, u32[]{:S(2)}, u32[]{:S(2)}) collective-permute-start(bf16[2,32,64,128]{3,2,1,0:T(8,128)(2,1)} %get-tuple-element.2155), channel_id=1, source_target_pairs={{0,1},{1,0},{2,3},{3,2},{4,5},{5,4},{6,7},{7,6}} | collective-permute-start | bytes 3145736 | tf_op jit(solution)/shard_map/cond/branch_1_fun/while/body/ppermute | solution.py:670
  646.2 25.8 %collective-permute-start.79 = (bf16[2,32,64,128]{3,2,1,0:T(8,128)(2,1)}, bf16[2,32,64,128]{3,2,1,0:T(8,128)(2,1)S(1)}, u32[]{:S(2)}, u32[]{:S(2)}) collective-permute-start(bf16[2,32,64,128]{3,2,1,0:T(8,128)(2,1)} %get-tuple-element.2172), channel_id=1, source_target_pairs={{0,1},{1,0},{2,3},{3,2},{4,5},{5,4},{6,7},{7,6}} | collective-permute-start | bytes 3145736 | tf_op jit(solution)/shard_map/cond/branch_1_fun/while/body/ppermute | solution.py:670
  647.8 48.6 %collective-permute-start.74 = (bf16[2,60,64,128]{3,2,1,0:T(8,128)(2,1)}, bf16[2,60,64,128]{3,2,1,0:T(8,128)(2,1)}, u32[]{:S(2)}, u32[]{:S(2)}) collective-permute-start(bf16[2,60,64,128]{3,2,1,0:T(8,128)(2,1)} %get-tuple-element.2169), channel_id=1, source_target_pairs={{0,1},{1,0},{2,3},{3,2},{4,5},{5,4},{6,7},{7,6}} | collective-permute-start | bytes 5898248 | tf_op jit(solution)/shard_map/cond/branch_1_fun/while/body/ppermute | solution.py:667
  699.2 32.1 %collective-permute-start.56 = (bf16[2,60,64,128]{3,2,1,0:T(8,128)(2,1)}, bf16[2,60,64,128]{3,2,1,0:T(8,128)(2,1)S(1)}, u32[]{:S(2)}, u32[]{:S(2)}) collective-permute-start(bf16[2,60,64,128]{3,2,1,0:T(8,128)(2,1)} %get-tuple-element.2445), channel_id=1, source_target_pairs={{0,1},{1,0},{2,3},{3,2},{4,5},{5,4},{6,7},{7,6}} | collective-permute-start | bytes 5898248 | tf_op jit(solution)/shard_map/cond/branch_1_fun/while/body/ppermute | solution.py:667
  699.2 30.8 %collective-permute-start.61 = (bf16[2,32,64,128]{3,2,1,0:T(8,128)(2,1)}, bf16[2,32,64,128]{3,2,1,0:T(8,128)(2,1)}, u32[]{:S(2)}, u32[]{:S(2)}) collective-permute-start(bf16[2,32,64,128]{3,2,1,0:T(8,128)(2,1)} %get-tuple-element.2446), channel_id=1, source_target_pairs={{0,1},{1,0},{2,3},{3,2},{4,5},{5,4},{6,7},{7,6}} | collective-permute-start | bytes 3145736 | tf_op jit(solution)/shard_map/cond/branch_1_fun/while/body/ppermute | solution.py:670
  699.7 29.8 %collective-permute-start.60 = (bf16[60,64,128]{2,1,0:T(8,128)(2,1)}, bf16[60,64,128]{2,1,0:T(8,128)(2,1)}, u32[]{:S(2)}, u32[]{:S(2)}) collective-permute-start(bf16[60,64,128]{2,1,0:T(8,128)(2,1)} %get-tuple-element.2449.rc1), channel_id=1, source_target_pairs={{0,1},{1,0},{2,3},{3,2},{4,5},{5,4},{6,7},{7,6}} | collective-permute-start | bytes 2949128 | tf_op jit(solution)/shard_map/cond/branch_1_fun/while/body/ppermute | solution.py:669
  729.5 32.4 %collective-permute-start.62 = (bf16[2,60,64,128]{3,2,1,0:T(8,128)(2,1)}, bf16[2,60,64,128]{3,2,1,0:T(8,128)(2,1)}, u32[]{:S(2)}, u32[]{:S(2)}) collective-permute-start(bf16[2,60,64,128]{3,2,1,0:T(8,128)(2,1)} %get-tuple-element.2131), channel_id=1, source_target_pairs={{0,1},{1,0},{2,3},{3,2},{4,5},{5,4},{6,7},{7,6}} | collective-permute-start | bytes 5898248 | tf_op jit(solution)/shard_map/cond/branch_1_fun/while/body/ppermute | solution.py:667
  730.0 25.0 %collective-permute-start.67 = (bf16[2,32,64,128]{3,2,1,0:T(8,128)(2,1)}, bf16[2,32,64,128]{3,2,1,0:T(8,128)(2,1)}, u32[]{:S(2)}, u32[]{:S(2)}) collective-permute-start(bf16[2,32,64,128]{3,2,1,0:T(8,128)(2,1)} %get-tuple-element.2138), channel_id=1, source_target_pairs={{0,1},{1,0},{2,3},{3,2},{4,5},{5,4},{6,7},{7,6}} | collective-permute-start | bytes 3145736 | tf_op jit(solution)/shard_map/cond/branch_1_fun/while/body/ppermute | solution.py:670
  746.5 29.1 %collective-permute-start.69 = (bf16[60,64,128]{2,1,0:T(8,128)(2,1)}, bf16[60,64,128]{2,1,0:T(8,128)(2,1)}, u32[]{:S(2)}, u32[]{:S(2)}) collective-permute-start(bf16[60,64,128]{2,1,0:T(8,128)(2,1)} %get-tuple-element.2149), channel_id=1, source_target_pairs={{0,2},{1,3},{2,6},{3,7},{6,4},{7,5},{4,0},{5,1}} | collective-permute-start | bytes 2949128 | tf_op jit(solution)/shard_map/cond/branch_1_fun/while/body/ppermute | solution.py:665
  755.0 46.4 %collective-permute-start.68 = (bf16[2,60,64,128]{3,2,1,0:T(8,128)(2,1)}, bf16[2,60,64,128]{3,2,1,0:T(8,128)(2,1)}, u32[]{:S(2)}, u32[]{:S(2)}) collective-permute-start(bf16[2,60,64,128]{3,2,1,0:T(8,128)(2,1)} %get-tuple-element.2148), channel_id=1, source_target_pairs={{0,1},{1,0},{2,3},{3,2},{4,5},{5,4},{6,7},{7,6}} | collective-permute-start | bytes 5898248 | tf_op jit(solution)/shard_map/cond/branch_1_fun/while/body/ppermute | solution.py:667
  761.9 39.0 %collective-permute-start.73 = (bf16[2,32,64,128]{3,2,1,0:T(8,128)(2,1)}, bf16[2,32,64,128]{3,2,1,0:T(8,128)(2,1)S(1)}, u32[]{:S(2)}, u32[]{:S(2)}) collective-permute-start(bf16[2,32,64,128]{3,2,1,0:T(8,128)(2,1)} %get-tuple-element.2155), channel_id=1, source_target_pairs={{0,1},{1,0},{2,3},{3,2},{4,5},{5,4},{6,7},{7,6}} | collective-permute-start | bytes 3145736 | tf_op jit(solution)/shard_map/cond/branch_1_fun/while/body/ppermute | solution.py:670
  775.6 25.3 %collective-permute-start.79 = (bf16[2,32,64,128]{3,2,1,0:T(8,128)(2,1)}, bf16[2,32,64,128]{3,2,1,0:T(8,128)(2,1)S(1)}, u32[]{:S(2)}, u32[]{:S(2)}) collective-permute-start(bf16[2,32,64,128]{3,2,1,0:T(8,128)(2,1)} %get-tuple-element.2172), channel_id=1, source_target_pairs={{0,1},{1,0},{2,3},{3,2},{4,5},{5,4},{6,7},{7,6}} | collective-permute-start | bytes 3145736 | tf_op jit(solution)/shard_map/cond/branch_1_fun/while/body/ppermute | solution.py:670
  777.1 48.3 %collective-permute-start.74 = (bf16[2,60,64,128]{3,2,1,0:T(8,128)(2,1)}, bf16[2,60,64,128]{3,2,1,0:T(8,128)(2,1)}, u32[]{:S(2)}, u32[]{:S(2)}) collective-permute-start(bf16[2,60,64,128]{3,2,1,0:T(8,128)(2,1)} %get-tuple-element.2169), channel_id=1, source_target_pairs={{0,1},{1,0},{2,3},{3,2},{4,5},{5,4},{6,7},{7,6}} | collective-permute-start | bytes 5898248 | tf_op jit(solution)/shard_map/cond/branch_1_fun/while/body/ppermute | solution.py:667
  (114 other events, 1868.3 us)

commit v4 on v3

--- a/solution.py
+++ b/solution.py
@@ -9,7 +9,7 @@
 
 
 BP, SHIFT = 8, 3
-SIZES = (66, 60, 54, 48)
+SIZES = range(84, 56, -4)
 NX = 32
 A = 4
 SL = 32
@@ -20,7 +20,7 @@
 CORE, PICK, SHARE, DUMP = range(ROUNDS + 1, ROUNDS + 5)
 TAB = ROUNDS + 8
 FWD, NONE = 2, 3
-TURN = 4
+TURN = 2
 SEGS = 6
 IDLE = 4 * SEGS
 HALF = 1 << 16
@@ -118,6 +118,11 @@
 
     lax.fori_loop(0, far, choose, 0)
 
+    def largest():
+        return functools.reduce(jnp.maximum, [load[x] for x in range(8)])
+
+    at[0] = largest()
+
     def detour(n, c):
         i = near[n]
         nb = nbv[i]
@@ -127,9 +132,8 @@
         b = [jnp.where(cw, y, x) for x, y in zip(cws, ccws)]
         lb = [load[x] for x in b]
         la = load[a]
-        top = functools.reduce(jnp.maximum, [load[x] for x in range(8)])
-
-        @pl.when((la - nb >= functools.reduce(jnp.maximum, lb) + nb) & (la * 10 >= top * 9))
+
+        @pl.when((la - nb >= functools.reduce(jnp.maximum, lb) + nb) & (la * 10 >= at[0] * 9))
         def _():
             load[a] = la - nb
             one[a] = one[a] - nb - HALF
@@ -137,6 +141,7 @@
                 load[x] = l + nb
             three[b[0]] = three[b[0]] + nb + HALF
             kindv[i] = jnp.where(cw, 6, 3)
+            at[0] = largest()
 
         return c
 
@@ -184,14 +189,22 @@
     for d in range(8):
         cross = jnp.maximum(cross, (swap[d] + NX - 1) // NX)
     best, pick, turns, chunk = zero + END, zero, zero, zero
+    all_links = [(two[x] + three[x], three[x], one[x] + two[x] + three[x]) for x in range(8)]
+    parts = []
+    for d in range(2):
+        ring = all_links[4 * d:][:4][::1 - 2 * d]
+        for x in range(4):
+            (_, _, own), (fwd, _, own_up), (fwd_up, fwd2, _) = ring[x], ring[x - 1], ring[x - 2]
+            parts.append([n & LOW for n in (own, fwd, own_up, fwd_up, fwd2)])
     for o, size in enumerate(SIZES):
         longest = zero
-        for d in range(2):
-            for x in range(4):
-                _, _, fwd2, _, _, start2 = link(d, x, size)
-                longest = jnp.maximum(longest, start2 + (fwd2 & LOW))
+        for own, fwd, own_up, fwd_up, fwd2 in parts:
+            wait, wait_up = jnp.where(fwd > 0, 2 * size, 0), jnp.where(fwd_up > 0, 2 * size, 0)
+            total = jnp.maximum(own, wait) + fwd
+            late = jnp.maximum(own_up, wait_up) + 2 * size
+            longest = jnp.maximum(longest, jnp.where(fwd2 > 0, jnp.maximum(total, late) + fwd2, total))
         trips = (jnp.maximum((longest + size - 1) // size, cross) + TURN - 1) // TURN
-        price = trips * (TURN * size + 12)
+        price = trips * (TURN * size + 7)
         better = price < best
         best, pick, turns, chunk = [jnp.where(better, n, o) for n, o in (
             (price, best), (o, pick), (trips * TURN, turns), (size, chunk))]
@@ -599,7 +612,7 @@
 
 ST = sds((STATE,), i32)
 DMA = [pltpu.SemaphoreType.DMA]
-TAGS = ('ra', 'rb', 'rc', 'rd')
+TAGS = ('ra', 'rb')
 
 
 def solution(mesh):

time: 850 us -> 712 us (0.84)
  waiting for transfers between devices: 357 us -> 302 us
  Pallas kernels: 400 us -> 347 us
  starting transfers between devices: 74.6 us -> 48 us
    ppermute x24 -> x18, waiting for transfers between devices: 272 us -> 168 us  [one_round(): nrc1 = lax.ppermute(s1, 'dp', ccw)]
    ppermute x24 -> x18, waiting for transfers between devices: 0.06 us -> 63.6 us  [one_round(): ndxr = lax.ppermute(dxs, 'dp', swap)]
    pallas_call x24 -> x18, Pallas kernels: 214 us -> 182 us  [one_round(): pl.pallas_call(functools.partial(round_kernel, NB), out_shape=(ST, chunk,...]
    pallas_call x25 -> x19, Pallas kernels: 139 us -> 114 us  [attend(): pl.pallas_call(functools.partial(attn_kernel, NB, batches), out_shape=(ST...]
    ppermute x24 -> x18, waiting for transfers between devices: 85.3 us -> 69.3 us  [one_round(): nrc0 = lax.ppermute(s0, 'dp', cw)]
    ppermute x24 -> x18, starting transfers between devices: 33.3 us -> 18.3 us  [one_round(): nrc1 = lax.ppermute(s1, 'dp', ccw)]
    ppermute x24 -> x18, starting transfers between devices: 15.2 us -> 3.8 us  [one_round(): ndxr = lax.ppermute(dxs, 'dp', swap)]
    ppermute x24 -> x18, starting transfers between devices: 13.3 us -> 18.4 us  [one_round(): nrc0 = lax.ppermute(s0, 'dp', cw)]
  transfers between devices with their start and end apart: 148 -> 112, of which waited for: 41 -> 44; matrix products, arithmetic and copies ran while one was open for 0% -> 0% of each run, Pallas kernels for 42% -> 43%
where the time goes in v4:
time: 712 us; the launch traced here: 707 us
  Pallas kernels  347 us (49%)
  waiting for transfers between devices  302 us (42%)
  starting transfers between devices  48 us (7%)
  loops' own time  7.26 us (1%)
    pallas_call x18, Pallas kernels, one_round(): pl.pallas_call(functools.partial(round_kernel, NB), out_shape=(ST, chunk,...  182 us
    ppermute x18, waiting for transfers between devices, one_round(): nrc1 = lax.ppermute(s1, 'dp', ccw)  168 us
    pallas_call x19, Pallas kernels, attend(): pl.pallas_call(functools.partial(attn_kernel, NB, batches), out_shape=(ST...  114 us
    ppermute x18, waiting for transfers between devices, one_round(): nrc0 = lax.ppermute(s0, 'dp', cw)  69.3 us
    ppermute x18, waiting for transfers between devices, one_round(): ndxr = lax.ppermute(dxs, 'dp', swap)  63.6 us
    pallas_call x1, Pallas kernels, local(): pl.pallas_call(plan_kernel, out_shape=(sds((TAB,), i32), sds((SL,), i32))...  20.2 us
    ppermute x18, starting transfers between devices, one_round(): nrc0 = lax.ppermute(s0, 'dp', cw)  18.4 us
    ppermute x18, starting transfers between devices, one_round(): nrc1 = lax.ppermute(s1, 'dp', ccw)  18.3 us
  transfers between devices with their start and end apart: 112, of which 44 were waited for; matrix products, arithmetic and copies ran while one was open for 0% of the time, Pallas kernels for 43%

profile of v4, /device:TPU:0, one launch (start us, length us, event | category | flops | bytes accessed | tf_op | source)
XLA Modules:
  0.0 707.0 jit_solution(14379517142242200677)
XLA Ops:
  0.6 7.8 %lens.1.len_ref = s32[8,1,32]{2,1,0:T(1,128)} custom-call(s32[1,32]{1,0:T(1,128)} %bitcast.30), custom_call_target="tpu_custom_call" | custom-call | tf_op jit(solution)/shard_map/lens/pallas_call | solution.py:628
  8.4 20.2 %plan.1 = (s32[2568]{0:T(1024)S(1)}, s32[32]{0:T(128)}) custom-call(s32[1]{0:T(128)} %bitcast.7.me_ref, s32[256]{0:T(256)} %dest_ref.1, s32[8,1,32]{2,1,0:T(1,128)} %lens.1.len_ref), custom_call_target="tpu_custom_call" | custom-call | tf_op jit(solution)/shard_map/plan/pallas_call | solution.py:634
  29.8 677.0 %conditional.1 = (bf16[32,24,128]{2,1,0:T(8,128)(2,1)}, bf16[2048,64,128]{2,1,0:T(8,128)(2,1)}, bf16[2048,64,128]{2,1,0:T(8,128)(2,1)}) conditional(s32[]{:T(128)} %bitcast.9, (s32[2568]{0:T(1024)S(1)}, bf16[2048,64,128]{2,1,0:T(8,128)(2,1)}, bf16[2048,64,128]{2,1,0:T(8,128)(2,1)}, bf16[32,24,128]{2,1,0:T(8,128)(2,1)}, ...), branch_computations={%region_0.0_spmd, %region_3.0_spmd, %region_6.0_spmd, %region_9.0_... | conditional | flops 152000000 | bytes 287005728 | solution.py:720
  34.7 6.1 open_more.8
  41.6 5.4 open_merge.8
  47.1 641.0 %while.274 = (s32[]{:T(128)}, s32[64]{0:T(128)S(1)}, bf16[80,64,128]{2,1,0:T(8,128)(2,1)}, bf16[80,64,128]{2,1,0:T(8,128)(2,1)}, bf16[2,80,64,128]{3,2,1,0:T(8,1...) while((s32[]{:T(128)}, s32[64]{0:T(128)S(1)}, ...), condition=%wide.region_5.0_spmd, body=%wide.region_4.0_spmd.sunk | while | flops 128000000 | bytes 224469808 | solution.py:700
  50.2 8.8 %round.24 = (s32[64]{0:T(128)}, bf16[80,64,128]{2,1,0:T(8,128)(2,1)}, bf16[80,64,128]{2,1,0:T(8,128)(2,1)}, bf16[2,80,64,128]{3,2,1,0:T(8,128)(2,1)}, bf16[2,32,...) custom-call(s32[2568]{0:T(1024)S(1)} %get-tuple-element.3684.tab, ...), custom_call_target="tpu_custom_call", output_to_operand_aliasing={{5}: (10, {}), {6}: (11, {}), {7}: (12, {}), {8}: (13, {})} | custom-call | flops 40000000 | bytes 40000000 | tf_op jit(solution)/shard_map/cond/branch_1_fun/while/body/round/pallas_call | solution.py:684
  59.0 19.7 %collective-permute-done.82.rc1 = bf16[80,64,128]{2,1,0:T(8,128)(2,1)} collective-permute-done((bf16[80,64,128]{2,1,0:T(8,128)(2,1)}, bf16[80,64,128]{2,1,0:T(8,128)(2,1)}, u32[]{:S(2)}, u32[]{:S(2)}) %collective-permute-start.82) | collective-permute-done | bytes 1310752 | tf_op jit(solution)/shard_map/cond/branch_1_fun/while/body/ppermute | solution.py:679
  80.5 6.7 collective-permute-done.85.dxr
  89.3 6.8 attend.38
  96.1 11.2 %round.25 = (s32[64]{0:T(128)}, bf16[80,64,128]{2,1,0:T(8,128)(2,1)}, bf16[80,64,128]{2,1,0:T(8,128)(2,1)}, bf16[2,80,64,128]{3,2,1,0:T(8,128)(2,1)}, bf16[2,32,...) custom-call(s32[2568]{0:T(1024)S(1)} %get-tuple-element.3684.tab, ...), custom_call_target="tpu_custom_call", output_to_operand_aliasing={{5}: (10, {}), {6}: (11, {}), {7}: (12, {}), {8}: (13, {})} | custom-call | flops 40000000 | bytes 40000000 | tf_op jit(solution)/shard_map/cond/branch_1_fun/while/body/round/pallas_call | solution.py:684
  110.0 8.4 %collective-permute-done.87 = bf16[80,64,128]{2,1,0:T(8,128)(2,1)} collective-permute-done((bf16[80,64,128]{2,1,0:T(8,128)(2,1)}, bf16[80,64,128]{2,1,0:T(8,128)(2,1)}, u32[]{:S(2)}, u32[]{:S(2)}) %collective-permute-start.87) | collective-permute-done | bytes 1310752 | tf_op jit(solution)/shard_map/cond/branch_1_fun/while/body/ppermute | solution.py:678
  122.7 10.6 %round.24 = (s32[64]{0:T(128)}, bf16[80,64,128]{2,1,0:T(8,128)(2,1)}, bf16[80,64,128]{2,1,0:T(8,128)(2,1)}, bf16[2,80,64,128]{3,2,1,0:T(8,128)(2,1)}, bf16[2,32,...) custom-call(s32[2568]{0:T(1024)S(1)} %get-tuple-element.3684.tab, ...), custom_call_target="tpu_custom_call", output_to_operand_aliasing={{5}: (10, {}), {6}: (11, {}), {7}: (12, {}), {8}: (13, {})} | custom-call | flops 40000000 | bytes 40000000 | tf_op jit(solution)/shard_map/cond/branch_1_fun/while/body/round/pallas_call | solution.py:684
  133.4 16.9 %collective-permute-done.82.rc1 = bf16[80,64,128]{2,1,0:T(8,128)(2,1)} collective-permute-done((bf16[80,64,128]{2,1,0:T(8,128)(2,1)}, bf16[80,64,128]{2,1,0:T(8,128)(2,1)}, u32[]{:S(2)}, u32[]{:S(2)}) %collective-permute-start.82) | collective-permute-done | bytes 1310752 | tf_op jit(solution)/shard_map/cond/branch_1_fun/while/body/ppermute | solution.py:679
  151.2 7.5 %collective-permute-done.85.dxr = bf16[2,32,64,128]{3,2,1,0:T(8,128)(2,1)S(1)} collective-permute-done((bf16[2,32,64,128]{3,2,1,0:T(8,128)(2,1)}, bf16[2,32,64,128]{3,2,1,0:T(8,128)(2,1)S(1)}, u32[]{:S(2)}, u32[]{:S(2)}) %collective-permute-start.85) | collective-permute-done | bytes 1048608 | tf_op jit(solution)/shard_map/cond/branch_1_fun/while/body/ppermute | solution.py:683
  160.8 5.4 attend.38
  166.2 11.4 %round.25 = (s32[64]{0:T(128)}, bf16[80,64,128]{2,1,0:T(8,128)(2,1)}, bf16[80,64,128]{2,1,0:T(8,128)(2,1)}, bf16[2,80,64,128]{3,2,1,0:T(8,128)(2,1)}, bf16[2,32,...) custom-call(s32[2568]{0:T(1024)S(1)} %get-tuple-element.3684.tab, ...), custom_call_target="tpu_custom_call", output_to_operand_aliasing={{5}: (10, {}), {6}: (11, {}), {7}: (12, {}), {8}: (13, {})} | custom-call | flops 40000000 | bytes 40000000 | tf_op jit(solution)/shard_map/cond/branch_1_fun/while/body/round/pallas_call | solution.py:684
  180.2 9.6 %collective-permute-done.87 = bf16[80,64,128]{2,1,0:T(8,128)(2,1)} collective-permute-done((bf16[80,64,128]{2,1,0:T(8,128)(2,1)}, bf16[80,64,128]{2,1,0:T(8,128)(2,1)}, u32[]{:S(2)}, u32[]{:S(2)}) %collective-permute-start.87) | collective-permute-done | bytes 1310752 | tf_op jit(solution)/shard_map/cond/branch_1_fun/while/body/ppermute | solution.py:678
  194.5 10.7 %round.24 = (s32[64]{0:T(128)}, bf16[80,64,128]{2,1,0:T(8,128)(2,1)}, bf16[80,64,128]{2,1,0:T(8,128)(2,1)}, bf16[2,80,64,128]{3,2,1,0:T(8,128)(2,1)}, bf16[2,32,...) custom-call(s32[2568]{0:T(1024)S(1)} %get-tuple-element.3684.tab, ...), custom_call_target="tpu_custom_call", output_to_operand_aliasing={{5}: (10, {}), {6}: (11, {}), {7}: (12, {}), {8}: (13, {})} | custom-call | flops 40000000 | bytes 40000000 | tf_op jit(solution)/shard_map/cond/branch_1_fun/while/body/round/pallas_call | solution.py:684
  205.1 16.8 %collective-permute-done.82.rc1 = bf16[80,64,128]{2,1,0:T(8,128)(2,1)} collective-permute-done((bf16[80,64,128]{2,1,0:T(8,128)(2,1)}, bf16[80,64,128]{2,1,0:T(8,128)(2,1)}, u32[]{:S(2)}, u32[]{:S(2)}) %collective-permute-start.82) | collective-permute-done | bytes 1310752 | tf_op jit(solution)/shard_map/cond/branch_1_fun/while/body/ppermute | solution.py:679
  222.9 7.5 %collective-permute-done.85.dxr = bf16[2,32,64,128]{3,2,1,0:T(8,128)(2,1)S(1)} collective-permute-done((bf16[2,32,64,128]{3,2,1,0:T(8,128)(2,1)}, bf16[2,32,64,128]{3,2,1,0:T(8,128)(2,1)S(1)}, u32[]{:S(2)}, u32[]{:S(2)}) %collective-permute-start.85) | collective-permute-done | bytes 1048608 | tf_op jit(solution)/shard_map/cond/branch_1_fun/while/body/ppermute | solution.py:683
  232.5 5.3 attend.38
  237.9 10.8 %round.25 = (s32[64]{0:T(128)}, bf16[80,64,128]{2,1,0:T(8,128)(2,1)}, bf16[80,64,128]{2,1,0:T(8,128)(2,1)}, bf16[2,80,64,128]{3,2,1,0:T(8,128)(2,1)}, bf16[2,32,...) custom-call(s32[2568]{0:T(1024)S(1)} %get-tuple-element.3684.tab, ...), custom_call_target="tpu_custom_call", output_to_operand_aliasing={{5}: (10, {}), {6}: (11, {}), {7}: (12, {}), {8}: (13, {})} | custom-call | flops 40000000 | bytes 40000000 | tf_op jit(solution)/shard_map/cond/branch_1_fun/while/body/round/pallas_call | solution.py:684
  251.2 10.3 %collective-permute-done.87 = bf16[80,64,128]{2,1,0:T(8,128)(2,1)} collective-permute-done((bf16[80,64,128]{2,1,0:T(8,128)(2,1)}, bf16[80,64,128]{2,1,0:T(8,128)(2,1)}, u32[]{:S(2)}, u32[]{:S(2)}) %collective-permute-start.87) | collective-permute-done | bytes 1310752 | tf_op jit(solution)/shard_map/cond/branch_1_fun/while/body/ppermute | solution.py:678
  265.0 9.9 %round.24 = (s32[64]{0:T(128)}, bf16[80,64,128]{2,1,0:T(8,128)(2,1)}, bf16[80,64,128]{2,1,0:T(8,128)(2,1)}, bf16[2,80,64,128]{3,2,1,0:T(8,128)(2,1)}, bf16[2,32,...) custom-call(s32[2568]{0:T(1024)S(1)} %get-tuple-element.3684.tab, ...), custom_call_target="tpu_custom_call", output_to_operand_aliasing={{5}: (10, {}), {6}: (11, {}), {7}: (12, {}), {8}: (13, {})} | custom-call | flops 40000000 | bytes 40000000 | tf_op jit(solution)/shard_map/cond/branch_1_fun/while/body/round/pallas_call | solution.py:684
  274.9 17.5 %collective-permute-done.82.rc1 = bf16[80,64,128]{2,1,0:T(8,128)(2,1)} collective-permute-done((bf16[80,64,128]{2,1,0:T(8,128)(2,1)}, bf16[80,64,128]{2,1,0:T(8,128)(2,1)}, u32[]{:S(2)}, u32[]{:S(2)}) %collective-permute-start.82) | collective-permute-done | bytes 1310752 | tf_op jit(solution)/shard_map/cond/branch_1_fun/while/body/ppermute | solution.py:679
  294.2 6.8 collective-permute-done.85.dxr
  308.4 10.9 %round.25 = (s32[64]{0:T(128)}, bf16[80,64,128]{2,1,0:T(8,128)(2,1)}, bf16[80,64,128]{2,1,0:T(8,128)(2,1)}, bf16[2,80,64,128]{3,2,1,0:T(8,128)(2,1)}, bf16[2,32,...) custom-call(s32[2568]{0:T(1024)S(1)} %get-tuple-element.3684.tab, ...), custom_call_target="tpu_custom_call", output_to_operand_aliasing={{5}: (10, {}), {6}: (11, {}), {7}: (12, {}), {8}: (13, {})} | custom-call | flops 40000000 | bytes 40000000 | tf_op jit(solution)/shard_map/cond/branch_1_fun/while/body/round/pallas_call | solution.py:684
  319.3 7.4 %attend.39 = (s32[64]{0:T(128)S(1)}, bf16[2048,64,128]{2,1,0:T(8,128)(2,1)}, bf16[2048,64,128]{2,1,0:T(8,128)(2,1)}, bf16[32,24,128]{2,1,0:T(8,128)(2,1)}) custom-call(s32[2568]{0:T(1024)S(1)} %get-tuple-element.3684.tab, s32[64]{0:T(128)} %get-tuple-element.3169.st_in, ...), custom_call_target="tpu_custom_call", output_to_operand_aliasing={{1}: (7, {}), {2}: (8, {}), {3}: (9, {})} | custom-call | flops 24000000 | bytes 24000000 | tf_op jit(solution)/shard_map/cond/branch_1_fun/while/body/attend/pallas_call | solution.py:667
  326.7 5.3 collective-permute-done.87
  335.5 10.1 %round.24 = (s32[64]{0:T(128)}, bf16[80,64,128]{2,1,0:T(8,128)(2,1)}, bf16[80,64,128]{2,1,0:T(8,128)(2,1)}, bf16[2,80,64,128]{3,2,1,0:T(8,128)(2,1)}, bf16[2,32,...) custom-call(s32[2568]{0:T(1024)S(1)} %get-tuple-element.3684.tab, ...), custom_call_target="tpu_custom_call", output_to_operand_aliasing={{5}: (10, {}), {6}: (11, {}), {7}: (12, {}), {8}: (13, {})} | custom-call | flops 40000000 | bytes 40000000 | tf_op jit(solution)/shard_map/cond/branch_1_fun/while/body/round/pallas_call | solution.py:684
  345.6 17.4 %collective-permute-done.82.rc1 = bf16[80,64,128]{2,1,0:T(8,128)(2,1)} collective-permute-done((bf16[80,64,128]{2,1,0:T(8,128)(2,1)}, bf16[80,64,128]{2,1,0:T(8,128)(2,1)}, u32[]{:S(2)}, u32[]{:S(2)}) %collective-permute-start.82) | collective-permute-done | bytes 1310752 | tf_op jit(solution)/shard_map/cond/branch_1_fun/while/body/ppermute | solution.py:679
  364.7 6.8 collective-permute-done.85.dxr
  373.5 7.6 %attend.38 = (s32[64]{0:T(128)}, bf16[2048,64,128]{2,1,0:T(8,128)(2,1)}, bf16[2048,64,128]{2,1,0:T(8,128)(2,1)}, bf16[32,24,128]{2,1,0:T(8,128)(2,1)}) custom-call(s32[2568]{0:T(1024)S(1)} %get-tuple-element.3684.tab, s32[64]{0:T(128)} %get-tuple-element.3157.st_in, ...), custom_call_target="tpu_custom_call", output_to_operand_aliasing={{1}: (7, {}), {2}: (8, {}), {3}: (9, {})} | custom-call | flops 24000000 | bytes 24000000 | tf_op jit(solution)/shard_map/cond/branch_1_fun/while/body/attend/pallas_call | solution.py:667
  381.1 10.7 %round.25 = (s32[64]{0:T(128)}, bf16[80,64,128]{2,1,0:T(8,128)(2,1)}, bf16[80,64,128]{2,1,0:T(8,128)(2,1)}, bf16[2,80,64,128]{3,2,1,0:T(8,128)(2,1)}, bf16[2,32,...) custom-call(s32[2568]{0:T(1024)S(1)} %get-tuple-element.3684.tab, ...), custom_call_target="tpu_custom_call", output_to_operand_aliasing={{5}: (10, {}), {6}: (11, {}), {7}: (12, {}), {8}: (13, {})} | custom-call | flops 40000000 | bytes 40000000 | tf_op jit(solution)/shard_map/cond/branch_1_fun/while/body/round/pallas_call | solution.py:684
  391.9 6.7 attend.39
  406.7 9.2 %round.24 = (s32[64]{0:T(128)}, bf16[80,64,128]{2,1,0:T(8,128)(2,1)}, bf16[80,64,128]{2,1,0:T(8,128)(2,1)}, bf16[2,80,64,128]{3,2,1,0:T(8,128)(2,1)}, bf16[2,32,...) custom-call(s32[2568]{0:T(1024)S(1)} %get-tuple-element.3684.tab, ...), custom_call_target="tpu_custom_call", output_to_operand_aliasing={{5}: (10, {}), {6}: (11, {}), {7}: (12, {}), {8}: (13, {})} | custom-call | flops 40000000 | bytes 40000000 | tf_op jit(solution)/shard_map/cond/branch_1_fun/while/body/round/pallas_call | solution.py:684
  415.9 18.3 %collective-permute-done.82.rc1 = bf16[80,64,128]{2,1,0:T(8,128)(2,1)} collective-permute-done((bf16[80,64,128]{2,1,0:T(8,128)(2,1)}, bf16[80,64,128]{2,1,0:T(8,128)(2,1)}, u32[]{:S(2)}, u32[]{:S(2)}) %collective-permute-start.82) | collective-permute-done | bytes 1310752 | tf_op jit(solution)/shard_map/cond/branch_1_fun/while/body/ppermute | solution.py:679
  435.2 7.4 %collective-permute-done.85.dxr = bf16[2,32,64,128]{3,2,1,0:T(8,128)(2,1)S(1)} collective-permute-done((bf16[2,32,64,128]{3,2,1,0:T(8,128)(2,1)}, bf16[2,32,64,128]{3,2,1,0:T(8,128)(2,1)S(1)}, u32[]{:S(2)}, u32[]{:S(2)}) %collective-permute-start.85) | collective-permute-done | bytes 1048608 | tf_op jit(solution)/shard_map/cond/branch_1_fun/while/body/ppermute | solution.py:683
  444.7 6.3 attend.38
  451.0 9.9 %round.25 = (s32[64]{0:T(128)}, bf16[80,64,128]{2,1,0:T(8,128)(2,1)}, bf16[80,64,128]{2,1,0:T(8,128)(2,1)}, bf16[2,80,64,128]{3,2,1,0:T(8,128)(2,1)}, bf16[2,32,...) custom-call(s32[2568]{0:T(1024)S(1)} %get-tuple-element.3684.tab, ...), custom_call_target="tpu_custom_call", output_to_operand_aliasing={{5}: (10, {}), {6}: (11, {}), {7}: (12, {}), {8}: (13, {})} | custom-call | flops 40000000 | bytes 40000000 | tf_op jit(solution)/shard_map/cond/branch_1_fun/while/body/round/pallas_call | solution.py:684
  461.0 5.9 attend.39
  466.9 6.9 collective-permute-done.87
  478.4 9.5 %round.24 = (s32[64]{0:T(128)}, bf16[80,64,128]{2,1,0:T(8,128)(2,1)}, bf16[80,64,128]{2,1,0:T(8,128)(2,1)}, bf16[2,80,64,128]{3,2,1,0:T(8,128)(2,1)}, bf16[2,32,...) custom-call(s32[2568]{0:T(1024)S(1)} %get-tuple-element.3684.tab, ...), custom_call_target="tpu_custom_call", output_to_operand_aliasing={{5}: (10, {}), {6}: (11, {}), {7}: (12, {}), {8}: (13, {})} | custom-call | flops 40000000 | bytes 40000000 | tf_op jit(solution)/shard_map/cond/branch_1_fun/while/body/round/pallas_call | solution.py:684
  487.9 18.0 %collective-permute-done.82.rc1 = bf16[80,64,128]{2,1,0:T(8,128)(2,1)} collective-permute-done((bf16[80,64,128]{2,1,0:T(8,128)(2,1)}, bf16[80,64,128]{2,1,0:T(8,128)(2,1)}, u32[]{:S(2)}, u32[]{:S(2)}) %collective-permute-start.82) | collective-permute-done | bytes 1310752 | tf_op jit(solution)/shard_map/cond/branch_1_fun/while/body/ppermute | solution.py:679
  506.9 7.5 %collective-permute-done.85.dxr = bf16[2,32,64,128]{3,2,1,0:T(8,128)(2,1)S(1)} collective-permute-done((bf16[2,32,64,128]{3,2,1,0:T(8,128)(2,1)}, bf16[2,32,64,128]{3,2,1,0:T(8,128)(2,1)S(1)}, u32[]{:S(2)}, u32[]{:S(2)}) %collective-permute-start.85) | collective-permute-done | bytes 1048608 | tf_op jit(solution)/shard_map/cond/branch_1_fun/while/body/ppermute | solution.py:683
  516.4 7.6 %attend.38 = (s32[64]{0:T(128)}, bf16[2048,64,128]{2,1,0:T(8,128)(2,1)}, bf16[2048,64,128]{2,1,0:T(8,128)(2,1)}, bf16[32,24,128]{2,1,0:T(8,128)(2,1)}) custom-call(s32[2568]{0:T(1024)S(1)} %get-tuple-element.3684.tab, s32[64]{0:T(128)} %get-tuple-element.3157.st_in, ...), custom_call_target="tpu_custom_call", output_to_operand_aliasing={{1}: (7, {}), {2}: (8, {}), {3}: (9, {})} | custom-call | flops 24000000 | bytes 24000000 | tf_op jit(solution)/shard_map/cond/branch_1_fun/while/body/attend/pallas_call | solution.py:667
  524.0 10.2 %round.25 = (s32[64]{0:T(128)}, bf16[80,64,128]{2,1,0:T(8,128)(2,1)}, bf16[80,64,128]{2,1,0:T(8,128)(2,1)}, bf16[2,80,64,128]{3,2,1,0:T(8,128)(2,1)}, bf16[2,32,...) custom-call(s32[2568]{0:T(1024)S(1)} %get-tuple-element.3684.tab, ...), custom_call_target="tpu_custom_call", output_to_operand_aliasing={{5}: (10, {}), {6}: (11, {}), {7}: (12, {}), {8}: (13, {})} | custom-call | flops 40000000 | bytes 40000000 | tf_op jit(solution)/shard_map/cond/branch_1_fun/while/body/round/pallas_call | solution.py:684
  534.2 5.5 attend.39
  539.8 5.7 collective-permute-done.87
  548.9 9.2 %round.24 = (s32[64]{0:T(128)}, bf16[80,64,128]{2,1,0:T(8,128)(2,1)}, bf16[80,64,128]{2,1,0:T(8,128)(2,1)}, bf16[2,80,64,128]{3,2,1,0:T(8,128)(2,1)}, bf16[2,32,...) custom-call(s32[2568]{0:T(1024)S(1)} %get-tuple-element.3684.tab, ...), custom_call_target="tpu_custom_call", output_to_operand_aliasing={{5}: (10, {}), {6}: (11, {}), {7}: (12, {}), {8}: (13, {})} | custom-call | flops 40000000 | bytes 40000000 | tf_op jit(solution)/shard_map/cond/branch_1_fun/while/body/round/pallas_call | solution.py:684
  558.1 18.3 %collective-permute-done.82.rc1 = bf16[80,64,128]{2,1,0:T(8,128)(2,1)} collective-permute-done((bf16[80,64,128]{2,1,0:T(8,128)(2,1)}, bf16[80,64,128]{2,1,0:T(8,128)(2,1)}, u32[]{:S(2)}, u32[]{:S(2)}) %collective-permute-start.82) | collective-permute-done | bytes 1310752 | tf_op jit(solution)/shard_map/cond/branch_1_fun/while/body/ppermute | solution.py:679
  578.1 6.8 collective-permute-done.85.dxr
  586.9 7.3 %attend.38 = (s32[64]{0:T(128)}, bf16[2048,64,128]{2,1,0:T(8,128)(2,1)}, bf16[2048,64,128]{2,1,0:T(8,128)(2,1)}, bf16[32,24,128]{2,1,0:T(8,128)(2,1)}) custom-call(s32[2568]{0:T(1024)S(1)} %get-tuple-element.3684.tab, s32[64]{0:T(128)} %get-tuple-element.3157.st_in, ...), custom_call_target="tpu_custom_call", output_to_operand_aliasing={{1}: (7, {}), {2}: (8, {}), {3}: (9, {})} | custom-call | flops 24000000 | bytes 24000000 | tf_op jit(solution)/shard_map/cond/branch_1_fun/while/body/attend/pallas_call | solution.py:667
  594.2 10.4 %round.25 = (s32[64]{0:T(128)}, bf16[80,64,128]{2,1,0:T(8,128)(2,1)}, bf16[80,64,128]{2,1,0:T(8,128)(2,1)}, bf16[2,80,64,128]{3,2,1,0:T(8,128)(2,1)}, bf16[2,32,...) custom-call(s32[2568]{0:T(1024)S(1)} %get-tuple-element.3684.tab, ...), custom_call_target="tpu_custom_call", output_to_operand_aliasing={{5}: (10, {}), {6}: (11, {}), {7}: (12, {}), {8}: (13, {})} | custom-call | flops 40000000 | bytes 40000000 | tf_op jit(solution)/shard_map/cond/branch_1_fun/while/body/round/pallas_call | solution.py:684
  604.7 6.5 attend.39
  619.4 9.4 %round.24 = (s32[64]{0:T(128)}, bf16[80,64,128]{2,1,0:T(8,128)(2,1)}, bf16[80,64,128]{2,1,0:T(8,128)(2,1)}, bf16[2,80,64,128]{3,2,1,0:T(8,128)(2,1)}, bf16[2,32,...) custom-call(s32[2568]{0:T(1024)S(1)} %get-tuple-element.3684.tab, ...), custom_call_target="tpu_custom_call", output_to_operand_aliasing={{5}: (10, {}), {6}: (11, {}), {7}: (12, {}), {8}: (13, {})} | custom-call | flops 40000000 | bytes 40000000 | tf_op jit(solution)/shard_map/cond/branch_1_fun/while/body/round/pallas_call | solution.py:684
  628.8 18.0 %collective-permute-done.82.rc1 = bf16[80,64,128]{2,1,0:T(8,128)(2,1)} collective-permute-done((bf16[80,64,128]{2,1,0:T(8,128)(2,1)}, bf16[80,64,128]{2,1,0:T(8,128)(2,1)}, u32[]{:S(2)}, u32[]{:S(2)}) %collective-permute-start.82) | collective-permute-done | bytes 1310752 | tf_op jit(solution)/shard_map/cond/branch_1_fun/while/body/ppermute | solution.py:679
  648.6 6.8 collective-permute-done.85.dxr
  657.5 6.3 attend.38
  663.8 9.0 %round.25 = (s32[64]{0:T(128)}, bf16[80,64,128]{2,1,0:T(8,128)(2,1)}, bf16[80,64,128]{2,1,0:T(8,128)(2,1)}, bf16[2,80,64,128]{3,2,1,0:T(8,128)(2,1)}, bf16[2,32,...) custom-call(s32[2568]{0:T(1024)S(1)} %get-tuple-element.3684.tab, ...), custom_call_target="tpu_custom_call", output_to_operand_aliasing={{5}: (10, {}), {6}: (11, {}), {7}: (12, {}), {8}: (13, {})} | custom-call | flops 40000000 | bytes 40000000 | tf_op jit(solution)/shard_map/cond/branch_1_fun/while/body/round/pallas_call | solution.py:684
  672.8 6.5 attend.39
  679.3 7.2 %collective-permute-done.87 = bf16[80,64,128]{2,1,0:T(8,128)(2,1)} collective-permute-done((bf16[80,64,128]{2,1,0:T(8,128)(2,1)}, bf16[80,64,128]{2,1,0:T(8,128)(2,1)}, u32[]{:S(2)}, u32[]{:S(2)}) %collective-permute-start.87) | collective-permute-done | bytes 1310752 | tf_op jit(solution)/shard_map/cond/branch_1_fun/while/body/ppermute | solution.py:678
  696.1 10.3 %attend.22 = (s32[64]{0:T(128)}, bf16[2048,64,128]{2,1,0:T(8,128)(2,1)}, bf16[2048,64,128]{2,1,0:T(8,128)(2,1)}, bf16[32,24,128]{2,1,0:T(8,128)(2,1)}) custom-call(s32[2568]{0:T(1024)S(1)} %get-tuple-element.3809, s32[64]{0:T(128)} %get-tuple-element.947.st_in, ...), custom_call_target="tpu_custom_call", output_to_operand_aliasing={{1}: (7, {}), {2}: (8, {}), {3}: (9, {})} | custom-call | flops 24000000 | bytes 24000000 | tf_op jit(solution)/shard_map/cond/branch_1_fun/attend/pallas_call | solution.py:667
  (306 shorter events, 97.7 us)
Async XLA Ops:
  47.6 31.1 %collective-permute-start.82 = (bf16[80,64,128]{2,1,0:T(8,128)(2,1)}, bf16[80,64,128]{2,1,0:T(8,128)(2,1)}, u32[]{:S(2)}, u32[]{:S(2)}) collective-permute-start(bf16[80,64,128]{2,1,0:T(8,128)(2,1)} %get-tuple-element.3644), channel_id=1, source_target_pairs={{2,0},{3,1},{6,2},{7,3},{4,6},{5,7},{0,4},{1,5}} | collective-permute-start | bytes 3932168 | tf_op jit(solution)/shard_map/cond/branch_1_fun/while/body/ppermute | solution.py:679
  49.3 30.7 %collective-permute-start.81 = (bf16[80,64,128]{2,1,0:T(8,128)(2,1)}, bf16[80,64,128]{2,1,0:T(8,128)(2,1)}, u32[]{:S(2)}, u32[]{:S(2)}) collective-permute-start(bf16[80,64,128]{2,1,0:T(8,128)(2,1)} %get-tuple-element.3643), channel_id=1, source_target_pairs={{0,2},{1,3},{2,6},{3,7},{6,4},{7,5},{4,0},{5,1}} | collective-permute-start | bytes 3932168 | tf_op jit(solution)/shard_map/cond/branch_1_fun/while/body/ppermute | solution.py:678
  49.7 30.3 %collective-permute-start.84 = (bf16[80,64,128]{2,1,0:T(8,128)(2,1)}, bf16[80,64,128]{2,1,0:T(8,128)(2,1)}, u32[]{:S(2)}, u32[]{:S(2)}) collective-permute-start(bf16[80,64,128]{2,1,0:T(8,128)(2,1)} %get-tuple-element.3649.rc1), channel_id=1, source_target_pairs={{0,1},{1,0},{2,3},{3,2},{4,5},{5,4},{6,7},{7,6}} | collective-permute-start | bytes 3932168 | tf_op jit(solution)/shard_map/cond/branch_1_fun/while/body/ppermute | solution.py:682
  49.7 30.8 %collective-permute-start.83 = (bf16[80,64,128]{2,1,0:T(8,128)(2,1)}, bf16[80,64,128]{2,1,0:T(8,128)(2,1)}, u32[]{:S(2)}, u32[]{:S(2)}) collective-permute-start(bf16[80,64,128]{2,1,0:T(8,128)(2,1)} %get-tuple-element.3648.rc0), channel_id=1, source_target_pairs={{0,1},{1,0},{2,3},{3,2},{4,5},{5,4},{6,7},{7,6}} | collective-permute-start | bytes 3932168 | tf_op jit(solution)/shard_map/cond/branch_1_fun/while/body/ppermute | solution.py:681
  50.2 45.9 %collective-permute-start.80 = (bf16[2,80,64,128]{3,2,1,0:T(8,128)(2,1)}, bf16[2,80,64,128]{3,2,1,0:T(8,128)(2,1)}, u32[]{:S(2)}, u32[]{:S(2)}) collective-permute-start(bf16[2,80,64,128]{3,2,1,0:T(8,128)(2,1)} %get-tuple-element.3645), channel_id=1, source_target_pairs={{0,1},{1,0},{2,3},{3,2},{4,5},{5,4},{6,7},{7,6}} | collective-permute-start | bytes 7864328 | tf_op jit(solution)/shard_map/cond/branch_1_fun/while/body/ppermute | solution.py:680
  80.0 39.6 %collective-permute-start.86 = (bf16[2,80,64,128]{3,2,1,0:T(8,128)(2,1)}, bf16[2,80,64,128]{3,2,1,0:T(8,128)(2,1)}, u32[]{:S(2)}, u32[]{:S(2)}) collective-permute-start(bf16[2,80,64,128]{3,2,1,0:T(8,128)(2,1)} %get-tuple-element.3178), channel_id=1, source_target_pairs={{0,1},{1,0},{2,3},{3,2},{4,5},{5,4},{6,7},{7,6}} | collective-permute-start | bytes 7864328 | tf_op jit(solution)/shard_map/cond/branch_1_fun/while/body/ppermute | solution.py:680
  87.2 31.1 %collective-permute-start.87 = (bf16[80,64,128]{2,1,0:T(8,128)(2,1)}, bf16[80,64,128]{2,1,0:T(8,128)(2,1)}, u32[]{:S(2)}, u32[]{:S(2)}) collective-permute-start(bf16[80,64,128]{2,1,0:T(8,128)(2,1)} %get-tuple-element.3179), channel_id=1, source_target_pairs={{0,2},{1,3},{2,6},{3,7},{6,4},{7,5},{4,0},{5,1}} | collective-permute-start | bytes 3932168 | tf_op jit(solution)/shard_map/cond/branch_1_fun/while/body/ppermute | solution.py:678
  88.7 30.9 %collective-permute-start.88 = (bf16[80,64,128]{2,1,0:T(8,128)(2,1)}, bf16[80,64,128]{2,1,0:T(8,128)(2,1)}, u32[]{:S(2)}, u32[]{:S(2)}) collective-permute-start(bf16[80,64,128]{2,1,0:T(8,128)(2,1)} %get-tuple-element.3180), channel_id=1, source_target_pairs={{2,0},{3,1},{6,2},{7,3},{4,6},{5,7},{0,4},{1,5}} | collective-permute-start | bytes 3932168 | tf_op jit(solution)/shard_map/cond/branch_1_fun/while/body/ppermute | solution.py:679
  120.2 30.0 %collective-permute-start.82 = (bf16[80,64,128]{2,1,0:T(8,128)(2,1)}, bf16[80,64,128]{2,1,0:T(8,128)(2,1)}, u32[]{:S(2)}, u32[]{:S(2)}) collective-permute-start(bf16[80,64,128]{2,1,0:T(8,128)(2,1)} %get-tuple-element.3644), channel_id=1, source_target_pairs={{2,0},{3,1},{6,2},{7,3},{4,6},{5,7},{0,4},{1,5}} | collective-permute-start | bytes 3932168 | tf_op jit(solution)/shard_map/cond/branch_1_fun/while/body/ppermute | solution.py:679
  120.7 30.0 %collective-permute-start.81 = (bf16[80,64,128]{2,1,0:T(8,128)(2,1)}, bf16[80,64,128]{2,1,0:T(8,128)(2,1)}, u32[]{:S(2)}, u32[]{:S(2)}) collective-permute-start(bf16[80,64,128]{2,1,0:T(8,128)(2,1)} %get-tuple-element.3643), channel_id=1, source_target_pairs={{0,2},{1,3},{2,6},{3,7},{6,4},{7,5},{4,0},{5,1}} | collective-permute-start | bytes 3932168 | tf_op jit(solution)/shard_map/cond/branch_1_fun/while/body/ppermute | solution.py:678
  122.7 43.5 %collective-permute-start.80 = (bf16[2,80,64,128]{3,2,1,0:T(8,128)(2,1)}, bf16[2,80,64,128]{3,2,1,0:T(8,128)(2,1)}, u32[]{:S(2)}, u32[]{:S(2)}) collective-permute-start(bf16[2,80,64,128]{3,2,1,0:T(8,128)(2,1)} %get-tuple-element.3645), channel_id=1, source_target_pairs={{0,1},{1,0},{2,3},{3,2},{4,5},{5,4},{6,7},{7,6}} | collective-permute-start | bytes 7864328 | tf_op jit(solution)/shard_map/cond/branch_1_fun/while/body/ppermute | solution.py:680
  150.7 40.6 %collective-permute-start.86 = (bf16[2,80,64,128]{3,2,1,0:T(8,128)(2,1)}, bf16[2,80,64,128]{3,2,1,0:T(8,128)(2,1)}, u32[]{:S(2)}, u32[]{:S(2)}) collective-permute-start(bf16[2,80,64,128]{3,2,1,0:T(8,128)(2,1)} %get-tuple-element.3178), channel_id=1, source_target_pairs={{0,1},{1,0},{2,3},{3,2},{4,5},{5,4},{6,7},{7,6}} | collective-permute-start | bytes 7864328 | tf_op jit(solution)/shard_map/cond/branch_1_fun/while/body/ppermute | solution.py:680
  158.7 31.1 %collective-permute-start.87 = (bf16[80,64,128]{2,1,0:T(8,128)(2,1)}, bf16[80,64,128]{2,1,0:T(8,128)(2,1)}, u32[]{:S(2)}, u32[]{:S(2)}) collective-permute-start(bf16[80,64,128]{2,1,0:T(8,128)(2,1)} %get-tuple-element.3179), channel_id=1, source_target_pairs={{0,2},{1,3},{2,6},{3,7},{6,4},{7,5},{4,0},{5,1}} | collective-permute-start | bytes 3932168 | tf_op jit(solution)/shard_map/cond/branch_1_fun/while/body/ppermute | solution.py:678
  160.5 30.9 %collective-permute-start.88 = (bf16[80,64,128]{2,1,0:T(8,128)(2,1)}, bf16[80,64,128]{2,1,0:T(8,128)(2,1)}, u32[]{:S(2)}, u32[]{:S(2)}) collective-permute-start(bf16[80,64,128]{2,1,0:T(8,128)(2,1)} %get-tuple-element.3180), channel_id=1, source_target_pairs={{2,0},{3,1},{6,2},{7,3},{4,6},{5,7},{0,4},{1,5}} | collective-permute-start | bytes 3932168 | tf_op jit(solution)/shard_map/cond/branch_1_fun/while/body/ppermute | solution.py:679
  191.9 30.0 %collective-permute-start.82 = (bf16[80,64,128]{2,1,0:T(8,128)(2,1)}, bf16[80,64,128]{2,1,0:T(8,128)(2,1)}, u32[]{:S(2)}, u32[]{:S(2)}) collective-permute-start(bf16[80,64,128]{2,1,0:T(8,128)(2,1)} %get-tuple-element.3644), channel_id=1, source_target_pairs={{2,0},{3,1},{6,2},{7,3},{4,6},{5,7},{0,4},{1,5}} | collective-permute-start | bytes 3932168 | tf_op jit(solution)/shard_map/cond/branch_1_fun/while/body/ppermute | solution.py:679
  192.2 29.8 %collective-permute-start.81 = (bf16[80,64,128]{2,1,0:T(8,128)(2,1)}, bf16[80,64,128]{2,1,0:T(8,128)(2,1)}, u32[]{:S(2)}, u32[]{:S(2)}) collective-permute-start(bf16[80,64,128]{2,1,0:T(8,128)(2,1)} %get-tuple-element.3643), channel_id=1, source_target_pairs={{0,2},{1,3},{2,6},{3,7},{6,4},{7,5},{4,0},{5,1}} | collective-permute-start | bytes 3932168 | tf_op jit(solution)/shard_map/cond/branch_1_fun/while/body/ppermute | solution.py:678
  194.5 43.4 %collective-permute-start.80 = (bf16[2,80,64,128]{3,2,1,0:T(8,128)(2,1)}, bf16[2,80,64,128]{3,2,1,0:T(8,128)(2,1)}, u32[]{:S(2)}, u32[]{:S(2)}) collective-permute-start(bf16[2,80,64,128]{3,2,1,0:T(8,128)(2,1)} %get-tuple-element.3645), channel_id=1, source_target_pairs={{0,1},{1,0},{2,3},{3,2},{4,5},{5,4},{6,7},{7,6}} | collective-permute-start | bytes 7864328 | tf_op jit(solution)/shard_map/cond/branch_1_fun/while/body/ppermute | solution.py:680
  222.0 39.9 %collective-permute-start.86 = (bf16[2,80,64,128]{3,2,1,0:T(8,128)(2,1)}, bf16[2,80,64,128]{3,2,1,0:T(8,128)(2,1)}, u32[]{:S(2)}, u32[]{:S(2)}) collective-permute-start(bf16[2,80,64,128]{3,2,1,0:T(8,128)(2,1)} %get-tuple-element.3178), channel_id=1, source_target_pairs={{0,1},{1,0},{2,3},{3,2},{4,5},{5,4},{6,7},{7,6}} | collective-permute-start | bytes 7864328 | tf_op jit(solution)/shard_map/cond/branch_1_fun/while/body/ppermute | solution.py:680
  230.4 31.1 %collective-permute-start.87 = (bf16[80,64,128]{2,1,0:T(8,128)(2,1)}, bf16[80,64,128]{2,1,0:T(8,128)(2,1)}, u32[]{:S(2)}, u32[]{:S(2)}) collective-permute-start(bf16[80,64,128]{2,1,0:T(8,128)(2,1)} %get-tuple-element.3179), channel_id=1, source_target_pairs={{0,2},{1,3},{2,6},{3,7},{6,4},{7,5},{4,0},{5,1}} | collective-permute-start | bytes 3932168 | tf_op jit(solution)/shard_map/cond/branch_1_fun/while/body/ppermute | solution.py:678
  231.0 30.9 %collective-permute-start.88 = (bf16[80,64,128]{2,1,0:T(8,128)(2,1)}, bf16[80,64,128]{2,1,0:T(8,128)(2,1)}, u32[]{:S(2)}, u32[]{:S(2)}) collective-permute-start(bf16[80,64,128]{2,1,0:T(8,128)(2,1)} %get-tuple-element.3180), channel_id=1, source_target_pairs={{2,0},{3,1},{6,2},{7,3},{4,6},{5,7},{0,4},{1,5}} | collective-permute-start | bytes 3932168 | tf_op jit(solution)/shard_map/cond/branch_1_fun/while/body/ppermute | solution.py:679
  262.4 30.0 %collective-permute-start.82 = (bf16[80,64,128]{2,1,0:T(8,128)(2,1)}, bf16[80,64,128]{2,1,0:T(8,128)(2,1)}, u32[]{:S(2)}, u32[]{:S(2)}) collective-permute-start(bf16[80,64,128]{2,1,0:T(8,128)(2,1)} %get-tuple-element.3644), channel_id=1, source_target_pairs={{2,0},{3,1},{6,2},{7,3},{4,6},{5,7},{0,4},{1,5}} | collective-permute-start | bytes 3932168 | tf_op jit(solution)/shard_map/cond/branch_1_fun/while/body/ppermute | solution.py:679
  263.9 29.7 %collective-permute-start.81 = (bf16[80,64,128]{2,1,0:T(8,128)(2,1)}, bf16[80,64,128]{2,1,0:T(8,128)(2,1)}, u32[]{:S(2)}, u32[]{:S(2)}) collective-permute-start(bf16[80,64,128]{2,1,0:T(8,128)(2,1)} %get-tuple-element.3643), channel_id=1, source_target_pairs={{0,2},{1,3},{2,6},{3,7},{6,4},{7,5},{4,0},{5,1}} | collective-permute-start | bytes 3932168 | tf_op jit(solution)/shard_map/cond/branch_1_fun/while/body/ppermute | solution.py:678
  264.5 29.2 %collective-permute-start.84 = (bf16[80,64,128]{2,1,0:T(8,128)(2,1)}, bf16[80,64,128]{2,1,0:T(8,128)(2,1)}, u32[]{:S(2)}, u32[]{:S(2)}) collective-permute-start(bf16[80,64,128]{2,1,0:T(8,128)(2,1)} %get-tuple-element.3649.rc1), channel_id=1, source_target_pairs={{0,1},{1,0},{2,3},{3,2},{4,5},{5,4},{6,7},{7,6}} | collective-permute-start | bytes 3932168 | tf_op jit(solution)/shard_map/cond/branch_1_fun/while/body/ppermute | solution.py:682
  264.5 29.7 %collective-permute-start.83 = (bf16[80,64,128]{2,1,0:T(8,128)(2,1)}, bf16[80,64,128]{2,1,0:T(8,128)(2,1)}, u32[]{:S(2)}, u32[]{:S(2)}) collective-permute-start(bf16[80,64,128]{2,1,0:T(8,128)(2,1)} %get-tuple-element.3648.rc0), channel_id=1, source_target_pairs={{0,1},{1,0},{2,3},{3,2},{4,5},{5,4},{6,7},{7,6}} | collective-permute-start | bytes 3932168 | tf_op jit(solution)/shard_map/cond/branch_1_fun/while/body/ppermute | solution.py:681
  265.0 43.4 %collective-permute-start.80 = (bf16[2,80,64,128]{3,2,1,0:T(8,128)(2,1)}, bf16[2,80,64,128]{3,2,1,0:T(8,128)(2,1)}, u32[]{:S(2)}, u32[]{:S(2)}) collective-permute-start(bf16[2,80,64,128]{3,2,1,0:T(8,128)(2,1)} %get-tuple-element.3645), channel_id=1, source_target_pairs={{0,1},{1,0},{2,3},{3,2},{4,5},{5,4},{6,7},{7,6}} | collective-permute-start | bytes 7864328 | tf_op jit(solution)/shard_map/cond/branch_1_fun/while/body/ppermute | solution.py:680
  293.6 38.7 %collective-permute-start.86 = (bf16[2,80,64,128]{3,2,1,0:T(8,128)(2,1)}, bf16[2,80,64,128]{3,2,1,0:T(8,128)(2,1)}, u32[]{:S(2)}, u32[]{:S(2)}) collective-permute-start(bf16[2,80,64,128]{3,2,1,0:T(8,128)(2,1)} %get-tuple-element.3178), channel_id=1, source_target_pairs={{0,1},{1,0},{2,3},{3,2},{4,5},{5,4},{6,7},{7,6}} | collective-permute-start | bytes 7864328 | tf_op jit(solution)/shard_map/cond/branch_1_fun/while/body/ppermute | solution.py:680
  300.9 31.1 %collective-permute-start.87 = (bf16[80,64,128]{2,1,0:T(8,128)(2,1)}, bf16[80,64,128]{2,1,0:T(8,128)(2,1)}, u32[]{:S(2)}, u32[]{:S(2)}) collective-permute-start(bf16[80,64,128]{2,1,0:T(8,128)(2,1)} %get-tuple-element.3179), channel_id=1, source_target_pairs={{0,2},{1,3},{2,6},{3,7},{6,4},{7,5},{4,0},{5,1}} | collective-permute-start | bytes 3932168 | tf_op jit(solution)/shard_map/cond/branch_1_fun/while/body/ppermute | solution.py:678
  301.5 30.9 %collective-permute-start.88 = (bf16[80,64,128]{2,1,0:T(8,128)(2,1)}, bf16[80,64,128]{2,1,0:T(8,128)(2,1)}, u32[]{:S(2)}, u32[]{:S(2)}) collective-permute-start(bf16[80,64,128]{2,1,0:T(8,128)(2,1)} %get-tuple-element.3180), channel_id=1, source_target_pairs={{2,0},{3,1},{6,2},{7,3},{4,6},{5,7},{0,4},{1,5}} | collective-permute-start | bytes 3932168 | tf_op jit(solution)/shard_map/cond/branch_1_fun/while/body/ppermute | solution.py:679
  332.9 30.0 %collective-permute-start.82 = (bf16[80,64,128]{2,1,0:T(8,128)(2,1)}, bf16[80,64,128]{2,1,0:T(8,128)(2,1)}, u32[]{:S(2)}, u32[]{:S(2)}) collective-permute-start(bf16[80,64,128]{2,1,0:T(8,128)(2,1)} %get-tuple-element.3644), channel_id=1, source_target_pairs={{2,0},{3,1},{6,2},{7,3},{4,6},{5,7},{0,4},{1,5}} | collective-permute-start | bytes 3932168 | tf_op jit(solution)/shard_map/cond/branch_1_fun/while/body/ppermute | solution.py:679
  334.4 29.7 %collective-permute-start.81 = (bf16[80,64,128]{2,1,0:T(8,128)(2,1)}, bf16[80,64,128]{2,1,0:T(8,128)(2,1)}, u32[]{:S(2)}, u32[]{:S(2)}) collective-permute-start(bf16[80,64,128]{2,1,0:T(8,128)(2,1)} %get-tuple-element.3643), channel_id=1, source_target_pairs={{0,2},{1,3},{2,6},{3,7},{6,4},{7,5},{4,0},{5,1}} | collective-permute-start | bytes 3932168 | tf_op jit(solution)/shard_map/cond/branch_1_fun/while/body/ppermute | solution.py:678
  335.0 29.2 %collective-permute-start.84 = (bf16[80,64,128]{2,1,0:T(8,128)(2,1)}, bf16[80,64,128]{2,1,0:T(8,128)(2,1)}, u32[]{:S(2)}, u32[]{:S(2)}) collective-permute-start(bf16[80,64,128]{2,1,0:T(8,128)(2,1)} %get-tuple-element.3649.rc1), channel_id=1, source_target_pairs={{0,1},{1,0},{2,3},{3,2},{4,5},{5,4},{6,7},{7,6}} | collective-permute-start | bytes 3932168 | tf_op jit(solution)/shard_map/cond/branch_1_fun/while/body/ppermute | solution.py:682
  335.0 29.7 %collective-permute-start.83 = (bf16[80,64,128]{2,1,0:T(8,128)(2,1)}, bf16[80,64,128]{2,1,0:T(8,128)(2,1)}, u32[]{:S(2)}, u32[]{:S(2)}) collective-permute-start(bf16[80,64,128]{2,1,0:T(8,128)(2,1)} %get-tuple-element.3648.rc0), channel_id=1, source_target_pairs={{0,1},{1,0},{2,3},{3,2},{4,5},{5,4},{6,7},{7,6}} | collective-permute-start | bytes 3932168 | tf_op jit(solution)/shard_map/cond/branch_1_fun/while/body/ppermute | solution.py:681
  335.5 45.6 %collective-permute-start.80 = (bf16[2,80,64,128]{3,2,1,0:T(8,128)(2,1)}, bf16[2,80,64,128]{3,2,1,0:T(8,128)(2,1)}, u32[]{:S(2)}, u32[]{:S(2)}) collective-permute-start(bf16[2,80,64,128]{3,2,1,0:T(8,128)(2,1)} %get-tuple-element.3645), channel_id=1, source_target_pairs={{0,1},{1,0},{2,3},{3,2},{4,5},{5,4},{6,7},{7,6}} | collective-permute-start | bytes 7864328 | tf_op jit(solution)/shard_map/cond/branch_1_fun/while/body/ppermute | solution.py:680
  364.2 39.4 %collective-permute-start.86 = (bf16[2,80,64,128]{3,2,1,0:T(8,128)(2,1)}, bf16[2,80,64,128]{3,2,1,0:T(8,128)(2,1)}, u32[]{:S(2)}, u32[]{:S(2)}) collective-permute-start(bf16[2,80,64,128]{3,2,1,0:T(8,128)(2,1)} %get-tuple-element.3178), channel_id=1, source_target_pairs={{0,1},{1,0},{2,3},{3,2},{4,5},{5,4},{6,7},{7,6}} | collective-permute-start | bytes 7864328 | tf_op jit(solution)/shard_map/cond/branch_1_fun/while/body/ppermute | solution.py:680
  371.5 31.1 %collective-permute-start.87 = (bf16[80,64,128]{2,1,0:T(8,128)(2,1)}, bf16[80,64,128]{2,1,0:T(8,128)(2,1)}, u32[]{:S(2)}, u32[]{:S(2)}) collective-permute-start(bf16[80,64,128]{2,1,0:T(8,128)(2,1)} %get-tuple-element.3179), channel_id=1, source_target_pairs={{0,2},{1,3},{2,6},{3,7},{6,4},{7,5},{4,0},{5,1}} | collective-permute-start | bytes 3932168 | tf_op jit(solution)/shard_map/cond/branch_1_fun/while/body/ppermute | solution.py:678
  372.7 30.9 %collective-permute-start.88 = (bf16[80,64,128]{2,1,0:T(8,128)(2,1)}, bf16[80,64,128]{2,1,0:T(8,128)(2,1)}, u32[]{:S(2)}, u32[]{:S(2)}) collective-permute-start(bf16[80,64,128]{2,1,0:T(8,128)(2,1)} %get-tuple-element.3180), channel_id=1, source_target_pairs={{2,0},{3,1},{6,2},{7,3},{4,6},{5,7},{0,4},{1,5}} | collective-permute-start | bytes 3932168 | tf_op jit(solution)/shard_map/cond/branch_1_fun/while/body/ppermute | solution.py:679
  404.1 30.0 %collective-permute-start.82 = (bf16[80,64,128]{2,1,0:T(8,128)(2,1)}, bf16[80,64,128]{2,1,0:T(8,128)(2,1)}, u32[]{:S(2)}, u32[]{:S(2)}) collective-permute-start(bf16[80,64,128]{2,1,0:T(8,128)(2,1)} %get-tuple-element.3644), channel_id=1, source_target_pairs={{2,0},{3,1},{6,2},{7,3},{4,6},{5,7},{0,4},{1,5}} | collective-permute-start | bytes 3932168 | tf_op jit(solution)/shard_map/cond/branch_1_fun/while/body/ppermute | solution.py:679
  405.0 29.7 %collective-permute-start.81 = (bf16[80,64,128]{2,1,0:T(8,128)(2,1)}, bf16[80,64,128]{2,1,0:T(8,128)(2,1)}, u32[]{:S(2)}, u32[]{:S(2)}) collective-permute-start(bf16[80,64,128]{2,1,0:T(8,128)(2,1)} %get-tuple-element.3643), channel_id=1, source_target_pairs={{0,2},{1,3},{2,6},{3,7},{6,4},{7,5},{4,0},{5,1}} | collective-permute-start | bytes 3932168 | tf_op jit(solution)/shard_map/cond/branch_1_fun/while/body/ppermute | solution.py:678
  406.7 44.3 %collective-permute-start.80 = (bf16[2,80,64,128]{3,2,1,0:T(8,128)(2,1)}, bf16[2,80,64,128]{3,2,1,0:T(8,128)(2,1)}, u32[]{:S(2)}, u32[]{:S(2)}) collective-permute-start(bf16[2,80,64,128]{3,2,1,0:T(8,128)(2,1)} %get-tuple-element.3645), channel_id=1, source_target_pairs={{0,1},{1,0},{2,3},{3,2},{4,5},{5,4},{6,7},{7,6}} | collective-permute-start | bytes 7864328 | tf_op jit(solution)/shard_map/cond/branch_1_fun/while/body/ppermute | solution.py:680
  434.7 40.6 %collective-permute-start.86 = (bf16[2,80,64,128]{3,2,1,0:T(8,128)(2,1)}, bf16[2,80,64,128]{3,2,1,0:T(8,128)(2,1)}, u32[]{:S(2)}, u32[]{:S(2)}) collective-permute-start(bf16[2,80,64,128]{3,2,1,0:T(8,128)(2,1)} %get-tuple-element.3178), channel_id=1, source_target_pairs={{0,1},{1,0},{2,3},{3,2},{4,5},{5,4},{6,7},{7,6}} | collective-permute-start | bytes 7864328 | tf_op jit(solution)/shard_map/cond/branch_1_fun/while/body/ppermute | solution.py:680
  442.6 31.1 %collective-permute-start.87 = (bf16[80,64,128]{2,1,0:T(8,128)(2,1)}, bf16[80,64,128]{2,1,0:T(8,128)(2,1)}, u32[]{:S(2)}, u32[]{:S(2)}) collective-permute-start(bf16[80,64,128]{2,1,0:T(8,128)(2,1)} %get-tuple-element.3179), channel_id=1, source_target_pairs={{0,2},{1,3},{2,6},{3,7},{6,4},{7,5},{4,0},{5,1}} | collective-permute-start | bytes 3932168 | tf_op jit(solution)/shard_map/cond/branch_1_fun/while/body/ppermute | solution.py:678
  444.4 30.9 %collective-permute-start.88 = (bf16[80,64,128]{2,1,0:T(8,128)(2,1)}, bf16[80,64,128]{2,1,0:T(8,128)(2,1)}, u32[]{:S(2)}, u32[]{:S(2)}) collective-permute-start(bf16[80,64,128]{2,1,0:T(8,128)(2,1)} %get-tuple-element.3180), channel_id=1, source_target_pairs={{2,0},{3,1},{6,2},{7,3},{4,6},{5,7},{0,4},{1,5}} | collective-permute-start | bytes 3932168 | tf_op jit(solution)/shard_map/cond/branch_1_fun/while/body/ppermute | solution.py:679
  475.8 30.0 %collective-permute-start.82 = (bf16[80,64,128]{2,1,0:T(8,128)(2,1)}, bf16[80,64,128]{2,1,0:T(8,128)(2,1)}, u32[]{:S(2)}, u32[]{:S(2)}) collective-permute-start(bf16[80,64,128]{2,1,0:T(8,128)(2,1)} %get-tuple-element.3644), channel_id=1, source_target_pairs={{2,0},{3,1},{6,2},{7,3},{4,6},{5,7},{0,4},{1,5}} | collective-permute-start | bytes 3932168 | tf_op jit(solution)/shard_map/cond/branch_1_fun/while/body/ppermute | solution.py:679
  476.1 29.8 %collective-permute-start.81 = (bf16[80,64,128]{2,1,0:T(8,128)(2,1)}, bf16[80,64,128]{2,1,0:T(8,128)(2,1)}, u32[]{:S(2)}, u32[]{:S(2)}) collective-permute-start(bf16[80,64,128]{2,1,0:T(8,128)(2,1)} %get-tuple-element.3643), channel_id=1, source_target_pairs={{0,2},{1,3},{2,6},{3,7},{6,4},{7,5},{4,0},{5,1}} | collective-permute-start | bytes 3932168 | tf_op jit(solution)/shard_map/cond/branch_1_fun/while/body/ppermute | solution.py:678
  478.4 45.7 %collective-permute-start.80 = (bf16[2,80,64,128]{3,2,1,0:T(8,128)(2,1)}, bf16[2,80,64,128]{3,2,1,0:T(8,128)(2,1)}, u32[]{:S(2)}, u32[]{:S(2)}) collective-permute-start(bf16[2,80,64,128]{3,2,1,0:T(8,128)(2,1)} %get-tuple-element.3645), channel_id=1, source_target_pairs={{0,1},{1,0},{2,3},{3,2},{4,5},{5,4},{6,7},{7,6}} | collective-permute-start | bytes 7864328 | tf_op jit(solution)/shard_map/cond/branch_1_fun/while/body/ppermute | solution.py:680
  505.9 39.9 %collective-permute-start.86 = (bf16[2,80,64,128]{3,2,1,0:T(8,128)(2,1)}, bf16[2,80,64,128]{3,2,1,0:T(8,128)(2,1)}, u32[]{:S(2)}, u32[]{:S(2)}) collective-permute-start(bf16[2,80,64,128]{3,2,1,0:T(8,128)(2,1)} %get-tuple-element.3178), channel_id=1, source_target_pairs={{0,1},{1,0},{2,3},{3,2},{4,5},{5,4},{6,7},{7,6}} | collective-permute-start | bytes 7864328 | tf_op jit(solution)/shard_map/cond/branch_1_fun/while/body/ppermute | solution.py:680
  514.3 31.1 %collective-permute-start.87 = (bf16[80,64,128]{2,1,0:T(8,128)(2,1)}, bf16[80,64,128]{2,1,0:T(8,128)(2,1)}, u32[]{:S(2)}, u32[]{:S(2)}) collective-permute-start(bf16[80,64,128]{2,1,0:T(8,128)(2,1)} %get-tuple-element.3179), channel_id=1, source_target_pairs={{0,2},{1,3},{2,6},{3,7},{6,4},{7,5},{4,0},{5,1}} | collective-permute-start | bytes 3932168 | tf_op jit(solution)/shard_map/cond/branch_1_fun/while/body/ppermute | solution.py:678
  514.9 30.9 %collective-permute-start.88 = (bf16[80,64,128]{2,1,0:T(8,128)(2,1)}, bf16[80,64,128]{2,1,0:T(8,128)(2,1)}, u32[]{:S(2)}, u32[]{:S(2)}) collective-permute-start(bf16[80,64,128]{2,1,0:T(8,128)(2,1)} %get-tuple-element.3180), channel_id=1, source_target_pairs={{2,0},{3,1},{6,2},{7,3},{4,6},{5,7},{0,4},{1,5}} | collective-permute-start | bytes 3932168 | tf_op jit(solution)/shard_map/cond/branch_1_fun/while/body/ppermute | solution.py:679
  546.3 30.0 %collective-permute-start.82 = (bf16[80,64,128]{2,1,0:T(8,128)(2,1)}, bf16[80,64,128]{2,1,0:T(8,128)(2,1)}, u32[]{:S(2)}, u32[]{:S(2)}) collective-permute-start(bf16[80,64,128]{2,1,0:T(8,128)(2,1)} %get-tuple-element.3644), channel_id=1, source_target_pairs={{2,0},{3,1},{6,2},{7,3},{4,6},{5,7},{0,4},{1,5}} | collective-permute-start | bytes 3932168 | tf_op jit(solution)/shard_map/cond/branch_1_fun/while/body/ppermute | solution.py:679
  547.8 29.7 %collective-permute-start.81 = (bf16[80,64,128]{2,1,0:T(8,128)(2,1)}, bf16[80,64,128]{2,1,0:T(8,128)(2,1)}, u32[]{:S(2)}, u32[]{:S(2)}) collective-permute-start(bf16[80,64,128]{2,1,0:T(8,128)(2,1)} %get-tuple-element.3643), channel_id=1, source_target_pairs={{0,2},{1,3},{2,6},{3,7},{6,4},{7,5},{4,0},{5,1}} | collective-permute-start | bytes 3932168 | tf_op jit(solution)/shard_map/cond/branch_1_fun/while/body/ppermute | solution.py:678
  548.4 29.2 %collective-permute-start.84 = (bf16[80,64,128]{2,1,0:T(8,128)(2,1)}, bf16[80,64,128]{2,1,0:T(8,128)(2,1)}, u32[]{:S(2)}, u32[]{:S(2)}) collective-permute-start(bf16[80,64,128]{2,1,0:T(8,128)(2,1)} %get-tuple-element.3649.rc1), channel_id=1, source_target_pairs={{0,1},{1,0},{2,3},{3,2},{4,5},{5,4},{6,7},{7,6}} | collective-permute-start | bytes 3932168 | tf_op jit(solution)/shard_map/cond/branch_1_fun/while/body/ppermute | solution.py:682
  548.4 29.7 %collective-permute-start.83 = (bf16[80,64,128]{2,1,0:T(8,128)(2,1)}, bf16[80,64,128]{2,1,0:T(8,128)(2,1)}, u32[]{:S(2)}, u32[]{:S(2)}) collective-permute-start(bf16[80,64,128]{2,1,0:T(8,128)(2,1)} %get-tuple-element.3648.rc0), channel_id=1, source_target_pairs={{0,1},{1,0},{2,3},{3,2},{4,5},{5,4},{6,7},{7,6}} | collective-permute-start | bytes 3932168 | tf_op jit(solution)/shard_map/cond/branch_1_fun/while/body/ppermute | solution.py:681
  548.9 45.3 %collective-permute-start.80 = (bf16[2,80,64,128]{3,2,1,0:T(8,128)(2,1)}, bf16[2,80,64,128]{3,2,1,0:T(8,128)(2,1)}, u32[]{:S(2)}, u32[]{:S(2)}) collective-permute-start(bf16[2,80,64,128]{3,2,1,0:T(8,128)(2,1)} %get-tuple-element.3645), channel_id=1, source_target_pairs={{0,1},{1,0},{2,3},{3,2},{4,5},{5,4},{6,7},{7,6}} | collective-permute-start | bytes 7864328 | tf_op jit(solution)/shard_map/cond/branch_1_fun/while/body/ppermute | solution.py:680
  577.6 38.7 %collective-permute-start.86 = (bf16[2,80,64,128]{3,2,1,0:T(8,128)(2,1)}, bf16[2,80,64,128]{3,2,1,0:T(8,128)(2,1)}, u32[]{:S(2)}, u32[]{:S(2)}) collective-permute-start(bf16[2,80,64,128]{3,2,1,0:T(8,128)(2,1)} %get-tuple-element.3178), channel_id=1, source_target_pairs={{0,1},{1,0},{2,3},{3,2},{4,5},{5,4},{6,7},{7,6}} | collective-permute-start | bytes 7864328 | tf_op jit(solution)/shard_map/cond/branch_1_fun/while/body/ppermute | solution.py:680
  584.9 31.1 %collective-permute-start.87 = (bf16[80,64,128]{2,1,0:T(8,128)(2,1)}, bf16[80,64,128]{2,1,0:T(8,128)(2,1)}, u32[]{:S(2)}, u32[]{:S(2)}) collective-permute-start(bf16[80,64,128]{2,1,0:T(8,128)(2,1)} %get-tuple-element.3179), channel_id=1, source_target_pairs={{0,2},{1,3},{2,6},{3,7},{6,4},{7,5},{4,0},{5,1}} | collective-permute-start | bytes 3932168 | tf_op jit(solution)/shard_map/cond/branch_1_fun/while/body/ppermute | solution.py:678
  585.4 30.9 %collective-permute-start.88 = (bf16[80,64,128]{2,1,0:T(8,128)(2,1)}, bf16[80,64,128]{2,1,0:T(8,128)(2,1)}, u32[]{:S(2)}, u32[]{:S(2)}) collective-permute-start(bf16[80,64,128]{2,1,0:T(8,128)(2,1)} %get-tuple-element.3180), channel_id=1, source_target_pairs={{2,0},{3,1},{6,2},{7,3},{4,6},{5,7},{0,4},{1,5}} | collective-permute-start | bytes 3932168 | tf_op jit(solution)/shard_map/cond/branch_1_fun/while/body/ppermute | solution.py:679
  616.9 30.0 %collective-permute-start.82 = (bf16[80,64,128]{2,1,0:T(8,128)(2,1)}, bf16[80,64,128]{2,1,0:T(8,128)(2,1)}, u32[]{:S(2)}, u32[]{:S(2)}) collective-permute-start(bf16[80,64,128]{2,1,0:T(8,128)(2,1)} %get-tuple-element.3644), channel_id=1, source_target_pairs={{2,0},{3,1},{6,2},{7,3},{4,6},{5,7},{0,4},{1,5}} | collective-permute-start | bytes 3932168 | tf_op jit(solution)/shard_map/cond/branch_1_fun/while/body/ppermute | solution.py:679
  618.4 29.7 %collective-permute-start.81 = (bf16[80,64,128]{2,1,0:T(8,128)(2,1)}, bf16[80,64,128]{2,1,0:T(8,128)(2,1)}, u32[]{:S(2)}, u32[]{:S(2)}) collective-permute-start(bf16[80,64,128]{2,1,0:T(8,128)(2,1)} %get-tuple-element.3643), channel_id=1, source_target_pairs={{0,2},{1,3},{2,6},{3,7},{6,4},{7,5},{4,0},{5,1}} | collective-permute-start | bytes 3932168 | tf_op jit(solution)/shard_map/cond/branch_1_fun/while/body/ppermute | solution.py:678
  618.9 29.2 %collective-permute-start.84 = (bf16[80,64,128]{2,1,0:T(8,128)(2,1)}, bf16[80,64,128]{2,1,0:T(8,128)(2,1)}, u32[]{:S(2)}, u32[]{:S(2)}) collective-permute-start(bf16[80,64,128]{2,1,0:T(8,128)(2,1)} %get-tuple-element.3649.rc1), channel_id=1, source_target_pairs={{0,1},{1,0},{2,3},{3,2},{4,5},{5,4},{6,7},{7,6}} | collective-permute-start | bytes 3932168 | tf_op jit(solution)/shard_map/cond/branch_1_fun/while/body/ppermute | solution.py:682
  618.9 29.7 %collective-permute-start.83 = (bf16[80,64,128]{2,1,0:T(8,128)(2,1)}, bf16[80,64,128]{2,1,0:T(8,128)(2,1)}, u32[]{:S(2)}, u32[]{:S(2)}) collective-permute-start(bf16[80,64,128]{2,1,0:T(8,128)(2,1)} %get-tuple-element.3648.rc0), channel_id=1, source_target_pairs={{0,1},{1,0},{2,3},{3,2},{4,5},{5,4},{6,7},{7,6}} | collective-permute-start | bytes 3932168 | tf_op jit(solution)/shard_map/cond/branch_1_fun/while/body/ppermute | solution.py:681
  619.4 44.4 %collective-permute-start.80 = (bf16[2,80,64,128]{3,2,1,0:T(8,128)(2,1)}, bf16[2,80,64,128]{3,2,1,0:T(8,128)(2,1)}, u32[]{:S(2)}, u32[]{:S(2)}) collective-permute-start(bf16[2,80,64,128]{3,2,1,0:T(8,128)(2,1)} %get-tuple-element.3645), channel_id=1, source_target_pairs={{0,1},{1,0},{2,3},{3,2},{4,5},{5,4},{6,7},{7,6}} | collective-permute-start | bytes 7864328 | tf_op jit(solution)/shard_map/cond/branch_1_fun/while/body/ppermute | solution.py:680
  648.1 39.4 %collective-permute-start.86 = (bf16[2,80,64,128]{3,2,1,0:T(8,128)(2,1)}, bf16[2,80,64,128]{3,2,1,0:T(8,128)(2,1)}, u32[]{:S(2)}, u32[]{:S(2)}) collective-permute-start(bf16[2,80,64,128]{3,2,1,0:T(8,128)(2,1)} %get-tuple-element.3178), channel_id=1, source_target_pairs={{0,1},{1,0},{2,3},{3,2},{4,5},{5,4},{6,7},{7,6}} | collective-permute-start | bytes 7864328 | tf_op jit(solution)/shard_map/cond/branch_1_fun/while/body/ppermute | solution.py:680
  655.4 31.1 %collective-permute-start.87 = (bf16[80,64,128]{2,1,0:T(8,128)(2,1)}, bf16[80,64,128]{2,1,0:T(8,128)(2,1)}, u32[]{:S(2)}, u32[]{:S(2)}) collective-permute-start(bf16[80,64,128]{2,1,0:T(8,128)(2,1)} %get-tuple-element.3179), channel_id=1, source_target_pairs={{0,2},{1,3},{2,6},{3,7},{6,4},{7,5},{4,0},{5,1}} | collective-permute-start | bytes 3932168 | tf_op jit(solution)/shard_map/cond/branch_1_fun/while/body/ppermute | solution.py:678
  656.6 30.9 %collective-permute-start.88 = (bf16[80,64,128]{2,1,0:T(8,128)(2,1)}, bf16[80,64,128]{2,1,0:T(8,128)(2,1)}, u32[]{:S(2)}, u32[]{:S(2)}) collective-permute-start(bf16[80,64,128]{2,1,0:T(8,128)(2,1)} %get-tuple-element.3180), channel_id=1, source_target_pairs={{2,0},{3,1},{6,2},{7,3},{4,6},{5,7},{0,4},{1,5}} | collective-permute-start | bytes 3932168 | tf_op jit(solution)/shard_map/cond/branch_1_fun/while/body/ppermute | solution.py:679
  (96 other events, 1080.9 us)

commit v5 on v4

--- a/solution.py
+++ b/solution.py
@@ -57,11 +57,11 @@
         c.wait()
 
 
-def plan_kernel(me_ref, dest_ref, len_ref, tab, lens_out, nbv, kindv, todo, near, load, one, two, three, swap, addr, at):
+def plan_kernel(me_ref, dest_ref, len_ref, tab, lens_out, nbv, kindv, todo, near, load, one, two, three, addr, at):
     me = me_ref[0]
     zero = me - me
-    for i in range(9):
-        for ref in (load, one, two, three, swap):
+    for i in range(17):
+        for ref in (one, two, three):
             ref[i] = zero
     tab[CORE] = me & 1
     for j in range(SL):
@@ -78,20 +78,19 @@
         beside = (delta & 1) == 1
         ccw = delta == 3
         kindv[i] = jnp.where(beside, jnp.where(ccw, 4, 1), 0)
-        slot = jnp.where(beside, jnp.where(ccw, 4, 0) + ra, 8)
-        one[slot] = one[slot] + nb + HALF
-        load[slot] = load[slot] + nb
         todo[c[0]] = i
         near[c[1]] = i
         cross = (delta == 0) & ((i >> 5) != (d >> 5))
-        xslot = jnp.where(cross, i >> 5, 8)
-        swap[xslot] = swap[xslot] + nb
+        slot = jnp.where(beside, jnp.where(ccw, 4, 0) + ra, jnp.where(cross, 9 + (i >> 5), 8))
+        one[slot] = one[slot] + nb + HALF
         mine = jnp.where((d >> 5) == me, d & 31, SL)
         tab[MLEN + mine] = size
         tab[SRC + mine] = jnp.where((i >> 5) == me, i & 31, -1)
         return c[0] + jnp.where(delta == 2, 1, 0), c[1] + jnp.where(beside, 1, 0)
 
-    far, side = lax.fori_loop(0, 8 * SL, first, (zero, zero), unroll=4)
+    far, side = lax.fori_loop(0, 8 * SL, first, (zero, zero), unroll=8)
+    for i in range(8):
+        load[i] = one[i] & LOW
 
     def lens(j, c):
         lens_out[j] = tab[MLEN + j] + 1
@@ -187,7 +186,7 @@
 
     cross = zero
     for d in range(8):
-        cross = jnp.maximum(cross, (swap[d] + NX - 1) // NX)
+        cross = jnp.maximum(cross, ((one[9 + d] & LOW) + NX - 1) // NX)
     best, pick, turns, chunk = zero + END, zero, zero, zero
     all_links = [(two[x] + three[x], three[x], one[x] + two[x] + three[x]) for x in range(8)]
     parts = []
@@ -444,12 +443,6 @@
     mv.drain(sum(mv.partial(d, kc, vc, part.at[d], sem) for d in range(2)), kc, sem)
 
 
-def open_more_kernel(NB, tab, st_in, kc, vc, st, part1, part2, dxs, sem):
-    mv = Mover(tab, st_in, st, NB)
-    cnt = sum(mv.partial(d, kc, vc, part.at[d], sem) for part in (part1, part2) for d in range(2))
-    mv.drain(cnt + mv.cross_send(kc, vc, dxs, sem), kc, sem)
-
-
 def open_merge_kernel(NB, tab, st_in, kc, vc, pre, st, send0, send1, sem):
     mv = Mover(tab, st_in, st, NB)
     mv.drain(sum(mv.merge(d, kc, vc, pre, None, buf, sem) for d, buf in enumerate((send0, send1))), kc, sem)
@@ -491,13 +484,14 @@
     mv.drain(cnt, ko, sem)
 
 
-def attn_kernel(NB, batches, tab, st_in, q, kn, vn, kc, vc, koi, voi, aoi, st, ko, vo, ao,
-                kb, vb, ob, sel, lsem, wsem, osem):
+def attn_kernel(NB, last, tab, st_in, q, kn, vn, kc, vc, koi, voi, aoi, st, ko, vo, ao,
+                kb, vb, ob, sel, lsem, wsem):
     def cp(i, _):
         st[i] = st_in[i]
         return 0
 
     lax.fori_loop(0, STATE, cp, 0)
+    share = SL if last else tab[SHARE]
     link_end = jnp.maximum((st_in[STEP] - 2) * NB, 0)
     swap_end = jnp.maximum((st_in[STEP] - 1) * NX, 0)
 
@@ -518,7 +512,6 @@
         pltpu.make_async_copy(kb.at[a], kb.at[a], lsem.at[a]).wait()
         pltpu.make_async_copy(vb.at[a], vb.at[a], lsem.at[a]).wait()
         m = tab[MLEN + j]
-        s = tab[SRC + j]
         b0 = m >> SHIFT
         row = lax.broadcasted_iota(i32, BLOCK, 0) >> 3
         for buf, new in ((kb, kn), (vb, vn)):
@@ -545,47 +538,54 @@
         tot = jnp.sum(w, axis=1, keepdims=True)
         acc = lax.dot_general(w.astype(bf16), vf, (((1,), (0,)), ((), ())), preferred_element_type=f32)
         ob[a] = (acc / tot).astype(bf16)
-        bw = jnp.where(s >= 0, 0, b0)
-
-        tail = pl.ds(bw, BL - bw)
-        home = pl.ds(j * BL + bw, BL - bw)
-        pltpu.make_async_copy(kb.at[a, tail], ko.at[home], wsem.at[0]).start()
-        pltpu.make_async_copy(vb.at[a, tail], vo.at[home], wsem.at[0]).start()
-        pltpu.make_async_copy(ob.at[a], ao.at[j], osem.at[0]).start()
-        return 2 * (BL - bw)
-
-    share = tab[SHARE] if batches == 1 else A
-
-    def batch(_, c):
-        def pick(j, n):
-            hit = (st[DONE + j] == 0) & (tab[RDY + j] <= link_end) & (tab[RDX + j] <= swap_end) & (n < share)
-            sel[jnp.where(hit, n, A)] = j
-            st[DONE + j] = jnp.where(hit, 1, st[DONE + j])
-            return n + jnp.where(hit, 1, 0)
-
-        n = lax.fori_loop(0, SL, pick, jnp.int32(0))
-
-        def loads(a, _):
-            load(a, sel[a])
-            return 0
-
-        lax.fori_loop(0, n, loads, 0)
-
-        def computes(a, cnt):
-            return cnt + compute(a, sel[a])
-
-        cnt = lax.fori_loop(0, n, computes, jnp.int32(0))
-
-        @pl.when(n > 0)
+        for src, dst in writes(a, j):
+            pltpu.make_async_copy(src, dst, wsem.at[a]).start()
+
+    def writes(a, j):
+        bw = jnp.where(tab[SRC + j] >= 0, 0, tab[MLEN + j] >> SHIFT)
+        tail, home = pl.ds(bw, BL - bw), pl.ds(j * BL + bw, BL - bw)
+        return (kb.at[a, tail], ko.at[home]), (vb.at[a, tail], vo.at[home]), (ob.at[a], ao.at[j])
+
+    def settle(k):
+        a, j = k & (A - 1), sel[k]
+        for src, dst in writes(a, j):
+            pltpu.make_async_copy(src, dst, wsem.at[a]).wait()
+
+    def pick(j, n):
+        hit = (st[DONE + j] == 0) & (tab[RDY + j] <= link_end) & (tab[RDX + j] <= swap_end) & (n < share)
+        sel[n] = j
+        st[DONE + j] = jnp.where(hit, 1, st[DONE + j])
+        return n + jnp.where(hit, 1, 0)
+
+    n = lax.fori_loop(0, SL, pick, jnp.int32(0))
+
+    def early(k, c):
+        load(k, sel[k])
+        return c
+
+    lax.fori_loop(0, jnp.minimum(n, A - 1), early, 0)
+
+    def step(k, c):
+        compute(k & (A - 1), sel[k])
+        later = k + A - 1
+
+        @pl.when(later < n)
         def _():
-            done = ko.at[pl.ds(0, cnt)]
-            pltpu.make_async_copy(done, done, wsem.at[0]).wait()
-            rows = ob.at[pl.ds(0, n)]
-            pltpu.make_async_copy(rows, rows, osem.at[0]).wait()
-
-        return c
-
-    lax.fori_loop(0, batches, batch, 0)
+            @pl.when(k >= 1)
+            def _():
+                settle(k - 1)
+
+            load(later & (A - 1), sel[later])
+
+        return c
+
+    lax.fori_loop(0, n, step, 0)
+
+    def wind_up(k, c):
+        settle(k)
+        return c
+
+    lax.fori_loop(jnp.maximum(n - A, 0), n, wind_up, 0)
 
 
 SMEM = pl.BlockSpec(memory_space=pltpu.SMEM)
@@ -633,7 +633,7 @@
         me = jnp.full((1,), lax.axis_index('dp'), i32)
         tab, lens_out = pl.pallas_call(
             plan_kernel, out_shape=(sds((TAB,), i32), sds((SL,), i32)), in_specs=[SMEM] * 3, out_specs=(SMEM, SMEM),
-            scratch_shapes=[pltpu.SMEM((8 * SL + 1,), i32)] * 4 + [pltpu.SMEM((IDLE + 1,), i32)] * 7,
+            scratch_shapes=[pltpu.SMEM((8 * SL + 1,), i32)] * 4 + [pltpu.SMEM((IDLE + 1,), i32)] * 6,
             name='plan')(me, dest_slot, lens_all)
 
         def run(NB):
@@ -648,49 +648,50 @@
 
             st = jnp.zeros((STATE,), i32)
             caches = [SMEM, SMEM, ANY, ANY]
-            st, part = pl.pallas_call(
-                functools.partial(open_kernel, NB), out_shape=(ST, both), in_specs=caches, out_specs=(SMEM, VMEM),
-                scratch_shapes=DMA, name='open')(tab, st, kc, vc)
+
+            def opened(st):
+                return pl.pallas_call(
+                    functools.partial(open_kernel, NB), out_shape=(ST, both), in_specs=caches, out_specs=(SMEM, VMEM),
+                    scratch_shapes=DMA, name='open')(tab, st, kc, vc)
+
+            st, part = opened(st)
             pre = lax.ppermute(part, 'dp', swap)
-            st, part1, part, dxs = pl.pallas_call(
-                functools.partial(open_more_kernel, NB), out_shape=(ST, both, both, cross), in_specs=caches,
-                out_specs=(SMEM,) + (VMEM,) * 3, scratch_shapes=DMA,
-                name='open_more')(tab, st, kc, vc)
-            pre1 = lax.ppermute(part1, 'dp', swap)
+            st, part = opened(st)
+            pre1 = lax.ppermute(part, 'dp', swap)
             st, s0, s1 = pl.pallas_call(
                 functools.partial(open_merge_kernel, NB), out_shape=(ST, chunk, chunk), in_specs=caches + [VMEM],
                 out_specs=(SMEM, VMEM, VMEM), scratch_shapes=DMA,
                 name='open_merge')(tab, st, kc, vc, pre)
             pre = pre1
 
-            def attend(st, ko, vo, ao, batches):
+            def attend(st, ko, vo, ao, last):
                 return pl.pallas_call(
-                    functools.partial(attn_kernel, NB, batches),
+                    functools.partial(attn_kernel, NB, last),
                     out_shape=(ST, cache, cache, sds((SL, 24, 128))),
                     in_specs=[SMEM, SMEM, VMEM, VMEM, VMEM, ANY, ANY, ANY, ANY, ANY], out_specs=(SMEM, ANY, ANY, ANY),
                     input_output_aliases={7: 1, 8: 2, 9: 3},
-                    scratch_shapes=[buf(A, BL), buf(A, BL), pltpu.VMEM((A, 24, 128), bf16), pltpu.SMEM((A + 1,), i32),
-                                    dma(A), dma(1), dma(1)],
+                    scratch_shapes=[buf(A, BL), buf(A, BL), pltpu.VMEM((A, 24, 128), bf16), pltpu.SMEM((SL + 1,), i32),
+                                    dma(A), dma(A)],
                     cost_estimate=cost(6), name='attend')(tab, st, query, k_new, v_new, kc, vc, ko, vo, ao)
 
             def one_round(tag, c):
-                st, s0, s1, part, dxs, pre, rc0, rc1, po0, po1, dxr, f0, f1, ko, vo, ao = c
+                st, s0, s1, pre, rc0, rc1, po0, po1, dxr, f0, f1, ko, vo, ao = c
                 nrc0 = lax.ppermute(s0, 'dp', cw)
                 nrc1 = lax.ppermute(s1, 'dp', ccw)
-                npre = lax.ppermute(part, 'dp', swap)
                 npo0 = lax.ppermute(rc0, 'dp', swap)
                 npo1 = lax.ppermute(rc1, 'dp', swap)
-                ndxr = lax.ppermute(dxs, 'dp', swap)
                 st, s0, s1, part, dxs, f0, f1, ko, vo = pl.pallas_call(
                     functools.partial(round_kernel, NB), out_shape=(ST, chunk, chunk, both, cross, store, store, cache, cache),
                     in_specs=caches + [VMEM] * 6 + [ANY] * 4, out_specs=(SMEM,) + (VMEM,) * 4 + (ANY,) * 4,
                     input_output_aliases={10: 5, 11: 6, 12: 7, 13: 8},
                     scratch_shapes=DMA * 3,
                     cost_estimate=cost(10), name='round')(tab, st, kc, vc, pre, rc0, rc1, po0, po1, dxr, f0, f1, ko, vo)
-                st, ko, vo, ao = attend(st, ko, vo, ao, 1)
+                npre = lax.ppermute(part, 'dp', swap)
+                ndxr = lax.ppermute(dxs, 'dp', swap)
+                st, ko, vo, ao = attend(st, ko, vo, ao, False)
                 if tag != TAGS[-1]:
                     s0, s1, npo0, npo1 = lax.optimization_barrier((s0, s1, npo0, npo1))
-                return st, s0, s1, part, dxs, npre, nrc0, nrc1, npo0, npo1, ndxr, f0, f1, ko, vo, ao
+                return st, s0, s1, npre, nrc0, nrc1, npo0, npo1, ndxr, f0, f1, ko, vo, ao
 
             rounds = tab[ROUNDS]
 
@@ -698,8 +699,8 @@
                 return (c[0] + TURN,) + functools.reduce(lambda c, tag: one_round(tag, c), TAGS, c[1:])
 
             c = lax.while_loop(lambda c: c[0] < rounds, body,
-                           (jnp.int32(0), st, s0, s1, part, dxs, pre, rc0, rc1, po0, po1, dxr, f0, f1, ko, vo, ao))
-            _, st, _, _, _, _, _, rc0, rc1, po0, po1, dxr, _, _, ko, vo, ao = c
+                           (jnp.int32(0), st, s0, s1, pre, rc0, rc1, po0, po1, dxr, f0, f1, ko, vo, ao))
+            _, st, _, _, _, rc0, rc1, po0, po1, dxr, _, _, ko, vo, ao = c
 
             def close(last, st, ko, vo, *ins):
                 n = len(ins)
@@ -714,7 +715,7 @@
             lpo1 = lax.ppermute(rc1, 'dp', swap)
             st, ko, vo = close(False, st, ko, vo, rc0, rc1, po0, po1, dxr)
             st, ko, vo = close(True, st, ko, vo, lpo0, lpo1)
-            st, ko, vo, ao = attend(st, ko, vo, ao, SL // A)
+            st, ko, vo, ao = attend(st, ko, vo, ao, True)
             return ao, ko, vo
 
         ao, ko, vo = lax.switch(tab[PICK], [functools.partial(run, size) for size in SIZES])

time: 712 us -> 857 us (1.20)
  waiting for transfers between devices: 302 us -> 435 us
  local copies, waits for them, and re-layouts: 1.79 us -> 16.9 us
    ppermute x18, waiting for transfers between devices: 69.3 us -> 171 us  [one_round(): nrc0 = lax.ppermute(s0, 'dp', cw)]
    ppermute x18, waiting for transfers between devices: 0.05 us -> 81.6 us  [one_round(): npo1 = lax.ppermute(rc1, 'dp', swap)]
    ppermute x18, waiting for transfers between devices: 63.6 us -> 0.05 us  [one_round(): ndxr = lax.ppermute(dxs, 'dp', swap)]
    ppermute x18, waiting for transfers between devices: 0.05 us -> 15.7 us  [one_round(): npo0 = lax.ppermute(rc0, 'dp', swap)]
    while x90 -> x18, local copies, waits for them, and re-layouts: 0.18 us -> 13.9 us
  transfers between devices with their start and end apart: 112 -> 112, of which waited for: 44 -> 60; matrix products, arithmetic and copies ran while one was open for 0% -> 0% of each run, Pallas kernels for 43% -> 13%
where the time goes in v5:
time: 857 us; the launch traced here: 854 us
  waiting for transfers between devices  435 us (51%)
  Pallas kernels  342 us (40%)
  starting transfers between devices  50.9 us (6%)
  local copies, waits for them, and re-layouts  16.9 us (2%)
    pallas_call x18, Pallas kernels, one_round(): pl.pallas_call(functools.partial(round_kernel, NB), out_shape=(ST, chunk,...  185 us
    ppermute x18, waiting for transfers between devices, one_round(): nrc0 = lax.ppermute(s0, 'dp', cw)  171 us
    ppermute x18, waiting for transfers between devices, one_round(): nrc1 = lax.ppermute(s1, 'dp', ccw)  167 us
    pallas_call x19, Pallas kernels, attend(): pl.pallas_call(functools.partial(attn_kernel, NB, last), out_shape=(ST, c...  108 us
    ppermute x18, waiting for transfers between devices, one_round(): npo1 = lax.ppermute(rc1, 'dp', swap)  81.6 us
    ppermute x18, starting transfers between devices, one_round(): nrc1 = lax.ppermute(s1, 'dp', ccw)  24.5 us
    pallas_call x1, Pallas kernels, local(): pl.pallas_call(plan_kernel, out_shape=(sds((TAB,), i32), sds((SL,), i32))...  19.5 us
  transfers between devices with their start and end apart: 112, of which 60 were waited for; matrix products, arithmetic and copies ran while one was open for 0% of the time, Pallas kernels for 13%

profile of v5, /device:TPU:0, one launch (start us, length us, event | category | flops | bytes accessed | tf_op | source)
XLA Modules:
  0.0 853.8 jit_solution(4935613951082795985)
XLA Ops:
  0.6 7.8 lens.1.len_ref
  8.4 19.5 %plan.1 = (s32[2568]{0:T(1024)S(1)}, s32[32]{0:T(128)}) custom-call(s32[1]{0:T(128)} %bitcast.7.me_ref, s32[256]{0:T(256)} %dest_ref.1, s32[8,1,32]{2,1,0:T(1,128)} %lens.1.len_ref), custom_call_target="tpu_custom_call" | custom-call | tf_op jit(solution)/shard_map/plan/pallas_call | solution.py:634
  29.1 824.5 %conditional.1 = (bf16[32,24,128]{2,1,0:T(8,128)(2,1)}, bf16[2048,64,128]{2,1,0:T(8,128)(2,1)}, bf16[2048,64,128]{2,1,0:T(8,128)(2,1)}) conditional(s32[]{:T(128)} %bitcast.9, (s32[2568]{0:T(1024)S(1)}, bf16[2048,64,128]{2,1,0:T(8,128)(2,1)}, bf16[2048,64,128]{2,1,0:T(8,128)(2,1)}, bf16[32,24,128]{2,1,0:T(8,128)(2,1)}, ...), branch_computations={%region_0.0_spmd, %region_3.0_spmd, %region_6.0_spmd, %region_9.0_... | conditional | flops 152000000 | bytes 282811328 | solution.py:721
  39.3 5.4 open_merge.8
  44.7 791.5 %while.246 = (s32[]{:T(128)}, s32[64]{0:T(128)S(1)}, bf16[80,64,128]{2,1,0:T(8,128)(2,1)}, bf16[80,64,128]{2,1,0:T(8,128)(2,1)}, bf16[2,80,64,128]{3,2,1,0:T(8,1...) while((s32[]{:T(128)}, s32[64]{0:T(128)S(1)}, ...), condition=%wide.region_5.0_spmd, body=%wide.region_4.0_spmd.sunk | while | flops 128000000 | bytes 209789616 | solution.py:701
  45.3 8.7 %round.24 = (s32[64]{0:T(128)}, bf16[80,64,128]{2,1,0:T(8,128)(2,1)}, bf16[80,64,128]{2,1,0:T(8,128)(2,1)}, bf16[2,80,64,128]{3,2,1,0:T(8,128)(2,1)}, bf16[2,32,...) custom-call(s32[2568]{0:T(1024)S(1)} %get-tuple-element.3452.tab, ...), custom_call_target="tpu_custom_call", output_to_operand_aliasing={{5}: (10, {}), {6}: (11, {}), {7}: (12, {}), {8}: (13, {})} | custom-call | flops 40000000 | bytes 40000000 | tf_op jit(solution)/shard_map/cond/branch_1_fun/while/body/round/pallas_call | solution.py:683
  56.6 4.6 collective-permute-done.84.po1
  61.3 6.7 attend.38
  68.0 18.0 %collective-permute-done.82.rc1 = bf16[80,64,128]{2,1,0:T(8,128)(2,1)} collective-permute-done((bf16[80,64,128]{2,1,0:T(8,128)(2,1)}, bf16[80,64,128]{2,1,0:T(8,128)(2,1)}, u32[]{:S(2)}, u32[]{:S(2)}) %collective-permute-start.82) | collective-permute-done | bytes 1310752 | tf_op jit(solution)/shard_map/cond/branch_1_fun/while/body/ppermute | solution.py:680
  88.7 11.3 %round.25 = (s32[64]{0:T(128)}, bf16[80,64,128]{2,1,0:T(8,128)(2,1)}, bf16[80,64,128]{2,1,0:T(8,128)(2,1)}, bf16[2,80,64,128]{3,2,1,0:T(8,128)(2,1)}, bf16[2,32,...) custom-call(s32[2568]{0:T(1024)S(1)} %get-tuple-element.3452.tab, ...), custom_call_target="tpu_custom_call", output_to_operand_aliasing={{5}: (10, {}), {6}: (11, {}), {7}: (12, {}), {8}: (13, {})} | custom-call | flops 40000000 | bytes 40000000 | tf_op jit(solution)/shard_map/cond/branch_1_fun/while/body/round/pallas_call | solution.py:683
  102.5 4.6 collective-permute-done.90
  111.2 20.7 %collective-permute-done.87 = bf16[80,64,128]{2,1,0:T(8,128)(2,1)} collective-permute-done((bf16[80,64,128]{2,1,0:T(8,128)(2,1)}, bf16[80,64,128]{2,1,0:T(8,128)(2,1)}, u32[]{:S(2)}, u32[]{:S(2)}) %collective-permute-start.87) | collective-permute-done | bytes 1310752 | tf_op jit(solution)/shard_map/cond/branch_1_fun/while/body/ppermute | solution.py:679
  132.9 10.7 %round.24 = (s32[64]{0:T(128)}, bf16[80,64,128]{2,1,0:T(8,128)(2,1)}, bf16[80,64,128]{2,1,0:T(8,128)(2,1)}, bf16[2,80,64,128]{3,2,1,0:T(8,128)(2,1)}, bf16[2,32,...) custom-call(s32[2568]{0:T(1024)S(1)} %get-tuple-element.3452.tab, ...), custom_call_target="tpu_custom_call", output_to_operand_aliasing={{5}: (10, {}), {6}: (11, {}), {7}: (12, {}), {8}: (13, {})} | custom-call | flops 40000000 | bytes 40000000 | tf_op jit(solution)/shard_map/cond/branch_1_fun/while/body/round/pallas_call | solution.py:683
  146.2 4.6 collective-permute-done.84.po1
  150.9 5.3 attend.38
  156.2 19.4 %collective-permute-done.82.rc1 = bf16[80,64,128]{2,1,0:T(8,128)(2,1)} collective-permute-done((bf16[80,64,128]{2,1,0:T(8,128)(2,1)}, bf16[80,64,128]{2,1,0:T(8,128)(2,1)}, u32[]{:S(2)}, u32[]{:S(2)}) %collective-permute-start.82) | collective-permute-done | bytes 1310752 | tf_op jit(solution)/shard_map/cond/branch_1_fun/while/body/ppermute | solution.py:680
  178.0 11.5 %round.25 = (s32[64]{0:T(128)}, bf16[80,64,128]{2,1,0:T(8,128)(2,1)}, bf16[80,64,128]{2,1,0:T(8,128)(2,1)}, bf16[2,80,64,128]{3,2,1,0:T(8,128)(2,1)}, bf16[2,32,...) custom-call(s32[2568]{0:T(1024)S(1)} %get-tuple-element.3452.tab, ...), custom_call_target="tpu_custom_call", output_to_operand_aliasing={{5}: (10, {}), {6}: (11, {}), {7}: (12, {}), {8}: (13, {})} | custom-call | flops 40000000 | bytes 40000000 | tf_op jit(solution)/shard_map/cond/branch_1_fun/while/body/round/pallas_call | solution.py:683
  192.1 4.6 collective-permute-done.90
  200.8 20.7 %collective-permute-done.87 = bf16[80,64,128]{2,1,0:T(8,128)(2,1)} collective-permute-done((bf16[80,64,128]{2,1,0:T(8,128)(2,1)}, bf16[80,64,128]{2,1,0:T(8,128)(2,1)}, u32[]{:S(2)}, u32[]{:S(2)}) %collective-permute-start.87) | collective-permute-done | bytes 1310752 | tf_op jit(solution)/shard_map/cond/branch_1_fun/while/body/ppermute | solution.py:679
  222.2 10.8 %round.24 = (s32[64]{0:T(128)}, bf16[80,64,128]{2,1,0:T(8,128)(2,1)}, bf16[80,64,128]{2,1,0:T(8,128)(2,1)}, bf16[2,80,64,128]{3,2,1,0:T(8,128)(2,1)}, bf16[2,32,...) custom-call(s32[2568]{0:T(1024)S(1)} %get-tuple-element.3452.tab, ...), custom_call_target="tpu_custom_call", output_to_operand_aliasing={{5}: (10, {}), {6}: (11, {}), {7}: (12, {}), {8}: (13, {})} | custom-call | flops 40000000 | bytes 40000000 | tf_op jit(solution)/shard_map/cond/branch_1_fun/while/body/round/pallas_call | solution.py:683
  235.6 4.6 collective-permute-done.84.po1
  240.3 5.2 attend.38
  245.5 19.5 %collective-permute-done.82.rc1 = bf16[80,64,128]{2,1,0:T(8,128)(2,1)} collective-permute-done((bf16[80,64,128]{2,1,0:T(8,128)(2,1)}, bf16[80,64,128]{2,1,0:T(8,128)(2,1)}, u32[]{:S(2)}, u32[]{:S(2)}) %collective-permute-start.82) | collective-permute-done | bytes 1310752 | tf_op jit(solution)/shard_map/cond/branch_1_fun/while/body/ppermute | solution.py:680
  267.2 11.3 %round.25 = (s32[64]{0:T(128)}, bf16[80,64,128]{2,1,0:T(8,128)(2,1)}, bf16[80,64,128]{2,1,0:T(8,128)(2,1)}, bf16[2,80,64,128]{3,2,1,0:T(8,128)(2,1)}, bf16[2,32,...) custom-call(s32[2568]{0:T(1024)S(1)} %get-tuple-element.3452.tab, ...), custom_call_target="tpu_custom_call", output_to_operand_aliasing={{5}: (10, {}), {6}: (11, {}), {7}: (12, {}), {8}: (13, {})} | custom-call | flops 40000000 | bytes 40000000 | tf_op jit(solution)/shard_map/cond/branch_1_fun/while/body/round/pallas_call | solution.py:683
  281.1 4.6 collective-permute-done.90
  289.9 20.7 %collective-permute-done.87 = bf16[80,64,128]{2,1,0:T(8,128)(2,1)} collective-permute-done((bf16[80,64,128]{2,1,0:T(8,128)(2,1)}, bf16[80,64,128]{2,1,0:T(8,128)(2,1)}, u32[]{:S(2)}, u32[]{:S(2)}) %collective-permute-start.87) | collective-permute-done | bytes 1310752 | tf_op jit(solution)/shard_map/cond/branch_1_fun/while/body/ppermute | solution.py:679
  311.6 10.4 %round.24 = (s32[64]{0:T(128)}, bf16[80,64,128]{2,1,0:T(8,128)(2,1)}, bf16[80,64,128]{2,1,0:T(8,128)(2,1)}, bf16[2,80,64,128]{3,2,1,0:T(8,128)(2,1)}, bf16[2,32,...) custom-call(s32[2568]{0:T(1024)S(1)} %get-tuple-element.3452.tab, ...), custom_call_target="tpu_custom_call", output_to_operand_aliasing={{5}: (10, {}), {6}: (11, {}), {7}: (12, {}), {8}: (13, {})} | custom-call | flops 40000000 | bytes 40000000 | tf_op jit(solution)/shard_map/cond/branch_1_fun/while/body/round/pallas_call | solution.py:683
  329.3 5.2 attend.38
  334.5 19.5 %collective-permute-done.82.rc1 = bf16[80,64,128]{2,1,0:T(8,128)(2,1)} collective-permute-done((bf16[80,64,128]{2,1,0:T(8,128)(2,1)}, bf16[80,64,128]{2,1,0:T(8,128)(2,1)}, u32[]{:S(2)}, u32[]{:S(2)}) %collective-permute-start.82) | collective-permute-done | bytes 1310752 | tf_op jit(solution)/shard_map/cond/branch_1_fun/while/body/ppermute | solution.py:680
  356.2 11.1 %round.25 = (s32[64]{0:T(128)}, bf16[80,64,128]{2,1,0:T(8,128)(2,1)}, bf16[80,64,128]{2,1,0:T(8,128)(2,1)}, bf16[2,80,64,128]{3,2,1,0:T(8,128)(2,1)}, bf16[2,32,...) custom-call(s32[2568]{0:T(1024)S(1)} %get-tuple-element.3452.tab, ...), custom_call_target="tpu_custom_call", output_to_operand_aliasing={{5}: (10, {}), {6}: (11, {}), {7}: (12, {}), {8}: (13, {})} | custom-call | flops 40000000 | bytes 40000000 | tf_op jit(solution)/shard_map/cond/branch_1_fun/while/body/round/pallas_call | solution.py:683
  376.3 7.2 attend.39
  383.6 15.8 %collective-permute-done.87 = bf16[80,64,128]{2,1,0:T(8,128)(2,1)} collective-permute-done((bf16[80,64,128]{2,1,0:T(8,128)(2,1)}, bf16[80,64,128]{2,1,0:T(8,128)(2,1)}, u32[]{:S(2)}, u32[]{:S(2)}) %collective-permute-start.87) | collective-permute-done | bytes 1310752 | tf_op jit(solution)/shard_map/cond/branch_1_fun/while/body/ppermute | solution.py:679
  400.3 10.1 %round.24 = (s32[64]{0:T(128)}, bf16[80,64,128]{2,1,0:T(8,128)(2,1)}, bf16[80,64,128]{2,1,0:T(8,128)(2,1)}, bf16[2,80,64,128]{3,2,1,0:T(8,128)(2,1)}, bf16[2,32,...) custom-call(s32[2568]{0:T(1024)S(1)} %get-tuple-element.3452.tab, ...), custom_call_target="tpu_custom_call", output_to_operand_aliasing={{5}: (10, {}), {6}: (11, {}), {7}: (12, {}), {8}: (13, {})} | custom-call | flops 40000000 | bytes 40000000 | tf_op jit(solution)/shard_map/cond/branch_1_fun/while/body/round/pallas_call | solution.py:683
  417.7 7.5 attend.38
  425.2 17.3 %collective-permute-done.82.rc1 = bf16[80,64,128]{2,1,0:T(8,128)(2,1)} collective-permute-done((bf16[80,64,128]{2,1,0:T(8,128)(2,1)}, bf16[80,64,128]{2,1,0:T(8,128)(2,1)}, u32[]{:S(2)}, u32[]{:S(2)}) %collective-permute-start.82) | collective-permute-done | bytes 1310752 | tf_op jit(solution)/shard_map/cond/branch_1_fun/while/body/ppermute | solution.py:680
  444.6 10.8 %round.25 = (s32[64]{0:T(128)}, bf16[80,64,128]{2,1,0:T(8,128)(2,1)}, bf16[80,64,128]{2,1,0:T(8,128)(2,1)}, bf16[2,80,64,128]{3,2,1,0:T(8,128)(2,1)}, bf16[2,32,...) custom-call(s32[2568]{0:T(1024)S(1)} %get-tuple-element.3452.tab, ...), custom_call_target="tpu_custom_call", output_to_operand_aliasing={{5}: (10, {}), {6}: (11, {}), {7}: (12, {}), {8}: (13, {})} | custom-call | flops 40000000 | bytes 40000000 | tf_op jit(solution)/shard_map/cond/branch_1_fun/while/body/round/pallas_call | solution.py:683
  464.5 6.5 attend.39
  471.0 16.5 %collective-permute-done.87 = bf16[80,64,128]{2,1,0:T(8,128)(2,1)} collective-permute-done((bf16[80,64,128]{2,1,0:T(8,128)(2,1)}, bf16[80,64,128]{2,1,0:T(8,128)(2,1)}, u32[]{:S(2)}, u32[]{:S(2)}) %collective-permute-start.87) | collective-permute-done | bytes 1310752 | tf_op jit(solution)/shard_map/cond/branch_1_fun/while/body/ppermute | solution.py:679
  488.1 9.4 %round.24 = (s32[64]{0:T(128)}, bf16[80,64,128]{2,1,0:T(8,128)(2,1)}, bf16[80,64,128]{2,1,0:T(8,128)(2,1)}, bf16[2,80,64,128]{3,2,1,0:T(8,128)(2,1)}, bf16[2,32,...) custom-call(s32[2568]{0:T(1024)S(1)} %get-tuple-element.3452.tab, ...), custom_call_target="tpu_custom_call", output_to_operand_aliasing={{5}: (10, {}), {6}: (11, {}), {7}: (12, {}), {8}: (13, {})} | custom-call | flops 40000000 | bytes 40000000 | tf_op jit(solution)/shard_map/cond/branch_1_fun/while/body/round/pallas_call | solution.py:683
  505.4 6.2 attend.38
  511.6 18.2 %collective-permute-done.82.rc1 = bf16[80,64,128]{2,1,0:T(8,128)(2,1)} collective-permute-done((bf16[80,64,128]{2,1,0:T(8,128)(2,1)}, bf16[80,64,128]{2,1,0:T(8,128)(2,1)}, u32[]{:S(2)}, u32[]{:S(2)}) %collective-permute-start.82) | collective-permute-done | bytes 1310752 | tf_op jit(solution)/shard_map/cond/branch_1_fun/while/body/ppermute | solution.py:680
  532.2 10.5 %round.25 = (s32[64]{0:T(128)}, bf16[80,64,128]{2,1,0:T(8,128)(2,1)}, bf16[80,64,128]{2,1,0:T(8,128)(2,1)}, bf16[2,80,64,128]{3,2,1,0:T(8,128)(2,1)}, bf16[2,32,...) custom-call(s32[2568]{0:T(1024)S(1)} %get-tuple-element.3452.tab, ...), custom_call_target="tpu_custom_call", output_to_operand_aliasing={{5}: (10, {}), {6}: (11, {}), {7}: (12, {}), {8}: (13, {})} | custom-call | flops 40000000 | bytes 40000000 | tf_op jit(solution)/shard_map/cond/branch_1_fun/while/body/round/pallas_call | solution.py:683
  551.7 5.7 attend.39
  557.4 17.3 %collective-permute-done.87 = bf16[80,64,128]{2,1,0:T(8,128)(2,1)} collective-permute-done((bf16[80,64,128]{2,1,0:T(8,128)(2,1)}, bf16[80,64,128]{2,1,0:T(8,128)(2,1)}, u32[]{:S(2)}, u32[]{:S(2)}) %collective-permute-start.87) | collective-permute-done | bytes 1310752 | tf_op jit(solution)/shard_map/cond/branch_1_fun/while/body/ppermute | solution.py:679
  575.4 9.5 %round.24 = (s32[64]{0:T(128)}, bf16[80,64,128]{2,1,0:T(8,128)(2,1)}, bf16[80,64,128]{2,1,0:T(8,128)(2,1)}, bf16[2,80,64,128]{3,2,1,0:T(8,128)(2,1)}, bf16[2,32,...) custom-call(s32[2568]{0:T(1024)S(1)} %get-tuple-element.3452.tab, ...), custom_call_target="tpu_custom_call", output_to_operand_aliasing={{5}: (10, {}), {6}: (11, {}), {7}: (12, {}), {8}: (13, {})} | custom-call | flops 40000000 | bytes 40000000 | tf_op jit(solution)/shard_map/cond/branch_1_fun/while/body/round/pallas_call | solution.py:683
  592.2 7.5 attend.38
  599.7 17.2 %collective-permute-done.82.rc1 = bf16[80,64,128]{2,1,0:T(8,128)(2,1)} collective-permute-done((bf16[80,64,128]{2,1,0:T(8,128)(2,1)}, bf16[80,64,128]{2,1,0:T(8,128)(2,1)}, u32[]{:S(2)}, u32[]{:S(2)}) %collective-permute-start.82) | collective-permute-done | bytes 1310752 | tf_op jit(solution)/shard_map/cond/branch_1_fun/while/body/ppermute | solution.py:680
  619.5 10.3 %round.25 = (s32[64]{0:T(128)}, bf16[80,64,128]{2,1,0:T(8,128)(2,1)}, bf16[80,64,128]{2,1,0:T(8,128)(2,1)}, bf16[2,80,64,128]{3,2,1,0:T(8,128)(2,1)}, bf16[2,32,...) custom-call(s32[2568]{0:T(1024)S(1)} %get-tuple-element.3452.tab, ...), custom_call_target="tpu_custom_call", output_to_operand_aliasing={{5}: (10, {}), {6}: (11, {}), {7}: (12, {}), {8}: (13, {})} | custom-call | flops 40000000 | bytes 40000000 | tf_op jit(solution)/shard_map/cond/branch_1_fun/while/body/round/pallas_call | solution.py:683
  638.9 5.3 attend.39
  644.1 17.8 %collective-permute-done.87 = bf16[80,64,128]{2,1,0:T(8,128)(2,1)} collective-permute-done((bf16[80,64,128]{2,1,0:T(8,128)(2,1)}, bf16[80,64,128]{2,1,0:T(8,128)(2,1)}, u32[]{:S(2)}, u32[]{:S(2)}) %collective-permute-start.87) | collective-permute-done | bytes 1310752 | tf_op jit(solution)/shard_map/cond/branch_1_fun/while/body/ppermute | solution.py:679
  662.5 9.2 %round.24 = (s32[64]{0:T(128)}, bf16[80,64,128]{2,1,0:T(8,128)(2,1)}, bf16[80,64,128]{2,1,0:T(8,128)(2,1)}, bf16[2,80,64,128]{3,2,1,0:T(8,128)(2,1)}, bf16[2,32,...) custom-call(s32[2568]{0:T(1024)S(1)} %get-tuple-element.3452.tab, ...), custom_call_target="tpu_custom_call", output_to_operand_aliasing={{5}: (10, {}), {6}: (11, {}), {7}: (12, {}), {8}: (13, {})} | custom-call | flops 40000000 | bytes 40000000 | tf_op jit(solution)/shard_map/cond/branch_1_fun/while/body/round/pallas_call | solution.py:683
  679.0 7.2 attend.38
  686.2 17.6 %collective-permute-done.82.rc1 = bf16[80,64,128]{2,1,0:T(8,128)(2,1)} collective-permute-done((bf16[80,64,128]{2,1,0:T(8,128)(2,1)}, bf16[80,64,128]{2,1,0:T(8,128)(2,1)}, u32[]{:S(2)}, u32[]{:S(2)}) %collective-permute-start.82) | collective-permute-done | bytes 1310752 | tf_op jit(solution)/shard_map/cond/branch_1_fun/while/body/ppermute | solution.py:680
  707.0 10.6 %round.25 = (s32[64]{0:T(128)}, bf16[80,64,128]{2,1,0:T(8,128)(2,1)}, bf16[80,64,128]{2,1,0:T(8,128)(2,1)}, bf16[2,80,64,128]{3,2,1,0:T(8,128)(2,1)}, bf16[2,32,...) custom-call(s32[2568]{0:T(1024)S(1)} %get-tuple-element.3452.tab, ...), custom_call_target="tpu_custom_call", output_to_operand_aliasing={{5}: (10, {}), {6}: (11, {}), {7}: (12, {}), {8}: (13, {})} | custom-call | flops 40000000 | bytes 40000000 | tf_op jit(solution)/shard_map/cond/branch_1_fun/while/body/round/pallas_call | solution.py:683
  726.6 6.2 attend.39
  732.8 16.8 %collective-permute-done.87 = bf16[80,64,128]{2,1,0:T(8,128)(2,1)} collective-permute-done((bf16[80,64,128]{2,1,0:T(8,128)(2,1)}, bf16[80,64,128]{2,1,0:T(8,128)(2,1)}, u32[]{:S(2)}, u32[]{:S(2)}) %collective-permute-start.87) | collective-permute-done | bytes 1310752 | tf_op jit(solution)/shard_map/cond/branch_1_fun/while/body/ppermute | solution.py:679
  750.2 9.4 %round.24 = (s32[64]{0:T(128)}, bf16[80,64,128]{2,1,0:T(8,128)(2,1)}, bf16[80,64,128]{2,1,0:T(8,128)(2,1)}, bf16[2,80,64,128]{3,2,1,0:T(8,128)(2,1)}, bf16[2,32,...) custom-call(s32[2568]{0:T(1024)S(1)} %get-tuple-element.3452.tab, ...), custom_call_target="tpu_custom_call", output_to_operand_aliasing={{5}: (10, {}), {6}: (11, {}), {7}: (12, {}), {8}: (13, {})} | custom-call | flops 40000000 | bytes 40000000 | tf_op jit(solution)/shard_map/cond/branch_1_fun/while/body/round/pallas_call | solution.py:683
  767.0 6.2 attend.38
  773.2 18.5 %collective-permute-done.82.rc1 = bf16[80,64,128]{2,1,0:T(8,128)(2,1)} collective-permute-done((bf16[80,64,128]{2,1,0:T(8,128)(2,1)}, bf16[80,64,128]{2,1,0:T(8,128)(2,1)}, u32[]{:S(2)}, u32[]{:S(2)}) %collective-permute-start.82) | collective-permute-done | bytes 1310752 | tf_op jit(solution)/shard_map/cond/branch_1_fun/while/body/ppermute | solution.py:680
  793.9 9.2 %round.25 = (s32[64]{0:T(128)}, bf16[80,64,128]{2,1,0:T(8,128)(2,1)}, bf16[80,64,128]{2,1,0:T(8,128)(2,1)}, bf16[2,80,64,128]{3,2,1,0:T(8,128)(2,1)}, bf16[2,32,...) custom-call(s32[2568]{0:T(1024)S(1)} %get-tuple-element.3452.tab, ...), custom_call_target="tpu_custom_call", output_to_operand_aliasing={{5}: (10, {}), {6}: (11, {}), {7}: (12, {}), {8}: (13, {})} | custom-call | flops 40000000 | bytes 40000000 | tf_op jit(solution)/shard_map/cond/branch_1_fun/while/body/round/pallas_call | solution.py:683
  812.1 6.2 attend.39
  818.3 16.8 %collective-permute-done.87 = bf16[80,64,128]{2,1,0:T(8,128)(2,1)} collective-permute-done((bf16[80,64,128]{2,1,0:T(8,128)(2,1)}, bf16[80,64,128]{2,1,0:T(8,128)(2,1)}, u32[]{:S(2)}, u32[]{:S(2)}) %collective-permute-start.87) | collective-permute-done | bytes 1310752 | tf_op jit(solution)/shard_map/cond/branch_1_fun/while/body/ppermute | solution.py:679
  836.7 4.9 close.8
  845.9 7.3 attend.22
  (238 shorter events, 165.6 us)
Async XLA Ops:
  54.0 33.1 %collective-permute-start.80 = (bf16[2,80,64,128]{3,2,1,0:T(8,128)(2,1)}, bf16[2,80,64,128]{3,2,1,0:T(8,128)(2,1)S(1)}, u32[]{:S(2)}, u32[]{:S(2)}) collective-permute-start(bf16[2,80,64,128]{3,2,1,0:T(8,128)(2,1)} %get-tuple-element.2967), channel_id=1, source_target_pairs={{0,1},{1,0},{2,3},{3,2},{4,5},{5,4},{6,7},{7,6}} | collective-permute-start | bytes 7864328 | tf_op jit(solution)/shard_map/cond/branch_1_fun/while/body/ppermute | solution.py:689
  54.6 31.5 %collective-permute-start.82 = (bf16[80,64,128]{2,1,0:T(8,128)(2,1)}, bf16[80,64,128]{2,1,0:T(8,128)(2,1)}, u32[]{:S(2)}, u32[]{:S(2)}) collective-permute-start(bf16[80,64,128]{2,1,0:T(8,128)(2,1)} %get-tuple-element.3416), channel_id=1, source_target_pairs={{2,0},{3,1},{6,2},{7,3},{4,6},{5,7},{0,4},{1,5}} | collective-permute-start | bytes 3932168 | tf_op jit(solution)/shard_map/cond/branch_1_fun/while/body/ppermute | solution.py:680
  55.9 31.2 %collective-permute-start.81 = (bf16[80,64,128]{2,1,0:T(8,128)(2,1)}, bf16[80,64,128]{2,1,0:T(8,128)(2,1)}, u32[]{:S(2)}, u32[]{:S(2)}) collective-permute-start(bf16[80,64,128]{2,1,0:T(8,128)(2,1)} %get-tuple-element.3415), channel_id=1, source_target_pairs={{0,2},{1,3},{2,6},{3,7},{6,4},{7,5},{4,0},{5,1}} | collective-permute-start | bytes 3932168 | tf_op jit(solution)/shard_map/cond/branch_1_fun/while/body/ppermute | solution.py:679
  99.9 32.4 %collective-permute-start.86 = (bf16[2,80,64,128]{3,2,1,0:T(8,128)(2,1)}, bf16[2,80,64,128]{3,2,1,0:T(8,128)(2,1)S(1)}, u32[]{:S(2)}, u32[]{:S(2)}) collective-permute-start(bf16[2,80,64,128]{3,2,1,0:T(8,128)(2,1)} %get-tuple-element.2984), channel_id=1, source_target_pairs={{0,1},{1,0},{2,3},{3,2},{4,5},{5,4},{6,7},{7,6}} | collective-permute-start | bytes 7864328 | tf_op jit(solution)/shard_map/cond/branch_1_fun/while/body/ppermute | solution.py:689
  100.5 31.5 %collective-permute-start.87 = (bf16[80,64,128]{2,1,0:T(8,128)(2,1)}, bf16[80,64,128]{2,1,0:T(8,128)(2,1)}, u32[]{:S(2)}, u32[]{:S(2)}) collective-permute-start(bf16[80,64,128]{2,1,0:T(8,128)(2,1)} %get-tuple-element.2985), channel_id=1, source_target_pairs={{0,2},{1,3},{2,6},{3,7},{6,4},{7,5},{4,0},{5,1}} | collective-permute-start | bytes 3932168 | tf_op jit(solution)/shard_map/cond/branch_1_fun/while/body/ppermute | solution.py:679
  100.9 31.4 %collective-permute-start.88 = (bf16[80,64,128]{2,1,0:T(8,128)(2,1)}, bf16[80,64,128]{2,1,0:T(8,128)(2,1)}, u32[]{:S(2)}, u32[]{:S(2)}) collective-permute-start(bf16[80,64,128]{2,1,0:T(8,128)(2,1)} %get-tuple-element.2986), channel_id=1, source_target_pairs={{2,0},{3,1},{6,2},{7,3},{4,6},{5,7},{0,4},{1,5}} | collective-permute-start | bytes 3932168 | tf_op jit(solution)/shard_map/cond/branch_1_fun/while/body/ppermute | solution.py:680
  107.1 25.2 %collective-permute-start.91 = (bf16[2,32,64,128]{3,2,1,0:T(8,128)(2,1)}, bf16[2,32,64,128]{3,2,1,0:T(8,128)(2,1)}, u32[]{:S(2)}, u32[]{:S(2)}) collective-permute-start(bf16[2,32,64,128]{3,2,1,0:T(8,128)(2,1)} %get-tuple-element.2987), channel_id=1, source_target_pairs={{0,1},{1,0},{2,3},{3,2},{4,5},{5,4},{6,7},{7,6}} | collective-permute-start | bytes 3145736 | tf_op jit(solution)/shard_map/cond/branch_1_fun/while/body/ppermute | solution.py:690
  143.6 32.8 %collective-permute-start.80 = (bf16[2,80,64,128]{3,2,1,0:T(8,128)(2,1)}, bf16[2,80,64,128]{3,2,1,0:T(8,128)(2,1)S(1)}, u32[]{:S(2)}, u32[]{:S(2)}) collective-permute-start(bf16[2,80,64,128]{3,2,1,0:T(8,128)(2,1)} %get-tuple-element.2967), channel_id=1, source_target_pairs={{0,1},{1,0},{2,3},{3,2},{4,5},{5,4},{6,7},{7,6}} | collective-permute-start | bytes 7864328 | tf_op jit(solution)/shard_map/cond/branch_1_fun/while/body/ppermute | solution.py:689
  144.1 31.5 %collective-permute-start.82 = (bf16[80,64,128]{2,1,0:T(8,128)(2,1)}, bf16[80,64,128]{2,1,0:T(8,128)(2,1)}, u32[]{:S(2)}, u32[]{:S(2)}) collective-permute-start(bf16[80,64,128]{2,1,0:T(8,128)(2,1)} %get-tuple-element.3416), channel_id=1, source_target_pairs={{2,0},{3,1},{6,2},{7,3},{4,6},{5,7},{0,4},{1,5}} | collective-permute-start | bytes 3932168 | tf_op jit(solution)/shard_map/cond/branch_1_fun/while/body/ppermute | solution.py:680
  145.2 31.2 %collective-permute-start.81 = (bf16[80,64,128]{2,1,0:T(8,128)(2,1)}, bf16[80,64,128]{2,1,0:T(8,128)(2,1)}, u32[]{:S(2)}, u32[]{:S(2)}) collective-permute-start(bf16[80,64,128]{2,1,0:T(8,128)(2,1)} %get-tuple-element.3415), channel_id=1, source_target_pairs={{0,2},{1,3},{2,6},{3,7},{6,4},{7,5},{4,0},{5,1}} | collective-permute-start | bytes 3932168 | tf_op jit(solution)/shard_map/cond/branch_1_fun/while/body/ppermute | solution.py:679
  189.5 32.1 %collective-permute-start.86 = (bf16[2,80,64,128]{3,2,1,0:T(8,128)(2,1)}, bf16[2,80,64,128]{3,2,1,0:T(8,128)(2,1)S(1)}, u32[]{:S(2)}, u32[]{:S(2)}) collective-permute-start(bf16[2,80,64,128]{3,2,1,0:T(8,128)(2,1)} %get-tuple-element.2984), channel_id=1, source_target_pairs={{0,1},{1,0},{2,3},{3,2},{4,5},{5,4},{6,7},{7,6}} | collective-permute-start | bytes 7864328 | tf_op jit(solution)/shard_map/cond/branch_1_fun/while/body/ppermute | solution.py:689
  190.1 31.5 %collective-permute-start.87 = (bf16[80,64,128]{2,1,0:T(8,128)(2,1)}, bf16[80,64,128]{2,1,0:T(8,128)(2,1)}, u32[]{:S(2)}, u32[]{:S(2)}) collective-permute-start(bf16[80,64,128]{2,1,0:T(8,128)(2,1)} %get-tuple-element.2985), channel_id=1, source_target_pairs={{0,2},{1,3},{2,6},{3,7},{6,4},{7,5},{4,0},{5,1}} | collective-permute-start | bytes 3932168 | tf_op jit(solution)/shard_map/cond/branch_1_fun/while/body/ppermute | solution.py:679
  190.4 31.2 %collective-permute-start.88 = (bf16[80,64,128]{2,1,0:T(8,128)(2,1)}, bf16[80,64,128]{2,1,0:T(8,128)(2,1)}, u32[]{:S(2)}, u32[]{:S(2)}) collective-permute-start(bf16[80,64,128]{2,1,0:T(8,128)(2,1)} %get-tuple-element.2986), channel_id=1, source_target_pairs={{2,0},{3,1},{6,2},{7,3},{4,6},{5,7},{0,4},{1,5}} | collective-permute-start | bytes 3932168 | tf_op jit(solution)/shard_map/cond/branch_1_fun/while/body/ppermute | solution.py:680
  196.6 25.0 %collective-permute-start.91 = (bf16[2,32,64,128]{3,2,1,0:T(8,128)(2,1)}, bf16[2,32,64,128]{3,2,1,0:T(8,128)(2,1)}, u32[]{:S(2)}, u32[]{:S(2)}) collective-permute-start(bf16[2,32,64,128]{3,2,1,0:T(8,128)(2,1)} %get-tuple-element.2987), channel_id=1, source_target_pairs={{0,1},{1,0},{2,3},{3,2},{4,5},{5,4},{6,7},{7,6}} | collective-permute-start | bytes 3145736 | tf_op jit(solution)/shard_map/cond/branch_1_fun/while/body/ppermute | solution.py:690
  233.0 32.7 %collective-permute-start.80 = (bf16[2,80,64,128]{3,2,1,0:T(8,128)(2,1)}, bf16[2,80,64,128]{3,2,1,0:T(8,128)(2,1)S(1)}, u32[]{:S(2)}, u32[]{:S(2)}) collective-permute-start(bf16[2,80,64,128]{3,2,1,0:T(8,128)(2,1)} %get-tuple-element.2967), channel_id=1, source_target_pairs={{0,1},{1,0},{2,3},{3,2},{4,5},{5,4},{6,7},{7,6}} | collective-permute-start | bytes 7864328 | tf_op jit(solution)/shard_map/cond/branch_1_fun/while/body/ppermute | solution.py:689
  233.6 31.5 %collective-permute-start.82 = (bf16[80,64,128]{2,1,0:T(8,128)(2,1)}, bf16[80,64,128]{2,1,0:T(8,128)(2,1)}, u32[]{:S(2)}, u32[]{:S(2)}) collective-permute-start(bf16[80,64,128]{2,1,0:T(8,128)(2,1)} %get-tuple-element.3416), channel_id=1, source_target_pairs={{2,0},{3,1},{6,2},{7,3},{4,6},{5,7},{0,4},{1,5}} | collective-permute-start | bytes 3932168 | tf_op jit(solution)/shard_map/cond/branch_1_fun/while/body/ppermute | solution.py:680
  234.5 31.2 %collective-permute-start.81 = (bf16[80,64,128]{2,1,0:T(8,128)(2,1)}, bf16[80,64,128]{2,1,0:T(8,128)(2,1)}, u32[]{:S(2)}, u32[]{:S(2)}) collective-permute-start(bf16[80,64,128]{2,1,0:T(8,128)(2,1)} %get-tuple-element.3415), channel_id=1, source_target_pairs={{0,2},{1,3},{2,6},{3,7},{6,4},{7,5},{4,0},{5,1}} | collective-permute-start | bytes 3932168 | tf_op jit(solution)/shard_map/cond/branch_1_fun/while/body/ppermute | solution.py:679
  278.5 32.5 %collective-permute-start.86 = (bf16[2,80,64,128]{3,2,1,0:T(8,128)(2,1)}, bf16[2,80,64,128]{3,2,1,0:T(8,128)(2,1)S(1)}, u32[]{:S(2)}, u32[]{:S(2)}) collective-permute-start(bf16[2,80,64,128]{3,2,1,0:T(8,128)(2,1)} %get-tuple-element.2984), channel_id=1, source_target_pairs={{0,1},{1,0},{2,3},{3,2},{4,5},{5,4},{6,7},{7,6}} | collective-permute-start | bytes 7864328 | tf_op jit(solution)/shard_map/cond/branch_1_fun/while/body/ppermute | solution.py:689
  279.1 31.5 %collective-permute-start.87 = (bf16[80,64,128]{2,1,0:T(8,128)(2,1)}, bf16[80,64,128]{2,1,0:T(8,128)(2,1)}, u32[]{:S(2)}, u32[]{:S(2)}) collective-permute-start(bf16[80,64,128]{2,1,0:T(8,128)(2,1)} %get-tuple-element.2985), channel_id=1, source_target_pairs={{0,2},{1,3},{2,6},{3,7},{6,4},{7,5},{4,0},{5,1}} | collective-permute-start | bytes 3932168 | tf_op jit(solution)/shard_map/cond/branch_1_fun/while/body/ppermute | solution.py:679
  279.8 31.2 %collective-permute-start.88 = (bf16[80,64,128]{2,1,0:T(8,128)(2,1)}, bf16[80,64,128]{2,1,0:T(8,128)(2,1)}, u32[]{:S(2)}, u32[]{:S(2)}) collective-permute-start(bf16[80,64,128]{2,1,0:T(8,128)(2,1)} %get-tuple-element.2986), channel_id=1, source_target_pairs={{2,0},{3,1},{6,2},{7,3},{4,6},{5,7},{0,4},{1,5}} | collective-permute-start | bytes 3932168 | tf_op jit(solution)/shard_map/cond/branch_1_fun/while/body/ppermute | solution.py:680
  285.7 25.4 %collective-permute-start.91 = (bf16[2,32,64,128]{3,2,1,0:T(8,128)(2,1)}, bf16[2,32,64,128]{3,2,1,0:T(8,128)(2,1)}, u32[]{:S(2)}, u32[]{:S(2)}) collective-permute-start(bf16[2,32,64,128]{3,2,1,0:T(8,128)(2,1)} %get-tuple-element.2987), channel_id=1, source_target_pairs={{0,1},{1,0},{2,3},{3,2},{4,5},{5,4},{6,7},{7,6}} | collective-permute-start | bytes 3145736 | tf_op jit(solution)/shard_map/cond/branch_1_fun/while/body/ppermute | solution.py:690
  322.0 32.7 %collective-permute-start.80 = (bf16[2,80,64,128]{3,2,1,0:T(8,128)(2,1)}, bf16[2,80,64,128]{3,2,1,0:T(8,128)(2,1)S(1)}, u32[]{:S(2)}, u32[]{:S(2)}) collective-permute-start(bf16[2,80,64,128]{3,2,1,0:T(8,128)(2,1)} %get-tuple-element.2967), channel_id=1, source_target_pairs={{0,1},{1,0},{2,3},{3,2},{4,5},{5,4},{6,7},{7,6}} | collective-permute-start | bytes 7864328 | tf_op jit(solution)/shard_map/cond/branch_1_fun/while/body/ppermute | solution.py:689
  322.6 31.5 %collective-permute-start.82 = (bf16[80,64,128]{2,1,0:T(8,128)(2,1)}, bf16[80,64,128]{2,1,0:T(8,128)(2,1)}, u32[]{:S(2)}, u32[]{:S(2)}) collective-permute-start(bf16[80,64,128]{2,1,0:T(8,128)(2,1)} %get-tuple-element.3416), channel_id=1, source_target_pairs={{2,0},{3,1},{6,2},{7,3},{4,6},{5,7},{0,4},{1,5}} | collective-permute-start | bytes 3932168 | tf_op jit(solution)/shard_map/cond/branch_1_fun/while/body/ppermute | solution.py:680
  323.5 31.2 %collective-permute-start.81 = (bf16[80,64,128]{2,1,0:T(8,128)(2,1)}, bf16[80,64,128]{2,1,0:T(8,128)(2,1)}, u32[]{:S(2)}, u32[]{:S(2)}) collective-permute-start(bf16[80,64,128]{2,1,0:T(8,128)(2,1)} %get-tuple-element.3415), channel_id=1, source_target_pairs={{0,2},{1,3},{2,6},{3,7},{6,4},{7,5},{4,0},{5,1}} | collective-permute-start | bytes 3932168 | tf_op jit(solution)/shard_map/cond/branch_1_fun/while/body/ppermute | solution.py:679
  367.3 32.4 %collective-permute-start.86 = (bf16[2,80,64,128]{3,2,1,0:T(8,128)(2,1)}, bf16[2,80,64,128]{3,2,1,0:T(8,128)(2,1)S(1)}, u32[]{:S(2)}, u32[]{:S(2)}) collective-permute-start(bf16[2,80,64,128]{3,2,1,0:T(8,128)(2,1)} %get-tuple-element.2984), channel_id=1, source_target_pairs={{0,1},{1,0},{2,3},{3,2},{4,5},{5,4},{6,7},{7,6}} | collective-permute-start | bytes 7864328 | tf_op jit(solution)/shard_map/cond/branch_1_fun/while/body/ppermute | solution.py:689
  367.9 31.5 %collective-permute-start.87 = (bf16[80,64,128]{2,1,0:T(8,128)(2,1)}, bf16[80,64,128]{2,1,0:T(8,128)(2,1)}, u32[]{:S(2)}, u32[]{:S(2)}) collective-permute-start(bf16[80,64,128]{2,1,0:T(8,128)(2,1)} %get-tuple-element.2985), channel_id=1, source_target_pairs={{0,2},{1,3},{2,6},{3,7},{6,4},{7,5},{4,0},{5,1}} | collective-permute-start | bytes 3932168 | tf_op jit(solution)/shard_map/cond/branch_1_fun/while/body/ppermute | solution.py:679
  368.5 31.2 %collective-permute-start.88 = (bf16[80,64,128]{2,1,0:T(8,128)(2,1)}, bf16[80,64,128]{2,1,0:T(8,128)(2,1)}, u32[]{:S(2)}, u32[]{:S(2)}) collective-permute-start(bf16[80,64,128]{2,1,0:T(8,128)(2,1)} %get-tuple-element.2986), channel_id=1, source_target_pairs={{2,0},{3,1},{6,2},{7,3},{4,6},{5,7},{0,4},{1,5}} | collective-permute-start | bytes 3932168 | tf_op jit(solution)/shard_map/cond/branch_1_fun/while/body/ppermute | solution.py:680
  374.5 25.2 %collective-permute-start.91 = (bf16[2,32,64,128]{3,2,1,0:T(8,128)(2,1)}, bf16[2,32,64,128]{3,2,1,0:T(8,128)(2,1)}, u32[]{:S(2)}, u32[]{:S(2)}) collective-permute-start(bf16[2,32,64,128]{3,2,1,0:T(8,128)(2,1)} %get-tuple-element.2987), channel_id=1, source_target_pairs={{0,1},{1,0},{2,3},{3,2},{4,5},{5,4},{6,7},{7,6}} | collective-permute-start | bytes 3145736 | tf_op jit(solution)/shard_map/cond/branch_1_fun/while/body/ppermute | solution.py:690
  410.4 32.7 %collective-permute-start.80 = (bf16[2,80,64,128]{3,2,1,0:T(8,128)(2,1)}, bf16[2,80,64,128]{3,2,1,0:T(8,128)(2,1)S(1)}, u32[]{:S(2)}, u32[]{:S(2)}) collective-permute-start(bf16[2,80,64,128]{3,2,1,0:T(8,128)(2,1)} %get-tuple-element.2967), channel_id=1, source_target_pairs={{0,1},{1,0},{2,3},{3,2},{4,5},{5,4},{6,7},{7,6}} | collective-permute-start | bytes 7864328 | tf_op jit(solution)/shard_map/cond/branch_1_fun/while/body/ppermute | solution.py:689
  411.0 31.5 %collective-permute-start.82 = (bf16[80,64,128]{2,1,0:T(8,128)(2,1)}, bf16[80,64,128]{2,1,0:T(8,128)(2,1)}, u32[]{:S(2)}, u32[]{:S(2)}) collective-permute-start(bf16[80,64,128]{2,1,0:T(8,128)(2,1)} %get-tuple-element.3416), channel_id=1, source_target_pairs={{2,0},{3,1},{6,2},{7,3},{4,6},{5,7},{0,4},{1,5}} | collective-permute-start | bytes 3932168 | tf_op jit(solution)/shard_map/cond/branch_1_fun/while/body/ppermute | solution.py:680
  411.9 31.2 %collective-permute-start.81 = (bf16[80,64,128]{2,1,0:T(8,128)(2,1)}, bf16[80,64,128]{2,1,0:T(8,128)(2,1)}, u32[]{:S(2)}, u32[]{:S(2)}) collective-permute-start(bf16[80,64,128]{2,1,0:T(8,128)(2,1)} %get-tuple-element.3415), channel_id=1, source_target_pairs={{0,2},{1,3},{2,6},{3,7},{6,4},{7,5},{4,0},{5,1}} | collective-permute-start | bytes 3932168 | tf_op jit(solution)/shard_map/cond/branch_1_fun/while/body/ppermute | solution.py:679
  455.4 32.0 %collective-permute-start.86 = (bf16[2,80,64,128]{3,2,1,0:T(8,128)(2,1)}, bf16[2,80,64,128]{3,2,1,0:T(8,128)(2,1)S(1)}, u32[]{:S(2)}, u32[]{:S(2)}) collective-permute-start(bf16[2,80,64,128]{3,2,1,0:T(8,128)(2,1)} %get-tuple-element.2984), channel_id=1, source_target_pairs={{0,1},{1,0},{2,3},{3,2},{4,5},{5,4},{6,7},{7,6}} | collective-permute-start | bytes 7864328 | tf_op jit(solution)/shard_map/cond/branch_1_fun/while/body/ppermute | solution.py:689
  456.1 31.4 %collective-permute-start.87 = (bf16[80,64,128]{2,1,0:T(8,128)(2,1)}, bf16[80,64,128]{2,1,0:T(8,128)(2,1)}, u32[]{:S(2)}, u32[]{:S(2)}) collective-permute-start(bf16[80,64,128]{2,1,0:T(8,128)(2,1)} %get-tuple-element.2985), channel_id=1, source_target_pairs={{0,2},{1,3},{2,6},{3,7},{6,4},{7,5},{4,0},{5,1}} | collective-permute-start | bytes 3932168 | tf_op jit(solution)/shard_map/cond/branch_1_fun/while/body/ppermute | solution.py:679
  456.6 30.9 %collective-permute-start.88 = (bf16[80,64,128]{2,1,0:T(8,128)(2,1)}, bf16[80,64,128]{2,1,0:T(8,128)(2,1)}, u32[]{:S(2)}, u32[]{:S(2)}) collective-permute-start(bf16[80,64,128]{2,1,0:T(8,128)(2,1)} %get-tuple-element.2986), channel_id=1, source_target_pairs={{2,0},{3,1},{6,2},{7,3},{4,6},{5,7},{0,4},{1,5}} | collective-permute-start | bytes 3932168 | tf_op jit(solution)/shard_map/cond/branch_1_fun/while/body/ppermute | solution.py:680
  462.6 24.9 %collective-permute-start.91 = (bf16[2,32,64,128]{3,2,1,0:T(8,128)(2,1)}, bf16[2,32,64,128]{3,2,1,0:T(8,128)(2,1)}, u32[]{:S(2)}, u32[]{:S(2)}) collective-permute-start(bf16[2,32,64,128]{3,2,1,0:T(8,128)(2,1)} %get-tuple-element.2987), channel_id=1, source_target_pairs={{0,1},{1,0},{2,3},{3,2},{4,5},{5,4},{6,7},{7,6}} | collective-permute-start | bytes 3145736 | tf_op jit(solution)/shard_map/cond/branch_1_fun/while/body/ppermute | solution.py:690
  497.5 33.1 %collective-permute-start.80 = (bf16[2,80,64,128]{3,2,1,0:T(8,128)(2,1)}, bf16[2,80,64,128]{3,2,1,0:T(8,128)(2,1)S(1)}, u32[]{:S(2)}, u32[]{:S(2)}) collective-permute-start(bf16[2,80,64,128]{3,2,1,0:T(8,128)(2,1)} %get-tuple-element.2967), channel_id=1, source_target_pairs={{0,1},{1,0},{2,3},{3,2},{4,5},{5,4},{6,7},{7,6}} | collective-permute-start | bytes 7864328 | tf_op jit(solution)/shard_map/cond/branch_1_fun/while/body/ppermute | solution.py:689
  498.8 31.0 %collective-permute-start.82 = (bf16[80,64,128]{2,1,0:T(8,128)(2,1)}, bf16[80,64,128]{2,1,0:T(8,128)(2,1)}, u32[]{:S(2)}, u32[]{:S(2)}) collective-permute-start(bf16[80,64,128]{2,1,0:T(8,128)(2,1)} %get-tuple-element.3416), channel_id=1, source_target_pairs={{2,0},{3,1},{6,2},{7,3},{4,6},{5,7},{0,4},{1,5}} | collective-permute-start | bytes 3932168 | tf_op jit(solution)/shard_map/cond/branch_1_fun/while/body/ppermute | solution.py:680
  499.4 31.2 %collective-permute-start.81 = (bf16[80,64,128]{2,1,0:T(8,128)(2,1)}, bf16[80,64,128]{2,1,0:T(8,128)(2,1)}, u32[]{:S(2)}, u32[]{:S(2)}) collective-permute-start(bf16[80,64,128]{2,1,0:T(8,128)(2,1)} %get-tuple-element.3415), channel_id=1, source_target_pairs={{0,2},{1,3},{2,6},{3,7},{6,4},{7,5},{4,0},{5,1}} | collective-permute-start | bytes 3932168 | tf_op jit(solution)/shard_map/cond/branch_1_fun/while/body/ppermute | solution.py:679
  542.7 32.0 %collective-permute-start.86 = (bf16[2,80,64,128]{3,2,1,0:T(8,128)(2,1)}, bf16[2,80,64,128]{3,2,1,0:T(8,128)(2,1)S(1)}, u32[]{:S(2)}, u32[]{:S(2)}) collective-permute-start(bf16[2,80,64,128]{3,2,1,0:T(8,128)(2,1)} %get-tuple-element.2984), channel_id=1, source_target_pairs={{0,1},{1,0},{2,3},{3,2},{4,5},{5,4},{6,7},{7,6}} | collective-permute-start | bytes 7864328 | tf_op jit(solution)/shard_map/cond/branch_1_fun/while/body/ppermute | solution.py:689
  543.3 31.5 %collective-permute-start.87 = (bf16[80,64,128]{2,1,0:T(8,128)(2,1)}, bf16[80,64,128]{2,1,0:T(8,128)(2,1)}, u32[]{:S(2)}, u32[]{:S(2)}) collective-permute-start(bf16[80,64,128]{2,1,0:T(8,128)(2,1)} %get-tuple-element.2985), channel_id=1, source_target_pairs={{0,2},{1,3},{2,6},{3,7},{6,4},{7,5},{4,0},{5,1}} | collective-permute-start | bytes 3932168 | tf_op jit(solution)/shard_map/cond/branch_1_fun/while/body/ppermute | solution.py:679
  543.6 31.2 %collective-permute-start.88 = (bf16[80,64,128]{2,1,0:T(8,128)(2,1)}, bf16[80,64,128]{2,1,0:T(8,128)(2,1)}, u32[]{:S(2)}, u32[]{:S(2)}) collective-permute-start(bf16[80,64,128]{2,1,0:T(8,128)(2,1)} %get-tuple-element.2986), channel_id=1, source_target_pairs={{2,0},{3,1},{6,2},{7,3},{4,6},{5,7},{0,4},{1,5}} | collective-permute-start | bytes 3932168 | tf_op jit(solution)/shard_map/cond/branch_1_fun/while/body/ppermute | solution.py:680
  549.9 24.9 %collective-permute-start.91 = (bf16[2,32,64,128]{3,2,1,0:T(8,128)(2,1)}, bf16[2,32,64,128]{3,2,1,0:T(8,128)(2,1)}, u32[]{:S(2)}, u32[]{:S(2)}) collective-permute-start(bf16[2,32,64,128]{3,2,1,0:T(8,128)(2,1)} %get-tuple-element.2987), channel_id=1, source_target_pairs={{0,1},{1,0},{2,3},{3,2},{4,5},{5,4},{6,7},{7,6}} | collective-permute-start | bytes 3145736 | tf_op jit(solution)/shard_map/cond/branch_1_fun/while/body/ppermute | solution.py:690
  584.9 33.1 %collective-permute-start.80 = (bf16[2,80,64,128]{3,2,1,0:T(8,128)(2,1)}, bf16[2,80,64,128]{3,2,1,0:T(8,128)(2,1)S(1)}, u32[]{:S(2)}, u32[]{:S(2)}) collective-permute-start(bf16[2,80,64,128]{3,2,1,0:T(8,128)(2,1)} %get-tuple-element.2967), channel_id=1, source_target_pairs={{0,1},{1,0},{2,3},{3,2},{4,5},{5,4},{6,7},{7,6}} | collective-permute-start | bytes 7864328 | tf_op jit(solution)/shard_map/cond/branch_1_fun/while/body/ppermute | solution.py:689
  585.4 14.3 %collective-permute-start.83 = (bf16[80,64,128]{2,1,0:T(8,128)(2,1)}, bf16[80,64,128]{2,1,0:T(8,128)(2,1)}, u32[]{:S(2)}, u32[]{:S(2)}) collective-permute-start(bf16[80,64,128]{2,1,0:T(8,128)(2,1)} %get-tuple-element.3418.rc0), channel_id=1, source_target_pairs={{0,1},{1,0},{2,3},{3,2},{4,5},{5,4},{6,7},{7,6}} | collective-permute-start | bytes 3932168 | tf_op jit(solution)/shard_map/cond/branch_1_fun/while/body/ppermute | solution.py:681
  585.5 31.5 %collective-permute-start.82 = (bf16[80,64,128]{2,1,0:T(8,128)(2,1)}, bf16[80,64,128]{2,1,0:T(8,128)(2,1)}, u32[]{:S(2)}, u32[]{:S(2)}) collective-permute-start(bf16[80,64,128]{2,1,0:T(8,128)(2,1)} %get-tuple-element.3416), channel_id=1, source_target_pairs={{2,0},{3,1},{6,2},{7,3},{4,6},{5,7},{0,4},{1,5}} | collective-permute-start | bytes 3932168 | tf_op jit(solution)/shard_map/cond/branch_1_fun/while/body/ppermute | solution.py:680
  587.2 30.8 %collective-permute-start.81 = (bf16[80,64,128]{2,1,0:T(8,128)(2,1)}, bf16[80,64,128]{2,1,0:T(8,128)(2,1)}, u32[]{:S(2)}, u32[]{:S(2)}) collective-permute-start(bf16[80,64,128]{2,1,0:T(8,128)(2,1)} %get-tuple-element.3415), channel_id=1, source_target_pairs={{0,2},{1,3},{2,6},{3,7},{6,4},{7,5},{4,0},{5,1}} | collective-permute-start | bytes 3932168 | tf_op jit(solution)/shard_map/cond/branch_1_fun/while/body/ppermute | solution.py:679
  629.9 32.0 %collective-permute-start.86 = (bf16[2,80,64,128]{3,2,1,0:T(8,128)(2,1)}, bf16[2,80,64,128]{3,2,1,0:T(8,128)(2,1)S(1)}, u32[]{:S(2)}, u32[]{:S(2)}) collective-permute-start(bf16[2,80,64,128]{3,2,1,0:T(8,128)(2,1)} %get-tuple-element.2984), channel_id=1, source_target_pairs={{0,1},{1,0},{2,3},{3,2},{4,5},{5,4},{6,7},{7,6}} | collective-permute-start | bytes 7864328 | tf_op jit(solution)/shard_map/cond/branch_1_fun/while/body/ppermute | solution.py:689
  630.4 31.5 %collective-permute-start.87 = (bf16[80,64,128]{2,1,0:T(8,128)(2,1)}, bf16[80,64,128]{2,1,0:T(8,128)(2,1)}, u32[]{:S(2)}, u32[]{:S(2)}) collective-permute-start(bf16[80,64,128]{2,1,0:T(8,128)(2,1)} %get-tuple-element.2985), channel_id=1, source_target_pairs={{0,2},{1,3},{2,6},{3,7},{6,4},{7,5},{4,0},{5,1}} | collective-permute-start | bytes 3932168 | tf_op jit(solution)/shard_map/cond/branch_1_fun/while/body/ppermute | solution.py:679
  630.8 31.1 %collective-permute-start.88 = (bf16[80,64,128]{2,1,0:T(8,128)(2,1)}, bf16[80,64,128]{2,1,0:T(8,128)(2,1)}, u32[]{:S(2)}, u32[]{:S(2)}) collective-permute-start(bf16[80,64,128]{2,1,0:T(8,128)(2,1)} %get-tuple-element.2986), channel_id=1, source_target_pairs={{2,0},{3,1},{6,2},{7,3},{4,6},{5,7},{0,4},{1,5}} | collective-permute-start | bytes 3932168 | tf_op jit(solution)/shard_map/cond/branch_1_fun/while/body/ppermute | solution.py:680
  637.0 24.9 %collective-permute-start.91 = (bf16[2,32,64,128]{3,2,1,0:T(8,128)(2,1)}, bf16[2,32,64,128]{3,2,1,0:T(8,128)(2,1)}, u32[]{:S(2)}, u32[]{:S(2)}) collective-permute-start(bf16[2,32,64,128]{3,2,1,0:T(8,128)(2,1)} %get-tuple-element.2987), channel_id=1, source_target_pairs={{0,1},{1,0},{2,3},{3,2},{4,5},{5,4},{6,7},{7,6}} | collective-permute-start | bytes 3145736 | tf_op jit(solution)/shard_map/cond/branch_1_fun/while/body/ppermute | solution.py:690
  671.8 33.7 %collective-permute-start.80 = (bf16[2,80,64,128]{3,2,1,0:T(8,128)(2,1)}, bf16[2,80,64,128]{3,2,1,0:T(8,128)(2,1)S(1)}, u32[]{:S(2)}, u32[]{:S(2)}) collective-permute-start(bf16[2,80,64,128]{3,2,1,0:T(8,128)(2,1)} %get-tuple-element.2967), channel_id=1, source_target_pairs={{0,1},{1,0},{2,3},{3,2},{4,5},{5,4},{6,7},{7,6}} | collective-permute-start | bytes 7864328 | tf_op jit(solution)/shard_map/cond/branch_1_fun/while/body/ppermute | solution.py:689
  672.3 31.5 %collective-permute-start.82 = (bf16[80,64,128]{2,1,0:T(8,128)(2,1)}, bf16[80,64,128]{2,1,0:T(8,128)(2,1)}, u32[]{:S(2)}, u32[]{:S(2)}) collective-permute-start(bf16[80,64,128]{2,1,0:T(8,128)(2,1)} %get-tuple-element.3416), channel_id=1, source_target_pairs={{2,0},{3,1},{6,2},{7,3},{4,6},{5,7},{0,4},{1,5}} | collective-permute-start | bytes 3932168 | tf_op jit(solution)/shard_map/cond/branch_1_fun/while/body/ppermute | solution.py:680
  674.2 31.2 %collective-permute-start.81 = (bf16[80,64,128]{2,1,0:T(8,128)(2,1)}, bf16[80,64,128]{2,1,0:T(8,128)(2,1)}, u32[]{:S(2)}, u32[]{:S(2)}) collective-permute-start(bf16[80,64,128]{2,1,0:T(8,128)(2,1)} %get-tuple-element.3415), channel_id=1, source_target_pairs={{0,2},{1,3},{2,6},{3,7},{6,4},{7,5},{4,0},{5,1}} | collective-permute-start | bytes 3932168 | tf_op jit(solution)/shard_map/cond/branch_1_fun/while/body/ppermute | solution.py:679
  717.6 32.0 %collective-permute-start.86 = (bf16[2,80,64,128]{3,2,1,0:T(8,128)(2,1)}, bf16[2,80,64,128]{3,2,1,0:T(8,128)(2,1)S(1)}, u32[]{:S(2)}, u32[]{:S(2)}) collective-permute-start(bf16[2,80,64,128]{3,2,1,0:T(8,128)(2,1)} %get-tuple-element.2984), channel_id=1, source_target_pairs={{0,1},{1,0},{2,3},{3,2},{4,5},{5,4},{6,7},{7,6}} | collective-permute-start | bytes 7864328 | tf_op jit(solution)/shard_map/cond/branch_1_fun/while/body/ppermute | solution.py:689
  718.1 31.5 %collective-permute-start.87 = (bf16[80,64,128]{2,1,0:T(8,128)(2,1)}, bf16[80,64,128]{2,1,0:T(8,128)(2,1)}, u32[]{:S(2)}, u32[]{:S(2)}) collective-permute-start(bf16[80,64,128]{2,1,0:T(8,128)(2,1)} %get-tuple-element.2985), channel_id=1, source_target_pairs={{0,2},{1,3},{2,6},{3,7},{6,4},{7,5},{4,0},{5,1}} | collective-permute-start | bytes 3932168 | tf_op jit(solution)/shard_map/cond/branch_1_fun/while/body/ppermute | solution.py:679
  718.1 31.5 %collective-permute-start.88 = (bf16[80,64,128]{2,1,0:T(8,128)(2,1)}, bf16[80,64,128]{2,1,0:T(8,128)(2,1)}, u32[]{:S(2)}, u32[]{:S(2)}) collective-permute-start(bf16[80,64,128]{2,1,0:T(8,128)(2,1)} %get-tuple-element.2986), channel_id=1, source_target_pairs={{2,0},{3,1},{6,2},{7,3},{4,6},{5,7},{0,4},{1,5}} | collective-permute-start | bytes 3932168 | tf_op jit(solution)/shard_map/cond/branch_1_fun/while/body/ppermute | solution.py:680
  724.7 24.9 %collective-permute-start.91 = (bf16[2,32,64,128]{3,2,1,0:T(8,128)(2,1)}, bf16[2,32,64,128]{3,2,1,0:T(8,128)(2,1)}, u32[]{:S(2)}, u32[]{:S(2)}) collective-permute-start(bf16[2,32,64,128]{3,2,1,0:T(8,128)(2,1)} %get-tuple-element.2987), channel_id=1, source_target_pairs={{0,1},{1,0},{2,3},{3,2},{4,5},{5,4},{6,7},{7,6}} | collective-permute-start | bytes 3145736 | tf_op jit(solution)/shard_map/cond/branch_1_fun/while/body/ppermute | solution.py:690
  759.7 32.7 %collective-permute-start.80 = (bf16[2,80,64,128]{3,2,1,0:T(8,128)(2,1)}, bf16[2,80,64,128]{3,2,1,0:T(8,128)(2,1)S(1)}, u32[]{:S(2)}, u32[]{:S(2)}) collective-permute-start(bf16[2,80,64,128]{3,2,1,0:T(8,128)(2,1)} %get-tuple-element.2967), channel_id=1, source_target_pairs={{0,1},{1,0},{2,3},{3,2},{4,5},{5,4},{6,7},{7,6}} | collective-permute-start | bytes 7864328 | tf_op jit(solution)/shard_map/cond/branch_1_fun/while/body/ppermute | solution.py:689
  760.2 31.5 %collective-permute-start.82 = (bf16[80,64,128]{2,1,0:T(8,128)(2,1)}, bf16[80,64,128]{2,1,0:T(8,128)(2,1)}, u32[]{:S(2)}, u32[]{:S(2)}) collective-permute-start(bf16[80,64,128]{2,1,0:T(8,128)(2,1)} %get-tuple-element.3416), channel_id=1, source_target_pairs={{2,0},{3,1},{6,2},{7,3},{4,6},{5,7},{0,4},{1,5}} | collective-permute-start | bytes 3932168 | tf_op jit(solution)/shard_map/cond/branch_1_fun/while/body/ppermute | solution.py:680
  761.2 31.2 %collective-permute-start.81 = (bf16[80,64,128]{2,1,0:T(8,128)(2,1)}, bf16[80,64,128]{2,1,0:T(8,128)(2,1)}, u32[]{:S(2)}, u32[]{:S(2)}) collective-permute-start(bf16[80,64,128]{2,1,0:T(8,128)(2,1)} %get-tuple-element.3415), channel_id=1, source_target_pairs={{0,2},{1,3},{2,6},{3,7},{6,4},{7,5},{4,0},{5,1}} | collective-permute-start | bytes 3932168 | tf_op jit(solution)/shard_map/cond/branch_1_fun/while/body/ppermute | solution.py:679
  803.1 32.5 %collective-permute-start.86 = (bf16[2,80,64,128]{3,2,1,0:T(8,128)(2,1)}, bf16[2,80,64,128]{3,2,1,0:T(8,128)(2,1)S(1)}, u32[]{:S(2)}, u32[]{:S(2)}) collective-permute-start(bf16[2,80,64,128]{3,2,1,0:T(8,128)(2,1)} %get-tuple-element.2984), channel_id=1, source_target_pairs={{0,1},{1,0},{2,3},{3,2},{4,5},{5,4},{6,7},{7,6}} | collective-permute-start | bytes 7864328 | tf_op jit(solution)/shard_map/cond/branch_1_fun/while/body/ppermute | solution.py:689
  803.6 31.5 %collective-permute-start.87 = (bf16[80,64,128]{2,1,0:T(8,128)(2,1)}, bf16[80,64,128]{2,1,0:T(8,128)(2,1)}, u32[]{:S(2)}, u32[]{:S(2)}) collective-permute-start(bf16[80,64,128]{2,1,0:T(8,128)(2,1)} %get-tuple-element.2985), channel_id=1, source_target_pairs={{0,2},{1,3},{2,6},{3,7},{6,4},{7,5},{4,0},{5,1}} | collective-permute-start | bytes 3932168 | tf_op jit(solution)/shard_map/cond/branch_1_fun/while/body/ppermute | solution.py:679
  804.4 31.2 %collective-permute-start.88 = (bf16[80,64,128]{2,1,0:T(8,128)(2,1)}, bf16[80,64,128]{2,1,0:T(8,128)(2,1)}, u32[]{:S(2)}, u32[]{:S(2)}) collective-permute-start(bf16[80,64,128]{2,1,0:T(8,128)(2,1)} %get-tuple-element.2986), channel_id=1, source_target_pairs={{2,0},{3,1},{6,2},{7,3},{4,6},{5,7},{0,4},{1,5}} | collective-permute-start | bytes 3932168 | tf_op jit(solution)/shard_map/cond/branch_1_fun/while/body/ppermute | solution.py:680
  810.2 25.3 %collective-permute-start.91 = (bf16[2,32,64,128]{3,2,1,0:T(8,128)(2,1)}, bf16[2,32,64,128]{3,2,1,0:T(8,128)(2,1)}, u32[]{:S(2)}, u32[]{:S(2)}) collective-permute-start(bf16[2,32,64,128]{3,2,1,0:T(8,128)(2,1)} %get-tuple-element.2987), channel_id=1, source_target_pairs={{0,1},{1,0},{2,3},{3,2},{4,5},{5,4},{6,7},{7,6}} | collective-permute-start | bytes 3145736 | tf_op jit(solution)/shard_map/cond/branch_1_fun/while/body/ppermute | solution.py:690
  (62 other events, 421.5 us)

commit v6 on v5

--- a/solution.py
+++ b/solution.py
@@ -17,7 +17,7 @@
 WIDE = 400
 S0, S1, R0, R1, XS, XR, FREE = range(7)
 RDY, RDX, MLEN, SRC, ROUNDS = range(FREE * WIDE, FREE * WIDE + 200, 40)
-CORE, PICK, SHARE, DUMP = range(ROUNDS + 1, ROUNDS + 5)
+CORE, _, SHARE, DUMP = range(ROUNDS + 1, ROUNDS + 5)
 TAB = ROUNDS + 8
 FWD, NONE = 2, 3
 TURN = 2
@@ -57,7 +57,7 @@
         c.wait()
 
 
-def plan_kernel(me_ref, dest_ref, len_ref, tab, lens_out, nbv, kindv, todo, near, load, one, two, three, addr, at):
+def plan_kernel(me_ref, dest_ref, len_ref, tab, lens_out, state, rounds_out, pick_out, nbv, kindv, todo, near, load, one, two, three, cur):
     me = me_ref[0]
     zero = me - me
     for i in range(17):
@@ -120,7 +120,7 @@
     def largest():
         return functools.reduce(jnp.maximum, [load[x] for x in range(8)])
 
-    at[0] = largest()
+    cur[0] = largest()
 
     def detour(n, c):
         i = near[n]
@@ -132,7 +132,7 @@
         lb = [load[x] for x in b]
         la = load[a]
 
-        @pl.when((la - nb >= functools.reduce(jnp.maximum, lb) + nb) & (la * 10 >= at[0] * 9))
+        @pl.when((la - nb >= functools.reduce(jnp.maximum, lb) + nb) & (la * 10 >= cur[0] * 9))
         def _():
             load[a] = la - nb
             one[a] = one[a] - nb - HALF
@@ -140,7 +140,7 @@
                 load[x] = l + nb
             three[b[0]] = three[b[0]] + nb + HALF
             kindv[i] = jnp.where(cw, 6, 3)
-            at[0] = largest()
+            cur[0] = largest()
 
         return c
 
@@ -207,8 +207,10 @@
         better = price < best
         best, pick, turns, chunk = [jnp.where(better, n, o) for n, o in (
             (price, best), (o, pick), (trips * TURN, turns), (size, chunk))]
-    tab[ROUNDS] = turns
-    tab[PICK] = pick
+    rounds_out[0] = turns
+    pick_out[0] = pick
+    for i in range(STATE):
+        state[i] = zero
     tab[SHARE] = jnp.minimum(SL // jnp.maximum(turns - TURN, 1) + 1, A)
 
     x0 = gray(me >> 1)
@@ -231,26 +233,25 @@
         segs = ((base, zero), (base + wide, hop3 & LOW), (base + wide + 2 * (hop2 >> 16), (hop3 + hop2) & LOW),
                 (pad + 2, start), (pad + 2 + 2 * (three[up] >> 16), start + (three[up] & LOW)), (pad2 + 2, start2))
         for k, (where, pos) in enumerate(segs):
-            addr[SEGS * lid + k] = where
-            at[SEGS * lid + k] = pos
+            cur[SEGS * lid + k] = where * HALF + pos
         shift.append(((hop3 + hop2) & LOW) - start)
-    addr[IDLE] = zero + DUMP
-    at[IDLE] = zero
-
-    def append(seg, hit, nb, code):
+    cur[IDLE] = zero + DUMP * HALF
+
+    def append(seg, hit, nb, code_at):
         seg = jnp.where(hit, seg, IDLE)
-        a, p = addr[seg], at[seg]
+        c = cur[seg]
+        a, p = c >> 16, c & LOW
+        code = code_at(p)
         tab[a] = nb
         tab[a + 1] = code
-        addr[seg] = a + jnp.where(hit, 2, 0)
-        at[seg] = p + nb
-        return p + nb
+        cur[seg] = c + jnp.where(hit, 2 * HALF + nb, 0)
+        return p + nb, code
 
     def source(s, c):
         i = (me >> 1) * 2 * SL + s
         kind = kindv[i]
         seg = jnp.where(kind > 3, SEGS + 6, 3) - kind
-        append(seg, kind > 0, nbv[i], ((s >> 5) << 16) + (s & 31) * BL)
+        append(seg, kind > 0, nbv[i], lambda p: ((s >> 5) << 16) + (s & 31) * BL)
         return c
 
     lax.fori_loop(0, 2 * SL, source, 0, unroll=4)
@@ -258,9 +259,9 @@
     def visit(i, hit, seg, goes_on, seg_on, ahead):
         nb = nbv[i]
         dst = dest_ref[i]
-        code = jnp.where(goes_on, FWD * HALF + at[seg] + ahead, (((dst >> 5) & 1) << 16) + (dst & 31) * BL)
-        end = append(seg, hit, nb, code)
-        append(seg_on, goes_on, nb, code)
+        home = (((dst >> 5) & 1) << 16) + (dst & 31) * BL
+        end, code = append(seg, hit, nb, lambda p: jnp.where(goes_on, FWD * HALF + p + ahead, home))
+        append(seg_on, goes_on, nb, lambda p: code)
         mine = hit & ((dst >> 5) == me) & jnp.logical_not(goes_on)
         tab[RDY + jnp.where(mine, dst & 31, SL)] = end
 
@@ -485,7 +486,7 @@
 
 
 def attn_kernel(NB, last, tab, st_in, q, kn, vn, kc, vc, koi, voi, aoi, st, ko, vo, ao,
-                kb, vb, ob, sel, lsem, wsem):
+                kb, vb, ob, scores, sel, lsem, wsem):
     def cp(i, _):
         st[i] = st_in[i]
         return 0
@@ -526,17 +527,30 @@
             return 0
 
         lax.fori_loop(b0 + 1, BL, wipe, 0)
-        kf = kb[a].reshape(-1, 128)
-        vf = vb[a].reshape(-1, 128)
-        sc = lax.dot_general(q[j], kf, (((1,), (1,)), ((), ())), preferred_element_type=f32) * (128 ** -0.5)
-        col = lax.broadcasted_iota(i32, sc.shape, 1)
-        head = lax.broadcasted_iota(i32, sc.shape, 0) // 3
-        ok = ((col & 7) == head) & ((col >> 3) <= m)
-        sc = jnp.where(ok, sc, -1e30)
-        top = jnp.max(sc, axis=1, keepdims=True)
-        w = jnp.exp(sc - top)
-        tot = jnp.sum(w, axis=1, keepdims=True)
-        acc = lax.dot_general(w.astype(bf16), vf, (((1,), (0,)), ((), ())), preferred_element_type=f32)
+        pieces = (m >> 7) + 1
+        span = 128 // BP
+
+        def rows(buf, c):
+            return buf[a, pl.ds(c * span, span)].reshape(-1, 128)
+
+        def score(c, top):
+            sc = lax.dot_general(q[j], rows(kb, c), (((1,), (1,)), ((), ())), preferred_element_type=f32) * (128 ** -0.5)
+            col = lax.broadcasted_iota(i32, sc.shape, 1)
+            head = lax.broadcasted_iota(i32, sc.shape, 0) // 3
+            ok = ((col & 7) == head) & ((col >> 3) <= m - c * 128)
+            sc = jnp.where(ok, sc, -1e30)
+            scores[c] = sc
+            return jnp.maximum(top, jnp.max(sc, axis=1, keepdims=True))
+
+        top = lax.fori_loop(0, pieces, score, jnp.full((24, 1), -1e30, f32))
+
+        def weigh(c, carry):
+            tot, acc = carry
+            w = jnp.exp(scores[c] - top)
+            acc = acc + lax.dot_general(w.astype(bf16), rows(vb, c), (((1,), (0,)), ((), ())), preferred_element_type=f32)
+            return tot + jnp.sum(w, axis=1, keepdims=True), acc
+
+        tot, acc = lax.fori_loop(0, pieces, weigh, (jnp.zeros((24, 1), f32), jnp.zeros((24, 128), f32)))
         ob[a] = (acc / tot).astype(bf16)
         for src, dst in writes(a, j):
             pltpu.make_async_copy(src, dst, wsem.at[a]).start()
@@ -631,9 +645,9 @@
             compiler_params=pltpu.CompilerParams(collective_id=0, has_side_effects=True),
             name='lens')(cache_lens.reshape(1, SL))
         me = jnp.full((1,), lax.axis_index('dp'), i32)
-        tab, lens_out = pl.pallas_call(
-            plan_kernel, out_shape=(sds((TAB,), i32), sds((SL,), i32)), in_specs=[SMEM] * 3, out_specs=(SMEM, SMEM),
-            scratch_shapes=[pltpu.SMEM((8 * SL + 1,), i32)] * 4 + [pltpu.SMEM((IDLE + 1,), i32)] * 6,
+        tab, lens_out, state, rounds, pick = pl.pallas_call(
+            plan_kernel, out_shape=[sds((n,), i32) for n in (TAB, SL, STATE, 1, 1)], in_specs=[SMEM] * 3, out_specs=[SMEM] * 5,
+            scratch_shapes=[pltpu.SMEM((8 * SL + 1,), i32)] * 4 + [pltpu.SMEM((IDLE + 1,), i32)] * 5,
             name='plan')(me, dest_slot, lens_all)
 
         def run(NB):
@@ -646,7 +660,7 @@
                 nothing, out_shape=(cache, cache, sds((SL, 24, 128)), store, store, chunk, chunk, chunk, chunk, cross),
                 out_specs=(ANY,) * 10, name='blank')()
 
-            st = jnp.zeros((STATE,), i32)
+            st = state
             caches = [SMEM, SMEM, ANY, ANY]
 
             def opened(st):
@@ -670,7 +684,8 @@
                     out_shape=(ST, cache, cache, sds((SL, 24, 128))),
                     in_specs=[SMEM, SMEM, VMEM, VMEM, VMEM, ANY, ANY, ANY, ANY, ANY], out_specs=(SMEM, ANY, ANY, ANY),
                     input_output_aliases={7: 1, 8: 2, 9: 3},
-                    scratch_shapes=[buf(A, BL), buf(A, BL), pltpu.VMEM((A, 24, 128), bf16), pltpu.SMEM((SL + 1,), i32),
+                    scratch_shapes=[buf(A, BL), buf(A, BL), pltpu.VMEM((A, 24, 128), bf16),
+                                    pltpu.VMEM((4, 24, 1024), f32), pltpu.SMEM((SL + 1,), i32),
                                     dma(A), dma(A)],
                     cost_estimate=cost(6), name='attend')(tab, st, query, k_new, v_new, kc, vc, ko, vo, ao)
 
@@ -693,12 +708,12 @@
                     s0, s1, npo0, npo1 = lax.optimization_barrier((s0, s1, npo0, npo1))
                 return st, s0, s1, npre, nrc0, nrc1, npo0, npo1, ndxr, f0, f1, ko, vo, ao
 
-            rounds = tab[ROUNDS]
+            turns = rounds[0]
 
             def body(c):
                 return (c[0] + TURN,) + functools.reduce(lambda c, tag: one_round(tag, c), TAGS, c[1:])
 
-            c = lax.while_loop(lambda c: c[0] < rounds, body,
+            c = lax.while_loop(lambda c: c[0] < turns, body,
                            (jnp.int32(0), st, s0, s1, pre, rc0, rc1, po0, po1, dxr, f0, f1, ko, vo, ao))
             _, st, _, _, _, rc0, rc1, po0, po1, dxr, _, _, ko, vo, ao = c
 
@@ -718,7 +733,7 @@
             st, ko, vo, ao = attend(st, ko, vo, ao, True)
             return ao, ko, vo
 
-        ao, ko, vo = lax.switch(tab[PICK], [functools.partial(run, size) for size in SIZES])
+        ao, ko, vo = lax.switch(pick[0], [functools.partial(run, size) for size in SIZES])
         return ao, ko.reshape(k_cache.shape), vo.reshape(v_cache.shape), lens_out
 
     row_spec = P('dp')

time: 857 us -> 859 us (level)
  Pallas kernels: 342 us -> 370 us
  waiting for transfers between devices: 435 us -> 410 us
    pallas_call x19, Pallas kernels: 108 us -> 137 us  [attend(): pl.pallas_call(functools.partial(attn_kernel, NB, last), out_shape=(ST, c...]
    ppermute x18, waiting for transfers between devices: 167 us -> 151 us  [one_round(): nrc1 = lax.ppermute(s1, 'dp', ccw)]
    ppermute x18, waiting for transfers between devices: 171 us -> 161 us  [one_round(): nrc0 = lax.ppermute(s0, 'dp', cw)]
  transfers between devices with their start and end apart: 112 -> 112, of which waited for: 60 -> 60; matrix products, arithmetic and copies ran while one was open for 0% -> 0% of each run, Pallas kernels for 13% -> 16%
where the time goes in v6:
time: 859 us; the launch traced here: 855 us
  waiting for transfers between devices  410 us (48%)
  Pallas kernels  370 us (43%)
  starting transfers between devices  50.9 us (6%)
  local copies, waits for them, and re-layouts  15.3 us (2%)
    pallas_call x18, Pallas kernels, one_round(): pl.pallas_call(functools.partial(round_kernel, NB), out_shape=(ST, chunk,...  185 us
    ppermute x18, waiting for transfers between devices, one_round(): nrc0 = lax.ppermute(s0, 'dp', cw)  161 us
    ppermute x18, waiting for transfers between devices, one_round(): nrc1 = lax.ppermute(s1, 'dp', ccw)  151 us
    pallas_call x19, Pallas kernels, attend(): pl.pallas_call(functools.partial(attn_kernel, NB, last), out_shape=(ST, c...  137 us
    ppermute x18, waiting for transfers between devices, one_round(): npo1 = lax.ppermute(rc1, 'dp', swap)  81.6 us
    ppermute x18, starting transfers between devices, one_round(): nrc1 = lax.ppermute(s1, 'dp', ccw)  24.5 us
    pallas_call x1, Pallas kernels, local(): pl.pallas_call(plan_kernel, out_shape=[sds((n,), i32) for n in (TAB, SL,...  19 us
  transfers between devices with their start and end apart: 112, of which 60 were waited for; matrix products, arithmetic and copies ran while one was open for 0% of the time, Pallas kernels for 16%

profile of v6, /device:TPU:0, one launch (start us, length us, event | category | flops | bytes accessed | tf_op | source)
XLA Modules:
  0.0 855.1 jit_solution(12260612037531613837)
XLA Ops:
  0.6 7.8 lens.1.len_ref
  8.4 19.0 %plan.1 = (s32[2568]{0:T(1024)S(1)}, s32[32]{0:T(128)}, s32[64]{0:T(128)S(1)}, s32[1]{0:T(128)}, s32[1]{0:T(128)}) custom-call(s32[1]{0:T(128)} %bitcast.7.me_ref, s32[256]{0:T(256)} %dest_ref.1, s32[8,1,32]{2,1,0:T(1,128)} %lens.1.len_ref), custom_call_target="tpu_custom_call" | custom-call | tf_op jit(solution)/shard_map/plan/pallas_call | solution.py:648
  28.1 826.9 %conditional.1 = (bf16[32,24,128]{2,1,0:T(8,128)(2,1)}, bf16[2048,64,128]{2,1,0:T(8,128)(2,1)}, bf16[2048,64,128]{2,1,0:T(8,128)(2,1)}) conditional(s32[]{:T(128)} %bitcast.9, (s32[2568]{0:T(1024)S(1)}, s32[64]{0:T(128)S(1)}, bf16[2048,64,128]{2,1,0:T(8,128)(2,1)}, bf16[2048,64,128]{2,1,0:T(8,128)(2,1)}, s32[1]{0:T(128)}, ...), branch_computations={%region_0.0_spmd, %region_3.0_spmd, %region_6.0_spmd, %region_9.0_... | conditional | flops 152000000 | bytes 282811072 | solution.py:736
  37.5 5.4 open_merge.8
  43.0 792.0 %while.246 = (s32[]{:T(128)}, s32[64]{0:T(128)S(1)}, bf16[80,64,128]{2,1,0:T(8,128)(2,1)}, bf16[80,64,128]{2,1,0:T(8,128)(2,1)}, bf16[2,80,64,128]{3,2,1,0:T(8,1...) while((s32[]{:T(128)}, s32[64]{0:T(128)S(1)}, ...), condition=%wide.region_5.0_spmd, body=%wide.region_4.0_spmd.sunk | while | flops 128000000 | bytes 209789616 | solution.py:716
  43.6 8.7 %round.24 = (s32[64]{0:T(128)}, bf16[80,64,128]{2,1,0:T(8,128)(2,1)}, bf16[80,64,128]{2,1,0:T(8,128)(2,1)}, bf16[2,80,64,128]{3,2,1,0:T(8,128)(2,1)}, bf16[2,32,...) custom-call(s32[2568]{0:T(1024)S(1)} %get-tuple-element.3500.tab, ...), custom_call_target="tpu_custom_call", output_to_operand_aliasing={{5}: (10, {}), {6}: (11, {}), {7}: (12, {}), {8}: (13, {})} | custom-call | flops 40000000 | bytes 40000000 | tf_op jit(solution)/shard_map/cond/branch_1_fun/while/body/round/pallas_call | solution.py:698
  54.9 4.6 collective-permute-done.84.po1
  59.6 8.8 %attend.38 = (s32[64]{0:T(128)}, bf16[2048,64,128]{2,1,0:T(8,128)(2,1)}, bf16[2048,64,128]{2,1,0:T(8,128)(2,1)}, bf16[32,24,128]{2,1,0:T(8,128)(2,1)}) custom-call(s32[2568]{0:T(1024)S(1)} %get-tuple-element.3500.tab, s32[64]{0:T(128)} %get-tuple-element.3011.st_in, ...), custom_call_target="tpu_custom_call", output_to_operand_aliasing={{1}: (7, {}), {2}: (8, {}), {3}: (9, {})} | custom-call | flops 24000000 | bytes 24000000 | tf_op jit(solution)/shard_map/cond/branch_1_fun/while/body/attend/pallas_call | solution.py:682
  68.5 15.9 %collective-permute-done.82.rc1 = bf16[80,64,128]{2,1,0:T(8,128)(2,1)} collective-permute-done((bf16[80,64,128]{2,1,0:T(8,128)(2,1)}, bf16[80,64,128]{2,1,0:T(8,128)(2,1)}, u32[]{:S(2)}, u32[]{:S(2)}) %collective-permute-start.82) | collective-permute-done | bytes 1310752 | tf_op jit(solution)/shard_map/cond/branch_1_fun/while/body/ppermute | solution.py:695
  87.0 11.3 %round.25 = (s32[64]{0:T(128)}, bf16[80,64,128]{2,1,0:T(8,128)(2,1)}, bf16[80,64,128]{2,1,0:T(8,128)(2,1)}, bf16[2,80,64,128]{3,2,1,0:T(8,128)(2,1)}, bf16[2,32,...) custom-call(s32[2568]{0:T(1024)S(1)} %get-tuple-element.3500.tab, ...), custom_call_target="tpu_custom_call", output_to_operand_aliasing={{5}: (10, {}), {6}: (11, {}), {7}: (12, {}), {8}: (13, {})} | custom-call | flops 40000000 | bytes 40000000 | tf_op jit(solution)/shard_map/cond/branch_1_fun/while/body/round/pallas_call | solution.py:698
  100.8 4.6 collective-permute-done.90
  109.6 20.7 %collective-permute-done.87 = bf16[80,64,128]{2,1,0:T(8,128)(2,1)} collective-permute-done((bf16[80,64,128]{2,1,0:T(8,128)(2,1)}, bf16[80,64,128]{2,1,0:T(8,128)(2,1)}, u32[]{:S(2)}, u32[]{:S(2)}) %collective-permute-start.87) | collective-permute-done | bytes 1310752 | tf_op jit(solution)/shard_map/cond/branch_1_fun/while/body/ppermute | solution.py:694
  131.3 10.7 %round.24 = (s32[64]{0:T(128)}, bf16[80,64,128]{2,1,0:T(8,128)(2,1)}, bf16[80,64,128]{2,1,0:T(8,128)(2,1)}, bf16[2,80,64,128]{3,2,1,0:T(8,128)(2,1)}, bf16[2,32,...) custom-call(s32[2568]{0:T(1024)S(1)} %get-tuple-element.3500.tab, ...), custom_call_target="tpu_custom_call", output_to_operand_aliasing={{5}: (10, {}), {6}: (11, {}), {7}: (12, {}), {8}: (13, {})} | custom-call | flops 40000000 | bytes 40000000 | tf_op jit(solution)/shard_map/cond/branch_1_fun/while/body/round/pallas_call | solution.py:698
  149.3 6.4 attend.38
  155.7 18.3 %collective-permute-done.82.rc1 = bf16[80,64,128]{2,1,0:T(8,128)(2,1)} collective-permute-done((bf16[80,64,128]{2,1,0:T(8,128)(2,1)}, bf16[80,64,128]{2,1,0:T(8,128)(2,1)}, u32[]{:S(2)}, u32[]{:S(2)}) %collective-permute-start.82) | collective-permute-done | bytes 1310752 | tf_op jit(solution)/shard_map/cond/branch_1_fun/while/body/ppermute | solution.py:695
  176.3 11.5 %round.25 = (s32[64]{0:T(128)}, bf16[80,64,128]{2,1,0:T(8,128)(2,1)}, bf16[80,64,128]{2,1,0:T(8,128)(2,1)}, bf16[2,80,64,128]{3,2,1,0:T(8,128)(2,1)}, bf16[2,32,...) custom-call(s32[2568]{0:T(1024)S(1)} %get-tuple-element.3500.tab, ...), custom_call_target="tpu_custom_call", output_to_operand_aliasing={{5}: (10, {}), {6}: (11, {}), {7}: (12, {}), {8}: (13, {})} | custom-call | flops 40000000 | bytes 40000000 | tf_op jit(solution)/shard_map/cond/branch_1_fun/while/body/round/pallas_call | solution.py:698
  190.5 4.6 collective-permute-done.90
  199.2 20.7 %collective-permute-done.87 = bf16[80,64,128]{2,1,0:T(8,128)(2,1)} collective-permute-done((bf16[80,64,128]{2,1,0:T(8,128)(2,1)}, bf16[80,64,128]{2,1,0:T(8,128)(2,1)}, u32[]{:S(2)}, u32[]{:S(2)}) %collective-permute-start.87) | collective-permute-done | bytes 1310752 | tf_op jit(solution)/shard_map/cond/branch_1_fun/while/body/ppermute | solution.py:694
  220.6 10.8 %round.24 = (s32[64]{0:T(128)}, bf16[80,64,128]{2,1,0:T(8,128)(2,1)}, bf16[80,64,128]{2,1,0:T(8,128)(2,1)}, bf16[2,80,64,128]{3,2,1,0:T(8,128)(2,1)}, bf16[2,32,...) custom-call(s32[2568]{0:T(1024)S(1)} %get-tuple-element.3500.tab, ...), custom_call_target="tpu_custom_call", output_to_operand_aliasing={{5}: (10, {}), {6}: (11, {}), {7}: (12, {}), {8}: (13, {})} | custom-call | flops 40000000 | bytes 40000000 | tf_op jit(solution)/shard_map/cond/branch_1_fun/while/body/round/pallas_call | solution.py:698
  234.0 4.6 collective-permute-done.84.po1
  238.7 6.3 attend.38
  245.0 18.4 %collective-permute-done.82.rc1 = bf16[80,64,128]{2,1,0:T(8,128)(2,1)} collective-permute-done((bf16[80,64,128]{2,1,0:T(8,128)(2,1)}, bf16[80,64,128]{2,1,0:T(8,128)(2,1)}, u32[]{:S(2)}, u32[]{:S(2)}) %collective-permute-start.82) | collective-permute-done | bytes 1310752 | tf_op jit(solution)/shard_map/cond/branch_1_fun/while/body/ppermute | solution.py:695
  265.6 11.3 %round.25 = (s32[64]{0:T(128)}, bf16[80,64,128]{2,1,0:T(8,128)(2,1)}, bf16[80,64,128]{2,1,0:T(8,128)(2,1)}, bf16[2,80,64,128]{3,2,1,0:T(8,128)(2,1)}, bf16[2,32,...) custom-call(s32[2568]{0:T(1024)S(1)} %get-tuple-element.3500.tab, ...), custom_call_target="tpu_custom_call", output_to_operand_aliasing={{5}: (10, {}), {6}: (11, {}), {7}: (12, {}), {8}: (13, {})} | custom-call | flops 40000000 | bytes 40000000 | tf_op jit(solution)/shard_map/cond/branch_1_fun/while/body/round/pallas_call | solution.py:698
  279.6 4.6 collective-permute-done.90
  288.3 20.7 %collective-permute-done.87 = bf16[80,64,128]{2,1,0:T(8,128)(2,1)} collective-permute-done((bf16[80,64,128]{2,1,0:T(8,128)(2,1)}, bf16[80,64,128]{2,1,0:T(8,128)(2,1)}, u32[]{:S(2)}, u32[]{:S(2)}) %collective-permute-start.87) | collective-permute-done | bytes 1310752 | tf_op jit(solution)/shard_map/cond/branch_1_fun/while/body/ppermute | solution.py:694
  310.1 10.4 %round.24 = (s32[64]{0:T(128)}, bf16[80,64,128]{2,1,0:T(8,128)(2,1)}, bf16[80,64,128]{2,1,0:T(8,128)(2,1)}, bf16[2,80,64,128]{3,2,1,0:T(8,128)(2,1)}, bf16[2,32,...) custom-call(s32[2568]{0:T(1024)S(1)} %get-tuple-element.3500.tab, ...), custom_call_target="tpu_custom_call", output_to_operand_aliasing={{5}: (10, {}), {6}: (11, {}), {7}: (12, {}), {8}: (13, {})} | custom-call | flops 40000000 | bytes 40000000 | tf_op jit(solution)/shard_map/cond/branch_1_fun/while/body/round/pallas_call | solution.py:698
  323.1 4.6 collective-permute-done.84.po1
  327.8 6.3 attend.38
  334.1 18.4 %collective-permute-done.82.rc1 = bf16[80,64,128]{2,1,0:T(8,128)(2,1)} collective-permute-done((bf16[80,64,128]{2,1,0:T(8,128)(2,1)}, bf16[80,64,128]{2,1,0:T(8,128)(2,1)}, u32[]{:S(2)}, u32[]{:S(2)}) %collective-permute-start.82) | collective-permute-done | bytes 1310752 | tf_op jit(solution)/shard_map/cond/branch_1_fun/while/body/ppermute | solution.py:695
  354.7 11.1 %round.25 = (s32[64]{0:T(128)}, bf16[80,64,128]{2,1,0:T(8,128)(2,1)}, bf16[80,64,128]{2,1,0:T(8,128)(2,1)}, bf16[2,80,64,128]{3,2,1,0:T(8,128)(2,1)}, bf16[2,32,...) custom-call(s32[2568]{0:T(1024)S(1)} %get-tuple-element.3500.tab, ...), custom_call_target="tpu_custom_call", output_to_operand_aliasing={{5}: (10, {}), {6}: (11, {}), {7}: (12, {}), {8}: (13, {})} | custom-call | flops 40000000 | bytes 40000000 | tf_op jit(solution)/shard_map/cond/branch_1_fun/while/body/round/pallas_call | solution.py:698
  374.8 9.9 %attend.39 = (s32[64]{0:T(128)S(1)}, bf16[2048,64,128]{2,1,0:T(8,128)(2,1)}, bf16[2048,64,128]{2,1,0:T(8,128)(2,1)}, bf16[32,24,128]{2,1,0:T(8,128)(2,1)}) custom-call(s32[2568]{0:T(1024)S(1)} %get-tuple-element.3500.tab, s32[64]{0:T(128)} %get-tuple-element.3025.st_in, ...), custom_call_target="tpu_custom_call", output_to_operand_aliasing={{1}: (7, {}), {2}: (8, {}), {3}: (9, {})} | custom-call | flops 24000000 | bytes 24000000 | tf_op jit(solution)/shard_map/cond/branch_1_fun/while/body/attend/pallas_call | solution.py:682
  384.7 13.1 %collective-permute-done.87 = bf16[80,64,128]{2,1,0:T(8,128)(2,1)} collective-permute-done((bf16[80,64,128]{2,1,0:T(8,128)(2,1)}, bf16[80,64,128]{2,1,0:T(8,128)(2,1)}, u32[]{:S(2)}, u32[]{:S(2)}) %collective-permute-start.87) | collective-permute-done | bytes 1310752 | tf_op jit(solution)/shard_map/cond/branch_1_fun/while/body/ppermute | solution.py:694
  398.8 10.1 %round.24 = (s32[64]{0:T(128)}, bf16[80,64,128]{2,1,0:T(8,128)(2,1)}, bf16[80,64,128]{2,1,0:T(8,128)(2,1)}, bf16[2,80,64,128]{3,2,1,0:T(8,128)(2,1)}, bf16[2,32,...) custom-call(s32[2568]{0:T(1024)S(1)} %get-tuple-element.3500.tab, ...), custom_call_target="tpu_custom_call", output_to_operand_aliasing={{5}: (10, {}), {6}: (11, {}), {7}: (12, {}), {8}: (13, {})} | custom-call | flops 40000000 | bytes 40000000 | tf_op jit(solution)/shard_map/cond/branch_1_fun/while/body/round/pallas_call | solution.py:698
  416.2 9.3 %attend.38 = (s32[64]{0:T(128)}, bf16[2048,64,128]{2,1,0:T(8,128)(2,1)}, bf16[2048,64,128]{2,1,0:T(8,128)(2,1)}, bf16[32,24,128]{2,1,0:T(8,128)(2,1)}) custom-call(s32[2568]{0:T(1024)S(1)} %get-tuple-element.3500.tab, s32[64]{0:T(128)} %get-tuple-element.3011.st_in, ...), custom_call_target="tpu_custom_call", output_to_operand_aliasing={{1}: (7, {}), {2}: (8, {}), {3}: (9, {})} | custom-call | flops 24000000 | bytes 24000000 | tf_op jit(solution)/shard_map/cond/branch_1_fun/while/body/attend/pallas_call | solution.py:682
  425.5 15.5 %collective-permute-done.82.rc1 = bf16[80,64,128]{2,1,0:T(8,128)(2,1)} collective-permute-done((bf16[80,64,128]{2,1,0:T(8,128)(2,1)}, bf16[80,64,128]{2,1,0:T(8,128)(2,1)}, u32[]{:S(2)}, u32[]{:S(2)}) %collective-permute-start.82) | collective-permute-done | bytes 1310752 | tf_op jit(solution)/shard_map/cond/branch_1_fun/while/body/ppermute | solution.py:695
  443.2 10.8 %round.25 = (s32[64]{0:T(128)}, bf16[80,64,128]{2,1,0:T(8,128)(2,1)}, bf16[80,64,128]{2,1,0:T(8,128)(2,1)}, bf16[2,80,64,128]{3,2,1,0:T(8,128)(2,1)}, bf16[2,32,...) custom-call(s32[2568]{0:T(1024)S(1)} %get-tuple-element.3500.tab, ...), custom_call_target="tpu_custom_call", output_to_operand_aliasing={{5}: (10, {}), {6}: (11, {}), {7}: (12, {}), {8}: (13, {})} | custom-call | flops 40000000 | bytes 40000000 | tf_op jit(solution)/shard_map/cond/branch_1_fun/while/body/round/pallas_call | solution.py:698
  463.0 8.2 attend.39
  471.2 14.8 %collective-permute-done.87 = bf16[80,64,128]{2,1,0:T(8,128)(2,1)} collective-permute-done((bf16[80,64,128]{2,1,0:T(8,128)(2,1)}, bf16[80,64,128]{2,1,0:T(8,128)(2,1)}, u32[]{:S(2)}, u32[]{:S(2)}) %collective-permute-start.87) | collective-permute-done | bytes 1310752 | tf_op jit(solution)/shard_map/cond/branch_1_fun/while/body/ppermute | solution.py:694
  486.7 9.4 %round.24 = (s32[64]{0:T(128)}, bf16[80,64,128]{2,1,0:T(8,128)(2,1)}, bf16[80,64,128]{2,1,0:T(8,128)(2,1)}, bf16[2,80,64,128]{3,2,1,0:T(8,128)(2,1)}, bf16[2,32,...) custom-call(s32[2568]{0:T(1024)S(1)} %get-tuple-element.3500.tab, ...), custom_call_target="tpu_custom_call", output_to_operand_aliasing={{5}: (10, {}), {6}: (11, {}), {7}: (12, {}), {8}: (13, {})} | custom-call | flops 40000000 | bytes 40000000 | tf_op jit(solution)/shard_map/cond/branch_1_fun/while/body/round/pallas_call | solution.py:698
  504.1 8.3 attend.38
  512.3 16.1 %collective-permute-done.82.rc1 = bf16[80,64,128]{2,1,0:T(8,128)(2,1)} collective-permute-done((bf16[80,64,128]{2,1,0:T(8,128)(2,1)}, bf16[80,64,128]{2,1,0:T(8,128)(2,1)}, u32[]{:S(2)}, u32[]{:S(2)}) %collective-permute-start.82) | collective-permute-done | bytes 1310752 | tf_op jit(solution)/shard_map/cond/branch_1_fun/while/body/ppermute | solution.py:695
  530.8 10.5 %round.25 = (s32[64]{0:T(128)}, bf16[80,64,128]{2,1,0:T(8,128)(2,1)}, bf16[80,64,128]{2,1,0:T(8,128)(2,1)}, bf16[2,80,64,128]{3,2,1,0:T(8,128)(2,1)}, bf16[2,32,...) custom-call(s32[2568]{0:T(1024)S(1)} %get-tuple-element.3500.tab, ...), custom_call_target="tpu_custom_call", output_to_operand_aliasing={{5}: (10, {}), {6}: (11, {}), {7}: (12, {}), {8}: (13, {})} | custom-call | flops 40000000 | bytes 40000000 | tf_op jit(solution)/shard_map/cond/branch_1_fun/while/body/round/pallas_call | solution.py:698
  550.4 6.4 attend.39
  556.7 16.6 %collective-permute-done.87 = bf16[80,64,128]{2,1,0:T(8,128)(2,1)} collective-permute-done((bf16[80,64,128]{2,1,0:T(8,128)(2,1)}, bf16[80,64,128]{2,1,0:T(8,128)(2,1)}, u32[]{:S(2)}, u32[]{:S(2)}) %collective-permute-start.87) | collective-permute-done | bytes 1310752 | tf_op jit(solution)/shard_map/cond/branch_1_fun/while/body/ppermute | solution.py:694
  574.0 9.5 %round.24 = (s32[64]{0:T(128)}, bf16[80,64,128]{2,1,0:T(8,128)(2,1)}, bf16[80,64,128]{2,1,0:T(8,128)(2,1)}, bf16[2,80,64,128]{3,2,1,0:T(8,128)(2,1)}, bf16[2,32,...) custom-call(s32[2568]{0:T(1024)S(1)} %get-tuple-element.3500.tab, ...), custom_call_target="tpu_custom_call", output_to_operand_aliasing={{5}: (10, {}), {6}: (11, {}), {7}: (12, {}), {8}: (13, {})} | custom-call | flops 40000000 | bytes 40000000 | tf_op jit(solution)/shard_map/cond/branch_1_fun/while/body/round/pallas_call | solution.py:698
  590.8 9.3 %attend.38 = (s32[64]{0:T(128)}, bf16[2048,64,128]{2,1,0:T(8,128)(2,1)}, bf16[2048,64,128]{2,1,0:T(8,128)(2,1)}, bf16[32,24,128]{2,1,0:T(8,128)(2,1)}) custom-call(s32[2568]{0:T(1024)S(1)} %get-tuple-element.3500.tab, s32[64]{0:T(128)} %get-tuple-element.3011.st_in, ...), custom_call_target="tpu_custom_call", output_to_operand_aliasing={{1}: (7, {}), {2}: (8, {}), {3}: (9, {})} | custom-call | flops 24000000 | bytes 24000000 | tf_op jit(solution)/shard_map/cond/branch_1_fun/while/body/attend/pallas_call | solution.py:682
  600.2 15.4 %collective-permute-done.82.rc1 = bf16[80,64,128]{2,1,0:T(8,128)(2,1)} collective-permute-done((bf16[80,64,128]{2,1,0:T(8,128)(2,1)}, bf16[80,64,128]{2,1,0:T(8,128)(2,1)}, u32[]{:S(2)}, u32[]{:S(2)}) %collective-permute-start.82) | collective-permute-done | bytes 1310752 | tf_op jit(solution)/shard_map/cond/branch_1_fun/while/body/ppermute | solution.py:695
  618.2 10.3 %round.25 = (s32[64]{0:T(128)}, bf16[80,64,128]{2,1,0:T(8,128)(2,1)}, bf16[80,64,128]{2,1,0:T(8,128)(2,1)}, bf16[2,80,64,128]{3,2,1,0:T(8,128)(2,1)}, bf16[2,32,...) custom-call(s32[2568]{0:T(1024)S(1)} %get-tuple-element.3500.tab, ...), custom_call_target="tpu_custom_call", output_to_operand_aliasing={{5}: (10, {}), {6}: (11, {}), {7}: (12, {}), {8}: (13, {})} | custom-call | flops 40000000 | bytes 40000000 | tf_op jit(solution)/shard_map/cond/branch_1_fun/while/body/round/pallas_call | solution.py:698
  637.6 6.3 attend.39
  643.8 16.7 %collective-permute-done.87 = bf16[80,64,128]{2,1,0:T(8,128)(2,1)} collective-permute-done((bf16[80,64,128]{2,1,0:T(8,128)(2,1)}, bf16[80,64,128]{2,1,0:T(8,128)(2,1)}, u32[]{:S(2)}, u32[]{:S(2)}) %collective-permute-start.87) | collective-permute-done | bytes 1310752 | tf_op jit(solution)/shard_map/cond/branch_1_fun/while/body/ppermute | solution.py:694
  661.2 9.2 %round.24 = (s32[64]{0:T(128)}, bf16[80,64,128]{2,1,0:T(8,128)(2,1)}, bf16[80,64,128]{2,1,0:T(8,128)(2,1)}, bf16[2,80,64,128]{3,2,1,0:T(8,128)(2,1)}, bf16[2,32,...) custom-call(s32[2568]{0:T(1024)S(1)} %get-tuple-element.3500.tab, ...), custom_call_target="tpu_custom_call", output_to_operand_aliasing={{5}: (10, {}), {6}: (11, {}), {7}: (12, {}), {8}: (13, {})} | custom-call | flops 40000000 | bytes 40000000 | tf_op jit(solution)/shard_map/cond/branch_1_fun/while/body/round/pallas_call | solution.py:698
  677.8 9.9 %attend.38 = (s32[64]{0:T(128)}, bf16[2048,64,128]{2,1,0:T(8,128)(2,1)}, bf16[2048,64,128]{2,1,0:T(8,128)(2,1)}, bf16[32,24,128]{2,1,0:T(8,128)(2,1)}) custom-call(s32[2568]{0:T(1024)S(1)} %get-tuple-element.3500.tab, s32[64]{0:T(128)} %get-tuple-element.3011.st_in, ...), custom_call_target="tpu_custom_call", output_to_operand_aliasing={{1}: (7, {}), {2}: (8, {}), {3}: (9, {})} | custom-call | flops 24000000 | bytes 24000000 | tf_op jit(solution)/shard_map/cond/branch_1_fun/while/body/attend/pallas_call | solution.py:682
  687.7 14.9 %collective-permute-done.82.rc1 = bf16[80,64,128]{2,1,0:T(8,128)(2,1)} collective-permute-done((bf16[80,64,128]{2,1,0:T(8,128)(2,1)}, bf16[80,64,128]{2,1,0:T(8,128)(2,1)}, u32[]{:S(2)}, u32[]{:S(2)}) %collective-permute-start.82) | collective-permute-done | bytes 1310752 | tf_op jit(solution)/shard_map/cond/branch_1_fun/while/body/ppermute | solution.py:695
  705.7 10.6 %round.25 = (s32[64]{0:T(128)}, bf16[80,64,128]{2,1,0:T(8,128)(2,1)}, bf16[80,64,128]{2,1,0:T(8,128)(2,1)}, bf16[2,80,64,128]{3,2,1,0:T(8,128)(2,1)}, bf16[2,32,...) custom-call(s32[2568]{0:T(1024)S(1)} %get-tuple-element.3500.tab, ...), custom_call_target="tpu_custom_call", output_to_operand_aliasing={{5}: (10, {}), {6}: (11, {}), {7}: (12, {}), {8}: (13, {})} | custom-call | flops 40000000 | bytes 40000000 | tf_op jit(solution)/shard_map/cond/branch_1_fun/while/body/round/pallas_call | solution.py:698
  725.3 8.4 attend.39
  733.7 14.7 %collective-permute-done.87 = bf16[80,64,128]{2,1,0:T(8,128)(2,1)} collective-permute-done((bf16[80,64,128]{2,1,0:T(8,128)(2,1)}, bf16[80,64,128]{2,1,0:T(8,128)(2,1)}, u32[]{:S(2)}, u32[]{:S(2)}) %collective-permute-start.87) | collective-permute-done | bytes 1310752 | tf_op jit(solution)/shard_map/cond/branch_1_fun/while/body/ppermute | solution.py:694
  749.0 9.4 %round.24 = (s32[64]{0:T(128)}, bf16[80,64,128]{2,1,0:T(8,128)(2,1)}, bf16[80,64,128]{2,1,0:T(8,128)(2,1)}, bf16[2,80,64,128]{3,2,1,0:T(8,128)(2,1)}, bf16[2,32,...) custom-call(s32[2568]{0:T(1024)S(1)} %get-tuple-element.3500.tab, ...), custom_call_target="tpu_custom_call", output_to_operand_aliasing={{5}: (10, {}), {6}: (11, {}), {7}: (12, {}), {8}: (13, {})} | custom-call | flops 40000000 | bytes 40000000 | tf_op jit(solution)/shard_map/cond/branch_1_fun/while/body/round/pallas_call | solution.py:698
  765.7 8.3 attend.38
  774.1 16.4 %collective-permute-done.82.rc1 = bf16[80,64,128]{2,1,0:T(8,128)(2,1)} collective-permute-done((bf16[80,64,128]{2,1,0:T(8,128)(2,1)}, bf16[80,64,128]{2,1,0:T(8,128)(2,1)}, u32[]{:S(2)}, u32[]{:S(2)}) %collective-permute-start.82) | collective-permute-done | bytes 1310752 | tf_op jit(solution)/shard_map/cond/branch_1_fun/while/body/ppermute | solution.py:695
  792.7 9.2 %round.25 = (s32[64]{0:T(128)}, bf16[80,64,128]{2,1,0:T(8,128)(2,1)}, bf16[80,64,128]{2,1,0:T(8,128)(2,1)}, bf16[2,80,64,128]{3,2,1,0:T(8,128)(2,1)}, bf16[2,32,...) custom-call(s32[2568]{0:T(1024)S(1)} %get-tuple-element.3500.tab, ...), custom_call_target="tpu_custom_call", output_to_operand_aliasing={{5}: (10, {}), {6}: (11, {}), {7}: (12, {}), {8}: (13, {})} | custom-call | flops 40000000 | bytes 40000000 | tf_op jit(solution)/shard_map/cond/branch_1_fun/while/body/round/pallas_call | solution.py:698
  810.9 7.9 attend.39
  818.7 15.2 %collective-permute-done.87 = bf16[80,64,128]{2,1,0:T(8,128)(2,1)} collective-permute-done((bf16[80,64,128]{2,1,0:T(8,128)(2,1)}, bf16[80,64,128]{2,1,0:T(8,128)(2,1)}, u32[]{:S(2)}, u32[]{:S(2)}) %collective-permute-start.87) | collective-permute-done | bytes 1310752 | tf_op jit(solution)/shard_map/cond/branch_1_fun/while/body/ppermute | solution.py:694
  835.5 4.9 close.8
  844.7 10.0 %attend.22 = (s32[64]{0:T(128)}, bf16[2048,64,128]{2,1,0:T(8,128)(2,1)}, bf16[2048,64,128]{2,1,0:T(8,128)(2,1)}, bf16[32,24,128]{2,1,0:T(8,128)(2,1)}) custom-call(s32[2568]{0:T(1024)S(1)} %get-tuple-element.3619, s32[64]{0:T(128)} %get-tuple-element.915.st_in, ...), custom_call_target="tpu_custom_call", output_to_operand_aliasing={{1}: (7, {}), {2}: (8, {}), {3}: (9, {})} | custom-call | flops 24000000 | bytes 24000000 | tf_op jit(solution)/shard_map/cond/branch_1_fun/attend/pallas_call | solution.py:682
  (235 shorter events, 164.4 us)
Async XLA Ops:
  52.4 33.1 %collective-permute-start.80 = (bf16[2,80,64,128]{3,2,1,0:T(8,128)(2,1)}, bf16[2,80,64,128]{3,2,1,0:T(8,128)(2,1)S(1)}, u32[]{:S(2)}, u32[]{:S(2)}) collective-permute-start(bf16[2,80,64,128]{3,2,1,0:T(8,128)(2,1)} %get-tuple-element.3015), channel_id=1, source_target_pairs={{0,1},{1,0},{2,3},{3,2},{4,5},{5,4},{6,7},{7,6}} | collective-permute-start | bytes 7864328 | tf_op jit(solution)/shard_map/cond/branch_1_fun/while/body/ppermute | solution.py:704
  52.9 31.5 %collective-permute-start.82 = (bf16[80,64,128]{2,1,0:T(8,128)(2,1)}, bf16[80,64,128]{2,1,0:T(8,128)(2,1)}, u32[]{:S(2)}, u32[]{:S(2)}) collective-permute-start(bf16[80,64,128]{2,1,0:T(8,128)(2,1)} %get-tuple-element.3464), channel_id=1, source_target_pairs={{2,0},{3,1},{6,2},{7,3},{4,6},{5,7},{0,4},{1,5}} | collective-permute-start | bytes 3932168 | tf_op jit(solution)/shard_map/cond/branch_1_fun/while/body/ppermute | solution.py:695
  54.2 31.2 %collective-permute-start.81 = (bf16[80,64,128]{2,1,0:T(8,128)(2,1)}, bf16[80,64,128]{2,1,0:T(8,128)(2,1)}, u32[]{:S(2)}, u32[]{:S(2)}) collective-permute-start(bf16[80,64,128]{2,1,0:T(8,128)(2,1)} %get-tuple-element.3463), channel_id=1, source_target_pairs={{0,2},{1,3},{2,6},{3,7},{6,4},{7,5},{4,0},{5,1}} | collective-permute-start | bytes 3932168 | tf_op jit(solution)/shard_map/cond/branch_1_fun/while/body/ppermute | solution.py:694
  98.2 32.4 %collective-permute-start.86 = (bf16[2,80,64,128]{3,2,1,0:T(8,128)(2,1)}, bf16[2,80,64,128]{3,2,1,0:T(8,128)(2,1)S(1)}, u32[]{:S(2)}, u32[]{:S(2)}) collective-permute-start(bf16[2,80,64,128]{3,2,1,0:T(8,128)(2,1)} %get-tuple-element.3032), channel_id=1, source_target_pairs={{0,1},{1,0},{2,3},{3,2},{4,5},{5,4},{6,7},{7,6}} | collective-permute-start | bytes 7864328 | tf_op jit(solution)/shard_map/cond/branch_1_fun/while/body/ppermute | solution.py:704
  98.8 31.5 %collective-permute-start.87 = (bf16[80,64,128]{2,1,0:T(8,128)(2,1)}, bf16[80,64,128]{2,1,0:T(8,128)(2,1)}, u32[]{:S(2)}, u32[]{:S(2)}) collective-permute-start(bf16[80,64,128]{2,1,0:T(8,128)(2,1)} %get-tuple-element.3033), channel_id=1, source_target_pairs={{0,2},{1,3},{2,6},{3,7},{6,4},{7,5},{4,0},{5,1}} | collective-permute-start | bytes 3932168 | tf_op jit(solution)/shard_map/cond/branch_1_fun/while/body/ppermute | solution.py:694
  99.2 31.4 %collective-permute-start.88 = (bf16[80,64,128]{2,1,0:T(8,128)(2,1)}, bf16[80,64,128]{2,1,0:T(8,128)(2,1)}, u32[]{:S(2)}, u32[]{:S(2)}) collective-permute-start(bf16[80,64,128]{2,1,0:T(8,128)(2,1)} %get-tuple-element.3034), channel_id=1, source_target_pairs={{2,0},{3,1},{6,2},{7,3},{4,6},{5,7},{0,4},{1,5}} | collective-permute-start | bytes 3932168 | tf_op jit(solution)/shard_map/cond/branch_1_fun/while/body/ppermute | solution.py:695
  105.4 25.2 %collective-permute-start.91 = (bf16[2,32,64,128]{3,2,1,0:T(8,128)(2,1)}, bf16[2,32,64,128]{3,2,1,0:T(8,128)(2,1)}, u32[]{:S(2)}, u32[]{:S(2)}) collective-permute-start(bf16[2,32,64,128]{3,2,1,0:T(8,128)(2,1)} %get-tuple-element.3035), channel_id=1, source_target_pairs={{0,1},{1,0},{2,3},{3,2},{4,5},{5,4},{6,7},{7,6}} | collective-permute-start | bytes 3145736 | tf_op jit(solution)/shard_map/cond/branch_1_fun/while/body/ppermute | solution.py:705
  142.0 32.8 %collective-permute-start.80 = (bf16[2,80,64,128]{3,2,1,0:T(8,128)(2,1)}, bf16[2,80,64,128]{3,2,1,0:T(8,128)(2,1)S(1)}, u32[]{:S(2)}, u32[]{:S(2)}) collective-permute-start(bf16[2,80,64,128]{3,2,1,0:T(8,128)(2,1)} %get-tuple-element.3015), channel_id=1, source_target_pairs={{0,1},{1,0},{2,3},{3,2},{4,5},{5,4},{6,7},{7,6}} | collective-permute-start | bytes 7864328 | tf_op jit(solution)/shard_map/cond/branch_1_fun/while/body/ppermute | solution.py:704
  142.5 31.5 %collective-permute-start.82 = (bf16[80,64,128]{2,1,0:T(8,128)(2,1)}, bf16[80,64,128]{2,1,0:T(8,128)(2,1)}, u32[]{:S(2)}, u32[]{:S(2)}) collective-permute-start(bf16[80,64,128]{2,1,0:T(8,128)(2,1)} %get-tuple-element.3464), channel_id=1, source_target_pairs={{2,0},{3,1},{6,2},{7,3},{4,6},{5,7},{0,4},{1,5}} | collective-permute-start | bytes 3932168 | tf_op jit(solution)/shard_map/cond/branch_1_fun/while/body/ppermute | solution.py:695
  143.6 31.2 %collective-permute-start.81 = (bf16[80,64,128]{2,1,0:T(8,128)(2,1)}, bf16[80,64,128]{2,1,0:T(8,128)(2,1)}, u32[]{:S(2)}, u32[]{:S(2)}) collective-permute-start(bf16[80,64,128]{2,1,0:T(8,128)(2,1)} %get-tuple-element.3463), channel_id=1, source_target_pairs={{0,2},{1,3},{2,6},{3,7},{6,4},{7,5},{4,0},{5,1}} | collective-permute-start | bytes 3932168 | tf_op jit(solution)/shard_map/cond/branch_1_fun/while/body/ppermute | solution.py:694
  187.9 32.1 %collective-permute-start.86 = (bf16[2,80,64,128]{3,2,1,0:T(8,128)(2,1)}, bf16[2,80,64,128]{3,2,1,0:T(8,128)(2,1)S(1)}, u32[]{:S(2)}, u32[]{:S(2)}) collective-permute-start(bf16[2,80,64,128]{3,2,1,0:T(8,128)(2,1)} %get-tuple-element.3032), channel_id=1, source_target_pairs={{0,1},{1,0},{2,3},{3,2},{4,5},{5,4},{6,7},{7,6}} | collective-permute-start | bytes 7864328 | tf_op jit(solution)/shard_map/cond/branch_1_fun/while/body/ppermute | solution.py:704
  188.4 31.5 %collective-permute-start.87 = (bf16[80,64,128]{2,1,0:T(8,128)(2,1)}, bf16[80,64,128]{2,1,0:T(8,128)(2,1)}, u32[]{:S(2)}, u32[]{:S(2)}) collective-permute-start(bf16[80,64,128]{2,1,0:T(8,128)(2,1)} %get-tuple-element.3033), channel_id=1, source_target_pairs={{0,2},{1,3},{2,6},{3,7},{6,4},{7,5},{4,0},{5,1}} | collective-permute-start | bytes 3932168 | tf_op jit(solution)/shard_map/cond/branch_1_fun/while/body/ppermute | solution.py:694
  188.8 31.2 %collective-permute-start.88 = (bf16[80,64,128]{2,1,0:T(8,128)(2,1)}, bf16[80,64,128]{2,1,0:T(8,128)(2,1)}, u32[]{:S(2)}, u32[]{:S(2)}) collective-permute-start(bf16[80,64,128]{2,1,0:T(8,128)(2,1)} %get-tuple-element.3034), channel_id=1, source_target_pairs={{2,0},{3,1},{6,2},{7,3},{4,6},{5,7},{0,4},{1,5}} | collective-permute-start | bytes 3932168 | tf_op jit(solution)/shard_map/cond/branch_1_fun/while/body/ppermute | solution.py:695
  195.0 25.0 %collective-permute-start.91 = (bf16[2,32,64,128]{3,2,1,0:T(8,128)(2,1)}, bf16[2,32,64,128]{3,2,1,0:T(8,128)(2,1)}, u32[]{:S(2)}, u32[]{:S(2)}) collective-permute-start(bf16[2,32,64,128]{3,2,1,0:T(8,128)(2,1)} %get-tuple-element.3035), channel_id=1, source_target_pairs={{0,1},{1,0},{2,3},{3,2},{4,5},{5,4},{6,7},{7,6}} | collective-permute-start | bytes 3145736 | tf_op jit(solution)/shard_map/cond/branch_1_fun/while/body/ppermute | solution.py:705
  231.4 32.7 %collective-permute-start.80 = (bf16[2,80,64,128]{3,2,1,0:T(8,128)(2,1)}, bf16[2,80,64,128]{3,2,1,0:T(8,128)(2,1)S(1)}, u32[]{:S(2)}, u32[]{:S(2)}) collective-permute-start(bf16[2,80,64,128]{3,2,1,0:T(8,128)(2,1)} %get-tuple-element.3015), channel_id=1, source_target_pairs={{0,1},{1,0},{2,3},{3,2},{4,5},{5,4},{6,7},{7,6}} | collective-permute-start | bytes 7864328 | tf_op jit(solution)/shard_map/cond/branch_1_fun/while/body/ppermute | solution.py:704
  232.0 31.5 %collective-permute-start.82 = (bf16[80,64,128]{2,1,0:T(8,128)(2,1)}, bf16[80,64,128]{2,1,0:T(8,128)(2,1)}, u32[]{:S(2)}, u32[]{:S(2)}) collective-permute-start(bf16[80,64,128]{2,1,0:T(8,128)(2,1)} %get-tuple-element.3464), channel_id=1, source_target_pairs={{2,0},{3,1},{6,2},{7,3},{4,6},{5,7},{0,4},{1,5}} | collective-permute-start | bytes 3932168 | tf_op jit(solution)/shard_map/cond/branch_1_fun/while/body/ppermute | solution.py:695
  232.9 31.2 %collective-permute-start.81 = (bf16[80,64,128]{2,1,0:T(8,128)(2,1)}, bf16[80,64,128]{2,1,0:T(8,128)(2,1)}, u32[]{:S(2)}, u32[]{:S(2)}) collective-permute-start(bf16[80,64,128]{2,1,0:T(8,128)(2,1)} %get-tuple-element.3463), channel_id=1, source_target_pairs={{0,2},{1,3},{2,6},{3,7},{6,4},{7,5},{4,0},{5,1}} | collective-permute-start | bytes 3932168 | tf_op jit(solution)/shard_map/cond/branch_1_fun/while/body/ppermute | solution.py:694
  277.0 32.5 %collective-permute-start.86 = (bf16[2,80,64,128]{3,2,1,0:T(8,128)(2,1)}, bf16[2,80,64,128]{3,2,1,0:T(8,128)(2,1)S(1)}, u32[]{:S(2)}, u32[]{:S(2)}) collective-permute-start(bf16[2,80,64,128]{3,2,1,0:T(8,128)(2,1)} %get-tuple-element.3032), channel_id=1, source_target_pairs={{0,1},{1,0},{2,3},{3,2},{4,5},{5,4},{6,7},{7,6}} | collective-permute-start | bytes 7864328 | tf_op jit(solution)/shard_map/cond/branch_1_fun/while/body/ppermute | solution.py:704
  277.5 31.5 %collective-permute-start.87 = (bf16[80,64,128]{2,1,0:T(8,128)(2,1)}, bf16[80,64,128]{2,1,0:T(8,128)(2,1)}, u32[]{:S(2)}, u32[]{:S(2)}) collective-permute-start(bf16[80,64,128]{2,1,0:T(8,128)(2,1)} %get-tuple-element.3033), channel_id=1, source_target_pairs={{0,2},{1,3},{2,6},{3,7},{6,4},{7,5},{4,0},{5,1}} | collective-permute-start | bytes 3932168 | tf_op jit(solution)/shard_map/cond/branch_1_fun/while/body/ppermute | solution.py:694
  278.3 31.2 %collective-permute-start.88 = (bf16[80,64,128]{2,1,0:T(8,128)(2,1)}, bf16[80,64,128]{2,1,0:T(8,128)(2,1)}, u32[]{:S(2)}, u32[]{:S(2)}) collective-permute-start(bf16[80,64,128]{2,1,0:T(8,128)(2,1)} %get-tuple-element.3034), channel_id=1, source_target_pairs={{2,0},{3,1},{6,2},{7,3},{4,6},{5,7},{0,4},{1,5}} | collective-permute-start | bytes 3932168 | tf_op jit(solution)/shard_map/cond/branch_1_fun/while/body/ppermute | solution.py:695
  284.1 25.4 %collective-permute-start.91 = (bf16[2,32,64,128]{3,2,1,0:T(8,128)(2,1)}, bf16[2,32,64,128]{3,2,1,0:T(8,128)(2,1)}, u32[]{:S(2)}, u32[]{:S(2)}) collective-permute-start(bf16[2,32,64,128]{3,2,1,0:T(8,128)(2,1)} %get-tuple-element.3035), channel_id=1, source_target_pairs={{0,1},{1,0},{2,3},{3,2},{4,5},{5,4},{6,7},{7,6}} | collective-permute-start | bytes 3145736 | tf_op jit(solution)/shard_map/cond/branch_1_fun/while/body/ppermute | solution.py:705
  320.5 32.7 %collective-permute-start.80 = (bf16[2,80,64,128]{3,2,1,0:T(8,128)(2,1)}, bf16[2,80,64,128]{3,2,1,0:T(8,128)(2,1)S(1)}, u32[]{:S(2)}, u32[]{:S(2)}) collective-permute-start(bf16[2,80,64,128]{3,2,1,0:T(8,128)(2,1)} %get-tuple-element.3015), channel_id=1, source_target_pairs={{0,1},{1,0},{2,3},{3,2},{4,5},{5,4},{6,7},{7,6}} | collective-permute-start | bytes 7864328 | tf_op jit(solution)/shard_map/cond/branch_1_fun/while/body/ppermute | solution.py:704
  321.1 31.5 %collective-permute-start.82 = (bf16[80,64,128]{2,1,0:T(8,128)(2,1)}, bf16[80,64,128]{2,1,0:T(8,128)(2,1)}, u32[]{:S(2)}, u32[]{:S(2)}) collective-permute-start(bf16[80,64,128]{2,1,0:T(8,128)(2,1)} %get-tuple-element.3464), channel_id=1, source_target_pairs={{2,0},{3,1},{6,2},{7,3},{4,6},{5,7},{0,4},{1,5}} | collective-permute-start | bytes 3932168 | tf_op jit(solution)/shard_map/cond/branch_1_fun/while/body/ppermute | solution.py:695
  322.0 31.2 %collective-permute-start.81 = (bf16[80,64,128]{2,1,0:T(8,128)(2,1)}, bf16[80,64,128]{2,1,0:T(8,128)(2,1)}, u32[]{:S(2)}, u32[]{:S(2)}) collective-permute-start(bf16[80,64,128]{2,1,0:T(8,128)(2,1)} %get-tuple-element.3463), channel_id=1, source_target_pairs={{0,2},{1,3},{2,6},{3,7},{6,4},{7,5},{4,0},{5,1}} | collective-permute-start | bytes 3932168 | tf_op jit(solution)/shard_map/cond/branch_1_fun/while/body/ppermute | solution.py:694
  365.8 32.4 %collective-permute-start.86 = (bf16[2,80,64,128]{3,2,1,0:T(8,128)(2,1)}, bf16[2,80,64,128]{3,2,1,0:T(8,128)(2,1)S(1)}, u32[]{:S(2)}, u32[]{:S(2)}) collective-permute-start(bf16[2,80,64,128]{3,2,1,0:T(8,128)(2,1)} %get-tuple-element.3032), channel_id=1, source_target_pairs={{0,1},{1,0},{2,3},{3,2},{4,5},{5,4},{6,7},{7,6}} | collective-permute-start | bytes 7864328 | tf_op jit(solution)/shard_map/cond/branch_1_fun/while/body/ppermute | solution.py:704
  366.4 31.5 %collective-permute-start.87 = (bf16[80,64,128]{2,1,0:T(8,128)(2,1)}, bf16[80,64,128]{2,1,0:T(8,128)(2,1)}, u32[]{:S(2)}, u32[]{:S(2)}) collective-permute-start(bf16[80,64,128]{2,1,0:T(8,128)(2,1)} %get-tuple-element.3033), channel_id=1, source_target_pairs={{0,2},{1,3},{2,6},{3,7},{6,4},{7,5},{4,0},{5,1}} | collective-permute-start | bytes 3932168 | tf_op jit(solution)/shard_map/cond/branch_1_fun/while/body/ppermute | solution.py:694
  367.0 31.2 %collective-permute-start.88 = (bf16[80,64,128]{2,1,0:T(8,128)(2,1)}, bf16[80,64,128]{2,1,0:T(8,128)(2,1)}, u32[]{:S(2)}, u32[]{:S(2)}) collective-permute-start(bf16[80,64,128]{2,1,0:T(8,128)(2,1)} %get-tuple-element.3034), channel_id=1, source_target_pairs={{2,0},{3,1},{6,2},{7,3},{4,6},{5,7},{0,4},{1,5}} | collective-permute-start | bytes 3932168 | tf_op jit(solution)/shard_map/cond/branch_1_fun/while/body/ppermute | solution.py:695
  373.0 25.2 %collective-permute-start.91 = (bf16[2,32,64,128]{3,2,1,0:T(8,128)(2,1)}, bf16[2,32,64,128]{3,2,1,0:T(8,128)(2,1)}, u32[]{:S(2)}, u32[]{:S(2)}) collective-permute-start(bf16[2,32,64,128]{3,2,1,0:T(8,128)(2,1)} %get-tuple-element.3035), channel_id=1, source_target_pairs={{0,1},{1,0},{2,3},{3,2},{4,5},{5,4},{6,7},{7,6}} | collective-permute-start | bytes 3145736 | tf_op jit(solution)/shard_map/cond/branch_1_fun/while/body/ppermute | solution.py:705
  408.9 32.7 %collective-permute-start.80 = (bf16[2,80,64,128]{3,2,1,0:T(8,128)(2,1)}, bf16[2,80,64,128]{3,2,1,0:T(8,128)(2,1)S(1)}, u32[]{:S(2)}, u32[]{:S(2)}) collective-permute-start(bf16[2,80,64,128]{3,2,1,0:T(8,128)(2,1)} %get-tuple-element.3015), channel_id=1, source_target_pairs={{0,1},{1,0},{2,3},{3,2},{4,5},{5,4},{6,7},{7,6}} | collective-permute-start | bytes 7864328 | tf_op jit(solution)/shard_map/cond/branch_1_fun/while/body/ppermute | solution.py:704
  409.5 31.5 %collective-permute-start.82 = (bf16[80,64,128]{2,1,0:T(8,128)(2,1)}, bf16[80,64,128]{2,1,0:T(8,128)(2,1)}, u32[]{:S(2)}, u32[]{:S(2)}) collective-permute-start(bf16[80,64,128]{2,1,0:T(8,128)(2,1)} %get-tuple-element.3464), channel_id=1, source_target_pairs={{2,0},{3,1},{6,2},{7,3},{4,6},{5,7},{0,4},{1,5}} | collective-permute-start | bytes 3932168 | tf_op jit(solution)/shard_map/cond/branch_1_fun/while/body/ppermute | solution.py:695
  410.4 31.2 %collective-permute-start.81 = (bf16[80,64,128]{2,1,0:T(8,128)(2,1)}, bf16[80,64,128]{2,1,0:T(8,128)(2,1)}, u32[]{:S(2)}, u32[]{:S(2)}) collective-permute-start(bf16[80,64,128]{2,1,0:T(8,128)(2,1)} %get-tuple-element.3463), channel_id=1, source_target_pairs={{0,2},{1,3},{2,6},{3,7},{6,4},{7,5},{4,0},{5,1}} | collective-permute-start | bytes 3932168 | tf_op jit(solution)/shard_map/cond/branch_1_fun/while/body/ppermute | solution.py:694
  454.0 32.0 %collective-permute-start.86 = (bf16[2,80,64,128]{3,2,1,0:T(8,128)(2,1)}, bf16[2,80,64,128]{3,2,1,0:T(8,128)(2,1)S(1)}, u32[]{:S(2)}, u32[]{:S(2)}) collective-permute-start(bf16[2,80,64,128]{3,2,1,0:T(8,128)(2,1)} %get-tuple-element.3032), channel_id=1, source_target_pairs={{0,1},{1,0},{2,3},{3,2},{4,5},{5,4},{6,7},{7,6}} | collective-permute-start | bytes 7864328 | tf_op jit(solution)/shard_map/cond/branch_1_fun/while/body/ppermute | solution.py:704
  454.6 31.4 %collective-permute-start.87 = (bf16[80,64,128]{2,1,0:T(8,128)(2,1)}, bf16[80,64,128]{2,1,0:T(8,128)(2,1)}, u32[]{:S(2)}, u32[]{:S(2)}) collective-permute-start(bf16[80,64,128]{2,1,0:T(8,128)(2,1)} %get-tuple-element.3033), channel_id=1, source_target_pairs={{0,2},{1,3},{2,6},{3,7},{6,4},{7,5},{4,0},{5,1}} | collective-permute-start | bytes 3932168 | tf_op jit(solution)/shard_map/cond/branch_1_fun/while/body/ppermute | solution.py:694
  455.1 30.9 %collective-permute-start.88 = (bf16[80,64,128]{2,1,0:T(8,128)(2,1)}, bf16[80,64,128]{2,1,0:T(8,128)(2,1)}, u32[]{:S(2)}, u32[]{:S(2)}) collective-permute-start(bf16[80,64,128]{2,1,0:T(8,128)(2,1)} %get-tuple-element.3034), channel_id=1, source_target_pairs={{2,0},{3,1},{6,2},{7,3},{4,6},{5,7},{0,4},{1,5}} | collective-permute-start | bytes 3932168 | tf_op jit(solution)/shard_map/cond/branch_1_fun/while/body/ppermute | solution.py:695
  461.1 24.9 %collective-permute-start.91 = (bf16[2,32,64,128]{3,2,1,0:T(8,128)(2,1)}, bf16[2,32,64,128]{3,2,1,0:T(8,128)(2,1)}, u32[]{:S(2)}, u32[]{:S(2)}) collective-permute-start(bf16[2,32,64,128]{3,2,1,0:T(8,128)(2,1)} %get-tuple-element.3035), channel_id=1, source_target_pairs={{0,1},{1,0},{2,3},{3,2},{4,5},{5,4},{6,7},{7,6}} | collective-permute-start | bytes 3145736 | tf_op jit(solution)/shard_map/cond/branch_1_fun/while/body/ppermute | solution.py:705
  496.1 33.1 %collective-permute-start.80 = (bf16[2,80,64,128]{3,2,1,0:T(8,128)(2,1)}, bf16[2,80,64,128]{3,2,1,0:T(8,128)(2,1)S(1)}, u32[]{:S(2)}, u32[]{:S(2)}) collective-permute-start(bf16[2,80,64,128]{3,2,1,0:T(8,128)(2,1)} %get-tuple-element.3015), channel_id=1, source_target_pairs={{0,1},{1,0},{2,3},{3,2},{4,5},{5,4},{6,7},{7,6}} | collective-permute-start | bytes 7864328 | tf_op jit(solution)/shard_map/cond/branch_1_fun/while/body/ppermute | solution.py:704
  497.4 31.0 %collective-permute-start.82 = (bf16[80,64,128]{2,1,0:T(8,128)(2,1)}, bf16[80,64,128]{2,1,0:T(8,128)(2,1)}, u32[]{:S(2)}, u32[]{:S(2)}) collective-permute-start(bf16[80,64,128]{2,1,0:T(8,128)(2,1)} %get-tuple-element.3464), channel_id=1, source_target_pairs={{2,0},{3,1},{6,2},{7,3},{4,6},{5,7},{0,4},{1,5}} | collective-permute-start | bytes 3932168 | tf_op jit(solution)/shard_map/cond/branch_1_fun/while/body/ppermute | solution.py:695
  498.0 31.2 %collective-permute-start.81 = (bf16[80,64,128]{2,1,0:T(8,128)(2,1)}, bf16[80,64,128]{2,1,0:T(8,128)(2,1)}, u32[]{:S(2)}, u32[]{:S(2)}) collective-permute-start(bf16[80,64,128]{2,1,0:T(8,128)(2,1)} %get-tuple-element.3463), channel_id=1, source_target_pairs={{0,2},{1,3},{2,6},{3,7},{6,4},{7,5},{4,0},{5,1}} | collective-permute-start | bytes 3932168 | tf_op jit(solution)/shard_map/cond/branch_1_fun/while/body/ppermute | solution.py:694
  541.3 32.0 %collective-permute-start.86 = (bf16[2,80,64,128]{3,2,1,0:T(8,128)(2,1)}, bf16[2,80,64,128]{3,2,1,0:T(8,128)(2,1)S(1)}, u32[]{:S(2)}, u32[]{:S(2)}) collective-permute-start(bf16[2,80,64,128]{3,2,1,0:T(8,128)(2,1)} %get-tuple-element.3032), channel_id=1, source_target_pairs={{0,1},{1,0},{2,3},{3,2},{4,5},{5,4},{6,7},{7,6}} | collective-permute-start | bytes 7864328 | tf_op jit(solution)/shard_map/cond/branch_1_fun/while/body/ppermute | solution.py:704
  541.9 31.5 %collective-permute-start.87 = (bf16[80,64,128]{2,1,0:T(8,128)(2,1)}, bf16[80,64,128]{2,1,0:T(8,128)(2,1)}, u32[]{:S(2)}, u32[]{:S(2)}) collective-permute-start(bf16[80,64,128]{2,1,0:T(8,128)(2,1)} %get-tuple-element.3033), channel_id=1, source_target_pairs={{0,2},{1,3},{2,6},{3,7},{6,4},{7,5},{4,0},{5,1}} | collective-permute-start | bytes 3932168 | tf_op jit(solution)/shard_map/cond/branch_1_fun/while/body/ppermute | solution.py:694
  542.2 31.2 %collective-permute-start.88 = (bf16[80,64,128]{2,1,0:T(8,128)(2,1)}, bf16[80,64,128]{2,1,0:T(8,128)(2,1)}, u32[]{:S(2)}, u32[]{:S(2)}) collective-permute-start(bf16[80,64,128]{2,1,0:T(8,128)(2,1)} %get-tuple-element.3034), channel_id=1, source_target_pairs={{2,0},{3,1},{6,2},{7,3},{4,6},{5,7},{0,4},{1,5}} | collective-permute-start | bytes 3932168 | tf_op jit(solution)/shard_map/cond/branch_1_fun/while/body/ppermute | solution.py:695
  548.5 24.9 %collective-permute-start.91 = (bf16[2,32,64,128]{3,2,1,0:T(8,128)(2,1)}, bf16[2,32,64,128]{3,2,1,0:T(8,128)(2,1)}, u32[]{:S(2)}, u32[]{:S(2)}) collective-permute-start(bf16[2,32,64,128]{3,2,1,0:T(8,128)(2,1)} %get-tuple-element.3035), channel_id=1, source_target_pairs={{0,1},{1,0},{2,3},{3,2},{4,5},{5,4},{6,7},{7,6}} | collective-permute-start | bytes 3145736 | tf_op jit(solution)/shard_map/cond/branch_1_fun/while/body/ppermute | solution.py:705
  583.6 33.1 %collective-permute-start.80 = (bf16[2,80,64,128]{3,2,1,0:T(8,128)(2,1)}, bf16[2,80,64,128]{3,2,1,0:T(8,128)(2,1)S(1)}, u32[]{:S(2)}, u32[]{:S(2)}) collective-permute-start(bf16[2,80,64,128]{3,2,1,0:T(8,128)(2,1)} %get-tuple-element.3015), channel_id=1, source_target_pairs={{0,1},{1,0},{2,3},{3,2},{4,5},{5,4},{6,7},{7,6}} | collective-permute-start | bytes 7864328 | tf_op jit(solution)/shard_map/cond/branch_1_fun/while/body/ppermute | solution.py:704
  584.1 31.5 %collective-permute-start.82 = (bf16[80,64,128]{2,1,0:T(8,128)(2,1)}, bf16[80,64,128]{2,1,0:T(8,128)(2,1)}, u32[]{:S(2)}, u32[]{:S(2)}) collective-permute-start(bf16[80,64,128]{2,1,0:T(8,128)(2,1)} %get-tuple-element.3464), channel_id=1, source_target_pairs={{2,0},{3,1},{6,2},{7,3},{4,6},{5,7},{0,4},{1,5}} | collective-permute-start | bytes 3932168 | tf_op jit(solution)/shard_map/cond/branch_1_fun/while/body/ppermute | solution.py:695
  585.9 30.8 %collective-permute-start.81 = (bf16[80,64,128]{2,1,0:T(8,128)(2,1)}, bf16[80,64,128]{2,1,0:T(8,128)(2,1)}, u32[]{:S(2)}, u32[]{:S(2)}) collective-permute-start(bf16[80,64,128]{2,1,0:T(8,128)(2,1)} %get-tuple-element.3463), channel_id=1, source_target_pairs={{0,2},{1,3},{2,6},{3,7},{6,4},{7,5},{4,0},{5,1}} | collective-permute-start | bytes 3932168 | tf_op jit(solution)/shard_map/cond/branch_1_fun/while/body/ppermute | solution.py:694
  628.5 32.0 %collective-permute-start.86 = (bf16[2,80,64,128]{3,2,1,0:T(8,128)(2,1)}, bf16[2,80,64,128]{3,2,1,0:T(8,128)(2,1)S(1)}, u32[]{:S(2)}, u32[]{:S(2)}) collective-permute-start(bf16[2,80,64,128]{3,2,1,0:T(8,128)(2,1)} %get-tuple-element.3032), channel_id=1, source_target_pairs={{0,1},{1,0},{2,3},{3,2},{4,5},{5,4},{6,7},{7,6}} | collective-permute-start | bytes 7864328 | tf_op jit(solution)/shard_map/cond/branch_1_fun/while/body/ppermute | solution.py:704
  629.1 31.5 %collective-permute-start.87 = (bf16[80,64,128]{2,1,0:T(8,128)(2,1)}, bf16[80,64,128]{2,1,0:T(8,128)(2,1)}, u32[]{:S(2)}, u32[]{:S(2)}) collective-permute-start(bf16[80,64,128]{2,1,0:T(8,128)(2,1)} %get-tuple-element.3033), channel_id=1, source_target_pairs={{0,2},{1,3},{2,6},{3,7},{6,4},{7,5},{4,0},{5,1}} | collective-permute-start | bytes 3932168 | tf_op jit(solution)/shard_map/cond/branch_1_fun/while/body/ppermute | solution.py:694
  629.5 31.1 %collective-permute-start.88 = (bf16[80,64,128]{2,1,0:T(8,128)(2,1)}, bf16[80,64,128]{2,1,0:T(8,128)(2,1)}, u32[]{:S(2)}, u32[]{:S(2)}) collective-permute-start(bf16[80,64,128]{2,1,0:T(8,128)(2,1)} %get-tuple-element.3034), channel_id=1, source_target_pairs={{2,0},{3,1},{6,2},{7,3},{4,6},{5,7},{0,4},{1,5}} | collective-permute-start | bytes 3932168 | tf_op jit(solution)/shard_map/cond/branch_1_fun/while/body/ppermute | solution.py:695
  635.7 24.9 %collective-permute-start.91 = (bf16[2,32,64,128]{3,2,1,0:T(8,128)(2,1)}, bf16[2,32,64,128]{3,2,1,0:T(8,128)(2,1)}, u32[]{:S(2)}, u32[]{:S(2)}) collective-permute-start(bf16[2,32,64,128]{3,2,1,0:T(8,128)(2,1)} %get-tuple-element.3035), channel_id=1, source_target_pairs={{0,1},{1,0},{2,3},{3,2},{4,5},{5,4},{6,7},{7,6}} | collective-permute-start | bytes 3145736 | tf_op jit(solution)/shard_map/cond/branch_1_fun/while/body/ppermute | solution.py:705
  670.5 33.7 %collective-permute-start.80 = (bf16[2,80,64,128]{3,2,1,0:T(8,128)(2,1)}, bf16[2,80,64,128]{3,2,1,0:T(8,128)(2,1)S(1)}, u32[]{:S(2)}, u32[]{:S(2)}) collective-permute-start(bf16[2,80,64,128]{3,2,1,0:T(8,128)(2,1)} %get-tuple-element.3015), channel_id=1, source_target_pairs={{0,1},{1,0},{2,3},{3,2},{4,5},{5,4},{6,7},{7,6}} | collective-permute-start | bytes 7864328 | tf_op jit(solution)/shard_map/cond/branch_1_fun/while/body/ppermute | solution.py:704
  671.0 16.6 %collective-permute-start.83 = (bf16[80,64,128]{2,1,0:T(8,128)(2,1)}, bf16[80,64,128]{2,1,0:T(8,128)(2,1)}, u32[]{:S(2)}, u32[]{:S(2)}) collective-permute-start(bf16[80,64,128]{2,1,0:T(8,128)(2,1)} %get-tuple-element.3466.rc0), channel_id=1, source_target_pairs={{0,1},{1,0},{2,3},{3,2},{4,5},{5,4},{6,7},{7,6}} | collective-permute-start | bytes 3932168 | tf_op jit(solution)/shard_map/cond/branch_1_fun/while/body/ppermute | solution.py:696
  671.0 31.5 %collective-permute-start.82 = (bf16[80,64,128]{2,1,0:T(8,128)(2,1)}, bf16[80,64,128]{2,1,0:T(8,128)(2,1)}, u32[]{:S(2)}, u32[]{:S(2)}) collective-permute-start(bf16[80,64,128]{2,1,0:T(8,128)(2,1)} %get-tuple-element.3464), channel_id=1, source_target_pairs={{2,0},{3,1},{6,2},{7,3},{4,6},{5,7},{0,4},{1,5}} | collective-permute-start | bytes 3932168 | tf_op jit(solution)/shard_map/cond/branch_1_fun/while/body/ppermute | solution.py:695
  672.9 31.2 %collective-permute-start.81 = (bf16[80,64,128]{2,1,0:T(8,128)(2,1)}, bf16[80,64,128]{2,1,0:T(8,128)(2,1)}, u32[]{:S(2)}, u32[]{:S(2)}) collective-permute-start(bf16[80,64,128]{2,1,0:T(8,128)(2,1)} %get-tuple-element.3463), channel_id=1, source_target_pairs={{0,2},{1,3},{2,6},{3,7},{6,4},{7,5},{4,0},{5,1}} | collective-permute-start | bytes 3932168 | tf_op jit(solution)/shard_map/cond/branch_1_fun/while/body/ppermute | solution.py:694
  716.3 32.0 %collective-permute-start.86 = (bf16[2,80,64,128]{3,2,1,0:T(8,128)(2,1)}, bf16[2,80,64,128]{3,2,1,0:T(8,128)(2,1)S(1)}, u32[]{:S(2)}, u32[]{:S(2)}) collective-permute-start(bf16[2,80,64,128]{3,2,1,0:T(8,128)(2,1)} %get-tuple-element.3032), channel_id=1, source_target_pairs={{0,1},{1,0},{2,3},{3,2},{4,5},{5,4},{6,7},{7,6}} | collective-permute-start | bytes 7864328 | tf_op jit(solution)/shard_map/cond/branch_1_fun/while/body/ppermute | solution.py:704
  716.9 31.5 %collective-permute-start.87 = (bf16[80,64,128]{2,1,0:T(8,128)(2,1)}, bf16[80,64,128]{2,1,0:T(8,128)(2,1)}, u32[]{:S(2)}, u32[]{:S(2)}) collective-permute-start(bf16[80,64,128]{2,1,0:T(8,128)(2,1)} %get-tuple-element.3033), channel_id=1, source_target_pairs={{0,2},{1,3},{2,6},{3,7},{6,4},{7,5},{4,0},{5,1}} | collective-permute-start | bytes 3932168 | tf_op jit(solution)/shard_map/cond/branch_1_fun/while/body/ppermute | solution.py:694
  716.9 31.5 %collective-permute-start.88 = (bf16[80,64,128]{2,1,0:T(8,128)(2,1)}, bf16[80,64,128]{2,1,0:T(8,128)(2,1)}, u32[]{:S(2)}, u32[]{:S(2)}) collective-permute-start(bf16[80,64,128]{2,1,0:T(8,128)(2,1)} %get-tuple-element.3034), channel_id=1, source_target_pairs={{2,0},{3,1},{6,2},{7,3},{4,6},{5,7},{0,4},{1,5}} | collective-permute-start | bytes 3932168 | tf_op jit(solution)/shard_map/cond/branch_1_fun/while/body/ppermute | solution.py:695
  723.4 24.9 %collective-permute-start.91 = (bf16[2,32,64,128]{3,2,1,0:T(8,128)(2,1)}, bf16[2,32,64,128]{3,2,1,0:T(8,128)(2,1)}, u32[]{:S(2)}, u32[]{:S(2)}) collective-permute-start(bf16[2,32,64,128]{3,2,1,0:T(8,128)(2,1)} %get-tuple-element.3035), channel_id=1, source_target_pairs={{0,1},{1,0},{2,3},{3,2},{4,5},{5,4},{6,7},{7,6}} | collective-permute-start | bytes 3145736 | tf_op jit(solution)/shard_map/cond/branch_1_fun/while/body/ppermute | solution.py:705
  758.4 32.7 %collective-permute-start.80 = (bf16[2,80,64,128]{3,2,1,0:T(8,128)(2,1)}, bf16[2,80,64,128]{3,2,1,0:T(8,128)(2,1)S(1)}, u32[]{:S(2)}, u32[]{:S(2)}) collective-permute-start(bf16[2,80,64,128]{3,2,1,0:T(8,128)(2,1)} %get-tuple-element.3015), channel_id=1, source_target_pairs={{0,1},{1,0},{2,3},{3,2},{4,5},{5,4},{6,7},{7,6}} | collective-permute-start | bytes 7864328 | tf_op jit(solution)/shard_map/cond/branch_1_fun/while/body/ppermute | solution.py:704
  759.0 31.5 %collective-permute-start.82 = (bf16[80,64,128]{2,1,0:T(8,128)(2,1)}, bf16[80,64,128]{2,1,0:T(8,128)(2,1)}, u32[]{:S(2)}, u32[]{:S(2)}) collective-permute-start(bf16[80,64,128]{2,1,0:T(8,128)(2,1)} %get-tuple-element.3464), channel_id=1, source_target_pairs={{2,0},{3,1},{6,2},{7,3},{4,6},{5,7},{0,4},{1,5}} | collective-permute-start | bytes 3932168 | tf_op jit(solution)/shard_map/cond/branch_1_fun/while/body/ppermute | solution.py:695
  759.9 31.2 %collective-permute-start.81 = (bf16[80,64,128]{2,1,0:T(8,128)(2,1)}, bf16[80,64,128]{2,1,0:T(8,128)(2,1)}, u32[]{:S(2)}, u32[]{:S(2)}) collective-permute-start(bf16[80,64,128]{2,1,0:T(8,128)(2,1)} %get-tuple-element.3463), channel_id=1, source_target_pairs={{0,2},{1,3},{2,6},{3,7},{6,4},{7,5},{4,0},{5,1}} | collective-permute-start | bytes 3932168 | tf_op jit(solution)/shard_map/cond/branch_1_fun/while/body/ppermute | solution.py:694
  801.9 32.5 %collective-permute-start.86 = (bf16[2,80,64,128]{3,2,1,0:T(8,128)(2,1)}, bf16[2,80,64,128]{3,2,1,0:T(8,128)(2,1)S(1)}, u32[]{:S(2)}, u32[]{:S(2)}) collective-permute-start(bf16[2,80,64,128]{3,2,1,0:T(8,128)(2,1)} %get-tuple-element.3032), channel_id=1, source_target_pairs={{0,1},{1,0},{2,3},{3,2},{4,5},{5,4},{6,7},{7,6}} | collective-permute-start | bytes 7864328 | tf_op jit(solution)/shard_map/cond/branch_1_fun/while/body/ppermute | solution.py:704
  802.4 31.5 %collective-permute-start.87 = (bf16[80,64,128]{2,1,0:T(8,128)(2,1)}, bf16[80,64,128]{2,1,0:T(8,128)(2,1)}, u32[]{:S(2)}, u32[]{:S(2)}) collective-permute-start(bf16[80,64,128]{2,1,0:T(8,128)(2,1)} %get-tuple-element.3033), channel_id=1, source_target_pairs={{0,2},{1,3},{2,6},{3,7},{6,4},{7,5},{4,0},{5,1}} | collective-permute-start | bytes 3932168 | tf_op jit(solution)/shard_map/cond/branch_1_fun/while/body/ppermute | solution.py:694
  803.2 31.2 %collective-permute-start.88 = (bf16[80,64,128]{2,1,0:T(8,128)(2,1)}, bf16[80,64,128]{2,1,0:T(8,128)(2,1)}, u32[]{:S(2)}, u32[]{:S(2)}) collective-permute-start(bf16[80,64,128]{2,1,0:T(8,128)(2,1)} %get-tuple-element.3034), channel_id=1, source_target_pairs={{2,0},{3,1},{6,2},{7,3},{4,6},{5,7},{0,4},{1,5}} | collective-permute-start | bytes 3932168 | tf_op jit(solution)/shard_map/cond/branch_1_fun/while/body/ppermute | solution.py:695
  809.0 25.3 %collective-permute-start.91 = (bf16[2,32,64,128]{3,2,1,0:T(8,128)(2,1)}, bf16[2,32,64,128]{3,2,1,0:T(8,128)(2,1)}, u32[]{:S(2)}, u32[]{:S(2)}) collective-permute-start(bf16[2,32,64,128]{3,2,1,0:T(8,128)(2,1)} %get-tuple-element.3035), channel_id=1, source_target_pairs={{0,1},{1,0},{2,3},{3,2},{4,5},{5,4},{6,7},{7,6}} | collective-permute-start | bytes 3145736 | tf_op jit(solution)/shard_map/cond/branch_1_fun/while/body/ppermute | solution.py:705
  (62 other events, 451.1 us)

commit v7 on v6

--- a/solution.py
+++ b/solution.py
@@ -9,7 +9,7 @@
 
 
 BP, SHIFT = 8, 3
-SIZES = range(84, 56, -4)
+SIZES = range(88, 60, -4)
 NX = 32
 A = 4
 SL = 32
@@ -486,7 +486,7 @@
 
 
 def attn_kernel(NB, last, tab, st_in, q, kn, vn, kc, vc, koi, voi, aoi, st, ko, vo, ao,
-                kb, vb, ob, scores, sel, lsem, wsem):
+                kb, vb, ob, sel, lsem, wsem):
     def cp(i, _):
         st[i] = st_in[i]
         return 0
@@ -527,30 +527,17 @@
             return 0
 
         lax.fori_loop(b0 + 1, BL, wipe, 0)
-        pieces = (m >> 7) + 1
-        span = 128 // BP
-
-        def rows(buf, c):
-            return buf[a, pl.ds(c * span, span)].reshape(-1, 128)
-
-        def score(c, top):
-            sc = lax.dot_general(q[j], rows(kb, c), (((1,), (1,)), ((), ())), preferred_element_type=f32) * (128 ** -0.5)
-            col = lax.broadcasted_iota(i32, sc.shape, 1)
-            head = lax.broadcasted_iota(i32, sc.shape, 0) // 3
-            ok = ((col & 7) == head) & ((col >> 3) <= m - c * 128)
-            sc = jnp.where(ok, sc, -1e30)
-            scores[c] = sc
-            return jnp.maximum(top, jnp.max(sc, axis=1, keepdims=True))
-
-        top = lax.fori_loop(0, pieces, score, jnp.full((24, 1), -1e30, f32))
-
-        def weigh(c, carry):
-            tot, acc = carry
-            w = jnp.exp(scores[c] - top)
-            acc = acc + lax.dot_general(w.astype(bf16), rows(vb, c), (((1,), (0,)), ((), ())), preferred_element_type=f32)
-            return tot + jnp.sum(w, axis=1, keepdims=True), acc
-
-        tot, acc = lax.fori_loop(0, pieces, weigh, (jnp.zeros((24, 1), f32), jnp.zeros((24, 128), f32)))
+        kf = kb[a].reshape(-1, 128)
+        vf = vb[a].reshape(-1, 128)
+        sc = lax.dot_general(q[j], kf, (((1,), (1,)), ((), ())), preferred_element_type=f32) * (128 ** -0.5)
+        col = lax.broadcasted_iota(i32, sc.shape, 1)
+        head = lax.broadcasted_iota(i32, sc.shape, 0) // 3
+        ok = ((col & 7) == head) & ((col >> 3) <= m)
+        sc = jnp.where(ok, sc, -1e30)
+        top = jnp.max(sc, axis=1, keepdims=True)
+        w = jnp.exp(sc - top)
+        tot = jnp.sum(w, axis=1, keepdims=True)
+        acc = lax.dot_general(w.astype(bf16), vf, (((1,), (0,)), ((), ())), preferred_element_type=f32)
         ob[a] = (acc / tot).astype(bf16)
         for src, dst in writes(a, j):
             pltpu.make_async_copy(src, dst, wsem.at[a]).start()
@@ -684,8 +671,7 @@
                     out_shape=(ST, cache, cache, sds((SL, 24, 128))),
                     in_specs=[SMEM, SMEM, VMEM, VMEM, VMEM, ANY, ANY, ANY, ANY, ANY], out_specs=(SMEM, ANY, ANY, ANY),
                     input_output_aliases={7: 1, 8: 2, 9: 3},
-                    scratch_shapes=[buf(A, BL), buf(A, BL), pltpu.VMEM((A, 24, 128), bf16),
-                                    pltpu.VMEM((4, 24, 1024), f32), pltpu.SMEM((SL + 1,), i32),
+                    scratch_shapes=[buf(A, BL), buf(A, BL), pltpu.VMEM((A, 24, 128), bf16), pltpu.SMEM((SL + 1,), i32),
                                     dma(A), dma(A)],
                     cost_estimate=cost(6), name='attend')(tab, st, query, k_new, v_new, kc, vc, ko, vo, ao)
 

time: 859 us -> 856 us (level)
  Pallas kernels: 370 us -> 342 us
  waiting for transfers between devices: 410 us -> 436 us
    pallas_call x19, Pallas kernels: 137 us -> 108 us  [attend(): pl.pallas_call(functools.partial(attn_kernel, NB, last), out_shape=(ST, c...]
    ppermute x18, waiting for transfers between devices: 151 us -> 167 us  [one_round(): nrc1 = lax.ppermute(s1, 'dp', ccw)]
    ppermute x18, waiting for transfers between devices: 161 us -> 171 us  [one_round(): nrc0 = lax.ppermute(s0, 'dp', cw)]
  transfers between devices with their start and end apart: 112 -> 112, of which waited for: 60 -> 59; matrix products, arithmetic and copies ran while one was open for 0% -> 0% of each run, Pallas kernels for 16% -> 14%
where the time goes in v7:
time: 856 us; the launch traced here: 853 us
  waiting for transfers between devices  436 us (51%)
  Pallas kernels  342 us (40%)
  starting transfers between devices  50.9 us (6%)
  local copies, waits for them, and re-layouts  15.4 us (2%)
    pallas_call x18, Pallas kernels, one_round(): pl.pallas_call(functools.partial(round_kernel, NB), out_shape=(ST, chunk,...  185 us
    ppermute x18, waiting for transfers between devices, one_round(): nrc0 = lax.ppermute(s0, 'dp', cw)  171 us
    ppermute x18, waiting for transfers between devices, one_round(): nrc1 = lax.ppermute(s1, 'dp', ccw)  167 us
    pallas_call x19, Pallas kernels, attend(): pl.pallas_call(functools.partial(attn_kernel, NB, last), out_shape=(ST, c...  108 us
    ppermute x18, waiting for transfers between devices, one_round(): npo1 = lax.ppermute(rc1, 'dp', swap)  81.6 us
    ppermute x18, starting transfers between devices, one_round(): nrc1 = lax.ppermute(s1, 'dp', ccw)  24.5 us
    pallas_call x1, Pallas kernels, local(): pl.pallas_call(plan_kernel, out_shape=[sds((n,), i32) for n in (TAB, SL,...  19.1 us
  transfers between devices with their start and end apart: 112, of which 59 were waited for; matrix products, arithmetic and copies ran while one was open for 0% of the time, Pallas kernels for 14%

profile of v7, /device:TPU:0, one launch (start us, length us, event | category | flops | bytes accessed | tf_op | source)
XLA Modules:
  0.0 852.9 jit_solution(4394059343940231258)
XLA Ops:
  0.6 7.8 lens.1.len_ref
  8.4 19.1 %plan.1 = (s32[2568]{0:T(1024)S(1)}, s32[32]{0:T(128)}, s32[64]{0:T(128)S(1)}, s32[1]{0:T(128)}, s32[1]{0:T(128)}) custom-call(s32[1]{0:T(128)} %bitcast.7.me_ref, s32[256]{0:T(256)} %dest_ref.1, s32[8,1,32]{2,1,0:T(1,128)} %lens.1.len_ref), custom_call_target="tpu_custom_call" | custom-call | tf_op jit(solution)/shard_map/plan/pallas_call | solution.py:635
  28.2 824.5 %conditional.1 = (bf16[32,24,128]{2,1,0:T(8,128)(2,1)}, bf16[2048,64,128]{2,1,0:T(8,128)(2,1)}, bf16[2048,64,128]{2,1,0:T(8,128)(2,1)}) conditional(s32[]{:T(128)} %bitcast.9, (s32[2568]{0:T(1024)S(1)}, s32[64]{0:T(128)S(1)}, bf16[2048,64,128]{2,1,0:T(8,128)(2,1)}, bf16[2048,64,128]{2,1,0:T(8,128)(2,1)}, s32[1]{0:T(128)}, ...), branch_computations={%region_0.0_spmd, %region_3.0_spmd, %region_6.0_spmd, %region_9.0_... | conditional | flops 152000000 | bytes 288578240 | solution.py:722
  37.7 5.4 open_merge.9
  43.1 792.2 %while.247 = (s32[]{:T(128)}, s32[64]{0:T(128)S(1)}, bf16[80,64,128]{2,1,0:T(8,128)(2,1)}, bf16[80,64,128]{2,1,0:T(8,128)(2,1)}, bf16[2,80,64,128]{3,2,1,0:T(8,1...) while((s32[]{:T(128)}, s32[64]{0:T(128)S(1)}, ...), condition=%wide.region_8.0_spmd, body=%wide.region_7.0_spmd.sunk | while | flops 128000000 | bytes 209789616 | solution.py:702
  43.7 8.7 %round.22 = (s32[64]{0:T(128)}, bf16[80,64,128]{2,1,0:T(8,128)(2,1)}, bf16[80,64,128]{2,1,0:T(8,128)(2,1)}, bf16[2,80,64,128]{3,2,1,0:T(8,128)(2,1)}, bf16[2,32,...) custom-call(s32[2568]{0:T(1024)S(1)} %get-tuple-element.3431.tab, ...), custom_call_target="tpu_custom_call", output_to_operand_aliasing={{5}: (10, {}), {6}: (11, {}), {7}: (12, {}), {8}: (13, {})} | custom-call | flops 40000000 | bytes 40000000 | tf_op jit(solution)/shard_map/cond/branch_2_fun/while/body/round/pallas_call | solution.py:684
  55.1 4.6 collective-permute-done.68.po1
  59.7 6.7 attend.36
  66.5 18.0 %collective-permute-done.66.rc1 = bf16[80,64,128]{2,1,0:T(8,128)(2,1)} collective-permute-done((bf16[80,64,128]{2,1,0:T(8,128)(2,1)}, bf16[80,64,128]{2,1,0:T(8,128)(2,1)}, u32[]{:S(2)}, u32[]{:S(2)}) %collective-permute-start.66) | collective-permute-done | bytes 1310752 | tf_op jit(solution)/shard_map/cond/branch_2_fun/while/body/ppermute | solution.py:681
  87.1 11.3 %round.23 = (s32[64]{0:T(128)}, bf16[80,64,128]{2,1,0:T(8,128)(2,1)}, bf16[80,64,128]{2,1,0:T(8,128)(2,1)}, bf16[2,80,64,128]{3,2,1,0:T(8,128)(2,1)}, bf16[2,32,...) custom-call(s32[2568]{0:T(1024)S(1)} %get-tuple-element.3431.tab, ...), custom_call_target="tpu_custom_call", output_to_operand_aliasing={{5}: (10, {}), {6}: (11, {}), {7}: (12, {}), {8}: (13, {})} | custom-call | flops 40000000 | bytes 40000000 | tf_op jit(solution)/shard_map/cond/branch_2_fun/while/body/round/pallas_call | solution.py:684
  109.7 20.7 %collective-permute-done.71 = bf16[80,64,128]{2,1,0:T(8,128)(2,1)} collective-permute-done((bf16[80,64,128]{2,1,0:T(8,128)(2,1)}, bf16[80,64,128]{2,1,0:T(8,128)(2,1)}, u32[]{:S(2)}, u32[]{:S(2)}) %collective-permute-start.71) | collective-permute-done | bytes 1310752 | tf_op jit(solution)/shard_map/cond/branch_2_fun/while/body/ppermute | solution.py:680
  131.4 10.7 %round.22 = (s32[64]{0:T(128)}, bf16[80,64,128]{2,1,0:T(8,128)(2,1)}, bf16[80,64,128]{2,1,0:T(8,128)(2,1)}, bf16[2,80,64,128]{3,2,1,0:T(8,128)(2,1)}, bf16[2,32,...) custom-call(s32[2568]{0:T(1024)S(1)} %get-tuple-element.3431.tab, ...), custom_call_target="tpu_custom_call", output_to_operand_aliasing={{5}: (10, {}), {6}: (11, {}), {7}: (12, {}), {8}: (13, {})} | custom-call | flops 40000000 | bytes 40000000 | tf_op jit(solution)/shard_map/cond/branch_2_fun/while/body/round/pallas_call | solution.py:684
  144.7 4.6 collective-permute-done.68.po1
  149.4 5.3 attend.36
  154.7 19.4 %collective-permute-done.66.rc1 = bf16[80,64,128]{2,1,0:T(8,128)(2,1)} collective-permute-done((bf16[80,64,128]{2,1,0:T(8,128)(2,1)}, bf16[80,64,128]{2,1,0:T(8,128)(2,1)}, u32[]{:S(2)}, u32[]{:S(2)}) %collective-permute-start.66) | collective-permute-done | bytes 1310752 | tf_op jit(solution)/shard_map/cond/branch_2_fun/while/body/ppermute | solution.py:681
  176.5 11.6 %round.23 = (s32[64]{0:T(128)}, bf16[80,64,128]{2,1,0:T(8,128)(2,1)}, bf16[80,64,128]{2,1,0:T(8,128)(2,1)}, bf16[2,80,64,128]{3,2,1,0:T(8,128)(2,1)}, bf16[2,32,...) custom-call(s32[2568]{0:T(1024)S(1)} %get-tuple-element.3431.tab, ...), custom_call_target="tpu_custom_call", output_to_operand_aliasing={{5}: (10, {}), {6}: (11, {}), {7}: (12, {}), {8}: (13, {})} | custom-call | flops 40000000 | bytes 40000000 | tf_op jit(solution)/shard_map/cond/branch_2_fun/while/body/round/pallas_call | solution.py:684
  190.6 4.6 collective-permute-done.74
  199.4 20.7 %collective-permute-done.71 = bf16[80,64,128]{2,1,0:T(8,128)(2,1)} collective-permute-done((bf16[80,64,128]{2,1,0:T(8,128)(2,1)}, bf16[80,64,128]{2,1,0:T(8,128)(2,1)}, u32[]{:S(2)}, u32[]{:S(2)}) %collective-permute-start.71) | collective-permute-done | bytes 1310752 | tf_op jit(solution)/shard_map/cond/branch_2_fun/while/body/ppermute | solution.py:680
  220.8 10.8 %round.22 = (s32[64]{0:T(128)}, bf16[80,64,128]{2,1,0:T(8,128)(2,1)}, bf16[80,64,128]{2,1,0:T(8,128)(2,1)}, bf16[2,80,64,128]{3,2,1,0:T(8,128)(2,1)}, bf16[2,32,...) custom-call(s32[2568]{0:T(1024)S(1)} %get-tuple-element.3431.tab, ...), custom_call_target="tpu_custom_call", output_to_operand_aliasing={{5}: (10, {}), {6}: (11, {}), {7}: (12, {}), {8}: (13, {})} | custom-call | flops 40000000 | bytes 40000000 | tf_op jit(solution)/shard_map/cond/branch_2_fun/while/body/round/pallas_call | solution.py:684
  234.2 4.6 collective-permute-done.68.po1
  238.9 5.2 attend.36
  244.1 19.5 %collective-permute-done.66.rc1 = bf16[80,64,128]{2,1,0:T(8,128)(2,1)} collective-permute-done((bf16[80,64,128]{2,1,0:T(8,128)(2,1)}, bf16[80,64,128]{2,1,0:T(8,128)(2,1)}, u32[]{:S(2)}, u32[]{:S(2)}) %collective-permute-start.66) | collective-permute-done | bytes 1310752 | tf_op jit(solution)/shard_map/cond/branch_2_fun/while/body/ppermute | solution.py:681
  265.8 11.3 %round.23 = (s32[64]{0:T(128)}, bf16[80,64,128]{2,1,0:T(8,128)(2,1)}, bf16[80,64,128]{2,1,0:T(8,128)(2,1)}, bf16[2,80,64,128]{3,2,1,0:T(8,128)(2,1)}, bf16[2,32,...) custom-call(s32[2568]{0:T(1024)S(1)} %get-tuple-element.3431.tab, ...), custom_call_target="tpu_custom_call", output_to_operand_aliasing={{5}: (10, {}), {6}: (11, {}), {7}: (12, {}), {8}: (13, {})} | custom-call | flops 40000000 | bytes 40000000 | tf_op jit(solution)/shard_map/cond/branch_2_fun/while/body/round/pallas_call | solution.py:684
  279.8 4.6 collective-permute-done.74
  288.5 20.7 %collective-permute-done.71 = bf16[80,64,128]{2,1,0:T(8,128)(2,1)} collective-permute-done((bf16[80,64,128]{2,1,0:T(8,128)(2,1)}, bf16[80,64,128]{2,1,0:T(8,128)(2,1)}, u32[]{:S(2)}, u32[]{:S(2)}) %collective-permute-start.71) | collective-permute-done | bytes 1310752 | tf_op jit(solution)/shard_map/cond/branch_2_fun/while/body/ppermute | solution.py:680
  310.3 10.4 %round.22 = (s32[64]{0:T(128)}, bf16[80,64,128]{2,1,0:T(8,128)(2,1)}, bf16[80,64,128]{2,1,0:T(8,128)(2,1)}, bf16[2,80,64,128]{3,2,1,0:T(8,128)(2,1)}, bf16[2,32,...) custom-call(s32[2568]{0:T(1024)S(1)} %get-tuple-element.3431.tab, ...), custom_call_target="tpu_custom_call", output_to_operand_aliasing={{5}: (10, {}), {6}: (11, {}), {7}: (12, {}), {8}: (13, {})} | custom-call | flops 40000000 | bytes 40000000 | tf_op jit(solution)/shard_map/cond/branch_2_fun/while/body/round/pallas_call | solution.py:684
  323.3 4.6 collective-permute-done.68.po1
  328.0 5.2 attend.36
  333.2 19.5 %collective-permute-done.66.rc1 = bf16[80,64,128]{2,1,0:T(8,128)(2,1)} collective-permute-done((bf16[80,64,128]{2,1,0:T(8,128)(2,1)}, bf16[80,64,128]{2,1,0:T(8,128)(2,1)}, u32[]{:S(2)}, u32[]{:S(2)}) %collective-permute-start.66) | collective-permute-done | bytes 1310752 | tf_op jit(solution)/shard_map/cond/branch_2_fun/while/body/ppermute | solution.py:681
  354.9 11.1 %round.23 = (s32[64]{0:T(128)}, bf16[80,64,128]{2,1,0:T(8,128)(2,1)}, bf16[80,64,128]{2,1,0:T(8,128)(2,1)}, bf16[2,80,64,128]{3,2,1,0:T(8,128)(2,1)}, bf16[2,32,...) custom-call(s32[2568]{0:T(1024)S(1)} %get-tuple-element.3431.tab, ...), custom_call_target="tpu_custom_call", output_to_operand_aliasing={{5}: (10, {}), {6}: (11, {}), {7}: (12, {}), {8}: (13, {})} | custom-call | flops 40000000 | bytes 40000000 | tf_op jit(solution)/shard_map/cond/branch_2_fun/while/body/round/pallas_call | solution.py:684
  375.0 7.2 attend.37
  382.2 15.8 %collective-permute-done.71 = bf16[80,64,128]{2,1,0:T(8,128)(2,1)} collective-permute-done((bf16[80,64,128]{2,1,0:T(8,128)(2,1)}, bf16[80,64,128]{2,1,0:T(8,128)(2,1)}, u32[]{:S(2)}, u32[]{:S(2)}) %collective-permute-start.71) | collective-permute-done | bytes 1310752 | tf_op jit(solution)/shard_map/cond/branch_2_fun/while/body/ppermute | solution.py:680
  399.0 10.1 %round.22 = (s32[64]{0:T(128)}, bf16[80,64,128]{2,1,0:T(8,128)(2,1)}, bf16[80,64,128]{2,1,0:T(8,128)(2,1)}, bf16[2,80,64,128]{3,2,1,0:T(8,128)(2,1)}, bf16[2,32,...) custom-call(s32[2568]{0:T(1024)S(1)} %get-tuple-element.3431.tab, ...), custom_call_target="tpu_custom_call", output_to_operand_aliasing={{5}: (10, {}), {6}: (11, {}), {7}: (12, {}), {8}: (13, {})} | custom-call | flops 40000000 | bytes 40000000 | tf_op jit(solution)/shard_map/cond/branch_2_fun/while/body/round/pallas_call | solution.py:684
  416.4 7.5 attend.36
  423.9 17.3 %collective-permute-done.66.rc1 = bf16[80,64,128]{2,1,0:T(8,128)(2,1)} collective-permute-done((bf16[80,64,128]{2,1,0:T(8,128)(2,1)}, bf16[80,64,128]{2,1,0:T(8,128)(2,1)}, u32[]{:S(2)}, u32[]{:S(2)}) %collective-permute-start.66) | collective-permute-done | bytes 1310752 | tf_op jit(solution)/shard_map/cond/branch_2_fun/while/body/ppermute | solution.py:681
  443.4 10.8 %round.23 = (s32[64]{0:T(128)}, bf16[80,64,128]{2,1,0:T(8,128)(2,1)}, bf16[80,64,128]{2,1,0:T(8,128)(2,1)}, bf16[2,80,64,128]{3,2,1,0:T(8,128)(2,1)}, bf16[2,32,...) custom-call(s32[2568]{0:T(1024)S(1)} %get-tuple-element.3431.tab, ...), custom_call_target="tpu_custom_call", output_to_operand_aliasing={{5}: (10, {}), {6}: (11, {}), {7}: (12, {}), {8}: (13, {})} | custom-call | flops 40000000 | bytes 40000000 | tf_op jit(solution)/shard_map/cond/branch_2_fun/while/body/round/pallas_call | solution.py:684
  463.2 6.5 attend.37
  469.7 16.5 %collective-permute-done.71 = bf16[80,64,128]{2,1,0:T(8,128)(2,1)} collective-permute-done((bf16[80,64,128]{2,1,0:T(8,128)(2,1)}, bf16[80,64,128]{2,1,0:T(8,128)(2,1)}, u32[]{:S(2)}, u32[]{:S(2)}) %collective-permute-start.71) | collective-permute-done | bytes 1310752 | tf_op jit(solution)/shard_map/cond/branch_2_fun/while/body/ppermute | solution.py:680
  486.9 9.4 %round.22 = (s32[64]{0:T(128)}, bf16[80,64,128]{2,1,0:T(8,128)(2,1)}, bf16[80,64,128]{2,1,0:T(8,128)(2,1)}, bf16[2,80,64,128]{3,2,1,0:T(8,128)(2,1)}, bf16[2,32,...) custom-call(s32[2568]{0:T(1024)S(1)} %get-tuple-element.3431.tab, ...), custom_call_target="tpu_custom_call", output_to_operand_aliasing={{5}: (10, {}), {6}: (11, {}), {7}: (12, {}), {8}: (13, {})} | custom-call | flops 40000000 | bytes 40000000 | tf_op jit(solution)/shard_map/cond/branch_2_fun/while/body/round/pallas_call | solution.py:684
  504.3 6.1 attend.36
  510.4 18.2 %collective-permute-done.66.rc1 = bf16[80,64,128]{2,1,0:T(8,128)(2,1)} collective-permute-done((bf16[80,64,128]{2,1,0:T(8,128)(2,1)}, bf16[80,64,128]{2,1,0:T(8,128)(2,1)}, u32[]{:S(2)}, u32[]{:S(2)}) %collective-permute-start.66) | collective-permute-done | bytes 1310752 | tf_op jit(solution)/shard_map/cond/branch_2_fun/while/body/ppermute | solution.py:681
  531.0 10.6 %round.23 = (s32[64]{0:T(128)}, bf16[80,64,128]{2,1,0:T(8,128)(2,1)}, bf16[80,64,128]{2,1,0:T(8,128)(2,1)}, bf16[2,80,64,128]{3,2,1,0:T(8,128)(2,1)}, bf16[2,32,...) custom-call(s32[2568]{0:T(1024)S(1)} %get-tuple-element.3431.tab, ...), custom_call_target="tpu_custom_call", output_to_operand_aliasing={{5}: (10, {}), {6}: (11, {}), {7}: (12, {}), {8}: (13, {})} | custom-call | flops 40000000 | bytes 40000000 | tf_op jit(solution)/shard_map/cond/branch_2_fun/while/body/round/pallas_call | solution.py:684
  550.6 5.7 attend.37
  556.3 17.3 %collective-permute-done.71 = bf16[80,64,128]{2,1,0:T(8,128)(2,1)} collective-permute-done((bf16[80,64,128]{2,1,0:T(8,128)(2,1)}, bf16[80,64,128]{2,1,0:T(8,128)(2,1)}, u32[]{:S(2)}, u32[]{:S(2)}) %collective-permute-start.71) | collective-permute-done | bytes 1310752 | tf_op jit(solution)/shard_map/cond/branch_2_fun/while/body/ppermute | solution.py:680
  574.2 9.5 %round.22 = (s32[64]{0:T(128)}, bf16[80,64,128]{2,1,0:T(8,128)(2,1)}, bf16[80,64,128]{2,1,0:T(8,128)(2,1)}, bf16[2,80,64,128]{3,2,1,0:T(8,128)(2,1)}, bf16[2,32,...) custom-call(s32[2568]{0:T(1024)S(1)} %get-tuple-element.3431.tab, ...), custom_call_target="tpu_custom_call", output_to_operand_aliasing={{5}: (10, {}), {6}: (11, {}), {7}: (12, {}), {8}: (13, {})} | custom-call | flops 40000000 | bytes 40000000 | tf_op jit(solution)/shard_map/cond/branch_2_fun/while/body/round/pallas_call | solution.py:684
  591.1 7.5 attend.36
  598.6 17.2 %collective-permute-done.66.rc1 = bf16[80,64,128]{2,1,0:T(8,128)(2,1)} collective-permute-done((bf16[80,64,128]{2,1,0:T(8,128)(2,1)}, bf16[80,64,128]{2,1,0:T(8,128)(2,1)}, u32[]{:S(2)}, u32[]{:S(2)}) %collective-permute-start.66) | collective-permute-done | bytes 1310752 | tf_op jit(solution)/shard_map/cond/branch_2_fun/while/body/ppermute | solution.py:681
  618.4 10.4 %round.23 = (s32[64]{0:T(128)}, bf16[80,64,128]{2,1,0:T(8,128)(2,1)}, bf16[80,64,128]{2,1,0:T(8,128)(2,1)}, bf16[2,80,64,128]{3,2,1,0:T(8,128)(2,1)}, bf16[2,32,...) custom-call(s32[2568]{0:T(1024)S(1)} %get-tuple-element.3431.tab, ...), custom_call_target="tpu_custom_call", output_to_operand_aliasing={{5}: (10, {}), {6}: (11, {}), {7}: (12, {}), {8}: (13, {})} | custom-call | flops 40000000 | bytes 40000000 | tf_op jit(solution)/shard_map/cond/branch_2_fun/while/body/round/pallas_call | solution.py:684
  637.8 5.3 attend.37
  643.0 17.8 %collective-permute-done.71 = bf16[80,64,128]{2,1,0:T(8,128)(2,1)} collective-permute-done((bf16[80,64,128]{2,1,0:T(8,128)(2,1)}, bf16[80,64,128]{2,1,0:T(8,128)(2,1)}, u32[]{:S(2)}, u32[]{:S(2)}) %collective-permute-start.71) | collective-permute-done | bytes 1310752 | tf_op jit(solution)/shard_map/cond/branch_2_fun/while/body/ppermute | solution.py:680
  661.4 9.2 %round.22 = (s32[64]{0:T(128)}, bf16[80,64,128]{2,1,0:T(8,128)(2,1)}, bf16[80,64,128]{2,1,0:T(8,128)(2,1)}, bf16[2,80,64,128]{3,2,1,0:T(8,128)(2,1)}, bf16[2,32,...) custom-call(s32[2568]{0:T(1024)S(1)} %get-tuple-element.3431.tab, ...), custom_call_target="tpu_custom_call", output_to_operand_aliasing={{5}: (10, {}), {6}: (11, {}), {7}: (12, {}), {8}: (13, {})} | custom-call | flops 40000000 | bytes 40000000 | tf_op jit(solution)/shard_map/cond/branch_2_fun/while/body/round/pallas_call | solution.py:684
  678.0 7.2 attend.36
  685.2 17.6 %collective-permute-done.66.rc1 = bf16[80,64,128]{2,1,0:T(8,128)(2,1)} collective-permute-done((bf16[80,64,128]{2,1,0:T(8,128)(2,1)}, bf16[80,64,128]{2,1,0:T(8,128)(2,1)}, u32[]{:S(2)}, u32[]{:S(2)}) %collective-permute-start.66) | collective-permute-done | bytes 1310752 | tf_op jit(solution)/shard_map/cond/branch_2_fun/while/body/ppermute | solution.py:681
  705.9 10.6 %round.23 = (s32[64]{0:T(128)}, bf16[80,64,128]{2,1,0:T(8,128)(2,1)}, bf16[80,64,128]{2,1,0:T(8,128)(2,1)}, bf16[2,80,64,128]{3,2,1,0:T(8,128)(2,1)}, bf16[2,32,...) custom-call(s32[2568]{0:T(1024)S(1)} %get-tuple-element.3431.tab, ...), custom_call_target="tpu_custom_call", output_to_operand_aliasing={{5}: (10, {}), {6}: (11, {}), {7}: (12, {}), {8}: (13, {})} | custom-call | flops 40000000 | bytes 40000000 | tf_op jit(solution)/shard_map/cond/branch_2_fun/while/body/round/pallas_call | solution.py:684
  725.5 6.2 attend.37
  731.8 16.8 %collective-permute-done.71 = bf16[80,64,128]{2,1,0:T(8,128)(2,1)} collective-permute-done((bf16[80,64,128]{2,1,0:T(8,128)(2,1)}, bf16[80,64,128]{2,1,0:T(8,128)(2,1)}, u32[]{:S(2)}, u32[]{:S(2)}) %collective-permute-start.71) | collective-permute-done | bytes 1310752 | tf_op jit(solution)/shard_map/cond/branch_2_fun/while/body/ppermute | solution.py:680
  749.2 9.5 %round.22 = (s32[64]{0:T(128)}, bf16[80,64,128]{2,1,0:T(8,128)(2,1)}, bf16[80,64,128]{2,1,0:T(8,128)(2,1)}, bf16[2,80,64,128]{3,2,1,0:T(8,128)(2,1)}, bf16[2,32,...) custom-call(s32[2568]{0:T(1024)S(1)} %get-tuple-element.3431.tab, ...), custom_call_target="tpu_custom_call", output_to_operand_aliasing={{5}: (10, {}), {6}: (11, {}), {7}: (12, {}), {8}: (13, {})} | custom-call | flops 40000000 | bytes 40000000 | tf_op jit(solution)/shard_map/cond/branch_2_fun/while/body/round/pallas_call | solution.py:684
  766.0 6.2 attend.36
  772.2 18.5 %collective-permute-done.66.rc1 = bf16[80,64,128]{2,1,0:T(8,128)(2,1)} collective-permute-done((bf16[80,64,128]{2,1,0:T(8,128)(2,1)}, bf16[80,64,128]{2,1,0:T(8,128)(2,1)}, u32[]{:S(2)}, u32[]{:S(2)}) %collective-permute-start.66) | collective-permute-done | bytes 1310752 | tf_op jit(solution)/shard_map/cond/branch_2_fun/while/body/ppermute | solution.py:681
  792.9 9.2 %round.23 = (s32[64]{0:T(128)}, bf16[80,64,128]{2,1,0:T(8,128)(2,1)}, bf16[80,64,128]{2,1,0:T(8,128)(2,1)}, bf16[2,80,64,128]{3,2,1,0:T(8,128)(2,1)}, bf16[2,32,...) custom-call(s32[2568]{0:T(1024)S(1)} %get-tuple-element.3431.tab, ...), custom_call_target="tpu_custom_call", output_to_operand_aliasing={{5}: (10, {}), {6}: (11, {}), {7}: (12, {}), {8}: (13, {})} | custom-call | flops 40000000 | bytes 40000000 | tf_op jit(solution)/shard_map/cond/branch_2_fun/while/body/round/pallas_call | solution.py:684
  811.1 6.2 attend.37
  817.4 16.8 %collective-permute-done.71 = bf16[80,64,128]{2,1,0:T(8,128)(2,1)} collective-permute-done((bf16[80,64,128]{2,1,0:T(8,128)(2,1)}, bf16[80,64,128]{2,1,0:T(8,128)(2,1)}, u32[]{:S(2)}, u32[]{:S(2)}) %collective-permute-start.71) | collective-permute-done | bytes 1310752 | tf_op jit(solution)/shard_map/cond/branch_2_fun/while/body/ppermute | solution.py:680
  835.8 4.9 close.9
  844.9 7.3 attend.23
  (235 shorter events, 164.4 us)
Async XLA Ops:
  52.5 33.1 %collective-permute-start.64 = (bf16[2,80,64,128]{3,2,1,0:T(8,128)(2,1)}, bf16[2,80,64,128]{3,2,1,0:T(8,128)(2,1)S(1)}, u32[]{:S(2)}, u32[]{:S(2)}) collective-permute-start(bf16[2,80,64,128]{3,2,1,0:T(8,128)(2,1)} %get-tuple-element.2963), channel_id=1, source_target_pairs={{0,1},{1,0},{2,3},{3,2},{4,5},{5,4},{6,7},{7,6}} | collective-permute-start | bytes 7864328 | tf_op jit(solution)/shard_map/cond/branch_2_fun/while/body/ppermute | solution.py:690
  53.0 31.5 %collective-permute-start.66 = (bf16[80,64,128]{2,1,0:T(8,128)(2,1)}, bf16[80,64,128]{2,1,0:T(8,128)(2,1)}, u32[]{:S(2)}, u32[]{:S(2)}) collective-permute-start(bf16[80,64,128]{2,1,0:T(8,128)(2,1)} %get-tuple-element.3395), channel_id=1, source_target_pairs={{2,0},{3,1},{6,2},{7,3},{4,6},{5,7},{0,4},{1,5}} | collective-permute-start | bytes 3932168 | tf_op jit(solution)/shard_map/cond/branch_2_fun/while/body/ppermute | solution.py:681
  54.3 31.2 %collective-permute-start.65 = (bf16[80,64,128]{2,1,0:T(8,128)(2,1)}, bf16[80,64,128]{2,1,0:T(8,128)(2,1)}, u32[]{:S(2)}, u32[]{:S(2)}) collective-permute-start(bf16[80,64,128]{2,1,0:T(8,128)(2,1)} %get-tuple-element.3394), channel_id=1, source_target_pairs={{0,2},{1,3},{2,6},{3,7},{6,4},{7,5},{4,0},{5,1}} | collective-permute-start | bytes 3932168 | tf_op jit(solution)/shard_map/cond/branch_2_fun/while/body/ppermute | solution.py:680
  98.4 32.4 %collective-permute-start.70 = (bf16[2,80,64,128]{3,2,1,0:T(8,128)(2,1)}, bf16[2,80,64,128]{3,2,1,0:T(8,128)(2,1)S(1)}, u32[]{:S(2)}, u32[]{:S(2)}) collective-permute-start(bf16[2,80,64,128]{3,2,1,0:T(8,128)(2,1)} %get-tuple-element.2980), channel_id=1, source_target_pairs={{0,1},{1,0},{2,3},{3,2},{4,5},{5,4},{6,7},{7,6}} | collective-permute-start | bytes 7864328 | tf_op jit(solution)/shard_map/cond/branch_2_fun/while/body/ppermute | solution.py:690
  99.0 31.5 %collective-permute-start.71 = (bf16[80,64,128]{2,1,0:T(8,128)(2,1)}, bf16[80,64,128]{2,1,0:T(8,128)(2,1)}, u32[]{:S(2)}, u32[]{:S(2)}) collective-permute-start(bf16[80,64,128]{2,1,0:T(8,128)(2,1)} %get-tuple-element.2981), channel_id=1, source_target_pairs={{0,2},{1,3},{2,6},{3,7},{6,4},{7,5},{4,0},{5,1}} | collective-permute-start | bytes 3932168 | tf_op jit(solution)/shard_map/cond/branch_2_fun/while/body/ppermute | solution.py:680
  99.4 31.4 %collective-permute-start.72 = (bf16[80,64,128]{2,1,0:T(8,128)(2,1)}, bf16[80,64,128]{2,1,0:T(8,128)(2,1)}, u32[]{:S(2)}, u32[]{:S(2)}) collective-permute-start(bf16[80,64,128]{2,1,0:T(8,128)(2,1)} %get-tuple-element.2982), channel_id=1, source_target_pairs={{2,0},{3,1},{6,2},{7,3},{4,6},{5,7},{0,4},{1,5}} | collective-permute-start | bytes 3932168 | tf_op jit(solution)/shard_map/cond/branch_2_fun/while/body/ppermute | solution.py:681
  105.5 25.2 %collective-permute-start.75 = (bf16[2,32,64,128]{3,2,1,0:T(8,128)(2,1)}, bf16[2,32,64,128]{3,2,1,0:T(8,128)(2,1)}, u32[]{:S(2)}, u32[]{:S(2)}) collective-permute-start(bf16[2,32,64,128]{3,2,1,0:T(8,128)(2,1)} %get-tuple-element.2983), channel_id=1, source_target_pairs={{0,1},{1,0},{2,3},{3,2},{4,5},{5,4},{6,7},{7,6}} | collective-permute-start | bytes 3145736 | tf_op jit(solution)/shard_map/cond/branch_2_fun/while/body/ppermute | solution.py:691
  142.1 32.8 %collective-permute-start.64 = (bf16[2,80,64,128]{3,2,1,0:T(8,128)(2,1)}, bf16[2,80,64,128]{3,2,1,0:T(8,128)(2,1)S(1)}, u32[]{:S(2)}, u32[]{:S(2)}) collective-permute-start(bf16[2,80,64,128]{3,2,1,0:T(8,128)(2,1)} %get-tuple-element.2963), channel_id=1, source_target_pairs={{0,1},{1,0},{2,3},{3,2},{4,5},{5,4},{6,7},{7,6}} | collective-permute-start | bytes 7864328 | tf_op jit(solution)/shard_map/cond/branch_2_fun/while/body/ppermute | solution.py:690
  142.7 31.5 %collective-permute-start.66 = (bf16[80,64,128]{2,1,0:T(8,128)(2,1)}, bf16[80,64,128]{2,1,0:T(8,128)(2,1)}, u32[]{:S(2)}, u32[]{:S(2)}) collective-permute-start(bf16[80,64,128]{2,1,0:T(8,128)(2,1)} %get-tuple-element.3395), channel_id=1, source_target_pairs={{2,0},{3,1},{6,2},{7,3},{4,6},{5,7},{0,4},{1,5}} | collective-permute-start | bytes 3932168 | tf_op jit(solution)/shard_map/cond/branch_2_fun/while/body/ppermute | solution.py:681
  143.7 31.2 %collective-permute-start.65 = (bf16[80,64,128]{2,1,0:T(8,128)(2,1)}, bf16[80,64,128]{2,1,0:T(8,128)(2,1)}, u32[]{:S(2)}, u32[]{:S(2)}) collective-permute-start(bf16[80,64,128]{2,1,0:T(8,128)(2,1)} %get-tuple-element.3394), channel_id=1, source_target_pairs={{0,2},{1,3},{2,6},{3,7},{6,4},{7,5},{4,0},{5,1}} | collective-permute-start | bytes 3932168 | tf_op jit(solution)/shard_map/cond/branch_2_fun/while/body/ppermute | solution.py:680
  188.0 32.1 %collective-permute-start.70 = (bf16[2,80,64,128]{3,2,1,0:T(8,128)(2,1)}, bf16[2,80,64,128]{3,2,1,0:T(8,128)(2,1)S(1)}, u32[]{:S(2)}, u32[]{:S(2)}) collective-permute-start(bf16[2,80,64,128]{3,2,1,0:T(8,128)(2,1)} %get-tuple-element.2980), channel_id=1, source_target_pairs={{0,1},{1,0},{2,3},{3,2},{4,5},{5,4},{6,7},{7,6}} | collective-permute-start | bytes 7864328 | tf_op jit(solution)/shard_map/cond/branch_2_fun/while/body/ppermute | solution.py:690
  188.6 31.5 %collective-permute-start.71 = (bf16[80,64,128]{2,1,0:T(8,128)(2,1)}, bf16[80,64,128]{2,1,0:T(8,128)(2,1)}, u32[]{:S(2)}, u32[]{:S(2)}) collective-permute-start(bf16[80,64,128]{2,1,0:T(8,128)(2,1)} %get-tuple-element.2981), channel_id=1, source_target_pairs={{0,2},{1,3},{2,6},{3,7},{6,4},{7,5},{4,0},{5,1}} | collective-permute-start | bytes 3932168 | tf_op jit(solution)/shard_map/cond/branch_2_fun/while/body/ppermute | solution.py:680
  188.9 31.2 %collective-permute-start.72 = (bf16[80,64,128]{2,1,0:T(8,128)(2,1)}, bf16[80,64,128]{2,1,0:T(8,128)(2,1)}, u32[]{:S(2)}, u32[]{:S(2)}) collective-permute-start(bf16[80,64,128]{2,1,0:T(8,128)(2,1)} %get-tuple-element.2982), channel_id=1, source_target_pairs={{2,0},{3,1},{6,2},{7,3},{4,6},{5,7},{0,4},{1,5}} | collective-permute-start | bytes 3932168 | tf_op jit(solution)/shard_map/cond/branch_2_fun/while/body/ppermute | solution.py:681
  195.2 24.9 %collective-permute-start.75 = (bf16[2,32,64,128]{3,2,1,0:T(8,128)(2,1)}, bf16[2,32,64,128]{3,2,1,0:T(8,128)(2,1)}, u32[]{:S(2)}, u32[]{:S(2)}) collective-permute-start(bf16[2,32,64,128]{3,2,1,0:T(8,128)(2,1)} %get-tuple-element.2983), channel_id=1, source_target_pairs={{0,1},{1,0},{2,3},{3,2},{4,5},{5,4},{6,7},{7,6}} | collective-permute-start | bytes 3145736 | tf_op jit(solution)/shard_map/cond/branch_2_fun/while/body/ppermute | solution.py:691
  231.6 32.7 %collective-permute-start.64 = (bf16[2,80,64,128]{3,2,1,0:T(8,128)(2,1)}, bf16[2,80,64,128]{3,2,1,0:T(8,128)(2,1)S(1)}, u32[]{:S(2)}, u32[]{:S(2)}) collective-permute-start(bf16[2,80,64,128]{3,2,1,0:T(8,128)(2,1)} %get-tuple-element.2963), channel_id=1, source_target_pairs={{0,1},{1,0},{2,3},{3,2},{4,5},{5,4},{6,7},{7,6}} | collective-permute-start | bytes 7864328 | tf_op jit(solution)/shard_map/cond/branch_2_fun/while/body/ppermute | solution.py:690
  232.2 31.5 %collective-permute-start.66 = (bf16[80,64,128]{2,1,0:T(8,128)(2,1)}, bf16[80,64,128]{2,1,0:T(8,128)(2,1)}, u32[]{:S(2)}, u32[]{:S(2)}) collective-permute-start(bf16[80,64,128]{2,1,0:T(8,128)(2,1)} %get-tuple-element.3395), channel_id=1, source_target_pairs={{2,0},{3,1},{6,2},{7,3},{4,6},{5,7},{0,4},{1,5}} | collective-permute-start | bytes 3932168 | tf_op jit(solution)/shard_map/cond/branch_2_fun/while/body/ppermute | solution.py:681
  233.1 31.2 %collective-permute-start.65 = (bf16[80,64,128]{2,1,0:T(8,128)(2,1)}, bf16[80,64,128]{2,1,0:T(8,128)(2,1)}, u32[]{:S(2)}, u32[]{:S(2)}) collective-permute-start(bf16[80,64,128]{2,1,0:T(8,128)(2,1)} %get-tuple-element.3394), channel_id=1, source_target_pairs={{0,2},{1,3},{2,6},{3,7},{6,4},{7,5},{4,0},{5,1}} | collective-permute-start | bytes 3932168 | tf_op jit(solution)/shard_map/cond/branch_2_fun/while/body/ppermute | solution.py:680
  277.2 32.5 %collective-permute-start.70 = (bf16[2,80,64,128]{3,2,1,0:T(8,128)(2,1)}, bf16[2,80,64,128]{3,2,1,0:T(8,128)(2,1)S(1)}, u32[]{:S(2)}, u32[]{:S(2)}) collective-permute-start(bf16[2,80,64,128]{3,2,1,0:T(8,128)(2,1)} %get-tuple-element.2980), channel_id=1, source_target_pairs={{0,1},{1,0},{2,3},{3,2},{4,5},{5,4},{6,7},{7,6}} | collective-permute-start | bytes 7864328 | tf_op jit(solution)/shard_map/cond/branch_2_fun/while/body/ppermute | solution.py:690
  277.7 31.5 %collective-permute-start.71 = (bf16[80,64,128]{2,1,0:T(8,128)(2,1)}, bf16[80,64,128]{2,1,0:T(8,128)(2,1)}, u32[]{:S(2)}, u32[]{:S(2)}) collective-permute-start(bf16[80,64,128]{2,1,0:T(8,128)(2,1)} %get-tuple-element.2981), channel_id=1, source_target_pairs={{0,2},{1,3},{2,6},{3,7},{6,4},{7,5},{4,0},{5,1}} | collective-permute-start | bytes 3932168 | tf_op jit(solution)/shard_map/cond/branch_2_fun/while/body/ppermute | solution.py:680
  278.5 31.2 %collective-permute-start.72 = (bf16[80,64,128]{2,1,0:T(8,128)(2,1)}, bf16[80,64,128]{2,1,0:T(8,128)(2,1)}, u32[]{:S(2)}, u32[]{:S(2)}) collective-permute-start(bf16[80,64,128]{2,1,0:T(8,128)(2,1)} %get-tuple-element.2982), channel_id=1, source_target_pairs={{2,0},{3,1},{6,2},{7,3},{4,6},{5,7},{0,4},{1,5}} | collective-permute-start | bytes 3932168 | tf_op jit(solution)/shard_map/cond/branch_2_fun/while/body/ppermute | solution.py:681
  284.3 25.4 %collective-permute-start.75 = (bf16[2,32,64,128]{3,2,1,0:T(8,128)(2,1)}, bf16[2,32,64,128]{3,2,1,0:T(8,128)(2,1)}, u32[]{:S(2)}, u32[]{:S(2)}) collective-permute-start(bf16[2,32,64,128]{3,2,1,0:T(8,128)(2,1)} %get-tuple-element.2983), channel_id=1, source_target_pairs={{0,1},{1,0},{2,3},{3,2},{4,5},{5,4},{6,7},{7,6}} | collective-permute-start | bytes 3145736 | tf_op jit(solution)/shard_map/cond/branch_2_fun/while/body/ppermute | solution.py:691
  320.7 32.7 %collective-permute-start.64 = (bf16[2,80,64,128]{3,2,1,0:T(8,128)(2,1)}, bf16[2,80,64,128]{3,2,1,0:T(8,128)(2,1)S(1)}, u32[]{:S(2)}, u32[]{:S(2)}) collective-permute-start(bf16[2,80,64,128]{3,2,1,0:T(8,128)(2,1)} %get-tuple-element.2963), channel_id=1, source_target_pairs={{0,1},{1,0},{2,3},{3,2},{4,5},{5,4},{6,7},{7,6}} | collective-permute-start | bytes 7864328 | tf_op jit(solution)/shard_map/cond/branch_2_fun/while/body/ppermute | solution.py:690
  321.2 31.5 %collective-permute-start.66 = (bf16[80,64,128]{2,1,0:T(8,128)(2,1)}, bf16[80,64,128]{2,1,0:T(8,128)(2,1)}, u32[]{:S(2)}, u32[]{:S(2)}) collective-permute-start(bf16[80,64,128]{2,1,0:T(8,128)(2,1)} %get-tuple-element.3395), channel_id=1, source_target_pairs={{2,0},{3,1},{6,2},{7,3},{4,6},{5,7},{0,4},{1,5}} | collective-permute-start | bytes 3932168 | tf_op jit(solution)/shard_map/cond/branch_2_fun/while/body/ppermute | solution.py:681
  322.2 31.2 %collective-permute-start.65 = (bf16[80,64,128]{2,1,0:T(8,128)(2,1)}, bf16[80,64,128]{2,1,0:T(8,128)(2,1)}, u32[]{:S(2)}, u32[]{:S(2)}) collective-permute-start(bf16[80,64,128]{2,1,0:T(8,128)(2,1)} %get-tuple-element.3394), channel_id=1, source_target_pairs={{0,2},{1,3},{2,6},{3,7},{6,4},{7,5},{4,0},{5,1}} | collective-permute-start | bytes 3932168 | tf_op jit(solution)/shard_map/cond/branch_2_fun/while/body/ppermute | solution.py:680
  366.0 32.4 %collective-permute-start.70 = (bf16[2,80,64,128]{3,2,1,0:T(8,128)(2,1)}, bf16[2,80,64,128]{3,2,1,0:T(8,128)(2,1)S(1)}, u32[]{:S(2)}, u32[]{:S(2)}) collective-permute-start(bf16[2,80,64,128]{3,2,1,0:T(8,128)(2,1)} %get-tuple-element.2980), channel_id=1, source_target_pairs={{0,1},{1,0},{2,3},{3,2},{4,5},{5,4},{6,7},{7,6}} | collective-permute-start | bytes 7864328 | tf_op jit(solution)/shard_map/cond/branch_2_fun/while/body/ppermute | solution.py:690
  366.6 31.5 %collective-permute-start.71 = (bf16[80,64,128]{2,1,0:T(8,128)(2,1)}, bf16[80,64,128]{2,1,0:T(8,128)(2,1)}, u32[]{:S(2)}, u32[]{:S(2)}) collective-permute-start(bf16[80,64,128]{2,1,0:T(8,128)(2,1)} %get-tuple-element.2981), channel_id=1, source_target_pairs={{0,2},{1,3},{2,6},{3,7},{6,4},{7,5},{4,0},{5,1}} | collective-permute-start | bytes 3932168 | tf_op jit(solution)/shard_map/cond/branch_2_fun/while/body/ppermute | solution.py:680
  367.2 31.2 %collective-permute-start.72 = (bf16[80,64,128]{2,1,0:T(8,128)(2,1)}, bf16[80,64,128]{2,1,0:T(8,128)(2,1)}, u32[]{:S(2)}, u32[]{:S(2)}) collective-permute-start(bf16[80,64,128]{2,1,0:T(8,128)(2,1)} %get-tuple-element.2982), channel_id=1, source_target_pairs={{2,0},{3,1},{6,2},{7,3},{4,6},{5,7},{0,4},{1,5}} | collective-permute-start | bytes 3932168 | tf_op jit(solution)/shard_map/cond/branch_2_fun/while/body/ppermute | solution.py:681
  373.2 25.2 %collective-permute-start.75 = (bf16[2,32,64,128]{3,2,1,0:T(8,128)(2,1)}, bf16[2,32,64,128]{3,2,1,0:T(8,128)(2,1)}, u32[]{:S(2)}, u32[]{:S(2)}) collective-permute-start(bf16[2,32,64,128]{3,2,1,0:T(8,128)(2,1)} %get-tuple-element.2983), channel_id=1, source_target_pairs={{0,1},{1,0},{2,3},{3,2},{4,5},{5,4},{6,7},{7,6}} | collective-permute-start | bytes 3145736 | tf_op jit(solution)/shard_map/cond/branch_2_fun/while/body/ppermute | solution.py:691
  409.1 32.7 %collective-permute-start.64 = (bf16[2,80,64,128]{3,2,1,0:T(8,128)(2,1)}, bf16[2,80,64,128]{3,2,1,0:T(8,128)(2,1)S(1)}, u32[]{:S(2)}, u32[]{:S(2)}) collective-permute-start(bf16[2,80,64,128]{3,2,1,0:T(8,128)(2,1)} %get-tuple-element.2963), channel_id=1, source_target_pairs={{0,1},{1,0},{2,3},{3,2},{4,5},{5,4},{6,7},{7,6}} | collective-permute-start | bytes 7864328 | tf_op jit(solution)/shard_map/cond/branch_2_fun/while/body/ppermute | solution.py:690
  409.7 31.5 %collective-permute-start.66 = (bf16[80,64,128]{2,1,0:T(8,128)(2,1)}, bf16[80,64,128]{2,1,0:T(8,128)(2,1)}, u32[]{:S(2)}, u32[]{:S(2)}) collective-permute-start(bf16[80,64,128]{2,1,0:T(8,128)(2,1)} %get-tuple-element.3395), channel_id=1, source_target_pairs={{2,0},{3,1},{6,2},{7,3},{4,6},{5,7},{0,4},{1,5}} | collective-permute-start | bytes 3932168 | tf_op jit(solution)/shard_map/cond/branch_2_fun/while/body/ppermute | solution.py:681
  410.6 31.2 %collective-permute-start.65 = (bf16[80,64,128]{2,1,0:T(8,128)(2,1)}, bf16[80,64,128]{2,1,0:T(8,128)(2,1)}, u32[]{:S(2)}, u32[]{:S(2)}) collective-permute-start(bf16[80,64,128]{2,1,0:T(8,128)(2,1)} %get-tuple-element.3394), channel_id=1, source_target_pairs={{0,2},{1,3},{2,6},{3,7},{6,4},{7,5},{4,0},{5,1}} | collective-permute-start | bytes 3932168 | tf_op jit(solution)/shard_map/cond/branch_2_fun/while/body/ppermute | solution.py:680
  454.2 32.0 %collective-permute-start.70 = (bf16[2,80,64,128]{3,2,1,0:T(8,128)(2,1)}, bf16[2,80,64,128]{3,2,1,0:T(8,128)(2,1)S(1)}, u32[]{:S(2)}, u32[]{:S(2)}) collective-permute-start(bf16[2,80,64,128]{3,2,1,0:T(8,128)(2,1)} %get-tuple-element.2980), channel_id=1, source_target_pairs={{0,1},{1,0},{2,3},{3,2},{4,5},{5,4},{6,7},{7,6}} | collective-permute-start | bytes 7864328 | tf_op jit(solution)/shard_map/cond/branch_2_fun/while/body/ppermute | solution.py:690
  454.8 31.4 %collective-permute-start.71 = (bf16[80,64,128]{2,1,0:T(8,128)(2,1)}, bf16[80,64,128]{2,1,0:T(8,128)(2,1)}, u32[]{:S(2)}, u32[]{:S(2)}) collective-permute-start(bf16[80,64,128]{2,1,0:T(8,128)(2,1)} %get-tuple-element.2981), channel_id=1, source_target_pairs={{0,2},{1,3},{2,6},{3,7},{6,4},{7,5},{4,0},{5,1}} | collective-permute-start | bytes 3932168 | tf_op jit(solution)/shard_map/cond/branch_2_fun/while/body/ppermute | solution.py:680
  455.4 30.9 %collective-permute-start.72 = (bf16[80,64,128]{2,1,0:T(8,128)(2,1)}, bf16[80,64,128]{2,1,0:T(8,128)(2,1)}, u32[]{:S(2)}, u32[]{:S(2)}) collective-permute-start(bf16[80,64,128]{2,1,0:T(8,128)(2,1)} %get-tuple-element.2982), channel_id=1, source_target_pairs={{2,0},{3,1},{6,2},{7,3},{4,6},{5,7},{0,4},{1,5}} | collective-permute-start | bytes 3932168 | tf_op jit(solution)/shard_map/cond/branch_2_fun/while/body/ppermute | solution.py:681
  461.3 24.9 %collective-permute-start.75 = (bf16[2,32,64,128]{3,2,1,0:T(8,128)(2,1)}, bf16[2,32,64,128]{3,2,1,0:T(8,128)(2,1)}, u32[]{:S(2)}, u32[]{:S(2)}) collective-permute-start(bf16[2,32,64,128]{3,2,1,0:T(8,128)(2,1)} %get-tuple-element.2983), channel_id=1, source_target_pairs={{0,1},{1,0},{2,3},{3,2},{4,5},{5,4},{6,7},{7,6}} | collective-permute-start | bytes 3145736 | tf_op jit(solution)/shard_map/cond/branch_2_fun/while/body/ppermute | solution.py:691
  496.3 33.1 %collective-permute-start.64 = (bf16[2,80,64,128]{3,2,1,0:T(8,128)(2,1)}, bf16[2,80,64,128]{3,2,1,0:T(8,128)(2,1)S(1)}, u32[]{:S(2)}, u32[]{:S(2)}) collective-permute-start(bf16[2,80,64,128]{3,2,1,0:T(8,128)(2,1)} %get-tuple-element.2963), channel_id=1, source_target_pairs={{0,1},{1,0},{2,3},{3,2},{4,5},{5,4},{6,7},{7,6}} | collective-permute-start | bytes 7864328 | tf_op jit(solution)/shard_map/cond/branch_2_fun/while/body/ppermute | solution.py:690
  497.6 31.0 %collective-permute-start.66 = (bf16[80,64,128]{2,1,0:T(8,128)(2,1)}, bf16[80,64,128]{2,1,0:T(8,128)(2,1)}, u32[]{:S(2)}, u32[]{:S(2)}) collective-permute-start(bf16[80,64,128]{2,1,0:T(8,128)(2,1)} %get-tuple-element.3395), channel_id=1, source_target_pairs={{2,0},{3,1},{6,2},{7,3},{4,6},{5,7},{0,4},{1,5}} | collective-permute-start | bytes 3932168 | tf_op jit(solution)/shard_map/cond/branch_2_fun/while/body/ppermute | solution.py:681
  498.2 31.2 %collective-permute-start.65 = (bf16[80,64,128]{2,1,0:T(8,128)(2,1)}, bf16[80,64,128]{2,1,0:T(8,128)(2,1)}, u32[]{:S(2)}, u32[]{:S(2)}) collective-permute-start(bf16[80,64,128]{2,1,0:T(8,128)(2,1)} %get-tuple-element.3394), channel_id=1, source_target_pairs={{0,2},{1,3},{2,6},{3,7},{6,4},{7,5},{4,0},{5,1}} | collective-permute-start | bytes 3932168 | tf_op jit(solution)/shard_map/cond/branch_2_fun/while/body/ppermute | solution.py:680
  541.5 32.0 %collective-permute-start.70 = (bf16[2,80,64,128]{3,2,1,0:T(8,128)(2,1)}, bf16[2,80,64,128]{3,2,1,0:T(8,128)(2,1)S(1)}, u32[]{:S(2)}, u32[]{:S(2)}) collective-permute-start(bf16[2,80,64,128]{3,2,1,0:T(8,128)(2,1)} %get-tuple-element.2980), channel_id=1, source_target_pairs={{0,1},{1,0},{2,3},{3,2},{4,5},{5,4},{6,7},{7,6}} | collective-permute-start | bytes 7864328 | tf_op jit(solution)/shard_map/cond/branch_2_fun/while/body/ppermute | solution.py:690
  542.1 31.5 %collective-permute-start.71 = (bf16[80,64,128]{2,1,0:T(8,128)(2,1)}, bf16[80,64,128]{2,1,0:T(8,128)(2,1)}, u32[]{:S(2)}, u32[]{:S(2)}) collective-permute-start(bf16[80,64,128]{2,1,0:T(8,128)(2,1)} %get-tuple-element.2981), channel_id=1, source_target_pairs={{0,2},{1,3},{2,6},{3,7},{6,4},{7,5},{4,0},{5,1}} | collective-permute-start | bytes 3932168 | tf_op jit(solution)/shard_map/cond/branch_2_fun/while/body/ppermute | solution.py:680
  542.4 31.2 %collective-permute-start.72 = (bf16[80,64,128]{2,1,0:T(8,128)(2,1)}, bf16[80,64,128]{2,1,0:T(8,128)(2,1)}, u32[]{:S(2)}, u32[]{:S(2)}) collective-permute-start(bf16[80,64,128]{2,1,0:T(8,128)(2,1)} %get-tuple-element.2982), channel_id=1, source_target_pairs={{2,0},{3,1},{6,2},{7,3},{4,6},{5,7},{0,4},{1,5}} | collective-permute-start | bytes 3932168 | tf_op jit(solution)/shard_map/cond/branch_2_fun/while/body/ppermute | solution.py:681
  548.7 24.9 %collective-permute-start.75 = (bf16[2,32,64,128]{3,2,1,0:T(8,128)(2,1)}, bf16[2,32,64,128]{3,2,1,0:T(8,128)(2,1)}, u32[]{:S(2)}, u32[]{:S(2)}) collective-permute-start(bf16[2,32,64,128]{3,2,1,0:T(8,128)(2,1)} %get-tuple-element.2983), channel_id=1, source_target_pairs={{0,1},{1,0},{2,3},{3,2},{4,5},{5,4},{6,7},{7,6}} | collective-permute-start | bytes 3145736 | tf_op jit(solution)/shard_map/cond/branch_2_fun/while/body/ppermute | solution.py:691
  583.8 33.1 %collective-permute-start.64 = (bf16[2,80,64,128]{3,2,1,0:T(8,128)(2,1)}, bf16[2,80,64,128]{3,2,1,0:T(8,128)(2,1)S(1)}, u32[]{:S(2)}, u32[]{:S(2)}) collective-permute-start(bf16[2,80,64,128]{3,2,1,0:T(8,128)(2,1)} %get-tuple-element.2963), channel_id=1, source_target_pairs={{0,1},{1,0},{2,3},{3,2},{4,5},{5,4},{6,7},{7,6}} | collective-permute-start | bytes 7864328 | tf_op jit(solution)/shard_map/cond/branch_2_fun/while/body/ppermute | solution.py:690
  584.3 14.3 %collective-permute-start.67 = (bf16[80,64,128]{2,1,0:T(8,128)(2,1)}, bf16[80,64,128]{2,1,0:T(8,128)(2,1)}, u32[]{:S(2)}, u32[]{:S(2)}) collective-permute-start(bf16[80,64,128]{2,1,0:T(8,128)(2,1)} %get-tuple-element.3397.rc0), channel_id=1, source_target_pairs={{0,1},{1,0},{2,3},{3,2},{4,5},{5,4},{6,7},{7,6}} | collective-permute-start | bytes 3932168 | tf_op jit(solution)/shard_map/cond/branch_2_fun/while/body/ppermute | solution.py:682
  584.3 31.5 %collective-permute-start.66 = (bf16[80,64,128]{2,1,0:T(8,128)(2,1)}, bf16[80,64,128]{2,1,0:T(8,128)(2,1)}, u32[]{:S(2)}, u32[]{:S(2)}) collective-permute-start(bf16[80,64,128]{2,1,0:T(8,128)(2,1)} %get-tuple-element.3395), channel_id=1, source_target_pairs={{2,0},{3,1},{6,2},{7,3},{4,6},{5,7},{0,4},{1,5}} | collective-permute-start | bytes 3932168 | tf_op jit(solution)/shard_map/cond/branch_2_fun/while/body/ppermute | solution.py:681
  586.1 30.8 %collective-permute-start.65 = (bf16[80,64,128]{2,1,0:T(8,128)(2,1)}, bf16[80,64,128]{2,1,0:T(8,128)(2,1)}, u32[]{:S(2)}, u32[]{:S(2)}) collective-permute-start(bf16[80,64,128]{2,1,0:T(8,128)(2,1)} %get-tuple-element.3394), channel_id=1, source_target_pairs={{0,2},{1,3},{2,6},{3,7},{6,4},{7,5},{4,0},{5,1}} | collective-permute-start | bytes 3932168 | tf_op jit(solution)/shard_map/cond/branch_2_fun/while/body/ppermute | solution.py:680
  628.8 32.0 %collective-permute-start.70 = (bf16[2,80,64,128]{3,2,1,0:T(8,128)(2,1)}, bf16[2,80,64,128]{3,2,1,0:T(8,128)(2,1)S(1)}, u32[]{:S(2)}, u32[]{:S(2)}) collective-permute-start(bf16[2,80,64,128]{3,2,1,0:T(8,128)(2,1)} %get-tuple-element.2980), channel_id=1, source_target_pairs={{0,1},{1,0},{2,3},{3,2},{4,5},{5,4},{6,7},{7,6}} | collective-permute-start | bytes 7864328 | tf_op jit(solution)/shard_map/cond/branch_2_fun/while/body/ppermute | solution.py:690
  629.3 31.5 %collective-permute-start.71 = (bf16[80,64,128]{2,1,0:T(8,128)(2,1)}, bf16[80,64,128]{2,1,0:T(8,128)(2,1)}, u32[]{:S(2)}, u32[]{:S(2)}) collective-permute-start(bf16[80,64,128]{2,1,0:T(8,128)(2,1)} %get-tuple-element.2981), channel_id=1, source_target_pairs={{0,2},{1,3},{2,6},{3,7},{6,4},{7,5},{4,0},{5,1}} | collective-permute-start | bytes 3932168 | tf_op jit(solution)/shard_map/cond/branch_2_fun/while/body/ppermute | solution.py:680
  629.7 31.1 %collective-permute-start.72 = (bf16[80,64,128]{2,1,0:T(8,128)(2,1)}, bf16[80,64,128]{2,1,0:T(8,128)(2,1)}, u32[]{:S(2)}, u32[]{:S(2)}) collective-permute-start(bf16[80,64,128]{2,1,0:T(8,128)(2,1)} %get-tuple-element.2982), channel_id=1, source_target_pairs={{2,0},{3,1},{6,2},{7,3},{4,6},{5,7},{0,4},{1,5}} | collective-permute-start | bytes 3932168 | tf_op jit(solution)/shard_map/cond/branch_2_fun/while/body/ppermute | solution.py:681
  635.9 24.9 %collective-permute-start.75 = (bf16[2,32,64,128]{3,2,1,0:T(8,128)(2,1)}, bf16[2,32,64,128]{3,2,1,0:T(8,128)(2,1)}, u32[]{:S(2)}, u32[]{:S(2)}) collective-permute-start(bf16[2,32,64,128]{3,2,1,0:T(8,128)(2,1)} %get-tuple-element.2983), channel_id=1, source_target_pairs={{0,1},{1,0},{2,3},{3,2},{4,5},{5,4},{6,7},{7,6}} | collective-permute-start | bytes 3145736 | tf_op jit(solution)/shard_map/cond/branch_2_fun/while/body/ppermute | solution.py:691
  670.7 33.7 %collective-permute-start.64 = (bf16[2,80,64,128]{3,2,1,0:T(8,128)(2,1)}, bf16[2,80,64,128]{3,2,1,0:T(8,128)(2,1)S(1)}, u32[]{:S(2)}, u32[]{:S(2)}) collective-permute-start(bf16[2,80,64,128]{3,2,1,0:T(8,128)(2,1)} %get-tuple-element.2963), channel_id=1, source_target_pairs={{0,1},{1,0},{2,3},{3,2},{4,5},{5,4},{6,7},{7,6}} | collective-permute-start | bytes 7864328 | tf_op jit(solution)/shard_map/cond/branch_2_fun/while/body/ppermute | solution.py:690
  671.3 31.5 %collective-permute-start.66 = (bf16[80,64,128]{2,1,0:T(8,128)(2,1)}, bf16[80,64,128]{2,1,0:T(8,128)(2,1)}, u32[]{:S(2)}, u32[]{:S(2)}) collective-permute-start(bf16[80,64,128]{2,1,0:T(8,128)(2,1)} %get-tuple-element.3395), channel_id=1, source_target_pairs={{2,0},{3,1},{6,2},{7,3},{4,6},{5,7},{0,4},{1,5}} | collective-permute-start | bytes 3932168 | tf_op jit(solution)/shard_map/cond/branch_2_fun/while/body/ppermute | solution.py:681
  673.2 31.2 %collective-permute-start.65 = (bf16[80,64,128]{2,1,0:T(8,128)(2,1)}, bf16[80,64,128]{2,1,0:T(8,128)(2,1)}, u32[]{:S(2)}, u32[]{:S(2)}) collective-permute-start(bf16[80,64,128]{2,1,0:T(8,128)(2,1)} %get-tuple-element.3394), channel_id=1, source_target_pairs={{0,2},{1,3},{2,6},{3,7},{6,4},{7,5},{4,0},{5,1}} | collective-permute-start | bytes 3932168 | tf_op jit(solution)/shard_map/cond/branch_2_fun/while/body/ppermute | solution.py:680
  716.5 32.0 %collective-permute-start.70 = (bf16[2,80,64,128]{3,2,1,0:T(8,128)(2,1)}, bf16[2,80,64,128]{3,2,1,0:T(8,128)(2,1)S(1)}, u32[]{:S(2)}, u32[]{:S(2)}) collective-permute-start(bf16[2,80,64,128]{3,2,1,0:T(8,128)(2,1)} %get-tuple-element.2980), channel_id=1, source_target_pairs={{0,1},{1,0},{2,3},{3,2},{4,5},{5,4},{6,7},{7,6}} | collective-permute-start | bytes 7864328 | tf_op jit(solution)/shard_map/cond/branch_2_fun/while/body/ppermute | solution.py:690
  717.1 31.5 %collective-permute-start.71 = (bf16[80,64,128]{2,1,0:T(8,128)(2,1)}, bf16[80,64,128]{2,1,0:T(8,128)(2,1)}, u32[]{:S(2)}, u32[]{:S(2)}) collective-permute-start(bf16[80,64,128]{2,1,0:T(8,128)(2,1)} %get-tuple-element.2981), channel_id=1, source_target_pairs={{0,2},{1,3},{2,6},{3,7},{6,4},{7,5},{4,0},{5,1}} | collective-permute-start | bytes 3932168 | tf_op jit(solution)/shard_map/cond/branch_2_fun/while/body/ppermute | solution.py:680
  717.1 31.5 %collective-permute-start.72 = (bf16[80,64,128]{2,1,0:T(8,128)(2,1)}, bf16[80,64,128]{2,1,0:T(8,128)(2,1)}, u32[]{:S(2)}, u32[]{:S(2)}) collective-permute-start(bf16[80,64,128]{2,1,0:T(8,128)(2,1)} %get-tuple-element.2982), channel_id=1, source_target_pairs={{2,0},{3,1},{6,2},{7,3},{4,6},{5,7},{0,4},{1,5}} | collective-permute-start | bytes 3932168 | tf_op jit(solution)/shard_map/cond/branch_2_fun/while/body/ppermute | solution.py:681
  723.7 24.9 %collective-permute-start.75 = (bf16[2,32,64,128]{3,2,1,0:T(8,128)(2,1)}, bf16[2,32,64,128]{3,2,1,0:T(8,128)(2,1)}, u32[]{:S(2)}, u32[]{:S(2)}) collective-permute-start(bf16[2,32,64,128]{3,2,1,0:T(8,128)(2,1)} %get-tuple-element.2983), channel_id=1, source_target_pairs={{0,1},{1,0},{2,3},{3,2},{4,5},{5,4},{6,7},{7,6}} | collective-permute-start | bytes 3145736 | tf_op jit(solution)/shard_map/cond/branch_2_fun/while/body/ppermute | solution.py:691
  758.7 32.7 %collective-permute-start.64 = (bf16[2,80,64,128]{3,2,1,0:T(8,128)(2,1)}, bf16[2,80,64,128]{3,2,1,0:T(8,128)(2,1)S(1)}, u32[]{:S(2)}, u32[]{:S(2)}) collective-permute-start(bf16[2,80,64,128]{3,2,1,0:T(8,128)(2,1)} %get-tuple-element.2963), channel_id=1, source_target_pairs={{0,1},{1,0},{2,3},{3,2},{4,5},{5,4},{6,7},{7,6}} | collective-permute-start | bytes 7864328 | tf_op jit(solution)/shard_map/cond/branch_2_fun/while/body/ppermute | solution.py:690
  759.2 31.5 %collective-permute-start.66 = (bf16[80,64,128]{2,1,0:T(8,128)(2,1)}, bf16[80,64,128]{2,1,0:T(8,128)(2,1)}, u32[]{:S(2)}, u32[]{:S(2)}) collective-permute-start(bf16[80,64,128]{2,1,0:T(8,128)(2,1)} %get-tuple-element.3395), channel_id=1, source_target_pairs={{2,0},{3,1},{6,2},{7,3},{4,6},{5,7},{0,4},{1,5}} | collective-permute-start | bytes 3932168 | tf_op jit(solution)/shard_map/cond/branch_2_fun/while/body/ppermute | solution.py:681
  760.2 31.2 %collective-permute-start.65 = (bf16[80,64,128]{2,1,0:T(8,128)(2,1)}, bf16[80,64,128]{2,1,0:T(8,128)(2,1)}, u32[]{:S(2)}, u32[]{:S(2)}) collective-permute-start(bf16[80,64,128]{2,1,0:T(8,128)(2,1)} %get-tuple-element.3394), channel_id=1, source_target_pairs={{0,2},{1,3},{2,6},{3,7},{6,4},{7,5},{4,0},{5,1}} | collective-permute-start | bytes 3932168 | tf_op jit(solution)/shard_map/cond/branch_2_fun/while/body/ppermute | solution.py:680
  802.1 32.5 %collective-permute-start.70 = (bf16[2,80,64,128]{3,2,1,0:T(8,128)(2,1)}, bf16[2,80,64,128]{3,2,1,0:T(8,128)(2,1)S(1)}, u32[]{:S(2)}, u32[]{:S(2)}) collective-permute-start(bf16[2,80,64,128]{3,2,1,0:T(8,128)(2,1)} %get-tuple-element.2980), channel_id=1, source_target_pairs={{0,1},{1,0},{2,3},{3,2},{4,5},{5,4},{6,7},{7,6}} | collective-permute-start | bytes 7864328 | tf_op jit(solution)/shard_map/cond/branch_2_fun/while/body/ppermute | solution.py:690
  802.7 31.5 %collective-permute-start.71 = (bf16[80,64,128]{2,1,0:T(8,128)(2,1)}, bf16[80,64,128]{2,1,0:T(8,128)(2,1)}, u32[]{:S(2)}, u32[]{:S(2)}) collective-permute-start(bf16[80,64,128]{2,1,0:T(8,128)(2,1)} %get-tuple-element.2981), channel_id=1, source_target_pairs={{0,2},{1,3},{2,6},{3,7},{6,4},{7,5},{4,0},{5,1}} | collective-permute-start | bytes 3932168 | tf_op jit(solution)/shard_map/cond/branch_2_fun/while/body/ppermute | solution.py:680
  803.4 31.2 %collective-permute-start.72 = (bf16[80,64,128]{2,1,0:T(8,128)(2,1)}, bf16[80,64,128]{2,1,0:T(8,128)(2,1)}, u32[]{:S(2)}, u32[]{:S(2)}) collective-permute-start(bf16[80,64,128]{2,1,0:T(8,128)(2,1)} %get-tuple-element.2982), channel_id=1, source_target_pairs={{2,0},{3,1},{6,2},{7,3},{4,6},{5,7},{0,4},{1,5}} | collective-permute-start | bytes 3932168 | tf_op jit(solution)/shard_map/cond/branch_2_fun/while/body/ppermute | solution.py:681
  809.3 25.3 %collective-permute-start.75 = (bf16[2,32,64,128]{3,2,1,0:T(8,128)(2,1)}, bf16[2,32,64,128]{3,2,1,0:T(8,128)(2,1)}, u32[]{:S(2)}, u32[]{:S(2)}) collective-permute-start(bf16[2,32,64,128]{3,2,1,0:T(8,128)(2,1)} %get-tuple-element.2983), channel_id=1, source_target_pairs={{0,1},{1,0},{2,3},{3,2},{4,5},{5,4},{6,7},{7,6}} | collective-permute-start | bytes 3145736 | tf_op jit(solution)/shard_map/cond/branch_2_fun/while/body/ppermute | solution.py:691
  (62 other events, 421.6 us)
